TPU v7x, 32 devices: a whole 2x2x4 slice. The times are simulated.
32 devices in a mesh: dp: 4 (over z), seq: 4 (over y, x), tensor: 2 (over core).
Axes of the slice: x: 2, y: 2, z: 4, core: 2. Of those that a mesh axis runs over, the one named last changes fastest.
Arguments:
- block_input: float32 [8, 1024, 768], P(('dp', 'tensor'), 'seq'), may hold values from -6 to 6
- segments: int32 [8, 1024], P(('dp', 'tensor')), may hold values from 0 to 7, never falling along the last dimension, each value on 1 to 512 neighbouring positions
- routes: int32 [2, 8, 1024, 2], P(None, 'dp', 'seq'), may hold values from 0 to 3, all different within a row
- distance_bucket: int32 [1024], replicated, may hold values from 0 to 31
- first_gain: bfloat16 [2, 768], P(None, 'dp'), may hold values from 0.5 to 1.5
- query_key_value: bfloat16 [2, 768, 2304], P(None, 'dp'), may hold values from -0.21875 to 0.21875
- attention_out: bfloat16 [2, 768, 768], P(None, 'dp'), may hold values from -0.875 to 0.875
- bias_table: bfloat16 [2, 32, 12], P(None, 'dp'), may hold values from -4 to 4
- second_gain: bfloat16 [2, 768], P(None, 'dp'), may hold values from 0.5 to 1.5
- router_weights: bfloat16 [2, 768, 4], P(None, 'dp'), may hold values from -0.4375 to 0.4375
- expert_up: bfloat16 [2, 4, 768, 3072], P(None, None, 'dp', 'tensor'), may hold values from -0.21875 to 0.21875
- expert_down: bfloat16 [2, 4, 3072, 768], P(None, None, 'tensor', 'dp'), may hold values from -0.109375 to 0.109375
- cotangent: float32 [8, 1024, 768], P(('dp', 'tensor'), 'seq'), may hold values from -6 to 6
Outputs:
- block_output: float32 [8, 1024, 768], P(('dp', 'tensor'), 'seq')
- input_grad: float32 [8, 1024, 768], P(('dp', 'tensor'), 'seq')
- first_gain_grad: float32 [2, 768], P(None, 'dp')
- query_key_value_grad: float32 [2, 768, 2304], P(None, 'dp')
- attention_out_grad: float32 [2, 768, 768], P(None, 'dp')
- bias_table_grad: float32 [2, 32, 12], P(None, 'dp')
- second_gain_grad: float32 [2, 768], P(None, 'dp')
- router_weights_grad: float32 [2, 768, 4], P(None, 'dp')
- expert_up_grad: float32 [2, 4, 768, 3072], P(None, None, 'dp', 'tensor')
- expert_down_grad: float32 [2, 4, 3072, 768], P(None, None, 'tensor', 'dp')
Inputs may be any that keep to these rules, and one draw needn't show every extreme that they name: `segments`: within each sequence the numbers never fall; every document holds 1 to 512 positions, one exactly 512. `routes`: each token names 2 different experts.
All inputs are finite; a program needn't handle non-finite values.
Results may differ from a plain program's by a relative error of at most 0.025.
Values may be sent and summed in bfloat16 or wider, within the bound.
A program may use at most 256 MiB of HBM per device.

v0:
```python
import jax
import jax.numpy as jnp
from jax import lax
from jax.sharding import PartitionSpec as P

HEADS = 12
HD = 64
LAYERS = 2


epsilon = 1e-06
negative = -1e30
highest_precision = lax.Precision.HIGHEST


def scaled(values, gain_vec):
    return (
        values * lax.rsqrt(jnp.mean(values * values, axis=-1, keepdims=True) + epsilon) * gain_vec
    )


def gelu_tanh(values):
    return jax.nn.gelu(values, approximate=True)


def gate_shares(score_logits, picked):
    probs = jax.nn.softmax(score_logits, axis=-1)
    chosen = jnp.sum(probs[..., None, :] * picked, axis=-1)
    return chosen / jnp.sum(chosen, axis=-1, keepdims=True)


def band_bias(padded, row_start, block_rows, length):
    head_count = padded.shape[0]
    band_width = length + block_rows - 1
    band_line = lax.dynamic_slice_in_dim(padded, row_start + 1, band_width, 1)
    spread = jnp.broadcast_to(band_line[:, None, :], (head_count, block_rows, band_width))
    spread = jnp.pad(spread.reshape(head_count, block_rows * band_width), ((0, 0), (0, block_rows)))
    return spread.reshape(head_count, block_rows, length + block_rows)[:, :, :length][:, :, ::-1]


def band_sums(weights, block_rows, length):
    head_count = weights.shape[0]
    flipped = jnp.pad(weights[:, :, ::-1], ((0, 0), (0, 0), (0, block_rows)))
    flat_view = flipped.reshape(head_count, block_rows * (length + block_rows))
    flat_view = flat_view[:, : block_rows * (length + block_rows - 1)]
    return jnp.sum(flat_view.reshape(head_count, block_rows, length + block_rows - 1), axis=1)


def block_logits(query_block, key_seq, seg_rows, seg_seq, row_start, padded):
    block_rows = query_block.shape[0]
    length = key_seq.shape[0]
    score_logits = (
        jnp.einsum("qhd,khd->hqk", query_block, key_seq, preferred_element_type=jnp.float32) * 0.125
    )
    score_logits = score_logits + band_bias(padded, row_start, block_rows, length)
    row_index = row_start + lax.iota(jnp.int32, block_rows)
    col_index = lax.iota(jnp.int32, length)
    allowed = (seg_rows[:, None] == seg_seq[None, :]) & (col_index[None, :] <= row_index[:, None])
    return jnp.where(allowed[None], score_logits, negative)


def attend(queries, keys_all, values_all, segments, padded, block_rows):
    length = queries.shape[1]
    steps_count = length // block_rows

    def one_sequence(inputs):
        query_seq, key_seq, value_seq, seg_seq = inputs

        def one_block(carry, row_start):
            query_block = lax.dynamic_slice_in_dim(query_seq, row_start, block_rows, 0)
            seg_rows = lax.dynamic_slice_in_dim(seg_seq, row_start, block_rows, 0)
            score_logits = block_logits(query_block, key_seq, seg_rows, seg_seq, row_start, padded)
            largest = jnp.max(score_logits, axis=-1, keepdims=True)
            log_total = largest + jnp.log(
                jnp.sum(jnp.exp(score_logits - largest), axis=-1, keepdims=True)
            )
            weights = jnp.exp(score_logits - log_total).astype(jnp.bfloat16)
            mixed = jnp.einsum(
                "hqk,khd->qhd", weights, value_seq, preferred_element_type=jnp.float32
            )
            return (carry, (mixed.astype(jnp.bfloat16), log_total[:, :, 0]))

        _, (mixed, log_total) = lax.scan(
            one_block, jnp.zeros((), jnp.int32), lax.iota(jnp.int32, steps_count) * block_rows
        )
        return (mixed.reshape((length,) + mixed.shape[2:]), log_total)

    return lax.map(one_sequence, (queries, keys_all, values_all, segments))


def attend_back(queries, keys_all, values_all, segments, log_totals, grad_out, padded, block_rows):
    length = queries.shape[1]
    head_count = queries.shape[2]
    head_size = queries.shape[3]
    steps_count = length // block_rows

    def one_sequence(inputs):
        query_seq, key_seq, value_seq, seg_seq, log_seq, grad_seq = inputs

        def one_block(carry, block_index):
            grad_keys, grad_values, band_total = carry
            row_start = block_index * block_rows
            query_block = lax.dynamic_slice_in_dim(query_seq, row_start, block_rows, 0)
            seg_rows = lax.dynamic_slice_in_dim(seg_seq, row_start, block_rows, 0)
            grad_block = lax.dynamic_slice_in_dim(grad_seq, row_start, block_rows, 0)
            score_logits = block_logits(query_block, key_seq, seg_rows, seg_seq, row_start, padded)
            weights = jnp.exp(score_logits - log_seq[block_index][:, :, None])
            weights_low = weights.astype(jnp.bfloat16)
            grad_weights = jnp.einsum(
                "qhd,khd->hqk", grad_block, value_seq, preferred_element_type=jnp.float32
            )
            grad_values = grad_values + jnp.einsum(
                "hqk,qhd->khd", weights_low, grad_block, preferred_element_type=jnp.float32
            )
            inner_sum = jnp.sum(weights * grad_weights, axis=-1, keepdims=True)
            grad_logits = (weights * (grad_weights - inner_sum)).astype(jnp.bfloat16)
            grad_query = jnp.einsum(
                "hqk,khd->qhd", grad_logits, key_seq, preferred_element_type=jnp.float32
            )
            grad_query = (grad_query * 0.125).astype(jnp.bfloat16)
            grad_keys = (
                grad_keys
                + jnp.einsum(
                    "hqk,qhd->khd", grad_logits, query_block, preferred_element_type=jnp.float32
                )
                * 0.125
            )
            diagonal = band_sums(grad_logits.astype(jnp.float32), block_rows, length)
            previous = lax.dynamic_slice_in_dim(band_total, row_start + 1, diagonal.shape[1], 1)
            band_total = lax.dynamic_update_slice_in_dim(
                band_total, previous + diagonal, row_start + 1, 1
            )
            return ((grad_keys, grad_values, band_total), grad_query)

        start_state = (
            jnp.zeros((length, head_count, head_size), jnp.float32),
            jnp.zeros((length, head_count, head_size), jnp.float32),
            jnp.zeros((head_count, 2 * length + block_rows), jnp.float32),
        )
        (grad_keys, grad_values, band_total), grad_query = lax.scan(
            one_block, start_state, lax.iota(jnp.int32, steps_count)
        )
        return (
            grad_query.reshape(length, head_count, head_size),
            grad_keys.astype(jnp.bfloat16),
            grad_values.astype(jnp.bfloat16),
            band_total[:, length : 2 * length],
        )

    return lax.map(one_sequence, (queries, keys_all, values_all, segments, log_totals, grad_out))


def route_maps(picks, experts, capacity):
    flat_picks = picks.reshape(-1)
    pair_total = flat_picks.shape[0]
    onehot = (flat_picks[:, None] == lax.iota(jnp.int32, experts)[None, :]).astype(jnp.int32)
    places = jnp.sum((jnp.cumsum(onehot, axis=0) - 1) * onehot, axis=1)
    target = jnp.where(places < capacity, flat_picks * capacity + places, experts * capacity)
    source = jnp.full((experts * capacity + 1,), pair_total, jnp.int32)
    source = source.at[target].set(lax.iota(jnp.int32, pair_total))
    return (target, source[: experts * capacity])


def to_heads(values):
    return lax.all_to_all(values, "seq", split_axis=3, concat_axis=1, tiled=True)


def to_tokens(values):
    return lax.all_to_all(values, "seq", split_axis=1, concat_axis=3, tiled=True)


def tensor_whole(values):
    return lax.all_gather(values, "tensor", axis=0, tiled=True)


def tensor_parts(values):
    return lax.psum_scatter(
        values.astype(jnp.bfloat16), "tensor", scatter_dimension=0, tiled=True
    ).astype(jnp.float32)


def fetch(
    first_gain,
    query_key_value,
    attention_out,
    bias_table,
    second_gain,
    router_weights,
    expert_up,
    expert_down,
    decoder_layer,
):
    return (
        lax.all_gather(first_gain[decoder_layer], "dp", axis=0, tiled=True),
        lax.all_gather(query_key_value[decoder_layer], "dp", axis=0, tiled=True),
        lax.all_gather(attention_out[decoder_layer], "dp", axis=0, tiled=True),
        lax.all_gather(bias_table[decoder_layer], "dp", axis=0, tiled=True),
        lax.all_gather(second_gain[decoder_layer], "dp", axis=0, tiled=True),
        lax.all_gather(router_weights[decoder_layer], "dp", axis=0, tiled=True),
        lax.all_gather(expert_up[decoder_layer], "dp", axis=1, tiled=True),
        lax.all_gather(expert_down[decoder_layer], "dp", axis=2, tiled=True),
    )


def reduce_grads(grads):
    gain_one, grad_qkv, grad_proj, grad_table, gain_two, grad_router, grad_up, grad_down = grads
    shards = (
        lax.psum_scatter(
            gain_one.astype(jnp.bfloat16), "dp", scatter_dimension=0, tiled=True
        ).astype(jnp.float32),
        lax.psum_scatter(
            grad_qkv.astype(jnp.bfloat16), "dp", scatter_dimension=0, tiled=True
        ).astype(jnp.float32),
        lax.psum_scatter(
            grad_proj.astype(jnp.bfloat16), "dp", scatter_dimension=0, tiled=True
        ).astype(jnp.float32),
        lax.psum_scatter(
            grad_table.astype(jnp.bfloat16), "dp", scatter_dimension=0, tiled=True
        ).astype(jnp.float32),
        lax.psum_scatter(
            gain_two.astype(jnp.bfloat16), "dp", scatter_dimension=0, tiled=True
        ).astype(jnp.float32),
        lax.psum_scatter(
            grad_router.astype(jnp.bfloat16), "dp", scatter_dimension=0, tiled=True
        ).astype(jnp.float32),
    )
    totals = (
        lax.psum(shards[0].astype(jnp.bfloat16), ("seq", "tensor")).astype(jnp.float32),
        lax.psum(shards[1].astype(jnp.bfloat16), ("seq", "tensor")).astype(jnp.float32),
        lax.psum(shards[2].astype(jnp.bfloat16), ("seq", "tensor")).astype(jnp.float32),
        lax.psum(shards[3].astype(jnp.bfloat16), ("seq", "tensor")).astype(jnp.float32),
        lax.psum(shards[4].astype(jnp.bfloat16), ("seq", "tensor")).astype(jnp.float32),
        lax.psum(shards[5].astype(jnp.bfloat16), ("seq", "tensor")).astype(jnp.float32),
    )
    expert_pieces = (
        lax.psum_scatter(
            grad_up.astype(jnp.bfloat16), "dp", scatter_dimension=1, tiled=True
        ).astype(jnp.float32),
        lax.psum_scatter(
            grad_down.astype(jnp.bfloat16), "dp", scatter_dimension=2, tiled=True
        ).astype(jnp.float32),
    )
    expert_totals = (
        lax.psum(expert_pieces[0].astype(jnp.bfloat16), "seq").astype(jnp.float32),
        lax.psum(expert_pieces[1].astype(jnp.bfloat16), "seq").astype(jnp.float32),
    )
    return tuple(totals) + tuple(expert_totals)


def body(
    block_input,
    segments,
    routes,
    distance_bucket,
    first_gain,
    query_key_value,
    attention_out,
    bias_table,
    second_gain,
    router_weights,
    expert_up,
    expert_down,
    cotangent,
):
    seq_count, piece, width = block_input.shape
    split_count = lax.axis_size("seq")
    length = piece * split_count
    local_heads = HEADS // split_count
    head_width = local_heads * HD
    block_rows = min(512, length)
    experts = expert_up.shape[1]
    top_count = routes.shape[-1]
    group_seqs = routes.shape[1]
    group_rows = group_seqs * piece
    capacity = group_rows * top_count // experts
    bucket_count = bias_table.shape[1] * lax.axis_size("dp")
    head_start = lax.axis_index("seq") * local_heads
    own_start = lax.axis_index("tensor") * seq_count
    bucket_hot = (distance_bucket[:, None] == lax.iota(jnp.int32, bucket_count)[None, :]).astype(
        jnp.float32
    )

    def layer_weights_of(decoder_layer):
        return fetch(
            first_gain,
            query_key_value,
            attention_out,
            bias_table,
            second_gain,
            router_weights,
            expert_up,
            expert_down,
            decoder_layer,
        )

    def layer_backward(grad_in, saved, weights):
        (
            gain_one,
            query_key_value_weight,
            output_projection,
            table,
            gain_two,
            router_weight,
            up_proj,
            down_proj,
        ) = weights
        (
            layer_in,
            normalized_input,
            queries,
            keys_all,
            values_all,
            padded,
            log_totals,
            merged,
            middle_state,
            normalized_second,
            score_logits,
            picked,
            shares,
            target,
            source,
            slots,
            hidden_pre,
            hidden,
            per_pair,
        ) = saved
        share_grad = jnp.sum(grad_in[:, :, None, :] * per_pair, axis=-1)
        result_grad = (shares[..., None] * grad_in[:, :, None, :]).astype(jnp.bfloat16)
        pair_grads = tensor_whole(result_grad).reshape(group_rows * top_count, width)
        pair_grads = jnp.concatenate([pair_grads, jnp.zeros((1, width), jnp.bfloat16)], axis=0)
        slot_result_grad = pair_grads[source].reshape(experts, capacity, width)
        hidden_grad = jnp.einsum(
            "ecd,efd->ecf", slot_result_grad, down_proj, preferred_element_type=jnp.float32
        )
        down_grad = jnp.einsum(
            "ecf,ecd->efd", hidden, slot_result_grad, preferred_element_type=jnp.float32
        )
        _, gelu_pull = jax.vjp(gelu_tanh, hidden_pre)
        pre_grad = gelu_pull(hidden_grad)[0].astype(jnp.bfloat16)
        up_grad = jnp.einsum("ecd,ecf->edf", slots, pre_grad, preferred_element_type=jnp.float32)
        slot_grad = jnp.einsum(
            "ecf,edf->ecd", pre_grad, up_proj, preferred_element_type=jnp.float32
        )
        slot_grad = jnp.concatenate(
            [slot_grad.reshape(experts * capacity, width), jnp.zeros((1, width), jnp.float32)],
            axis=0,
        )
        token_grad = jnp.sum(slot_grad[target].reshape(group_rows, top_count, width), axis=1)
        normed_two_grad = tensor_parts(token_grad.reshape(group_seqs, piece, width))
        _, gate_pull = jax.vjp(lambda values: gate_shares(values, picked), score_logits)
        logit_grad = gate_pull(share_grad)[0].astype(jnp.bfloat16)
        router_grad = jnp.einsum(
            "spd,spe->de", normalized_second, logit_grad, preferred_element_type=jnp.float32
        )
        normed_two_grad = normed_two_grad + jnp.einsum(
            "spe,de->spd", logit_grad, router_weight, preferred_element_type=jnp.float32
        )
        _, norm_pull = jax.vjp(scaled, middle_state, gain_two.astype(jnp.float32))
        middle_part, gain_two_grad = norm_pull(normed_two_grad)
        middle_grad = grad_in + middle_part
        out_grad = middle_grad.astype(jnp.bfloat16)
        proj_out_grad = jnp.einsum(
            "spd,spe->de", merged, out_grad, preferred_element_type=jnp.float32
        )
        merged_grad = jnp.einsum(
            "spe,de->spd", out_grad, output_projection, preferred_element_type=jnp.float32
        )
        merged_grad = merged_grad.astype(jnp.bfloat16).reshape(
            seq_count, piece, 1, split_count, head_width
        )
        attn_grad = to_heads(merged_grad).reshape(seq_count, length, local_heads, HD)
        query_grad, key_grad, value_grad, band_grad = attend_back(
            queries, keys_all, values_all, segments, log_totals, attn_grad, padded, block_rows
        )
        head_grads = jnp.stack([query_grad, key_grad, value_grad], axis=2)
        head_grads = head_grads.reshape(seq_count, length, 3, 1, head_width)
        qkv_grad = to_tokens(head_grads).reshape(seq_count, piece, 3 * width)
        proj_qkv_grad = jnp.einsum(
            "spd,spe->de", normalized_input, qkv_grad, preferred_element_type=jnp.float32
        )
        normed_grad = jnp.einsum(
            "spe,de->spd", qkv_grad, query_key_value_weight, preferred_element_type=jnp.float32
        )
        _, norm_pull_one = jax.vjp(scaled, layer_in, gain_one.astype(jnp.float32))
        input_part, gain_one_grad = norm_pull_one(normed_grad)
        my_bias_grad = jnp.dot(
            bucket_hot.T, jnp.sum(band_grad, axis=0).T, precision=highest_precision
        )
        table_grad = lax.dynamic_update_slice_in_dim(
            jnp.zeros((bucket_count, HEADS), jnp.float32), my_bias_grad, head_start, 1
        )
        grads = (
            gain_one_grad,
            proj_qkv_grad,
            proj_out_grad,
            table_grad,
            gain_two_grad,
            router_grad,
            up_grad,
            down_grad,
        )
        return (middle_grad + input_part, grads)

    current = block_input
    kept_weights = []
    kept_states = []
    for decoder_layer in range(LAYERS):
        weights = layer_weights_of(decoder_layer)
        (
            layer_gain_one,
            layer_query_key_value_weight,
            layer_output_projection,
            layer_table,
            layer_gain_two,
            layer_router_weight,
            layer_up_proj,
            layer_down_proj,
        ) = weights
        layer_normalized_input = scaled(current, layer_gain_one.astype(jnp.float32)).astype(
            jnp.bfloat16
        )
        projected_rows = jnp.einsum(
            "spd,de->spe",
            layer_normalized_input,
            layer_query_key_value_weight,
            preferred_element_type=jnp.float32,
        )
        projected_rows = projected_rows.astype(jnp.bfloat16).reshape(
            seq_count, piece, 3, split_count, head_width
        )
        by_heads = to_heads(projected_rows).reshape(seq_count, length, 3, local_heads, HD)
        layer_queries = by_heads[:, :, 0]
        layer_keys_all = by_heads[:, :, 1]
        layer_values_all = by_heads[:, :, 2]
        my_table = lax.dynamic_slice_in_dim(
            layer_table.astype(jnp.float32), head_start, local_heads, 1
        )
        distance_bias = jnp.dot(bucket_hot, my_table, precision=highest_precision).T
        layer_padded = jnp.concatenate(
            [
                jnp.zeros((local_heads, length), jnp.float32),
                distance_bias,
                jnp.zeros((local_heads, block_rows), jnp.float32),
            ],
            axis=1,
        )
        mixed, layer_log_totals = attend(
            layer_queries, layer_keys_all, layer_values_all, segments, layer_padded, block_rows
        )
        layer_merged = to_tokens(mixed.reshape(seq_count, length, 1, 1, head_width)).reshape(
            seq_count, piece, width
        )
        layer_middle_state = current + jnp.einsum(
            "spd,de->spe", layer_merged, layer_output_projection, preferred_element_type=jnp.float32
        )
        layer_normalized_second = scaled(
            layer_middle_state, layer_gain_two.astype(jnp.float32)
        ).astype(jnp.bfloat16)
        layer_score_logits = jnp.einsum(
            "spd,de->spe",
            layer_normalized_second,
            layer_router_weight,
            preferred_element_type=jnp.float32,
        )
        layer_routes = routes[decoder_layer]
        layer_target, layer_source = route_maps(layer_routes, experts, capacity)
        own_routes = lax.dynamic_slice_in_dim(layer_routes, own_start, seq_count, 0)
        layer_picked = (own_routes[..., None] == lax.iota(jnp.int32, experts)).astype(jnp.float32)
        layer_shares = gate_shares(layer_score_logits, layer_picked)
        whole = tensor_whole(layer_normalized_second).reshape(group_rows, width)
        whole = jnp.concatenate([whole, jnp.zeros((1, width), jnp.bfloat16)], axis=0)
        layer_slots = whole[layer_source // top_count].reshape(experts, capacity, width)
        layer_hidden_pre = jnp.einsum(
            "ecd,edf->ecf", layer_slots, layer_up_proj, preferred_element_type=jnp.float32
        )
        layer_hidden = gelu_tanh(layer_hidden_pre).astype(jnp.bfloat16)
        part_sums = jnp.einsum(
            "ecf,efd->ecd", layer_hidden, layer_down_proj, preferred_element_type=jnp.float32
        )
        part_sums = jnp.concatenate(
            [part_sums.reshape(experts * capacity, width), jnp.zeros((1, width), jnp.float32)],
            axis=0,
        )
        layer_per_pair = tensor_parts(
            part_sums[layer_target].reshape(group_seqs, piece, top_count, width)
        )
        layer_out = layer_middle_state + jnp.sum(layer_shares[..., None] * layer_per_pair, axis=2)
        layer_saved = (
            current,
            layer_normalized_input,
            layer_queries,
            layer_keys_all,
            layer_values_all,
            layer_padded,
            layer_log_totals,
            layer_merged,
            layer_middle_state,
            layer_normalized_second,
            layer_score_logits,
            layer_picked,
            layer_shares,
            layer_target,
            layer_source,
            layer_slots,
            layer_hidden_pre,
            layer_hidden,
            layer_per_pair,
        )
        current = layer_out
        saved = layer_saved
        kept_weights.append(weights)
        kept_states.append(saved)
    grad_stream = cotangent
    reduced = [None] * LAYERS
    for decoder_layer in range(LAYERS - 1, -1, -1):
        weights = layer_weights_of(decoder_layer)
        grad_stream, grads = layer_backward(grad_stream, kept_states[decoder_layer], weights)
        reduced[decoder_layer] = reduce_grads(grads)
    stacked = [
        jnp.stack([reduced[decoder_layer][member] for decoder_layer in range(LAYERS)], axis=0)
        for member in range(8)
    ]
    return (
        current,
        grad_stream,
        stacked[0],
        stacked[1],
        stacked[2],
        stacked[3],
        stacked[4],
        stacked[5],
        stacked[6],
        stacked[7],
    )


def solution(mesh):
    in_specs = (
        P(("dp", "tensor"), "seq", None),
        P(("dp", "tensor"), None),
        P(None, "dp", "seq", None),
        P(),
        P(None, "dp"),
        P(None, "dp", None),
        P(None, "dp", None),
        P(None, "dp", None),
        P(None, "dp"),
        P(None, "dp", None),
        P(None, None, "dp", "tensor"),
        P(None, None, "tensor", "dp"),
        P(("dp", "tensor"), "seq", None),
    )
    out_specs = (
        P(("dp", "tensor"), "seq", None),
        P(("dp", "tensor"), "seq", None),
        P(None, "dp"),
        P(None, "dp", None),
        P(None, "dp", None),
        P(None, "dp", None),
        P(None, "dp"),
        P(None, "dp", None),
        P(None, None, "dp", "tensor"),
        P(None, None, "tensor", "dp"),
    )
    return jax.shard_map(body, mesh=mesh, in_specs=in_specs, out_specs=out_specs, check_vma=False)
```

profile of v0, /device:TPU:0, one launch (start us, length us, event | category | flops | bytes accessed | tf_op | source)
XLA Modules:
  0.0 3244.0 jit_solution(9610421378525381593)
XLA Ops:
  111.4 254.4 %while.110 = (s32[]{:T(128)}, bf16[2,512,3,64]{1,3,2,0:T(8,128)(2,1)}, f32[2,3,512]{2,1,0:T(4,128)}, s32[2]{0:T(128)S(1)}, s32[1024]{0:T(1024)S(1)}, /*index=5*/...) while((s32[]{:T(128)}, ...), condition=%wide.region_4.5_spmd, body=%wide.region_1.4_spmd.sunk | while | flops 416906240 | bytes 142299424 | solution.py:83
  181.1 50.8 %rev.46 = f32[3,512,1024]{2,1,0:T(8,128)} reverse(f32[3,512,1024]{2,1,0:T(8,128)} %slice.258), dimensions={2} | reverse | bytes 12582912 | tf_op jit(solution)/shard_map/while/body/eval_jaxpr/while/body/eval_jaxpr/rev | solution.py:38
  301.6 50.8 %rev.46 = f32[3,512,1024]{2,1,0:T(8,128)} reverse(f32[3,512,1024]{2,1,0:T(8,128)} %slice.258), dimensions={2} | reverse | bytes 12582912 | tf_op jit(solution)/shard_map/while/body/eval_jaxpr/while/body/eval_jaxpr/rev | solution.py:38
  411.9 36.6 %all-gather.35.cloned.1.call-done = bf16[1,4,768,1536]{3,2,1,0:T(8,128)(2,1)} async-done(((bf16[1,4,192,1536]{3,2,1,0:T(8,128)(2,1)}), bf16[1,4,768,1536]{3,2,1,0:T(8,128)(2,1)}) %all-gather.35.cloned.1.call-update) | async-done | bytes 9437200 | tf_op jit(solution)/shard_map/all_gather | solution.py:200
  495.6 53.2 %all-gather.39.cloned.1.call-done = bf16[1,768,2304]{2,1,0:T(8,128)(2,1)} async-done(((bf16[1,192,2304]{2,1,0:T(8,128)(2,1)}), bf16[1,768,2304]{2,1,0:T(8,128)(2,1)}) %all-gather.39.cloned.1.call-update) | async-done | bytes 3538960 | tf_op jit(solution)/shard_map/all_gather | solution.py:195
  576.8 240.8 %while.111 = (s32[]{:T(128)}, bf16[2,512,3,64]{1,3,2,0:T(8,128)(2,1)}, f32[2,3,512]{2,1,0:T(4,128)}, s32[2]{0:T(128)S(1)}, s32[1024]{0:T(1024)S(1)}, /*index=5*/...) while((s32[]{:T(128)}, ...), condition=%wide.region_20.21_spmd, body=%wide.region_17.20_spmd.sunk | while | flops 416906240 | bytes 142299424 | solution.py:83
  633.4 50.8 %rev.47 = f32[3,512,1024]{2,1,0:T(8,128)} reverse(f32[3,512,1024]{2,1,0:T(8,128)} %slice.259), dimensions={2} | reverse | bytes 12582912 | tf_op jit(solution)/shard_map/while/body/eval_jaxpr/while/body/eval_jaxpr/rev | solution.py:38
  753.6 50.9 %rev.47 = f32[3,512,1024]{2,1,0:T(8,128)} reverse(f32[3,512,1024]{2,1,0:T(8,128)} %slice.259), dimensions={2} | reverse | bytes 12582912 | tf_op jit(solution)/shard_map/while/body/eval_jaxpr/while/body/eval_jaxpr/rev | solution.py:38
  859.6 53.9 %all-gather.43.cloned.1.call-done = bf16[1,4,768,1536]{3,2,1,0:T(8,128)(2,1)} async-done(((bf16[1,4,192,1536]{3,2,1,0:T(8,128)(2,1)}), bf16[1,4,768,1536]{3,2,1,0:T(8,128)(2,1)}) %all-gather.43.cloned.1.call-update) | async-done | bytes 9437200 | tf_op jit(solution)/shard_map/all_gather | solution.py:200
  1032.5 496.9 %while.112 = (s32[]{:T(128)}, f32[1024,3,64]{0,2,1:T(8,128)}, f32[1024,3,64]{0,2,1:T(8,128)}, f32[3,2560]{1,0:T(4,128)}, bf16[2,512,3,64]{1,3,2,0:T(8,128)(2,1)}...) while((s32[]{:T(128)}, f32[1024,3,64]{0,2,1:T(8,128)}, ...), condition=%wide.region_42.43_spmd.clone, body=%wide.region_39.42_spmd.clone.sunk | while | flops 1027470848 | bytes 332073312 | solution.py:140
  1117.4 50.8 %rev.48 = f32[3,512,1024]{2,1,0:T(8,128)} reverse(f32[3,512,1024]{2,1,0:T(8,128)} %slice.260), dimensions={2} | reverse | bytes 12582912 | tf_op jit(solution)/shard_map/while/body/eval_jaxpr/while/body/eval_jaxpr/rev | solution.py:38
  1186.8 34.4 %rev.49 = f32[3,512,1024]{2,1,0:T(8,128)} reverse(bf16[3,512,1024]{2,1,0:T(8,128)(2,1)S(1)} %multiply_convert_fusion.22), dimensions={2} | reverse | bytes 9437184 | tf_op jit(solution)/shard_map/while/body/eval_jaxpr/while/body/eval_jaxpr/rev | solution.py:43
  1225.3 19.9 copy.378
  1352.3 50.8 %rev.48 = f32[3,512,1024]{2,1,0:T(8,128)} reverse(f32[3,512,1024]{2,1,0:T(8,128)} %slice.260), dimensions={2} | reverse | bytes 12582912 | tf_op jit(solution)/shard_map/while/body/eval_jaxpr/while/body/eval_jaxpr/rev | solution.py:38
  1422.2 34.4 %rev.49 = f32[3,512,1024]{2,1,0:T(8,128)} reverse(bf16[3,512,1024]{2,1,0:T(8,128)(2,1)S(1)} %multiply_convert_fusion.22), dimensions={2} | reverse | bytes 9437184 | tf_op jit(solution)/shard_map/while/body/eval_jaxpr/while/body/eval_jaxpr/rev | solution.py:43
  1537.5 28.4 all_to_all.120
  1657.2 500.1 %while.113 = (s32[]{:T(128)}, f32[1024,3,64]{0,2,1:T(8,128)}, f32[1024,3,64]{0,2,1:T(8,128)}, f32[3,2560]{1,0:T(4,128)}, bf16[2,512,3,64]{1,3,2,0:T(8,128)(2,1)}...) while((s32[]{:T(128)}, f32[1024,3,64]{0,2,1:T(8,128)}, ...), condition=%wide.region_54.55_spmd.clone, body=%wide.region_51.54_spmd.clone.sunk | while | flops 1027470848 | bytes 332073312 | solution.py:140
  1742.7 50.8 %rev.50 = f32[3,512,1024]{2,1,0:T(8,128)} reverse(f32[3,512,1024]{2,1,0:T(8,128)} %slice.262), dimensions={2} | reverse | bytes 12582912 | tf_op jit(solution)/shard_map/while/body/eval_jaxpr/while/body/eval_jaxpr/rev | solution.py:38
  1812.2 34.4 %rev.51 = f32[3,512,1024]{2,1,0:T(8,128)} reverse(bf16[3,512,1024]{2,1,0:T(8,128)(2,1)S(1)} %multiply_convert_fusion.23), dimensions={2} | reverse | bytes 9437184 | tf_op jit(solution)/shard_map/while/body/eval_jaxpr/while/body/eval_jaxpr/rev | solution.py:43
  1850.6 19.9 copy.380
  1977.9 50.8 %rev.50 = f32[3,512,1024]{2,1,0:T(8,128)} reverse(f32[3,512,1024]{2,1,0:T(8,128)} %slice.262), dimensions={2} | reverse | bytes 12582912 | tf_op jit(solution)/shard_map/while/body/eval_jaxpr/while/body/eval_jaxpr/rev | solution.py:38
  2047.8 34.4 %rev.51 = f32[3,512,1024]{2,1,0:T(8,128)} reverse(bf16[3,512,1024]{2,1,0:T(8,128)(2,1)S(1)} %multiply_convert_fusion.23), dimensions={2} | reverse | bytes 9437184 | tf_op jit(solution)/shard_map/while/body/eval_jaxpr/while/body/eval_jaxpr/rev | solution.py:43
  2086.3 19.9 copy.380
  2164.0 29.4 all_to_all.121
  2241.2 25.7 reduce-scatter.27.cloned.1.call-done
  2266.9 164.3 %reduce-scatter.37.cloned.1.call-done = bf16[4,192,1536]{2,1,0:T(8,128)(2,1)} async-done(((bf16[4,768,1536]{2,1,0:T(8,128)(2,1)}), bf16[4,192,1536]{2,1,0:T(8,128)(2,1)}) %reduce-scatter.37.cloned.1.call-update) | async-done | bytes 2359312 | tf_op jit(solution)/shard_map/reduce_scatter | solution.py:236
  2431.2 164.4 %reduce-scatter.41.cloned.1.call-done = bf16[4,1536,192]{1,2,0:T(8,128)(2,1)} async-done(((bf16[4,1536,768]{1,2,0:T(8,128)(2,1)}), bf16[4,1536,192]{1,2,0:T(8,128)(2,1)}) %reduce-scatter.41.cloned.1.call-update) | async-done | bytes 2359312 | tf_op jit(solution)/shard_map/reduce_scatter | solution.py:239
  2595.5 165.2 %reduce-scatter.35.cloned.1.call-done = bf16[4,192,1536]{2,1,0:T(8,128)(2,1)} async-done(((bf16[4,768,1536]{2,1,0:T(8,128)(2,1)}), bf16[4,192,1536]{2,1,0:T(8,128)(2,1)}) %reduce-scatter.35.cloned.1.call-update) | async-done | bytes 2359312 | tf_op jit(solution)/shard_map/reduce_scatter | solution.py:236
  2760.7 164.5 %reduce-scatter.39.cloned.1.call-done = bf16[4,1536,192]{1,2,0:T(8,128)(2,1)} async-done(((bf16[4,1536,768]{1,2,0:T(8,128)(2,1)}), bf16[4,1536,192]{1,2,0:T(8,128)(2,1)}) %reduce-scatter.39.cloned.1.call-update) | async-done | bytes 2359312 | tf_op jit(solution)/shard_map/reduce_scatter | solution.py:239
  2926.5 22.2 reduce-scatter.45.cloned.1.call-done
  2993.1 22.6 all-reduce.24
  3040.0 186.0 %all-reduce.34.cloned.1.call-done = (bf16[1,4,192,1536]{3,2,1,0:T(8,128)(2,1)}, bf16[1,4,192,1536]{3,2,1,0:T(8,128)(2,1)}, bf16[1,4,1536,192]{2,3,1,0:T(8,128)(2,1)}, bf16[1,4,1536,192]{2,3,1,0:T(8,128)(2,1)}) async-done(((bf16[1,4,192,1536]{3,2,1,0:T(8,128)(2,1)}, bf16[1,4,192,1536]{3,2,1,0:T(8,128)(2,1)}, bf16[1,4,1536,192]{2,3,1,0:T(8,128)(2,1)}, bf16[1,4,1536,192]{2,3,1,0:T(8,128)(2,1)}), ...) | async-done | bytes 9437200 | tf_op jit(solution)/shard_map/psum | solution.py:244
  (824 shorter events, 1411.6 us)
Async XLA Ops:
  7.2 76.3 %all-gather.31.cloned.1.call-start = ((), (), s32[]{:S(2)}) async-start(), calls=%async_computation.36 | async-start | bytes 4423680 | tf_op jit(solution)/shard_map/all_gather | solution.py:195
  10.1 376.3 %all-gather.33.cloned.1.call-start = ((), (), s32[]{:S(2)}) async-start(), calls=%async_computation.37 | async-start | bytes 1474560 | tf_op jit(solution)/shard_map/all_gather | solution.py:196
  11.0 385.4 %all-gather.37.cloned.1.call-start = ((), (), s32[]{:S(2)}) async-start(), calls=%async_computation.39 | async-start | bytes 11796480 | tf_op jit(solution)/shard_map/all_gather | solution.py:201
  18.6 429.9 %all-gather.35.cloned.1.call-start = ((), (), s32[]{:S(2)}) async-start(), calls=%async_computation.38 | async-start | bytes 11796480 | tf_op jit(solution)/shard_map/all_gather | solution.py:200
  88.4 18.8 all-to-all-start
  374.6 10.1 all-to-all-start.1
  378.0 116.0 %reduce-scatter.19.cloned.1.call-start = ((), (), s32[]{:S(2)}) async-start(), calls=%async_computation.22 | async-start | bytes 2359296 | tf_op jit(solution)/shard_map/reduce_scatter | solution.py:177
  468.4 80.4 %all-gather.39.cloned.1.call-start = ((), (), s32[]{:S(2)}) async-start(), calls=%async_computation.40 | async-start | bytes 4423680 | tf_op jit(solution)/shard_map/all_gather | solution.py:195
  469.0 364.7 %all-gather.45.cloned.1.call-start = ((), (), s32[]{:S(2)}) async-start(), calls=%async_computation.43 | async-start | bytes 11796480 | tf_op jit(solution)/shard_map/all_gather | solution.py:201
  474.0 376.8 %all-gather.41.cloned.1.call-start = ((), (), s32[]{:S(2)}) async-start(), calls=%async_computation.41 | async-start | bytes 1474560 | tf_op jit(solution)/shard_map/all_gather | solution.py:196
  474.8 438.8 %all-gather.43.cloned.1.call-start = ((), (), s32[]{:S(2)}) async-start(), calls=%async_computation.42 | async-start | bytes 11796480 | tf_op jit(solution)/shard_map/all_gather | solution.py:200
  553.7 18.8 all-to-all-start.2
  825.8 23.3 all-to-all-start.3
  829.2 124.9 %reduce-scatter.21.cloned.1.call-start = ((), (), s32[]{:S(2)}) async-start(), calls=%async_computation.23 | async-start | bytes 2359296 | tf_op jit(solution)/shard_map/reduce_scatter | solution.py:177
  938.1 27.9 all-gather.27.cloned.1.call-start
  957.5 53.7 %reduce-scatter.23.cloned.1.call-start = ((), (), s32[]{:S(2)}) async-start(), calls=%async_computation.25 | async-start | bytes 1179648 | tf_op jit(solution)/shard_map/reduce_scatter | solution.py:177
  1018.7 11.0 all-to-all-start.4
  1022.6 563.7 %all-gather.29.cloned.1.call-start = ((), (), s32[]{:S(2)}) async-start(), calls=%async_computation.26 | async-start | bytes 2359296 | tf_op jit(solution)/shard_map/all_gather | solution.py:173
  1576.7 58.0 %reduce-scatter.25.cloned.1.call-start = ((), (), s32[]{:S(2)}) async-start(), calls=%async_computation.27 | async-start | bytes 1179648 | tf_op jit(solution)/shard_map/reduce_scatter | solution.py:177
  1625.2 615.9 %reduce-scatter.33.cloned.1.call-start = ((), (), s32[]{:S(2)}) async-start(), calls=%async_computation.31 | async-start | bytes 1474560 | tf_op jit(solution)/shard_map/reduce_scatter | solution.py:214
  1626.8 614.3 %reduce-scatter.31.cloned.1.call-start = ((), (), s32[]{:S(2)}) async-start(), calls=%async_computation.30 | async-start | bytes 1474560 | tf_op jit(solution)/shard_map/reduce_scatter | solution.py:214
  1643.5 11.0 all-to-all-start.6
  1647.3 593.8 %reduce-scatter.29.cloned.1.call-start = ((), (), s32[]{:S(2)}) async-start(), calls=%async_computation.29 | async-start | bytes 4423680 | tf_op jit(solution)/shard_map/reduce_scatter | solution.py:211
  1650.4 616.4 %reduce-scatter.27.cloned.1.call-start = ((), (), s32[]{:S(2)}) async-start(), calls=%async_computation.28 | async-start | bytes 4423680 | tf_op jit(solution)/shard_map/reduce_scatter | solution.py:211
  2200.6 230.6 %reduce-scatter.37.cloned.1.call-start = ((), (), s32[]{:S(2)}) async-start(), calls=%async_computation.33 | async-start | bytes 11796480 | tf_op jit(solution)/shard_map/reduce_scatter | solution.py:236
  2207.8 387.8 %reduce-scatter.41.cloned.1.call-start = ((), (), s32[]{:S(2)}) async-start(), calls=%async_computation.35 | async-start | bytes 11796480 | tf_op jit(solution)/shard_map/reduce_scatter | solution.py:239
  2218.6 542.1 %reduce-scatter.35.cloned.1.call-start = ((), (), s32[]{:S(2)}) async-start(), calls=%async_computation.32 | async-start | bytes 11796480 | tf_op jit(solution)/shard_map/reduce_scatter | solution.py:236
  2227.1 698.2 %reduce-scatter.39.cloned.1.call-start = ((), (), s32[]{:S(2)}) async-start(), calls=%async_computation.34 | async-start | bytes 11796480 | tf_op jit(solution)/shard_map/reduce_scatter | solution.py:239
  2237.9 710.7 %reduce-scatter.45.cloned.1.call-start = ((), (), s32[]{:S(2)}) async-start(), calls=%async_computation.45 | async-start | bytes 245760
  2239.9 729.3 %reduce-scatter.43.cloned.1.call-start = ((), (), s32[]{:S(2)}) async-start(), calls=%async_computation.44 | async-start | bytes 245760
  2241.0 793.3 %all-reduce.32.cloned.1.call-start = ((), (), s32[]{:S(2)}) async-start(), calls=%async_computation.46 | async-start | bytes 4718592 | tf_op jit(solution)/shard_map/psum | solution.py:229
  2266.9 959.1 %all-reduce.34.cloned.1.call-start = ((), (), s32[]{:S(2)}) async-start(), calls=%async_computation.47 | async-start | bytes 18874368 | tf_op jit(solution)/shard_map/psum | solution.py:244
  (154 other events, 3158.2 us)
Sparse Core Ops, SparseCore 0:
  10.2 73.3 all-gather.30
  85.7 28.7 all-gather.32
  116.1 165.9 all-gather.36
  283.5 164.9 all-gather.34
  468.5 7.2 reduce-scatter.18
  477.2 71.5 all-gather.38
  550.4 165.5 all-gather.44
  717.5 28.4 all-gather.40
  747.5 165.9 all-gather.42
  938.2 7.2 reduce-scatter.20
  957.7 8.2 all-gather.26
  1001.9 9.3 reduce-scatter.22
  1576.8 9.3 all-gather.28
  1625.3 9.3 reduce-scatter.24
  1636.9 30.4 reduce-scatter.32
  1669.5 27.9 reduce-scatter.30
  1700.2 65.0 reduce-scatter.28
  2200.7 66.0 reduce-scatter.26
  2269.8 161.3 reduce-scatter.36
  2433.4 162.1 reduce-scatter.40
  2598.5 162.1 reduce-scatter.34
  2763.0 162.1 reduce-scatter.38
  2928.1 20.5 reduce-scatter.44
  2951.3 17.8 reduce-scatter.42
  2972.8 61.5 all-reduce.31
  3038.1 187.8 all-reduce.33
where the time goes:
time: 3290 us; the launch traced here: 3240 us
  local copies, waits for them, and re-layouts  1430 us (43%)
  waiting for transfers between devices  1160 us (35%)
  matrix products  218 us (7%)
  blocking collectives  173 us (5%)
  other arithmetic  129 us (4%)
  loops' own time  93.6 us (3%)
    rev x8, local copies, waits for them, and re-layouts, band_bias(): spread.reshape(head_count, block_rows, length + block_rows)[:, :, :length]  406 us
    reduce_scatter x2, waiting for transfers between devices, reduce_grads(): lax.psum_scatter(grad_up.astype(jnp.bfloat16), 'dp', scatter_dimension=1,...  329 us
    while x76, local copies, waits for them, and re-layouts  329 us
    reduce_scatter x2, waiting for transfers between devices, reduce_grads(): lax.psum_scatter(grad_down.astype(jnp.bfloat16), 'dp', scatter_dimension=...  329 us
    psum x1, waiting for transfers between devices, reduce_grads(): lax.psum(expert_pieces[0].astype(jnp.bfloat16), 'seq').astype(jnp.float32)  186 us
    rev x4, local copies, waits for them, and re-layouts, band_sums(): flipped = jnp.pad(weights[:, :, ::-1], ((0, 0), (0, 0), (0, block_rows)))  138 us
    reshape x8, local copies, waits for them, and re-layouts, band_bias(): spread.reshape(head_count, block_rows * band_width)  106 us
    all_gather x2, waiting for transfers between devices, fetch(): lax.all_gather(expert_up[decoder_layer], 'dp', axis=1, tiled=True)  90.6 us
  transfers between devices with their start and end apart: 32, of which 22 were waited for; matrix products, arithmetic and copies ran while one was open for 35% of the time, Pallas kernels for 0%

commit v1 on v0

v1 whole, which is shorter than its diff:
```python
import functools

import jax
import jax.numpy as jnp
from jax import lax
from jax.experimental import pallas as pl
from jax.experimental.pallas import tpu as pltpu
from jax.sharding import PartitionSpec as P

HEADS = 12
LAYERS = 2
epsilon = 1e-06
negative = -1e30
highest_precision = lax.Precision.HIGHEST


def scaled(values, gain_vec):
    return values * lax.rsqrt(jnp.mean(values * values, axis=-1, keepdims=True) + epsilon) * gain_vec


HD = 64
ROWS = 128
NT = (((1,), (1,)), ((), ()))
TN = (((0,), (0,)), ((), ()))


def visit_blocks(length, span, one_block):
    full = span // ROWS
    for i in range(min(full - 1, length // ROWS)):
        one_block(i * ROWS, 0, (i + 1) * ROWS)

    def step(i, carry):
        start = pl.multiple_of(i * ROWS, ROWS)
        one_block(start, pl.multiple_of(start + ROWS - span, ROWS), span)
        return carry

    lax.fori_loop(full - 1, length // ROWS, step, 0)


def fill_mask(mask_ref, segr_ref, segc_ref, start, low, width):
    same = segc_ref[pl.ds(start, ROWS), :] == segr_ref[:, pl.ds(low, width)]
    back = lax.broadcasted_iota(jnp.int32, (ROWS, width), 0) + (width - ROWS)
    allowed = same & (back >= lax.broadcasted_iota(jnp.int32, (ROWS, width), 1))
    mask_ref[:, :width] = jnp.where(allowed, 0.0, -1e30)


def fill_slab(slab_ref, line_ref, heads, span):
    for h in range(heads):
        spread = jnp.broadcast_to(line_ref[h : h + 1, :], (ROWS, span))
        slab_ref[h] = pltpu.roll(spread, 0, 1, stride=1, stride_axis=0)


def split_heads(qkv_ref, parts_ref, heads):
    for h in range(3 * heads):
        part = qkv_ref[:, h * HD : (h + 1) * HD]
        parts_ref[h] = part * jnp.bfloat16(0.125) if h < heads else part


def attn_fwd_kernel(heads, span, qkv_ref, segr_ref, segc_ref, line_ref, out_ref, lse_ref, parts_ref, mixed_ref, slab_ref, mask_ref):
    length = qkv_ref.shape[0]
    fill_slab(slab_ref, line_ref, heads, span)
    split_heads(qkv_ref, parts_ref, heads)

    def one_block(start, low, width):
        fill_mask(mask_ref, segr_ref, segc_ref, start, low, width)

        def one_head(h, carry):
            q = parts_ref[h, pl.ds(start, ROWS), :]
            k = parts_ref[heads + h, pl.ds(low, width), :]
            v = parts_ref[2 * heads + h, pl.ds(low, width), :]
            s = lax.dot_general(q, k, NT, preferred_element_type=jnp.float32)
            s = s + slab_ref[h, :, span - width :] + mask_ref[:, :width]
            top = jnp.max(s, axis=1, keepdims=True)
            e = jnp.exp(s - top)
            total = jnp.sum(e, axis=1, keepdims=True)
            mixed = jnp.dot(e.astype(jnp.bfloat16), v, preferred_element_type=jnp.float32)
            mixed_ref[h, pl.ds(start, ROWS), :] = (mixed / total).astype(jnp.bfloat16)
            lse_ref[h, pl.ds(start, ROWS), :] = top + jnp.log(total)
            return carry

        lax.fori_loop(0, heads, one_head, 0)

    visit_blocks(length, span, one_block)
    out_ref[...] = jnp.concatenate([mixed_ref[h] for h in range(heads)], axis=1)


def attn_bwd_kernel(heads, span, qkv_ref, segr_ref, segc_ref, line_ref, lse_ref, grad_ref, out_ref, band_ref,
                    parts_ref, gparts_ref, qgrad_ref, kgrad_ref, vgrad_ref, slab_ref, mask_ref, band_acc):
    length = qkv_ref.shape[0]
    fill_slab(slab_ref, line_ref, heads, span)
    split_heads(qkv_ref, parts_ref, heads)
    for h in range(heads):
        gparts_ref[h] = grad_ref[:, h * HD : (h + 1) * HD]
    kgrad_ref[...] = jnp.zeros_like(kgrad_ref)
    vgrad_ref[...] = jnp.zeros_like(vgrad_ref)
    band_acc[...] = jnp.zeros_like(band_acc)

    def one_block(start, low, width):
        fill_mask(mask_ref, segr_ref, segc_ref, start, low, width)

        def one_head(h, carry):
            rows = pl.ds(start, ROWS)
            window = pl.ds(low, width)
            q = parts_ref[h, rows, :]
            k = parts_ref[heads + h, window, :]
            v = parts_ref[2 * heads + h, window, :]
            grad = gparts_ref[h, rows, :]
            s = lax.dot_general(q, k, NT, preferred_element_type=jnp.float32)
            s = s + slab_ref[h, :, span - width :] + mask_ref[:, :width]
            p = jnp.exp(s - lse_ref[h, rows, :])
            dp = lax.dot_general(grad, v, NT, preferred_element_type=jnp.float32)
            inner = jnp.sum(p * dp, axis=1, keepdims=True)
            ds = p * (dp - inner)
            band_acc[h, :, span - width :] += ds
            ds = ds.astype(jnp.bfloat16)
            qgrad = jnp.dot(ds, k, preferred_element_type=jnp.float32)
            qgrad_ref[h, rows, :] = (qgrad * 0.125).astype(jnp.bfloat16)
            kgrad_ref[h, window, :] += lax.dot_general(ds, q, TN, preferred_element_type=jnp.float32)
            vgrad_ref[h, window, :] += lax.dot_general(p.astype(jnp.bfloat16), grad, TN, preferred_element_type=jnp.float32)
            return carry

        lax.fori_loop(0, heads, one_head, 0)

    visit_blocks(length, span, one_block)
    parts = [qgrad_ref[h] for h in range(heads)]
    parts += [kgrad_ref[h].astype(jnp.bfloat16) for h in range(heads)]
    parts += [vgrad_ref[h].astype(jnp.bfloat16) for h in range(heads)]
    out_ref[...] = jnp.concatenate(parts, axis=1)
    row = lax.broadcasted_iota(jnp.int32, (ROWS, span), 0)
    for h in range(heads):
        acc = band_acc[h]
        bit = 1
        while bit < ROWS:
            acc = jnp.where((row & bit) != 0, pltpu.roll(acc, span - bit, 1), acc)
            bit *= 2
        band_ref[h : h + 1, :] = jnp.sum(acc, axis=0, keepdims=True)


def vmem(count):
    return [pl.BlockSpec(memory_space=pltpu.VMEM)] * count


def attend(qkv, seg_row, seg_col, line):
    length, width = qkv.shape
    heads, span = line.shape
    return pl.pallas_call(
        functools.partial(attn_fwd_kernel, heads, span),
        out_shape=(
            jax.ShapeDtypeStruct((length, heads * HD), jnp.bfloat16),
            jax.ShapeDtypeStruct((heads, length, 1), jnp.float32),
        ),
        in_specs=vmem(4),
        out_specs=tuple(vmem(2)),
        scratch_shapes=[
            pltpu.VMEM((3 * heads, length, HD), jnp.bfloat16),
            pltpu.VMEM((heads, length, HD), jnp.bfloat16),
            pltpu.VMEM((heads, ROWS, span), jnp.float32),
            pltpu.VMEM((ROWS, span), jnp.float32),
        ],
        name="attend",
    )(qkv, seg_row, seg_col, line)


def attend_back(qkv, seg_row, seg_col, line, lse, grad):
    length, width = qkv.shape
    heads, span = line.shape
    return pl.pallas_call(
        functools.partial(attn_bwd_kernel, heads, span),
        out_shape=(
            jax.ShapeDtypeStruct((length, width), jnp.bfloat16),
            jax.ShapeDtypeStruct((heads, span), jnp.float32),
        ),
        in_specs=vmem(6),
        out_specs=tuple(vmem(2)),
        scratch_shapes=[
            pltpu.VMEM((3 * heads, length, HD), jnp.bfloat16),
            pltpu.VMEM((heads, length, HD), jnp.bfloat16),
            pltpu.VMEM((heads, length, HD), jnp.bfloat16),
            pltpu.VMEM((heads, length, HD), jnp.float32),
            pltpu.VMEM((heads, length, HD), jnp.float32),
            pltpu.VMEM((heads, ROWS, span), jnp.float32),
            pltpu.VMEM((ROWS, span), jnp.float32),
            pltpu.VMEM((heads, ROWS, span), jnp.float32),
        ],
        name="attend_back",
    )(qkv, seg_row, seg_col, line, lse, grad)


def plane_gather(values):
    return lax.all_gather(values, ("seq", "tensor"), axis=0, tiled=True)


def plane_sum(values):
    return lax.psum_scatter(values, ("seq", "tensor"), scatter_dimension=0, tiled=True)


def seq_gather(values):
    return lax.all_gather(values, "seq", axis=0, tiled=True)


def seq_sum(values):
    return lax.psum_scatter(values, "seq", scatter_dimension=0, tiled=True)


def heads_to_tokens(values):
    return lax.all_to_all(values, "seq", split_axis=0, concat_axis=1, tiled=True)


def tokens_to_heads(values):
    return lax.all_to_all(values, "seq", split_axis=1, concat_axis=0, tiled=True)


def norm_back(values, gain_vec, grad):
    inverse = lax.rsqrt(jnp.mean(values * values, axis=-1, keepdims=True) + epsilon)
    unit = values * inverse
    scaled_grad = grad * gain_vec
    gain_grad = jnp.sum(grad * unit, axis=0)
    return inverse * (scaled_grad - unit * jnp.mean(scaled_grad * unit, axis=-1, keepdims=True)), gain_grad


def gelu_parts(values):
    cubic = values * values * 0.044715
    inner = jnp.tanh(0.7978845608028654 * values * (1.0 + cubic))
    slope = 0.5 * (1.0 + inner) + 0.5 * values * (1.0 - inner * inner) * 0.7978845608028654 * (1.0 + 3.0 * cubic)
    return 0.5 * values * (1.0 + inner), slope


def dot(left, right):
    return jnp.dot(left, right, preferred_element_type=jnp.float32)


def dot_nt(left, right):
    return lax.dot_general(left, right, NT, preferred_element_type=jnp.float32)


def dot_tn(left, right):
    return lax.dot_general(left, right, TN, preferred_element_type=jnp.float32)


def body(
    block_input,
    segments,
    routes,
    distance_bucket,
    first_gain,
    query_key_value,
    attention_out,
    bias_table,
    second_gain,
    router_weights,
    expert_up,
    expert_down,
    cotangent,
):
    low = jnp.bfloat16
    seq_count, piece, width = block_input.shape
    n_dp, n_seq, n_tensor = (lax.axis_size(name) for name in ("dp", "seq", "tensor"))
    n_plane = n_seq * n_tensor
    length = piece * n_seq
    local_heads = HEADS // n_seq
    head_width = local_heads * HD
    experts = expert_up.shape[1]
    assert seq_count == 1 and experts == n_seq
    shard = width // n_dp
    bucket_count = bias_table.shape[1] * n_dp
    bucket_shard = bias_table.shape[1]
    group_rows = n_tensor * piece
    capacity = group_rows * routes.shape[-1] // experts
    seq_index = lax.axis_index("seq")
    plane_index = seq_index * n_tensor + lax.axis_index("tensor")
    span = ROWS + length // 2

    small = jnp.concatenate(
        [
            first_gain.reshape(LAYERS, -1),
            second_gain.reshape(LAYERS, -1),
            bias_table.reshape(LAYERS, -1),
            router_weights.reshape(LAYERS, -1),
        ],
        axis=1,
    )
    small = lax.all_gather(small, "dp", axis=0)
    cuts = [shard, 2 * shard, 2 * shard + bucket_shard * HEADS]
    gains_one, gains_two, tables, routers = jnp.split(small, cuts, axis=2)

    def whole(values, trailing):
        return jnp.moveaxis(values, 1, 0).reshape((LAYERS, -1) + trailing)

    gains_one = whole(gains_one, ()).astype(jnp.float32)
    gains_two = whole(gains_two, ()).astype(jnp.float32)
    tables = whole(tables, (HEADS,)).astype(jnp.float32)
    routers = whole(routers, (experts,))

    own_qkv = lax.dynamic_index_in_dim(
        query_key_value.reshape(LAYERS, shard, 3, n_seq, head_width), seq_index, 3, keepdims=False
    ).reshape(LAYERS, shard, 3 * head_width)
    out_columns = width // n_plane
    own_out = lax.dynamic_index_in_dim(
        attention_out.reshape(LAYERS, shard, n_plane, out_columns), plane_index, 2, keepdims=False
    )
    own_up = lax.dynamic_index_in_dim(expert_up, seq_index, 1, keepdims=False)
    own_down = lax.dynamic_index_in_dim(expert_down, seq_index, 1, keepdims=False).swapaxes(1, 2)

    def attention_weights(layer):
        qkv = lax.all_gather(own_qkv[layer], "dp", axis=0, tiled=True)
        out = lax.all_gather(own_out[layer], ("dp", "seq", "tensor"), axis=0)
        out = out.reshape(n_dp, n_plane, shard, out_columns)
        return qkv, jnp.moveaxis(out, 1, 2).reshape(width, width)

    def expert_weights(layer):
        up = lax.all_gather(own_up[layer], "dp", axis=0, tiled=True)
        down = lax.all_gather(own_down[layer], "dp", axis=0, tiled=True)
        return up, down

    routes_all = lax.all_gather(routes, "seq", axis=0)
    routes_all = jnp.moveaxis(routes_all, 0, 1).reshape(LAYERS, n_seq, group_rows, -1)
    seg_row = segments
    seg_col = segments.reshape(length, 1)
    bucket_line = distance_bucket[length // 2 - 1 :: -1][: length // 2]
    bucket_line = jnp.concatenate(
        [jnp.full((1,), -1, jnp.int32), bucket_line, jnp.full((span - 1 - length // 2,), -1, jnp.int32)]
    )
    line_hot = (bucket_line[None, :] == lax.iota(jnp.int32, bucket_count)[:, None]).astype(jnp.float32)
    strict_upper = (
        lax.iota(jnp.int32, group_rows)[:, None] < lax.iota(jnp.int32, group_rows)[None, :]
    ).astype(low)

    def routing(layer):
        layer_routes = routes_all[layer]
        mine = jnp.any(layer_routes == seq_index, axis=-1)
        slot = dot(mine.astype(low), strict_upper).astype(jnp.int32)
        slot = jnp.where(mine & (slot < capacity), slot, -1)
        hot = (slot[:, None, :] == lax.iota(jnp.int32, capacity)[None, :, None]).astype(low)
        chosen = jnp.any(layer_routes[..., None] == lax.iota(jnp.int32, experts), axis=2)
        return hot, chosen.reshape(n_seq * group_rows, experts)

    def to_slots(hot, rows):
        rows = rows.reshape(n_seq, group_rows, width)
        out = jnp.einsum("gct,gtd->gcd", hot, rows, preferred_element_type=jnp.float32)
        return out.astype(low).reshape(n_seq * capacity, width)

    def from_slots(hot, rows):
        rows = rows.reshape(n_seq, capacity, -1)
        out = jnp.einsum("gct,gcd->gtd", hot, rows, preferred_element_type=jnp.float32)
        return out.reshape(n_seq * group_rows, -1)

    current = block_input[0]
    grad = cotangent[0]
    saved = []
    for layer in range(LAYERS):
        qkv_weight, out_weight = attention_weights(layer)
        up, down = expert_weights(layer)
        normed = scaled(current, gains_one[layer]).astype(low)
        normed_all = seq_gather(normed)
        qkv = dot(normed_all, qkv_weight).astype(low)
        own_table = lax.dynamic_slice_in_dim(tables[layer], seq_index * local_heads, local_heads, 1)
        line = jnp.dot(own_table.T, line_hot, precision=highest_precision)
        mixed, log_total = attend(qkv, seg_row, seg_col, line)
        merged = heads_to_tokens(mixed)
        middle = current + dot(merged, out_weight)
        normed_two = scaled(middle, gains_two[layer]).astype(low)
        tokens = plane_gather(normed_two)
        hot, chosen = routing(layer)
        router_logits = dot(tokens, routers[layer])
        router_logits = jnp.where(chosen, router_logits, negative)
        raised = jnp.exp(router_logits - jnp.max(router_logits, axis=1, keepdims=True))
        shares = raised / jnp.sum(raised, axis=1, keepdims=True)
        own_share = lax.dynamic_slice_in_dim(shares, seq_index, 1, 1)
        slots = to_slots(hot, tokens)
        pre = dot(slots, up)
        hidden = gelu_parts(pre)[0].astype(low)
        pre = pre.astype(low)
        result = dot_nt(hidden, down).astype(low)
        part = (own_share * from_slots(hot, result)).astype(low)
        following = middle + plane_sum(part).astype(jnp.float32)
        saved.append(
            (current, normed_all, qkv, line, log_total, merged, middle, tokens, hot, shares, own_share, slots, pre, hidden,
             qkv_weight, out_weight, up, down)
        )
        current = following

    results = [None] * LAYERS
    for layer in range(LAYERS - 1, -1, -1):
        (layer_in, normed_all, qkv, line, log_total, merged, middle, tokens, hot, shares, own_share, slots, pre, hidden,
         qkv_weight, out_weight, up, down) = saved[layer]
        grad_rows = plane_gather(grad.astype(low)).astype(jnp.float32)
        result_grad = to_slots(hot, (own_share * grad_rows).astype(low))
        hidden_grad = dot(result_grad, down)
        down_grad = dot_tn(result_grad, hidden)
        pair_sum = jnp.sum(hidden.astype(jnp.float32) * hidden_grad, axis=1)
        pre_grad = (gelu_parts(pre.astype(jnp.float32))[1] * hidden_grad).astype(low)
        up_grad = dot_tn(slots, pre_grad)
        slot_grad = dot_nt(pre_grad, up).astype(low)
        token_pair = jnp.einsum(
            "gct,gc->gt", hot.astype(jnp.float32), pair_sum.reshape(n_seq, capacity), precision=highest_precision
        ).reshape(-1, 1)
        own_hot = (lax.iota(jnp.int32, experts) == seq_index).astype(jnp.float32)
        logit_grad = (token_pair * (own_hot[None, :] - shares)).astype(low)
        part = from_slots(hot, slot_grad) + dot_nt(logit_grad, routers[layer])
        router_grad = dot_tn(tokens, logit_grad)
        normed_two_grad = plane_sum(part.astype(low)).astype(jnp.float32)
        middle_part, gain_two_grad = norm_back(middle, gains_two[layer], normed_two_grad)
        middle_grad = grad + middle_part
        out_grad = middle_grad.astype(low)
        out_weight_grad = dot_tn(merged, out_grad)
        merged_grad = dot_nt(out_grad, out_weight).astype(low)
        mixed_grad = tokens_to_heads(merged_grad)
        qkv_grad, band = attend_back(qkv, seg_row, seg_col, line, log_total, mixed_grad)
        qkv_weight_grad = dot_tn(normed_all, qkv_grad)
        normed_grad = seq_sum(dot_nt(qkv_grad, qkv_weight).astype(low)).astype(jnp.float32)
        input_part, gain_one_grad = norm_back(layer_in, gains_one[layer], normed_grad)
        grad = middle_grad + input_part
        table_grad = jnp.dot(line_hot, band.T, precision=highest_precision)
        table_grad = lax.dynamic_update_slice_in_dim(
            jnp.zeros((bucket_count, HEADS), jnp.float32), table_grad, seq_index * local_heads, 1
        )

        expert_grads = []
        for piece_grad in (up_grad, down_grad):
            piece_grad = lax.psum_scatter(piece_grad.astype(low), "dp", scatter_dimension=0, tiled=True)
            expert_grads.append(lax.all_gather(piece_grad, "seq", axis=0).astype(jnp.float32))
        up_total, down_total = expert_grads[0], expert_grads[1].swapaxes(1, 2)

        packed = jnp.concatenate(
            [
                gain_one_grad.reshape(n_dp, -1),
                gain_two_grad.reshape(n_dp, -1),
                table_grad.reshape(n_dp, -1),
                router_grad.reshape(n_dp, -1),
            ],
            axis=1,
        )
        packed_width = packed.shape[1]
        lanes = width
        per_row = n_plane * lanes
        extra = -(-packed_width // per_row) * per_row - packed_width
        packed = jnp.pad(packed, ((0, 0), (0, extra))).reshape(n_dp, n_plane, -1, lanes)
        both = jnp.concatenate([out_weight_grad.reshape(n_dp, n_plane, -1, width), packed], axis=2).astype(low)
        both = lax.psum_scatter(both.reshape((n_dp * n_plane,) + both.shape[2:]), ("dp", "seq", "tensor"), scatter_dimension=0, tiled=True)
        both = lax.all_gather(both, ("seq", "tensor"), axis=0, tiled=True).astype(jnp.float32)
        out_rows = shard // n_plane
        out_total = both[:, :out_rows].reshape(shard, width)
        packed_total = both[:, out_rows:].reshape(-1)[:packed_width]
        gain_one_total = packed_total[: cuts[0]]
        gain_two_total = packed_total[cuts[0] : cuts[1]]
        table_total = packed_total[cuts[1] : cuts[2]].reshape(bucket_shard, HEADS)
        router_total = packed_total[cuts[2] :].reshape(shard, experts)

        qkv_total = lax.psum_scatter(qkv_weight_grad.astype(low), ("dp", "tensor"), scatter_dimension=0, tiled=True)
        qkv_total = lax.all_gather(qkv_total, ("seq", "tensor"), axis=0).astype(jnp.float32)
        qkv_total = qkv_total.reshape(n_seq, shard, 3, head_width)
        qkv_total = jnp.moveaxis(qkv_total, 0, 2).reshape(shard, 3 * width)
        results[layer] = (gain_one_total, qkv_total, out_total, table_total, gain_two_total, router_total, up_total, down_total)

    stacked = [jnp.stack([results[layer][member] for layer in range(LAYERS)]) for member in range(8)]
    return (current[None], grad[None]) + tuple(stacked)


def solution(mesh):
    in_specs = (
        P(("dp", "tensor"), "seq", None),
        P(("dp", "tensor"), None),
        P(None, "dp", "seq", None),
        P(),
        P(None, "dp"),
        P(None, "dp", None),
        P(None, "dp", None),
        P(None, "dp", None),
        P(None, "dp"),
        P(None, "dp", None),
        P(None, None, "dp", "tensor"),
        P(None, None, "tensor", "dp"),
        P(("dp", "tensor"), "seq", None),
    )
    out_specs = (
        P(("dp", "tensor"), "seq", None),
        P(("dp", "tensor"), "seq", None),
        P(None, "dp"),
        P(None, "dp", None),
        P(None, "dp", None),
        P(None, "dp", None),
        P(None, "dp"),
        P(None, "dp", None),
        P(None, None, "dp", "tensor"),
        P(None, None, "tensor", "dp"),
    )
    return jax.shard_map(body, mesh=mesh, in_specs=in_specs, out_specs=out_specs, check_vma=False)
```

time: 3290 us -> 1570 us (0.48); the launches traced: 3240 us -> 1560 us
  local copies, waits for them, and re-layouts: 1430 us -> 76.1 us
  waiting for transfers between devices: 1160 us -> 1050 us
  loops' own time: 93.6 us -> 0 us
  other arithmetic: 129 us -> 57.1 us
  Pallas kernels: 0 us -> 71.8 us
  matrix products: 218 us -> 148 us
  blocking collectives: 173 us -> 129 us
    rev x12 -> x1, local copies, waits for them, and re-layouts: 544 us -> 0.1 us  [body(): bucket_line = distance_bucket[length // 2 - 1::-1][:length // 2]]
    while x80 -> x0, local copies, waits for them, and re-layouts: 335 us -> none
    all_gather x10 -> x16, waiting for transfers between devices: 174 us -> 494 us  [the longest x4 142 us: body(): lax.all_gather(piece_grad, 'seq', axis=0).astype(jnp.float32)]
    psum x2 -> x0, waiting for transfers between devices: 200 us -> none  [the longest x1 186 us: reduce_grads(): lax.psum(expert_pieces[0].astype(jnp.bfloat16), 'seq').astype(jnp.float32)]
    reshape x24 -> x17, local copies, waits for them, and re-layouts: 186 us -> 24.3 us  [the longest x2 5.81 us: body(): qkv_total = qkv_total.reshape(n_seq, shard, 3, head_width)]
    reduce_scatter x12 -> x14, waiting for transfers between devices: 701 us -> 558 us  [the longest x2 177 us: body(): lax.psum_scatter(both.reshape((n_dp * n_plane,) + both.shape[2:]), ('dp',...]
    another operation x4 -> x0, loops' own time: 93.6 us -> none  [the longest x2 66.1 us: one_sequence(): lax.scan(one_block, start_state, lax.iota(jnp.int32, steps_count))]
    slice x22 -> x27, local copies, waits for them, and re-layouts: 91.1 us -> 9.88 us  [the longest x1 2.34 us: expert_weights(): up = lax.all_gather(own_up[layer], 'dp', axis=0, tiled=True)]
  transfers between devices with their start and end apart: 32 -> 32, of which waited for: 22 -> 27; matrix products, arithmetic and copies ran while one was open for 35% -> 12% of each run, Pallas kernels for 0% -> 3%
where the time goes in v1:
time: 1570 us; the launch traced here: 1560 us
  waiting for transfers between devices  1050 us (67%)
  matrix products  148 us (9%)
  blocking collectives  129 us (8%)
  local copies, waits for them, and re-layouts  76.1 us (5%)
  Pallas kernels  71.8 us (5%)
  other arithmetic  57.1 us (4%)
  between operations  15.8 us (1%)
    reduce_scatter x2, waiting for transfers between devices, body(): lax.psum_scatter(both.reshape((n_dp * n_plane,) + both.shape[2:]), ('dp',...  177 us
    reduce_scatter x4, waiting for transfers between devices, body(): lax.psum_scatter(piece_grad.astype(low), 'dp', scatter_dimension=0, tiled...  148 us
    all_gather x4, waiting for transfers between devices, body(): lax.all_gather(piece_grad, 'seq', axis=0).astype(jnp.float32)  142 us
    reduce_scatter x4, waiting for transfers between devices, plane_sum(): lax.psum_scatter(values, ('seq', 'tensor'), scatter_dimension=0, tiled=True)  139 us
    all_gather x4, waiting for transfers between devices, plane_gather(): return lax.all_gather(values, ('seq', 'tensor'), axis=0, tiled=True)  97.6 us
    all_gather x2, waiting for transfers between devices, expert_weights(): up = lax.all_gather(own_up[layer], 'dp', axis=0, tiled=True)  93.5 us
    all_gather x2, waiting for transfers between devices, expert_weights(): down = lax.all_gather(own_down[layer], 'dp', axis=0, tiled=True)  88.1 us
    all_gather x2, waiting for transfers between devices, attention_weights(): out = lax.all_gather(own_out[layer], ('dp', 'seq', 'tensor'), axis=0)  66.1 us
  transfers between devices with their start and end apart: 32, of which 27 were waited for; matrix products, arithmetic and copies ran while one was open for 12% of the time, Pallas kernels for 3%

profile of v1, /device:TPU:0, one launch (start us, length us, event | category | flops | bytes accessed | tf_op | source)
XLA Modules:
  0.0 1561.6 jit_solution(830181769475887909)
XLA Ops:
  9.8 14.9 all-gather.14
  41.8 20.4 %all_gather.99 = bf16[768,576]{1,0:T(8,128)(2,1)S(1)} all-gather(bf16[192,576]{1,0:T(8,128)(2,1)S(1)} %copy.142), channel_id=1, replica_groups=mesh['dp'=4,'seq'=4,'tensor'=2] {'dp'}, dimensions={0}, use_global_device_ids=true | all-gather | bytes 1105920 | tf_op jit(solution)/shard_map/all_gather | solution.py:305
  66.5 15.1 attend.2
  87.6 32.3 %all-gather.44.cloned.1.call-done = bf16[32,192,1,96]{3,1,2,0:T(8,128)(2,1)} async-done(((bf16[1,192,1,96]{3,1,2,0:T(8,128)(2,1)}), bf16[32,192,1,96]{3,1,2,0:T(8,128)(2,1)}) %all-gather.44.cloned.1.call-update) | async-done | bytes 1179664 | tf_op jit(solution)/shard_map/all_gather | solution.py:306
  143.4 16.1 %all-gather.34.cloned.1.call-done = bf16[2048,768]{1,0:T(8,128)(2,1)} async-done(((bf16[256,768]{1,0:T(8,128)(2,1)}), bf16[2048,768]{1,0:T(8,128)(2,1)}) %all-gather.34.cloned.1.call-update) | async-done | bytes 3145744 | tf_op jit(solution)/shard_map/all_gather | solution.py:190
  164.2 47.3 %all-gather.46.cloned.1.call-done = bf16[1,1,768,1536]{3,2,1,0:T(8,128)(2,1)} async-done(((bf16[1,1,192,1536]{3,2,1,0:T(8,128)(2,1)}), bf16[1,1,768,1536]{3,2,1,0:T(8,128)(2,1)}) %all-gather.46.cloned.1.call-update) | async-done | bytes 2359312 | tf_op jit(solution)/shard_map/all_gather | solution.py:311
  217.6 44.6 %all-gather.48.cloned.1.call-done = bf16[1,768,1536]{2,1,0:T(8,128)(2,1)} async-done(((bf16[1,192,1536]{2,1,0:T(8,128)(2,1)}), bf16[1,768,1536]{2,1,0:T(8,128)(2,1)}) %all-gather.48.cloned.1.call-update) | async-done | bytes 2359312 | tf_op jit(solution)/shard_map/all_gather | solution.py:312
  273.1 44.8 %reduce-scatter.15.cloned.1.call-done = bf16[256,768]{1,0:T(8,128)(2,1)} async-done(((bf16[2048,768]{1,0:T(8,128)(2,1)}), bf16[256,768]{1,0:T(8,128)(2,1)}) %reduce-scatter.15.cloned.1.call-update) | async-done | bytes 393232 | tf_op jit(solution)/shard_map/reduce_scatter | solution.py:194
  323.7 22.3 %all_gather.107 = bf16[768,576]{1,0:T(8,128)(2,1)S(1)} all-gather(bf16[192,576]{1,0:T(8,128)(2,1)S(1)} %copy.150), channel_id=1, replica_groups=mesh['dp'=4,'seq'=4,'tensor'=2] {'dp'}, dimensions={0}, use_global_device_ids=true | all-gather | bytes 1105920 | tf_op jit(solution)/shard_map/all_gather | solution.py:305
  355.8 15.1 attend.3
  376.5 33.8 %all-gather.50.cloned.1.call-done = bf16[32,192,1,96]{3,1,2,0:T(8,128)(2,1)} async-done(((bf16[1,192,1,96]{3,1,2,0:T(8,128)(2,1)}), bf16[32,192,1,96]{3,1,2,0:T(8,128)(2,1)}) %all-gather.50.cloned.1.call-update) | async-done | bytes 1179664 | tf_op jit(solution)/shard_map/all_gather | solution.py:306
  422.2 27.0 %all-gather.38.cloned.1.call-done = bf16[2048,768]{1,0:T(8,128)(2,1)} async-done(((bf16[256,768]{1,0:T(8,128)(2,1)}), bf16[2048,768]{1,0:T(8,128)(2,1)}) %all-gather.38.cloned.1.call-update) | async-done | bytes 3145744 | tf_op jit(solution)/shard_map/all_gather | solution.py:190
  454.9 46.2 %all-gather.52.cloned.1.call-done = bf16[1,1,768,1536]{3,2,1,0:T(8,128)(2,1)} async-done(((bf16[1,1,192,1536]{3,2,1,0:T(8,128)(2,1)}), bf16[1,1,768,1536]{3,2,1,0:T(8,128)(2,1)}) %all-gather.52.cloned.1.call-update) | async-done | bytes 2359312 | tf_op jit(solution)/shard_map/all_gather | solution.py:311
  508.6 43.5 %all-gather.54.cloned.1.call-done = bf16[1,768,1536]{2,1,0:T(8,128)(2,1)} async-done(((bf16[1,192,1536]{2,1,0:T(8,128)(2,1)}), bf16[1,768,1536]{2,1,0:T(8,128)(2,1)}) %all-gather.54.cloned.1.call-update) | async-done | bytes 2359312 | tf_op jit(solution)/shard_map/all_gather | solution.py:312
  562.7 22.7 %all-gather.40.cloned.1.call-done = bf16[2048,768]{1,0:T(8,128)(2,1)} async-done(((bf16[256,768]{1,0:T(8,128)(2,1)}), bf16[2048,768]{1,0:T(8,128)(2,1)}) %all-gather.40.cloned.1.call-update) | async-done | bytes 3145744 | tf_op jit(solution)/shard_map/all_gather | solution.py:190
  607.9 45.6 %reduce-scatter.19.cloned.1.call-done = bf16[256,768]{1,0:T(8,128)(2,1)} async-done(((bf16[2048,768]{1,0:T(8,128)(2,1)}), bf16[256,768]{1,0:T(8,128)(2,1)}) %reduce-scatter.19.cloned.1.call-update) | async-done | bytes 393232 | tf_op jit(solution)/shard_map/reduce_scatter | solution.py:194
  654.9 48.5 %reduce-scatter.17.cloned.1.call-done = bf16[256,768]{1,0:T(8,128)(2,1)} async-done(((bf16[2048,768]{1,0:T(8,128)(2,1)}), bf16[256,768]{1,0:T(8,128)(2,1)}) %reduce-scatter.17.cloned.1.call-update) | async-done | bytes 393232 | tf_op jit(solution)/shard_map/reduce_scatter | solution.py:194
  718.5 20.8 %attend_back.2 = (bf16[1024,576]{1,0:T(8,128)(2,1)}, f32[3,640]{1,0:T(4,128)}) custom-call(bf16[1024,576]{1,0:T(8,128)(2,1)} %convolution_convert_fusion.6.qkv_ref, s32[1,1024]{1,0:T(1,128)} %segr_ref.7, s32[1024,1]{1,0:T(8,128)} %copy.144.segc_ref, f32[3,640]{1,0:T(4,128)} %fusion.114.line_ref, f32[3,1024,1]{2,1,0:T(8,128)} %get-tuple-element.20.lse_ref, ...), custom_call_target="tpu_custom_call" | custom-call | tf_op jit(solution)/shard_map/attend_back/pallas_call | solution.py:167
  743.5 30.7 %reduce-scatter.21.cloned.1.call-done = bf16[256,768]{1,0:T(8,128)(2,1)} async-done(((bf16[1024,768]{1,0:T(8,128)(2,1)}), bf16[256,768]{1,0:T(8,128)(2,1)}) %reduce-scatter.21.cloned.1.call-update) | async-done | bytes 393232 | tf_op jit(solution)/shard_map/reduce_scatter | solution.py:202
  778.7 31.9 %all-gather.42.cloned.1.call-done = bf16[2048,768]{1,0:T(8,128)(2,1)} async-done(((bf16[256,768]{1,0:T(8,128)(2,1)}), bf16[2048,768]{1,0:T(8,128)(2,1)}) %all-gather.42.cloned.1.call-update) | async-done | bytes 3145744 | tf_op jit(solution)/shard_map/all_gather | solution.py:190
  900.6 20.8 %attend_back.3 = (bf16[1024,576]{1,0:T(8,128)(2,1)}, f32[3,640]{1,0:T(4,128)}) custom-call(bf16[1024,576]{1,0:T(8,128)(2,1)} %convolution_convert_fusion.7.qkv_ref, s32[1,1024]{1,0:T(1,128)} %segr_ref.7, s32[1024,1]{1,0:T(8,128)} %copy.144.segc_ref, f32[3,640]{1,0:T(4,128)} %fusion.115.line_ref, f32[3,1024,1]{2,1,0:T(8,128)} %get-tuple-element.22.lse_ref, ...), custom_call_target="tpu_custom_call" | custom-call | tf_op jit(solution)/shard_map/attend_back/pallas_call | solution.py:167
  930.3 48.2 %reduce-scatter.39.cloned.1.call-done = bf16[192,1536]{1,0:T(8,128)(2,1)} async-done(((bf16[768,1536]{1,0:T(8,128)(2,1)}), bf16[192,1536]{1,0:T(8,128)(2,1)}) %reduce-scatter.39.cloned.1.call-update) | async-done | bytes 589840 | tf_op jit(solution)/shard_map/reduce_scatter | solution.py:420
  978.6 49.8 %reduce-scatter.37.cloned.1.call-done = bf16[192,1536]{1,0:T(8,128)(2,1)} async-done(((bf16[768,1536]{1,0:T(8,128)(2,1)}), bf16[192,1536]{1,0:T(8,128)(2,1)}) %reduce-scatter.37.cloned.1.call-update) | async-done | bytes 589840 | tf_op jit(solution)/shard_map/reduce_scatter | solution.py:420
  1028.4 49.9 %reduce-scatter.35.cloned.1.call-done = bf16[192,1536]{1,0:T(8,128)(2,1)} async-done(((bf16[768,1536]{1,0:T(8,128)(2,1)}), bf16[192,1536]{1,0:T(8,128)(2,1)}) %reduce-scatter.35.cloned.1.call-update) | async-done | bytes 589840 | tf_op jit(solution)/shard_map/reduce_scatter | solution.py:420
  1078.4 34.5 %reduce-scatter.33.cloned.1.call-done = bf16[96,576]{1,0:T(8,128)(2,1)} async-done(((bf16[768,576]{1,0:T(8,128)(2,1)}), bf16[96,576]{1,0:T(8,128)(2,1)}) %reduce-scatter.33.cloned.1.call-update) | async-done | bytes 110608 | tf_op jit(solution)/shard_map/reduce_scatter | solution.py:449
  1133.9 80.7 %reduce-scatter.29.cloned.1.call-done = bf16[1,25,768]{2,1,0:T(8,128)(2,1)} async-done(((bf16[32,25,768]{2,1,0:T(8,128)(2,1)}), bf16[1,25,768]{2,1,0:T(8,128)(2,1)}) %reduce-scatter.29.cloned.1.call-update) | async-done | bytes 38416 | tf_op jit(solution)/shard_map/reduce_scatter | solution.py:439
  1230.0 18.0 %reduce-scatter.31.cloned.1.call-done = bf16[96,576]{1,0:T(8,128)(2,1)} async-done(((bf16[768,576]{1,0:T(8,128)(2,1)}), bf16[96,576]{1,0:T(8,128)(2,1)}) %reduce-scatter.31.cloned.1.call-update) | async-done | bytes 110608 | tf_op jit(solution)/shard_map/reduce_scatter | solution.py:449
  1288.7 31.4 %all-gather.62.cloned.1.call-done = bf16[768,1536]{1,0:T(8,128)(2,1)} async-done(((bf16[192,1536]{1,0:T(8,128)(2,1)}), bf16[768,1536]{1,0:T(8,128)(2,1)}) %all-gather.62.cloned.1.call-update) | async-done | bytes 2359312 | tf_op jit(solution)/shard_map/all_gather | solution.py:421
  1320.1 39.1 %all-gather.60.cloned.1.call-done = bf16[768,1536]{1,0:T(8,128)(2,1)} async-done(((bf16[192,1536]{1,0:T(8,128)(2,1)}), bf16[768,1536]{1,0:T(8,128)(2,1)}) %all-gather.60.cloned.1.call-update) | async-done | bytes 2359312 | tf_op jit(solution)/shard_map/all_gather | solution.py:421
  1365.9 32.5 %all-gather.58.cloned.1.call-done = bf16[768,1536]{1,0:T(8,128)(2,1)} async-done(((bf16[192,1536]{1,0:T(8,128)(2,1)}), bf16[768,1536]{1,0:T(8,128)(2,1)}) %all-gather.58.cloned.1.call-update) | async-done | bytes 2359312 | tf_op jit(solution)/shard_map/all_gather | solution.py:421
  1398.4 39.2 %all-gather.56.cloned.1.call-done = bf16[768,1536]{1,0:T(8,128)(2,1)} async-done(((bf16[192,1536]{1,0:T(8,128)(2,1)}), bf16[768,1536]{1,0:T(8,128)(2,1)}) %all-gather.56.cloned.1.call-update) | async-done | bytes 2359312 | tf_op jit(solution)/shard_map/all_gather | solution.py:421
  1444.3 96.3 %reduce-scatter.27.cloned.1.call-done = bf16[1,25,768]{2,1,0:T(8,128)(2,1)} async-done(((bf16[32,25,768]{2,1,0:T(8,128)(2,1)}), bf16[1,25,768]{2,1,0:T(8,128)(2,1)}) %reduce-scatter.27.cloned.1.call-update) | async-done | bytes 38416 | tf_op jit(solution)/shard_map/reduce_scatter | solution.py:439
  (393 shorter events, 381.7 us)
Async XLA Ops:
  7.2 55.0 %all-gather.32.cloned.1.call-start = ((), (), s32[]{:S(2)}) async-start(), calls=%async_computation.18 | async-start | bytes 1966080 | tf_op jit(solution)/shard_map/all_gather | solution.py:198
  28.8 91.0 %all-gather.44.cloned.1.call-start = ((), (), s32[]{:S(2)}) async-start(), calls=%async_computation.38 | async-start | bytes 1622016 | tf_op jit(solution)/shard_map/all_gather | solution.py:306
  83.6 42.9 %all-to-all-start = ((bf16[4,256,192]{1,2,0:T(8,128)(2,1)}), bf16[4,256,192]{1,2,0:T(8,128)(2,1)S(1)}, u32[]{:S(2)}, u32[]{:S(2)}) async-start(bf16[4,256,192]{1,2,0:T(8,128)(2,1)} %copy.145), calls=%async_computation | async-start | bytes 786432 | tf_op jit(solution)/shard_map/all_to_all | solution.py:206
  87.3 72.2 %all-gather.34.cloned.1.call-start = ((), (), s32[]{:S(2)}) async-start(), calls=%async_computation.19 | async-start | bytes 3538944 | tf_op jit(solution)/shard_map/all_gather | solution.py:190
  128.0 83.6 %all-gather.46.cloned.1.call-start = ((), (), s32[]{:S(2)}) async-start(), calls=%async_computation.39 | async-start | bytes 2949120 | tf_op jit(solution)/shard_map/all_gather | solution.py:311
  130.4 131.9 %all-gather.48.cloned.1.call-start = ((), (), s32[]{:S(2)}) async-start(), calls=%async_computation.40 | async-start | bytes 2949120 | tf_op jit(solution)/shard_map/all_gather | solution.py:312
  132.9 185.0 %reduce-scatter.15.cloned.1.call-start = ((), (), s32[]{:S(2)}) async-start(), calls=%async_computation.20 | async-start | bytes 3538944 | tf_op jit(solution)/shard_map/reduce_scatter | solution.py:194
  272.9 79.1 %all-gather.36.cloned.1.call-start = ((), (), s32[]{:S(2)}) async-start(), calls=%async_computation.21 | async-start | bytes 1966080 | tf_op jit(solution)/shard_map/all_gather | solution.py:198
  321.0 89.4 %all-gather.50.cloned.1.call-start = ((), (), s32[]{:S(2)}) async-start(), calls=%async_computation.41 | async-start | bytes 1622016 | tf_op jit(solution)/shard_map/all_gather | solution.py:306
  372.9 42.0 %all-to-all-start.1 = ((bf16[4,256,192]{1,2,0:T(8,128)(2,1)}), bf16[4,256,192]{1,2,0:T(8,128)(2,1)S(1)}, u32[]{:S(2)}, u32[]{:S(2)}) async-start(bf16[4,256,192]{1,2,0:T(8,128)(2,1)} %copy.153), calls=%async_computation.2 | async-start | bytes 786432 | tf_op jit(solution)/shard_map/all_to_all | solution.py:206
  376.4 72.7 %all-gather.38.cloned.1.call-start = ((), (), s32[]{:S(2)}) async-start(), calls=%async_computation.22 | async-start | bytes 3538944 | tf_op jit(solution)/shard_map/all_gather | solution.py:190
  417.8 83.3 %all-gather.52.cloned.1.call-start = ((), (), s32[]{:S(2)}) async-start(), calls=%async_computation.42 | async-start | bytes 2949120 | tf_op jit(solution)/shard_map/all_gather | solution.py:311
  418.4 133.7 %all-gather.54.cloned.1.call-start = ((), (), s32[]{:S(2)}) async-start(), calls=%async_computation.43 | async-start | bytes 2949120 | tf_op jit(solution)/shard_map/all_gather | solution.py:312
  419.1 166.2 %all-gather.40.cloned.1.call-start = ((), (), s32[]{:S(2)}) async-start(), calls=%async_computation.24 | async-start | bytes 3538944 | tf_op jit(solution)/shard_map/all_gather | solution.py:190
  420.0 233.5 %reduce-scatter.19.cloned.1.call-start = ((), (), s32[]{:S(2)}) async-start(), calls=%async_computation.25 | async-start | bytes 3538944 | tf_op jit(solution)/shard_map/reduce_scatter | solution.py:194
  607.3 96.1 %reduce-scatter.17.cloned.1.call-start = ((), (), s32[]{:S(2)}) async-start(), calls=%async_computation.23 | async-start | bytes 3538944 | tf_op jit(solution)/shard_map/reduce_scatter | solution.py:194
  607.9 166.4 %reduce-scatter.21.cloned.1.call-start = ((), (), s32[]{:S(2)}) async-start(), calls=%async_computation.26 | async-start | bytes 1966080 | tf_op jit(solution)/shard_map/reduce_scatter | solution.py:202
  743.5 67.1 %all-gather.42.cloned.1.call-start = ((), (), s32[]{:S(2)}) async-start(), calls=%async_computation.27 | async-start | bytes 3538944 | tf_op jit(solution)/shard_map/all_gather | solution.py:190
  778.3 105.3 %reduce-scatter.23.cloned.1.call-start = ((), (), s32[]{:S(2)}) async-start(), calls=%async_computation.28 | async-start | bytes 3538944 | tf_op jit(solution)/shard_map/reduce_scatter | solution.py:194
  833.0 96.8 %reduce-scatter.41.cloned.1.call-start = ((), (), s32[]{:S(2)}) async-start(), calls=%async_computation.37 | async-start | bytes 2949120 | tf_op jit(solution)/shard_map/reduce_scatter | solution.py:420
  840.5 138.0 %reduce-scatter.39.cloned.1.call-start = ((), (), s32[]{:S(2)}) async-start(), calls=%async_computation.36 | async-start | bytes 2949120 | tf_op jit(solution)/shard_map/reduce_scatter | solution.py:420
  848.8 179.5 %reduce-scatter.37.cloned.1.call-start = ((), (), s32[]{:S(2)}) async-start(), calls=%async_computation.35 | async-start | bytes 2949120 | tf_op jit(solution)/shard_map/reduce_scatter | solution.py:420
  855.3 223.0 %reduce-scatter.35.cloned.1.call-start = ((), (), s32[]{:S(2)}) async-start(), calls=%async_computation.34 | async-start | bytes 2949120 | tf_op jit(solution)/shard_map/reduce_scatter | solution.py:420
  861.8 251.1 %reduce-scatter.33.cloned.1.call-start = ((), (), s32[]{:S(2)}) async-start(), calls=%async_computation.33 | async-start | bytes 1105920 | tf_op jit(solution)/shard_map/reduce_scatter | solution.py:449
  866.1 348.4 %reduce-scatter.29.cloned.1.call-start = ((), (), s32[]{:S(2)}) async-start(), calls=%async_computation.31 | async-start | bytes 1622016 | tf_op jit(solution)/shard_map/reduce_scatter | solution.py:439
  883.5 364.5 %reduce-scatter.31.cloned.1.call-start = ((), (), s32[]{:S(2)}) async-start(), calls=%async_computation.32 | async-start | bytes 1105920 | tf_op jit(solution)/shard_map/reduce_scatter | solution.py:449
  925.7 355.3 %reduce-scatter.25.cloned.1.call-start = ((), (), s32[]{:S(2)}) async-start(), calls=%async_computation.29 | async-start | bytes 1966080 | tf_op jit(solution)/shard_map/reduce_scatter | solution.py:202
  929.7 390.4 %all-gather.62.cloned.1.call-start = ((), (), s32[]{:S(2)}) async-start(), calls=%async_computation.47 | async-start | bytes 2949120 | tf_op jit(solution)/shard_map/all_gather | solution.py:421
  930.2 428.9 %all-gather.60.cloned.1.call-start = ((), (), s32[]{:S(2)}) async-start(), calls=%async_computation.46 | async-start | bytes 2949120 | tf_op jit(solution)/shard_map/all_gather | solution.py:421
  978.5 419.8 %all-gather.58.cloned.1.call-start = ((), (), s32[]{:S(2)}) async-start(), calls=%async_computation.45 | async-start | bytes 2949120 | tf_op jit(solution)/shard_map/all_gather | solution.py:421
  1028.4 409.2 %all-gather.56.cloned.1.call-start = ((), (), s32[]{:S(2)}) async-start(), calls=%async_computation.44 | async-start | bytes 2949120 | tf_op jit(solution)/shard_map/all_gather | solution.py:421
  1078.4 462.2 %reduce-scatter.27.cloned.1.call-start = ((), (), s32[]{:S(2)}) async-start(), calls=%async_computation.30 | async-start | bytes 1622016 | tf_op jit(solution)/shard_map/reduce_scatter | solution.py:439
  (61 other events, 1803.9 us)
Sparse Core Ops, SparseCore 0:
  29.0 31.8 all-gather.31
  64.3 55.5 all-gather.43
  128.1 31.3 all-gather.33
  161.5 49.9 all-gather.45
  213.5 48.7 all-gather.47
  273.0 44.8 reduce-scatter.14
  321.1 30.8 all-gather.35
  354.8 55.4 all-gather.49
  417.9 31.1 all-gather.37
  451.1 49.9 all-gather.51
  503.3 48.7 all-gather.53
  554.4 30.9 all-gather.39
  607.4 46.0 reduce-scatter.18
  657.3 46.0 reduce-scatter.16
  743.6 30.5 reduce-scatter.20
  778.4 32.1 all-gather.41
  833.1 46.0 reduce-scatter.22
  881.4 47.6 reduce-scatter.40
  931.4 47.0 reduce-scatter.38
  981.2 47.0 reduce-scatter.36
  1031.3 47.0 reduce-scatter.34
  1081.2 31.6 reduce-scatter.32
  1118.2 96.2 reduce-scatter.28
  1216.7 31.3 reduce-scatter.30
  1251.6 29.3 reduce-scatter.24
  1282.7 37.3 all-gather.61
  1321.8 37.3 all-gather.59
  1361.0 37.3 all-gather.57
  1400.2 37.3 all-gather.55
  1442.7 97.9 reduce-scatter.26

commit v2 on v1

--- a/solution.py
+++ b/solution.py
@@ -24,7 +24,7 @@
 TN = (((0,), (0,)), ((), ()))
 
 
-def visit_blocks(length, span, one_block):
+def visit_blocks(length, span, one_block, midway=None):
     full = span // ROWS
     for i in range(min(full - 1, length // ROWS)):
         one_block(i * ROWS, 0, (i + 1) * ROWS)
@@ -34,7 +34,13 @@
         one_block(start, pl.multiple_of(start + ROWS - span, ROWS), span)
         return carry
 
-    lax.fori_loop(full - 1, length // ROWS, step, 0)
+    middle = (full + length // ROWS) // 2
+    if midway is None:
+        lax.fori_loop(full - 1, length // ROWS, step, 0)
+    else:
+        lax.fori_loop(full - 1, middle, step, 0)
+        midway()
+        lax.fori_loop(middle, length // ROWS, step, 0)
 
 
 def fill_mask(mask_ref, segr_ref, segc_ref, start, low, width):
@@ -56,7 +62,23 @@
         parts_ref[h] = part * jnp.bfloat16(0.125) if h < heads else part
 
 
-def attn_fwd_kernel(heads, span, qkv_ref, segr_ref, segc_ref, line_ref, out_ref, lse_ref, parts_ref, mixed_ref, slab_ref, mask_ref):
+def attn_fwd_kernel(heads, span, spread, *refs):
+    qkv_ref, segr_ref, segc_ref, line_ref = refs[:4]
+    midway = None
+    if spread:
+        rows_ref, out_ref, lse_ref, gathered_ref = refs[4:8]
+        wires = Wires(*refs[12:])
+        place = plane_place()
+        greet(*plane_peers(place))
+        gathered_ref[place[0], place[1]] = rows_ref[...].astype(jnp.bfloat16)
+        first = plane_gather_start(wires, gathered_ref, place)
+        second = []
+        midway = lambda: second.extend(plane_gather_forward(wires, gathered_ref, place, first))
+        refs = refs[8:12]
+    else:
+        out_ref, lse_ref = refs[4:6]
+        refs = refs[6:10]
+    parts_ref, mixed_ref, slab_ref, mask_ref = refs
     length = qkv_ref.shape[0]
     fill_slab(slab_ref, line_ref, heads, span)
     split_heads(qkv_ref, parts_ref, heads)
@@ -80,8 +102,11 @@
 
         lax.fori_loop(0, heads, one_head, 0)
 
-    visit_blocks(length, span, one_block)
+    visit_blocks(length, span, one_block, midway)
     out_ref[...] = jnp.concatenate([mixed_ref[h] for h in range(heads)], axis=1)
+    if spread:
+        plane_gather_finish(wires, gathered_ref, place, first, second)
+        wires.finish()
 
 
 def attn_bwd_kernel(heads, span, qkv_ref, segr_ref, segc_ref, line_ref, lse_ref, grad_ref, out_ref, band_ref,
@@ -140,23 +165,28 @@
     return [pl.BlockSpec(memory_space=pltpu.VMEM)] * count
 
 
+def attend_scratch(heads, length, span):
+    return [
+        pltpu.VMEM((3 * heads, length, HD), jnp.bfloat16),
+        pltpu.VMEM((heads, length, HD), jnp.bfloat16),
+        pltpu.VMEM((heads, ROWS, span), jnp.float32),
+        pltpu.VMEM((ROWS, span), jnp.float32),
+    ]
+
+
 def attend(qkv, seg_row, seg_col, line):
     length, width = qkv.shape
     heads, span = line.shape
     return pl.pallas_call(
-        functools.partial(attn_fwd_kernel, heads, span),
+        functools.partial(attn_fwd_kernel, heads, span, False),
         out_shape=(
             jax.ShapeDtypeStruct((length, heads * HD), jnp.bfloat16),
             jax.ShapeDtypeStruct((heads, length, 1), jnp.float32),
         ),
         in_specs=vmem(4),
         out_specs=tuple(vmem(2)),
-        scratch_shapes=[
-            pltpu.VMEM((3 * heads, length, HD), jnp.bfloat16),
-            pltpu.VMEM((heads, length, HD), jnp.bfloat16),
-            pltpu.VMEM((heads, ROWS, span), jnp.float32),
-            pltpu.VMEM((ROWS, span), jnp.float32),
-        ],
+        scratch_shapes=attend_scratch(heads, length, span),
+        cost_estimate=cost(15.0),
         name="attend",
     )(qkv, seg_row, seg_col, line)
 
@@ -182,40 +212,324 @@
             pltpu.VMEM((ROWS, span), jnp.float32),
             pltpu.VMEM((heads, ROWS, span), jnp.float32),
         ],
+        cost_estimate=cost(21.0),
         name="attend_back",
     )(qkv, seg_row, seg_col, line, lse, grad)
 
 
-def plane_gather(values):
-    return lax.all_gather(values, ("seq", "tensor"), axis=0, tiled=True)
-
-
-def plane_sum(values):
-    return lax.psum_scatter(values, ("seq", "tensor"), scatter_dimension=0, tiled=True)
-
-
-def seq_gather(values):
-    return lax.all_gather(values, "seq", axis=0, tiled=True)
-
-
-def seq_sum(values):
-    return lax.psum_scatter(values, "seq", scatter_dimension=0, tiled=True)
-
-
-def heads_to_tokens(values):
-    return lax.all_to_all(values, "seq", split_axis=0, concat_axis=1, tiled=True)
-
-
-def tokens_to_heads(values):
-    return lax.all_to_all(values, "seq", split_axis=1, concat_axis=0, tiled=True)
+MESH_ID = pl.DeviceIdType.MESH
+
+
+class Wires:
+    def __init__(self, send, recv):
+        self.send, self.recv, self.next, self.started = send, recv, 0, []
+
+    def copy(self, src, dst, where):
+        one = pltpu.make_async_remote_copy(
+            src_ref=src, dst_ref=dst, send_sem=self.send.at[self.next], recv_sem=self.recv.at[self.next],
+            device_id=where, device_id_type=MESH_ID,
+        )
+        self.next += 1
+        one.start()
+        self.started.append(one)
+        return one
+
+    def finish(self):
+        for one in self.started:
+            one.wait_send()
+
+
+def plane_place():
+    me = lax.axis_index("seq")
+    core = lax.axis_index("tensor")
+    near, far = me + 1 - 2 * lax.rem(me, 2), lax.rem(me + 2, 4)
+    cross = lax.rem(near + 2, 4)
+    return me, core, near, far, cross
+
+
+def greet(*places):
+    barrier = pltpu.get_barrier_semaphore()
+    for where in places:
+        pl.semaphore_signal(barrier, inc=1, device_id=where, device_id_type=MESH_ID)
+    pl.semaphore_wait(barrier, len(places))
+
+
+def seq_gather_start(wires, ref, place):
+    me, core, near, far, cross = place
+    mine = ref.at[me]
+    return wires.copy(mine, mine, {"seq": near}), wires.copy(mine, mine, {"seq": far})
+
+
+def seq_gather_forward(wires, ref, place, first):
+    me, core, near, far, cross = place
+    half = ref.shape[1] // 2
+    first[0].wait_recv()
+    upper = ref.at[near, pl.ds(0, half)]
+    one = wires.copy(upper, upper, {"seq": far})
+    first[1].wait_recv()
+    lower = ref.at[far, pl.ds(half, half)]
+    return one, wires.copy(lower, lower, {"seq": near})
+
+
+def plane_gather_start(wires, ref, place):
+    me, core, near, far, cross = place
+    mine = ref.at[me, core]
+    return (
+        wires.copy(mine, mine, {"seq": near}),
+        wires.copy(mine, mine, {"seq": far}),
+        wires.copy(mine, mine, {"tensor": 1 - core}),
+    )
+
+
+def plane_gather_forward(wires, ref, place, first):
+    me, core, near, far, cross = place
+    half = ref.shape[2] // 2
+    partner = {"tensor": 1 - core}
+    first[0].wait_recv()
+    upper = ref.at[near, core, pl.ds(0, half)]
+    one = wires.copy(upper, upper, {"seq": far})
+    first[1].wait_recv()
+    lower = ref.at[far, core, pl.ds(half, half)]
+    two = wires.copy(lower, lower, {"seq": near})
+    block = ref.at[near, core]
+    three = wires.copy(block, block, partner)
+    block = ref.at[far, core]
+    four = wires.copy(block, block, partner)
+    return one, two, three, four
+
+
+def plane_gather_finish(wires, ref, place, first, second):
+    me, core, near, far, cross = place
+    half = ref.shape[2] // 2
+    partner = {"tensor": 1 - core}
+    second[0].wait_recv()
+    upper = ref.at[cross, core, pl.ds(0, half)]
+    one = wires.copy(upper, upper, partner)
+    second[1].wait_recv()
+    lower = ref.at[cross, core, pl.ds(half, half)]
+    two = wires.copy(lower, lower, partner)
+    for other in (first[2], second[2], second[3], one, two):
+        other.wait_recv()
+
+
+def wide(values):
+    return values.astype(jnp.float32)
+
+
+def cross_sum(wires, place, total_of, out_refs):
+    me, core, near, far, cross = place
+    cross_ref, near_ref, far_ref, cross_in, near_in, far_in = out_refs
+    half = near_ref.shape[0] // 2
+    top, bottom = pl.ds(0, half), pl.ds(half, half)
+    cross_ref[...] = total_of(cross).astype(cross_ref.dtype)
+    to_near = wires.copy(cross_ref.at[top], cross_in.at[top], {"seq": near})
+    to_far = wires.copy(cross_ref.at[bottom], cross_in.at[bottom], {"seq": far})
+    near_ref[...] = total_of(near).astype(near_ref.dtype)
+    near_one = wires.copy(near_ref.at[top], near_in.at[top], {"seq": near})
+    far_ref[...] = total_of(far).astype(far_ref.dtype)
+    far_one = wires.copy(far_ref.at[bottom], far_in.at[bottom], {"seq": far})
+    own = total_of(me)
+    to_near.wait_recv()
+    far_ref[top, :] = (wide(far_ref[top, :]) + wide(cross_in[top, :])).astype(far_ref.dtype)
+    far_two = wires.copy(far_ref.at[top], far_in.at[top], {"seq": far})
+    to_far.wait_recv()
+    near_ref[bottom, :] = (wide(near_ref[bottom, :]) + wide(cross_in[bottom, :])).astype(near_ref.dtype)
+    near_two = wires.copy(near_ref.at[bottom], near_in.at[bottom], {"seq": near})
+    for one in (near_one, far_one, far_two, near_two):
+        one.wait_recv()
+    return own + wide(near_in[...]) + wide(far_in[...])
+
+
+def plane_sum(wires, place, part_ref, partner_in, out_refs):
+    me, core, near, far, cross = place
+    arrivals = {}
+    for name, spot in (("cross", cross), ("near", near), ("far", far), ("me", me)):
+        arrivals[name] = wires.copy(part_ref.at[spot, 1 - core], partner_in.at[spot], {"tensor": 1 - core})
+    order = iter(("cross", "near", "far", "me"))
+
+    def total_of(spot):
+        arrivals[next(order)].wait_recv()
+        return wide(part_ref[spot, core]) + wide(partner_in[spot])
+
+    return cross_sum(wires, place, total_of, out_refs)
+
+
+def sum_scratch(piece, width):
+    return [pltpu.VMEM((piece, width), jnp.bfloat16)] * 6
+
+
+def sems(count):
+    return [pltpu.SemaphoreType.DMA((count,)), pltpu.SemaphoreType.DMA((count,))]
+
+
+def plane_peers(place):
+    me, core, near, far, cross = place
+    return {"seq": near}, {"seq": far}, {"tensor": 1 - core}
+
+
+def norm_of(values, gain_vec):
+    return values * lax.rsqrt(jnp.mean(values * values, axis=-1, keepdims=True) + epsilon) * gain_vec
 
 
 def norm_back(values, gain_vec, grad):
     inverse = lax.rsqrt(jnp.mean(values * values, axis=-1, keepdims=True) + epsilon)
     unit = values * inverse
     scaled_grad = grad * gain_vec
-    gain_grad = jnp.sum(grad * unit, axis=0)
+    gain_grad = jnp.sum(grad * unit, axis=0, keepdims=True)
     return inverse * (scaled_grad - unit * jnp.mean(scaled_grad * unit, axis=-1, keepdims=True)), gain_grad
+
+
+def dot(left, right):
+    return jnp.dot(left, right, preferred_element_type=jnp.float32)
+
+
+def dot_nt(left, right):
+    return lax.dot_general(left, right, NT, preferred_element_type=jnp.float32)
+
+
+def dot_tn(left, right):
+    return lax.dot_general(left, right, TN, preferred_element_type=jnp.float32)
+
+
+def project_steps(place, x_ref, gain_ref, w_ref, normed_ref, qkv_ref, wires):
+    me, core, near, far, cross = place
+    normed_ref[me] = norm_of(x_ref[...], gain_ref[...]).astype(jnp.bfloat16)
+    first = seq_gather_start(wires, normed_ref, place)
+    qkv_ref[me] = dot(normed_ref[me], w_ref[...]).astype(jnp.bfloat16)
+    second = seq_gather_forward(wires, normed_ref, place, first)
+    qkv_ref[near] = dot(normed_ref[near], w_ref[...]).astype(jnp.bfloat16)
+    qkv_ref[far] = dot(normed_ref[far], w_ref[...]).astype(jnp.bfloat16)
+    second[0].wait_recv()
+    second[1].wait_recv()
+    qkv_ref[cross] = dot(normed_ref[cross], w_ref[...]).astype(jnp.bfloat16)
+
+
+def project_kernel(x_ref, gain_ref, w_ref, routes_ref, normed_ref, qkv_ref, routes_all_ref, send, recv):
+    place = plane_place()
+    me, core, near, far, cross = place
+    wires = Wires(send, recv)
+    greet({"seq": near}, {"seq": far}, {"seq": cross})
+    routes_all_ref[me] = routes_ref[...]
+    picks = [wires.copy(routes_ref, routes_all_ref.at[me], {"seq": spot}) for spot in (near, far, cross)]
+    project_steps(place, x_ref, gain_ref, w_ref, normed_ref, qkv_ref, wires)
+    for one in picks:
+        one.wait_recv()
+    wires.finish()
+
+
+def sum_project_kernel(part_ref, base_ref, gain_ref, w_ref, x_ref, normed_ref, qkv_ref, partner_in, *rest):
+    out_refs, (send, recv) = rest[:6], rest[6:]
+    place = plane_place()
+    wires = Wires(send, recv)
+    greet(*plane_peers(place))
+    x_ref[...] = base_ref[...] + plane_sum(wires, place, part_ref, partner_in, out_refs)
+    project_steps(place, x_ref, gain_ref, w_ref, normed_ref, qkv_ref, wires)
+    wires.finish()
+
+
+def sum_kernel(part_ref, base_ref, x_ref, partner_in, *rest):
+    out_refs, (send, recv) = rest[:6], rest[6:]
+    place = plane_place()
+    wires = Wires(send, recv)
+    greet(*plane_peers(place))
+    x_ref[...] = base_ref[...] + plane_sum(wires, place, part_ref, partner_in, out_refs)
+    wires.finish()
+
+
+def merge_kernel(mixed_ref, base_ref, w_ref, gain_ref, merged_ref, middle_ref, tokens_ref, send, recv):
+    place = plane_place()
+    me, core, near, far, cross = place
+    wires = Wires(send, recv)
+    greet({"seq": near}, {"seq": far}, {"seq": cross}, {"tensor": 1 - core})
+    copies = [wires.copy(mixed_ref.at[spot], merged_ref.at[me], {"seq": spot}) for spot in (cross, near, far)]
+    merged_ref[me] = mixed_ref[me]
+    total = base_ref[...] + dot(mixed_ref[me], w_ref[me])
+    for spot, one in ((near, copies[1]), (far, copies[2]), (cross, copies[0])):
+        one.wait_recv()
+        total = total + dot(merged_ref[spot], w_ref[spot])
+    middle_ref[...] = total
+    tokens_ref[me, core] = norm_of(total, gain_ref[...]).astype(jnp.bfloat16)
+    first = plane_gather_start(wires, tokens_ref, place)
+    second = plane_gather_forward(wires, tokens_ref, place, first)
+    plane_gather_finish(wires, tokens_ref, place, first, second)
+    wires.finish()
+
+
+def split_kernel(part_ref, middle_ref, gain_ref, grad_ref, w_ref, middle_grad_ref, out_grad_ref, gain_grad_ref, mixed_grad_ref,
+                 outgoing, partner_in, *rest):
+    out_refs, (send, recv) = rest[:6], rest[6:]
+    place = plane_place()
+    me, core, near, far, cross = place
+    wires = Wires(send, recv)
+    greet({"seq": near}, {"seq": far}, {"seq": cross}, {"tensor": 1 - core})
+    normed_grad = plane_sum(wires, place, part_ref, partner_in, out_refs)
+    part, gain_grad_ref[...] = norm_back(middle_ref[...], gain_ref[...], normed_grad)
+    middle_grad = grad_ref[...] + part
+    middle_grad_ref[...] = middle_grad
+    out_grad_ref[...] = middle_grad.astype(jnp.bfloat16)
+    copies = []
+    for spot in (cross, near, far):
+        outgoing[spot] = dot_nt(out_grad_ref[...], w_ref[spot]).astype(jnp.bfloat16)
+        copies.append(wires.copy(outgoing.at[spot], mixed_grad_ref.at[me], {"seq": spot}))
+    mixed_grad_ref[me] = dot_nt(out_grad_ref[...], w_ref[me]).astype(jnp.bfloat16)
+    for one in copies:
+        one.wait_recv()
+    wires.finish()
+
+
+def input_grad_kernel(spread, qkv_grad_ref, w_ref, x_ref, gain_ref, middle_grad_ref, *rest):
+    grad_ref, gain_grad_ref = rest[:2]
+    rows_ref = rest[2] if spread else None
+    rest = rest[3:] if spread else rest[2:]
+    out_refs, (send, recv) = rest[:6], rest[6:]
+    place = plane_place()
+    me, core, near, far, cross = place
+    wires = Wires(send, recv)
+    greet(*plane_peers(place)[: 3 if spread else 2])
+    normed_grad = cross_sum(wires, place, lambda spot: dot_nt(qkv_grad_ref[spot], w_ref[...]), out_refs)
+    part, gain_grad_ref[...] = norm_back(x_ref[...], gain_ref[...], normed_grad)
+    grad = middle_grad_ref[...] + part
+    grad_ref[...] = grad
+    if spread:
+        rows_ref[me, core] = grad.astype(jnp.bfloat16)
+        first = plane_gather_start(wires, rows_ref, place)
+        second = plane_gather_forward(wires, rows_ref, place, first)
+        plane_gather_finish(wires, rows_ref, place, first, second)
+    wires.finish()
+
+
+def comm_call(kernel, name, number, time, outs, scratch, wire_count, *operands):
+    return pl.pallas_call(
+        kernel,
+        out_shape=tuple(outs),
+        in_specs=vmem(len(operands)),
+        out_specs=tuple(vmem(len(outs))),
+        scratch_shapes=scratch + sems(wire_count),
+        compiler_params=pltpu.CompilerParams(collective_id=number, has_side_effects=True),
+        cost_estimate=cost(time),
+        name=name,
+    )(*operands)
+
+
+def cost(time):
+    return pl.CostEstimate(flops=0, bytes_accessed=int(time * 3e6), transcendentals=0)
+
+
+def low_array(*shape):
+    return jax.ShapeDtypeStruct(shape, jnp.bfloat16)
+
+
+def wide_array(*shape):
+    return jax.ShapeDtypeStruct(shape, jnp.float32)
+
+
+def attend_gather(qkv, seg_row, seg_col, line, rows, n_tensor):
+    length, width = qkv.shape
+    heads, span = line.shape
+    piece, depth = rows.shape
+    outs = [low_array(length, heads * HD), wide_array(heads, length, 1), low_array(length // piece, n_tensor, piece, depth)]
+    return comm_call(functools.partial(attn_fwd_kernel, heads, span, True), "attend_gather", 6, 16.0, outs,
+                     attend_scratch(heads, length, span), 9, qkv, seg_row, seg_col, line, rows)
 
 
 def gelu_parts(values):
@@ -223,18 +537,6 @@
     inner = jnp.tanh(0.7978845608028654 * values * (1.0 + cubic))
     slope = 0.5 * (1.0 + inner) + 0.5 * values * (1.0 - inner * inner) * 0.7978845608028654 * (1.0 + 3.0 * cubic)
     return 0.5 * values * (1.0 + inner), slope
-
-
-def dot(left, right):
-    return jnp.dot(left, right, preferred_element_type=jnp.float32)
-
-
-def dot_nt(left, right):
-    return lax.dot_general(left, right, NT, preferred_element_type=jnp.float32)
-
-
-def dot_tn(left, right):
-    return lax.dot_general(left, right, TN, preferred_element_type=jnp.float32)
 
 
 def body(
@@ -305,15 +607,15 @@
         qkv = lax.all_gather(own_qkv[layer], "dp", axis=0, tiled=True)
         out = lax.all_gather(own_out[layer], ("dp", "seq", "tensor"), axis=0)
         out = out.reshape(n_dp, n_plane, shard, out_columns)
-        return qkv, jnp.moveaxis(out, 1, 2).reshape(width, width)
+        return qkv, jnp.moveaxis(out, 1, 2).reshape(n_seq, head_width, width)
 
     def expert_weights(layer):
         up = lax.all_gather(own_up[layer], "dp", axis=0, tiled=True)
         down = lax.all_gather(own_down[layer], "dp", axis=0, tiled=True)
         return up, down
 
-    routes_all = lax.all_gather(routes, "seq", axis=0)
-    routes_all = jnp.moveaxis(routes_all, 0, 1).reshape(LAYERS, n_seq, group_rows, -1)
+    assert n_seq == 4 and n_tensor == 2
+    routes_own = routes.reshape(-1, 128)
     seg_row = segments
     seg_col = segments.reshape(length, 1)
     bucket_line = distance_bucket[length // 2 - 1 :: -1][: length // 2]
@@ -325,7 +627,7 @@
         lax.iota(jnp.int32, group_rows)[:, None] < lax.iota(jnp.int32, group_rows)[None, :]
     ).astype(low)
 
-    def routing(layer):
+    def routing(layer, routes_all):
         layer_routes = routes_all[layer]
         mine = jnp.any(layer_routes == seq_index, axis=-1)
         slot = dot(mine.astype(low), strict_upper).astype(jnp.int32)
@@ -350,17 +652,34 @@
     for layer in range(LAYERS):
         qkv_weight, out_weight = attention_weights(layer)
         up, down = expert_weights(layer)
-        normed = scaled(current, gains_one[layer]).astype(low)
-        normed_all = seq_gather(normed)
-        qkv = dot(normed_all, qkv_weight).astype(low)
+        gain_one, gain_two = gains_one[layer][None], gains_two[layer][None]
+        outs = [low_array(n_seq, piece, width), low_array(n_seq, piece, 3 * head_width)]
+        if layer == 0:
+            outs.append(jax.ShapeDtypeStruct((n_seq,) + routes_own.shape, jnp.int32))
+            normed_all, qkv, routes_all = comm_call(
+                project_kernel, "project", 1, 16.0, outs, [], 7, current, gain_one, qkv_weight, routes_own
+            )
+            routes_all = routes_all.reshape((n_seq,) + routes.shape)
+            routes_all = jnp.moveaxis(routes_all, 0, 1).reshape(LAYERS, n_seq, group_rows, -1)
+        else:
+            current, normed_all, qkv = comm_call(
+                sum_project_kernel, "sum_project", 2, 32.0, [wide_array(piece, width)] + outs,
+                [pltpu.VMEM((n_seq, piece, width), low)] + sum_scratch(piece, width), 14, part, middle, gain_one, qkv_weight
+            )
+        qkv = qkv.reshape(length, 3 * head_width)
         own_table = lax.dynamic_slice_in_dim(tables[layer], seq_index * local_heads, local_heads, 1)
         line = jnp.dot(own_table.T, line_hot, precision=highest_precision)
-        mixed, log_total = attend(qkv, seg_row, seg_col, line)
-        merged = heads_to_tokens(mixed)
-        middle = current + dot(merged, out_weight)
-        normed_two = scaled(middle, gains_two[layer]).astype(low)
-        tokens = plane_gather(normed_two)
-        hot, chosen = routing(layer)
+        if layer == 0:
+            mixed, log_total, grad_rows = attend_gather(qkv, seg_row, seg_col, line, grad, n_tensor)
+        else:
+            mixed, log_total = attend(qkv, seg_row, seg_col, line)
+        merged, middle, tokens = comm_call(
+            merge_kernel, "merge", 3, 21.0,
+            [low_array(n_seq, piece, head_width), wide_array(piece, width), low_array(n_seq, n_tensor, piece, width)], [], 12,
+            mixed.reshape(n_seq, piece, head_width), current, out_weight, gain_two
+        )
+        tokens = tokens.reshape(n_plane * piece, width)
+        hot, chosen = routing(layer, routes_all)
         router_logits = dot(tokens, routers[layer])
         router_logits = jnp.where(chosen, router_logits, negative)
         raised = jnp.exp(router_logits - jnp.max(router_logits, axis=1, keepdims=True))
@@ -372,18 +691,22 @@
         pre = pre.astype(low)
         result = dot_nt(hidden, down).astype(low)
         part = (own_share * from_slots(hot, result)).astype(low)
-        following = middle + plane_sum(part).astype(jnp.float32)
+        part = part.reshape(n_seq, n_tensor, piece, width)
         saved.append(
             (current, normed_all, qkv, line, log_total, merged, middle, tokens, hot, shares, own_share, slots, pre, hidden,
              qkv_weight, out_weight, up, down)
         )
-        current = following
-
+
+    (block_output,) = comm_call(
+        sum_kernel, "sum_last", 4, 16.0, [wide_array(piece, width)], [pltpu.VMEM((n_seq, piece, width), low)] + sum_scratch(piece, width),
+        10, part, middle
+    )
     results = [None] * LAYERS
     for layer in range(LAYERS - 1, -1, -1):
         (layer_in, normed_all, qkv, line, log_total, merged, middle, tokens, hot, shares, own_share, slots, pre, hidden,
          qkv_weight, out_weight, up, down) = saved[layer]
-        grad_rows = plane_gather(grad.astype(low)).astype(jnp.float32)
+        gain_one, gain_two = gains_one[layer][None], gains_two[layer][None]
+        grad_rows = grad_rows.reshape(n_plane * piece, width).astype(jnp.float32)
         result_grad = to_slots(hot, (own_share * grad_rows).astype(low))
         hidden_grad = dot(result_grad, down)
         down_grad = dot_tn(result_grad, hidden)
@@ -398,18 +721,25 @@
         logit_grad = (token_pair * (own_hot[None, :] - shares)).astype(low)
         part = from_slots(hot, slot_grad) + dot_nt(logit_grad, routers[layer])
         router_grad = dot_tn(tokens, logit_grad)
-        normed_two_grad = plane_sum(part.astype(low)).astype(jnp.float32)
-        middle_part, gain_two_grad = norm_back(middle, gains_two[layer], normed_two_grad)
-        middle_grad = grad + middle_part
-        out_grad = middle_grad.astype(low)
-        out_weight_grad = dot_tn(merged, out_grad)
-        merged_grad = dot_nt(out_grad, out_weight).astype(low)
-        mixed_grad = tokens_to_heads(merged_grad)
-        qkv_grad, band = attend_back(qkv, seg_row, seg_col, line, log_total, mixed_grad)
-        qkv_weight_grad = dot_tn(normed_all, qkv_grad)
-        normed_grad = seq_sum(dot_nt(qkv_grad, qkv_weight).astype(low)).astype(jnp.float32)
-        input_part, gain_one_grad = norm_back(layer_in, gains_one[layer], normed_grad)
-        grad = middle_grad + input_part
+        part = part.astype(low).reshape(n_seq, n_tensor, piece, width)
+        middle_grad, out_grad, gain_two_grad, mixed_grad = comm_call(
+            split_kernel, "split", 5, 22.0,
+            [wide_array(piece, width), low_array(piece, width), wide_array(1, width), low_array(n_seq, piece, head_width)],
+            [pltpu.VMEM((n_seq, piece, head_width), low), pltpu.VMEM((n_seq, piece, width), low)] + sum_scratch(piece, width), 13,
+            part, middle, gain_two, grad, out_weight
+        )
+        out_weight_grad = jnp.einsum("gtd,te->gde", merged, out_grad, preferred_element_type=jnp.float32).reshape(width, width)
+        qkv_grad, band = attend_back(qkv, seg_row, seg_col, line, log_total, mixed_grad.reshape(length, head_width))
+        qkv_weight_grad = dot_tn(normed_all.reshape(length, width), qkv_grad)
+        spread = layer > 0
+        outs = [wide_array(piece, width), wide_array(1, width)]
+        outs += [low_array(n_seq, n_tensor, piece, width)] if spread else []
+        outs = comm_call(
+            functools.partial(input_grad_kernel, spread), "input_grad_spread" if spread else "input_grad", 7 + spread, 32.0 if spread else 16.0,
+            outs, sum_scratch(piece, width), 15, qkv_grad.reshape(n_seq, piece, -1), qkv_weight, layer_in, gain_one, middle_grad
+        )
+        grad, gain_one_grad = outs[:2]
+        grad_rows = outs[2] if spread else None
         table_grad = jnp.dot(line_hot, band.T, precision=highest_precision)
         table_grad = lax.dynamic_update_slice_in_dim(
             jnp.zeros((bucket_count, HEADS), jnp.float32), table_grad, seq_index * local_heads, 1
@@ -453,7 +783,7 @@
         results[layer] = (gain_one_total, qkv_total, out_total, table_total, gain_two_total, router_total, up_total, down_total)
 
     stacked = [jnp.stack([results[layer][member] for layer in range(LAYERS)]) for member in range(8)]
-    return (current[None], grad[None]) + tuple(stacked)
+    return (block_output[None], grad[None]) + tuple(stacked)
 
 
 def solution(mesh):

time: 1570 us -> 1080 us (0.69)
  waiting for transfers between devices: 1050 us -> 386 us
  Pallas kernels: 71.8 us -> 334 us
  blocking collectives: 129 us -> 101 us
  other arithmetic: 57.1 us -> 32.5 us
  local copies, waits for them, and re-layouts: 76.1 us -> 60.1 us
    pallas_call x2 -> x11, Pallas kernels: 30.2 us -> 293 us  [the longest x10 277 us: comm_call(): pl.pallas_call(kernel, out_shape=tuple(outs), in_specs=vmem(len(operands)...]
    reduce_scatter x6 -> x0, waiting for transfers between devices: 181 us -> none  [the longest x4 139 us: plane_sum(): lax.psum_scatter(values, ('seq', 'tensor'), scatter_dimension=0, tiled=True)]
    reduce_scatter x4, waiting for transfers between devices: 148 us -> 11.6 us  [body(): lax.psum_scatter(piece_grad.astype(low), 'dp', scatter_dimension=0, tiled...]
    all_gather x6 -> x0, waiting for transfers between devices: 104 us -> none  [the longest x4 97.6 us: plane_gather(): return lax.all_gather(values, ('seq', 'tensor'), axis=0, tiled=True)]
    all_gather x2, waiting for transfers between devices: 93.5 us -> 0.01 us  [expert_weights(): up = lax.all_gather(own_up[layer], 'dp', axis=0, tiled=True)]
    all_gather x2, waiting for transfers between devices: 66.1 us -> 0.02 us  [attention_weights(): out = lax.all_gather(own_out[layer], ('dp', 'seq', 'tensor'), axis=0)]
    all_gather x2, waiting for transfers between devices: 88.1 us -> 32.8 us  [expert_weights(): down = lax.all_gather(own_down[layer], 'dp', axis=0, tiled=True)]
    all_to_all x2 -> x0, blocking collectives: 20.1 us -> none  [tokens_to_heads(): lax.all_to_all(values, 'seq', split_axis=1, concat_axis=0, tiled=True)]
  transfers between devices with their start and end apart: 32 -> 18, of which waited for: 27 -> 10; matrix products, arithmetic and copies ran while one was open for 12% -> 19% of each run, Pallas kernels for 3% -> 31%
where the time goes in v2:
time: 1080 us; the launch traced here: 1070 us
  waiting for transfers between devices  386 us (36%)
  Pallas kernels  334 us (31%)
  matrix products  139 us (13%)
  blocking collectives  101 us (9%)
  local copies, waits for them, and re-layouts  60.1 us (6%)
  other arithmetic  32.5 us (3%)
  between operations  15.9 us (1%)
    pallas_call x10, Pallas kernels, comm_call(): pl.pallas_call(kernel, out_shape=tuple(outs), in_specs=vmem(len(operands)...  277 us
    reduce_scatter x2, waiting for transfers between devices, body(): lax.psum_scatter(both.reshape((n_dp * n_plane,) + both.shape[2:]), ('dp',...  172 us
    all_gather x4, waiting for transfers between devices, body(): lax.all_gather(piece_grad, 'seq', axis=0).astype(jnp.float32)  131 us
    all_gather x2, blocking collectives, attention_weights(): qkv = lax.all_gather(own_qkv[layer], 'dp', axis=0, tiled=True)  44.7 us
    dot_general x8, matrix products, dot(): return jnp.dot(left, right, preferred_element_type=jnp.float32)  44.5 us
    pallas_call x2, Pallas kernels, attend_back(): pl.pallas_call(functools.partial(attn_bwd_kernel, heads, span), out_shape...  41.9 us
    reduce_scatter x2, waiting for transfers between devices, body(): lax.psum_scatter(qkv_weight_grad.astype(low), ('dp', 'tensor'), scatter_d...  36.4 us
    dot_general x8, matrix products, dot_tn(): return lax.dot_general(left, right, TN, preferred_element_type=jnp.float32)  35.2 us
  transfers between devices with their start and end apart: 18, of which 10 were waited for; matrix products, arithmetic and copies ran while one was open for 19% of the time, Pallas kernels for 31%

profile of v2, /device:TPU:0, one launch (start us, length us, event | category | flops | bytes accessed | tf_op | source)
XLA Modules:
  0.0 1071.3 jit_solution(14743477314553453412)
XLA Ops:
  17.6 14.9 %all-gather.13 = bf16[4,2,1248]{2,1,0:T(2,128)(2,1)S(1)} all-gather(bf16[1,2,1248]{2,1,0:T(2,128)(2,1)S(1)} %bitcast.267), channel_id=2, replica_groups=mesh['dp'=4,'seq'=4,'tensor'=2] {'dp'}, dimensions={0}, use_global_device_ids=true | all-gather | bytes 24960 | tf_op jit(solution)/shard_map/all_gather | solution.py:584
  42.7 23.9 %all_gather.74.w_ref = bf16[768,576]{1,0:T(8,128)(2,1)} all-gather(bf16[192,576]{1,0:T(8,128)(2,1)S(1)} %copy.135), channel_id=1, replica_groups=mesh['dp'=4,'seq'=4,'tensor'=2] {'dp'}, dimensions={0}, use_global_device_ids=true | all-gather | bytes 1105920 | tf_op jit(solution)/shard_map/all_gather | solution.py:607
  66.6 17.5 %project.1 = (bf16[4,256,768]{2,1,0:T(8,128)(2,1)}, bf16[4,256,576]{2,1,0:T(8,128)(2,1)}, s32[4,16,128]{2,1,0:T(8,128)}) custom-call(f32[256,768]{1,0:T(8,128)} %bitcast.213, f32[1,768]{1,0:T(1,128)} %slice.144.gain_ref, bf16[768,576]{1,0:T(8,128)(2,1)} %all_gather.74.w_ref, s32[16,128]{1,0:T(8,128)} %reshape.303.routes_ref), custom_call_target="tpu_custom_call" | custom-call | bytes 48000000 | tf_op jit(solution)/shard_map/project/pallas_call | solution.py:502
  94.2 20.9 %all_gather.78.w_ref = bf16[768,576]{1,0:T(8,128)(2,1)} all-gather(bf16[192,576]{1,0:T(8,128)(2,1)S(1)} %copy.145), channel_id=1, replica_groups=mesh['dp'=4,'seq'=4,'tensor'=2] {'dp'}, dimensions={0}, use_global_device_ids=true | all-gather | bytes 1105920 | tf_op jit(solution)/shard_map/all_gather | solution.py:607
  117.5 21.7 %attend_gather.1 = (bf16[1024,192]{1,0:T(8,128)(2,1)}, f32[3,1024,1]{2,1,0:T(8,128)}, bf16[4,2,256,768]{3,2,1,0:T(8,128)(2,1)}) custom-call(bf16[1024,576]{1,0:T(8,128)(2,1)} %bitcast.216, s32[1,1024]{1,0:T(1,128)} %segr_ref.3, s32[1024,1]{1,0:T(8,128)} %copy.140.refs_2_.segc_ref, f32[3,640]{1,0:T(4,128)} %fusion.93.refs_3_.line_ref, f32[256,768]{1,0:T(8,128)} %bitcast.225), custom_call_target="tpu_custom_call" | custom-call | bytes 48000000 | tf_op jit(solution)/shard_map/attend_gather/pallas_call | solution.py:502
  148.4 30.2 %merge.2 = (bf16[4,256,192]{2,1,0:T(8,128)(2,1)}, f32[256,768]{1,0:T(8,128)}, bf16[4,2,256,768]{3,2,1,0:T(8,128)(2,1)}) custom-call(bf16[4,256,192]{2,1,0:T(8,128)(2,1)} %bitcast.248, f32[256,768]{1,0:T(8,128)} %bitcast.214, bf16[4,192,768]{2,1,0:T(8,128)(2,1)} %reshape.312.w_ref, f32[1,768]{1,0:T(1,128)} %slice.153.gain_ref), custom_call_target="tpu_custom_call" | custom-call | bytes 63000000 | tf_op jit(solution)/shard_map/merge/pallas_call | solution.py:502
  196.6 32.8 %all-gather.29.cloned.1.call-done = bf16[1,768,1536]{2,1,0:T(8,128)(2,1)} async-done(((bf16[1,192,1536]{2,1,0:T(8,128)(2,1)}), bf16[1,768,1536]{2,1,0:T(8,128)(2,1)}) %all-gather.29.cloned.1.call-update) | async-done | bytes 2359312 | tf_op jit(solution)/shard_map/all_gather | solution.py:614
  240.4 39.8 %sum_project.1 = (f32[256,768]{1,0:T(8,128)}, bf16[4,256,768]{2,1,0:T(8,128)(2,1)}, bf16[4,256,576]{2,1,0:T(8,128)(2,1)}) custom-call(bf16[4,2,256,768]{3,2,1,0:T(8,128)(2,1)} %multiply_convert_fusion.2.part_ref, f32[256,768]{1,0:T(8,128)} %get-tuple-element.48.base_ref.middle_ref, f32[1,768]{1,0:T(1,128)} %slice.158.gain_ref, bf16[768,576]{1,0:T(8,128)(2,1)} %all_gather.78.w_ref), custom_call_target="tpu_custom_call" | custom-call | bytes 96000000 | tf_op jit(solution)/shard_map/sum_project/pallas_call | solution.py:502
  280.2 15.1 %attend.1 = (bf16[1024,192]{1,0:T(8,128)(2,1)}, f32[3,1024,1]{2,1,0:T(8,128)}) custom-call(bf16[1024,576]{1,0:T(8,128)(2,1)} %bitcast.218, s32[1,1024]{1,0:T(1,128)} %segr_ref.3, s32[1024,1]{1,0:T(8,128)} %copy.140.refs_2_.segc_ref, f32[3,640]{1,0:T(4,128)} %fusion.92.refs_3_.line_ref), custom_call_target="tpu_custom_call" | custom-call | bytes 45000000 | tf_op jit(solution)/shard_map/attend/pallas_call | solution.py:180
  295.3 28.9 %merge.3 = (bf16[4,256,192]{2,1,0:T(8,128)(2,1)}, f32[256,768]{1,0:T(8,128)}, bf16[4,2,256,768]{3,2,1,0:T(8,128)(2,1)}) custom-call(bf16[4,256,192]{2,1,0:T(8,128)(2,1)} %bitcast.249, f32[256,768]{1,0:T(8,128)} %get-tuple-element.51.base_ref.x_ref, bf16[4,192,768]{2,1,0:T(8,128)(2,1)} %reshape.320.w_ref, f32[1,768]{1,0:T(1,128)} %slice.164.gain_ref), custom_call_target="tpu_custom_call" | custom-call | bytes 63000000 | tf_op jit(solution)/shard_map/merge/pallas_call | solution.py:502
  344.9 12.4 %multiply_reduce_fusion.1 = (f32[1024]{0:T(1024)}, bf16[1024,1536]{1,0:T(8,128)(2,1)S(1)}) fusion(f32[1024,1536]{1,0:T(8,128)} %fusion.40, bf16[1024,768]{1,0:T(8,128)(2,1)} %bitcast.280, bf16[1,768,1536]{2,1,0:T(8,128)(2,1)} %all-gather.35.cloned.1.call-done), kind=kOutput, calls=%fused_computation.39 | convolution fusion | flops 2466249728 | bytes 13373440 | tf_op jit(solution)/shard_map/dot_general | solution.py:383
  375.7 31.8 %split.26 = (f32[256,768]{1,0:T(8,128)}, bf16[256,768]{1,0:T(8,128)(2,1)}, f32[1,768]{1,0:T(1,128)}, bf16[4,256,192]{2,1,0:T(8,128)(2,1)}) custom-call(bf16[4,2,256,768]{3,2,1,0:T(8,128)(2,1)} %bitcast.210, f32[256,768]{1,0:T(8,128)} %get-tuple-element.53.base_ref.middle_ref, f32[1,768]{1,0:T(1,128)} %slice.164.gain_ref, f32[256,768]{1,0:T(8,128)} %bitcast.226, ...), custom_call_target="tpu_custom_call" | custom-call | bytes 66000000 | tf_op jit(solution)/shard_map/split/pallas_call | solution.py:502
  407.5 21.1 %attend_back.2 = (bf16[1024,576]{1,0:T(8,128)(2,1)}, f32[3,640]{1,0:T(4,128)}) custom-call(bf16[1024,576]{1,0:T(8,128)(2,1)} %bitcast.219, s32[1,1024]{1,0:T(1,128)} %segr_ref.3, s32[1024,1]{1,0:T(8,128)} %copy.140.refs_2_.segc_ref, f32[3,640]{1,0:T(4,128)} %fusion.92.refs_3_.line_ref, f32[3,1024,1]{2,1,0:T(8,128)} %get-tuple-element.55.lse_ref, ...), custom_call_target="tpu_custom_call" | custom-call | bytes 63000000 | tf_op jit(solution)/shard_map/attend_back/pallas_call | solution.py:197
  428.6 36.4 %input_grad_spread.1 = (f32[256,768]{1,0:T(8,128)}, f32[1,768]{1,0:T(1,128)}, bf16[4,2,256,768]{3,2,1,0:T(8,128)(2,1)}) custom-call(bf16[4,256,576]{2,1,0:T(8,128)(2,1)} %bitcast.241, bf16[768,576]{1,0:T(8,128)(2,1)} %all_gather.78.w_ref, f32[256,768]{1,0:T(8,128)} %get-tuple-element.51.base_ref.x_ref, f32[1,768]{1,0:T(1,128)} %slice.158.gain_ref, ...), custom_call_target="tpu_custom_call" | custom-call | bytes 96000000 | tf_op jit(solution)/shard_map/input_grad_spread/pallas_call | solution.py:502
  468.8 10.9 %multiply_reduce_fusion = (f32[1024]{0:T(1024)}, bf16[1024,1536]{1,0:T(8,128)(2,1)S(1)}) fusion(f32[1024,1536]{1,0:T(8,128)} %fusion.48, bf16[1024,768]{1,0:T(8,128)(2,1)S(1)} %bitcast.282, bf16[1,768,1536]{2,1,0:T(8,128)(2,1)S(1)} %copy-done.38), kind=kOutput, calls=%fused_computation.38 | convolution fusion | flops 2466249728 | bytes 13373440 | tf_op jit(solution)/shard_map/dot_general | solution.py:383
  524.5 30.6 %split.27 = (f32[256,768]{1,0:T(8,128)}, bf16[256,768]{1,0:T(8,128)(2,1)}, f32[1,768]{1,0:T(1,128)}, bf16[4,256,192]{2,1,0:T(8,128)(2,1)}) custom-call(bf16[4,2,256,768]{3,2,1,0:T(8,128)(2,1)} %bitcast.209, f32[256,768]{1,0:T(8,128)} %get-tuple-element.48.base_ref.middle_ref, f32[1,768]{1,0:T(1,128)} %slice.153.gain_ref, ...), custom_call_target="tpu_custom_call" | custom-call | bytes 66000000 | tf_op jit(solution)/shard_map/split/pallas_call | solution.py:502
  555.1 20.8 %attend_back.3 = (bf16[1024,576]{1,0:T(8,128)(2,1)}, f32[3,640]{1,0:T(4,128)}) custom-call(bf16[1024,576]{1,0:T(8,128)(2,1)} %bitcast.217, s32[1,1024]{1,0:T(1,128)} %segr_ref.3, s32[1024,1]{1,0:T(8,128)} %copy.140.refs_2_.segc_ref, f32[3,640]{1,0:T(4,128)} %fusion.93.refs_3_.line_ref, f32[3,1024,1]{2,1,0:T(8,128)} %get-tuple-element.54.lse_ref, ...), custom_call_target="tpu_custom_call" | custom-call | bytes 63000000 | tf_op jit(solution)/shard_map/attend_back/pallas_call | solution.py:197
  577.1 20.2 %input_grad.1 = (f32[256,768]{1,0:T(8,128)}, f32[1,768]{1,0:T(1,128)}) custom-call(bf16[4,256,576]{2,1,0:T(8,128)(2,1)} %bitcast.242, bf16[768,576]{1,0:T(8,128)(2,1)} %all_gather.74.w_ref, f32[256,768]{1,0:T(8,128)} %bitcast.215, f32[1,768]{1,0:T(1,128)} %slice.144.gain_ref, f32[256,768]{1,0:T(8,128)} %get-tuple-element.64.middle_grad_ref), custom_call_target="tpu_custom_call" | custom-call | bytes 48000000 | tf_op jit(solution)/shard_map/input_grad/pallas_call | solution.py:502
  617.6 11.6 %reduce-scatter.21.cloned.1.call-done = bf16[192,1536]{1,0:T(8,128)(2,1)} async-done(((bf16[768,1536]{1,0:T(8,128)(2,1)}), bf16[192,1536]{1,0:T(8,128)(2,1)}) %reduce-scatter.21.cloned.1.call-update) | async-done | bytes 589840 | tf_op jit(solution)/shard_map/reduce_scatter | solution.py:750
  632.6 20.3 %sum_last.1 = f32[256,768]{1,0:T(8,128)} custom-call(bf16[4,2,256,768]{3,2,1,0:T(8,128)(2,1)} %multiply_convert_fusion.part_ref, f32[256,768]{1,0:T(8,128)} %get-tuple-element.53.base_ref.middle_ref), custom_call_target="tpu_custom_call" | custom-call | bytes 48000000 | tf_op jit(solution)/shard_map/sum_last/pallas_call | solution.py:502
  652.9 79.5 %reduce-scatter.11.cloned.1.call-done = bf16[1,25,768]{2,1,0:T(8,128)(2,1)} async-done(((bf16[32,25,768]{2,1,0:T(8,128)(2,1)}), bf16[1,25,768]{2,1,0:T(8,128)(2,1)}) %reduce-scatter.11.cloned.1.call-update) | async-done | bytes 38416 | tf_op jit(solution)/shard_map/reduce_scatter | solution.py:769
  732.3 9.7 all_gather.83
  742.1 92.3 %reduce-scatter.9.cloned.1.call-done = bf16[1,25,768]{2,1,0:T(8,128)(2,1)} async-done(((bf16[32,25,768]{2,1,0:T(8,128)(2,1)}), bf16[1,25,768]{2,1,0:T(8,128)(2,1)}) %reduce-scatter.9.cloned.1.call-update) | async-done | bytes 38416 | tf_op jit(solution)/shard_map/reduce_scatter | solution.py:769
  834.4 9.7 all_gather.82
  849.1 19.0 %reduce-scatter.15.cloned.1.call-done = bf16[96,576]{1,0:T(8,128)(2,1)} async-done(((bf16[768,576]{1,0:T(8,128)(2,1)}), bf16[96,576]{1,0:T(8,128)(2,1)}) %reduce-scatter.15.cloned.1.call-update) | async-done | bytes 110608 | tf_op jit(solution)/shard_map/reduce_scatter | solution.py:779
  868.1 11.3 %all-gather.8 = bf16[768,576]{1,0:T(8,128)(2,1)S(1)} all-gather(bf16[96,576]{1,0:T(8,128)(2,1)} %reduce-scatter.15.cloned.1.call-done), channel_id=10, replica_groups=mesh['dp'=4,'seq'=4,'tensor'=2] {'seq','tensor'}, dimensions={0}, use_global_device_ids=true | all-gather | bytes 995328 | tf_op jit(solution)/shard_map/all_gather | solution.py:780
  883.4 17.5 %reduce-scatter.13.cloned.1.call-done = bf16[96,576]{1,0:T(8,128)(2,1)} async-done(((bf16[768,576]{1,0:T(8,128)(2,1)}), bf16[96,576]{1,0:T(8,128)(2,1)}) %reduce-scatter.13.cloned.1.call-update) | async-done | bytes 110608 | tf_op jit(solution)/shard_map/reduce_scatter | solution.py:779
  900.9 11.1 %all-gather.7 = bf16[768,576]{1,0:T(8,128)(2,1)S(1)} all-gather(bf16[96,576]{1,0:T(8,128)(2,1)} %reduce-scatter.13.cloned.1.call-done), channel_id=9, replica_groups=mesh['dp'=4,'seq'=4,'tensor'=2] {'seq','tensor'}, dimensions={0}, use_global_device_ids=true | all-gather | bytes 995328 | tf_op jit(solution)/shard_map/all_gather | solution.py:780
  918.0 20.2 %all-gather.39.cloned.1.call-done = bf16[768,1536]{1,0:T(8,128)(2,1)} async-done(((bf16[192,1536]{1,0:T(8,128)(2,1)}), bf16[768,1536]{1,0:T(8,128)(2,1)}) %all-gather.39.cloned.1.call-update) | async-done | bytes 2359312 | tf_op jit(solution)/shard_map/all_gather | solution.py:751
  938.2 39.1 %all-gather.37.cloned.1.call-done = bf16[768,1536]{1,0:T(8,128)(2,1)} async-done(((bf16[192,1536]{1,0:T(8,128)(2,1)}), bf16[768,1536]{1,0:T(8,128)(2,1)}) %all-gather.37.cloned.1.call-update) | async-done | bytes 2359312 | tf_op jit(solution)/shard_map/all_gather | solution.py:751
  984.0 32.3 %all-gather.43.cloned.1.call-done = bf16[768,1536]{1,0:T(8,128)(2,1)} async-done(((bf16[192,1536]{1,0:T(8,128)(2,1)}), bf16[768,1536]{1,0:T(8,128)(2,1)}) %all-gather.43.cloned.1.call-update) | async-done | bytes 2359312 | tf_op jit(solution)/shard_map/all_gather | solution.py:751
  1016.4 39.1 %all-gather.41.cloned.1.call-done = bf16[768,1536]{1,0:T(8,128)(2,1)} async-done(((bf16[192,1536]{1,0:T(8,128)(2,1)}), bf16[768,1536]{1,0:T(8,128)(2,1)}) %all-gather.41.cloned.1.call-update) | async-done | bytes 2359312 | tf_op jit(solution)/shard_map/all_gather | solution.py:751
  (302 shorter events, 213.0 us)
Async XLA Ops:
  7.2 132.0 %all-gather.31.cloned.1.call-start = ((), (), s32[]{:S(2)}) async-start(), calls=%async_computation.19 | async-start | bytes 1622016 | tf_op jit(solution)/shard_map/all_gather | solution.py:608
  10.1 133.8 %all-gather.25.cloned.1.call-start = ((), (), s32[]{:S(2)}) async-start(), calls=%async_computation.16 | async-start | bytes 1622016 | tf_op jit(solution)/shard_map/all_gather | solution.py:608
  10.8 178.3 %all-gather.27.cloned.1.call-start = ((), (), s32[]{:S(2)}) async-start(), calls=%async_computation.17 | async-start | bytes 2949120 | tf_op jit(solution)/shard_map/all_gather | solution.py:613
  13.3 21.3 %copy-start.27 = (s32[2,2,256,2]{2,3,1,0:T(2,128)S(1)}, s32[2,2,256,2]{2,3,1,0:T(2,128)}, u32[]{:S(2)}) copy-start(s32[2,2,256,2]{2,3,1,0:T(2,128)} %param.15) | copy-start | bytes 24580
  13.3 216.1 %all-gather.29.cloned.1.call-start = ((), (), s32[]{:S(2)}) async-start(), calls=%async_computation.18 | async-start | bytes 2949120 | tf_op jit(solution)/shard_map/all_gather | solution.py:614
  15.8 321.6 %all-gather.33.cloned.1.call-start = ((), (), s32[]{:S(2)}) async-start(), calls=%async_computation.20 | async-start | bytes 2949120 | tf_op jit(solution)/shard_map/all_gather | solution.py:613
  16.4 328.5 %all-gather.35.cloned.1.call-start = ((), (), s32[]{:S(2)}) async-start(), calls=%async_computation.21 | async-start | bytes 2949120 | tf_op jit(solution)/shard_map/all_gather | solution.py:614
  17.0 591.6 %reduce-scatter.19.cloned.1.call-start = ((), (), s32[]{:S(2)}) async-start(), calls=%async_computation.13 | async-start | bytes 2949120 | tf_op jit(solution)/shard_map/reduce_scatter | solution.py:750
  66.6 22.6 %copy-start.26 = (f32[4,192]{1,0:T(4,128)S(1)}, f32[4,192]{1,0:T(4,128)}, u32[]{:S(2)}) copy-start(f32[4,192]{1,0:T(4,128)} %get-tuple-element.102) | copy-start | bytes 9220
  66.6 23.3 %copy-start.25 = (f32[4,192]{1,0:T(4,128)S(1)}, f32[4,192]{1,0:T(4,128)}, u32[]{:S(2)}) copy-start(f32[4,192]{1,0:T(4,128)} %get-tuple-element.103) | copy-start | bytes 9220
  66.6 24.0 %copy-start.24 = (f32[4,192]{1,0:T(4,128)S(1)}, f32[4,192]{1,0:T(4,128)}, u32[]{:S(2)}) copy-start(f32[4,192]{1,0:T(4,128)} %get-tuple-element.137) | copy-start | bytes 9220
  66.6 25.5 %copy-start.11 = (s32[1,1024]{1,0:T(1,128)S(1)}, s32[1,1024]{1,0:T(1,128)}, u32[]{:S(2)}) copy-start(s32[1,1024]{1,0:T(1,128)} %segr_ref.3) | copy-start | bytes 12292
  87.4 27.6 %copy-start.12 = (s32[640]{0:T(1024)}, s32[640]{0:T(1024)S(1)}, u32[]{:S(2)}) copy-start(s32[640]{0:T(1024)S(1)} %pad_add_fusion) | copy-start | bytes 7684
  117.2 254.3 %copy-start.14 = (s32[4,512]{1,0:T(4,128)}, s32[4,512]{1,0:T(4,128)S(1)}, u32[]{:S(2)}) copy-start(s32[4,512]{1,0:T(4,128)S(1)} %and_select_fusion) | copy-start | bytes 24580
  117.5 119.2 %copy-start.16 = (s32[4,512]{1,0:T(4,128)}, s32[4,512]{1,0:T(4,128)S(1)}, u32[]{:S(2)}) copy-start(s32[4,512]{1,0:T(4,128)S(1)} %and_select_fusion.1) | copy-start | bytes 24580
  280.2 44.0 %copy-start.19 = (pred[4,512,4]{1,2,0:T(4,128)(4,1)S(1)}, pred[4,512,4]{1,2,0:T(4,128)(4,1)}, u32[]{:S(2)}) copy-start(pred[4,512,4]{1,2,0:T(4,128)(4,1)} %fusion.94) | copy-start | bytes 24580
  363.0 246.2 %reduce-scatter.17.cloned.1.call-start = ((), (), s32[]{:S(2)}) async-start(), calls=%async_computation.12 | async-start | bytes 2949120 | tf_op jit(solution)/shard_map/reduce_scatter | solution.py:750
  407.5 57.5 %copy-start.17 = (s32[4,512]{1,0:T(4,128)S(1)}, s32[4,512]{1,0:T(4,128)}, u32[]{:S(2)}) copy-start(s32[4,512]{1,0:T(4,128)} %copy-done.16) | copy-start | bytes 24580
  407.5 57.5 %copy-start.30 = (f32[4,512]{1,0:T(4,128)S(1)}, f32[4,512]{1,0:T(4,128)}, u32[]{:S(2)}) copy-start(f32[4,512]{1,0:T(4,128)} %mul.221) | copy-start | bytes 24580
  485.3 124.4 %reduce-scatter.23.cloned.1.call-start = ((), (), s32[]{:S(2)}) async-start(), calls=%async_computation.15 | async-start | bytes 2949120 | tf_op jit(solution)/shard_map/reduce_scatter | solution.py:750
  493.0 136.2 %reduce-scatter.21.cloned.1.call-start = ((), (), s32[]{:S(2)}) async-start(), calls=%async_computation.14 | async-start | bytes 2949120 | tf_op jit(solution)/shard_map/reduce_scatter | solution.py:750
  501.0 231.3 %reduce-scatter.11.cloned.1.call-start = ((), (), s32[]{:S(2)}) async-start(), calls=%async_computation.9 | async-start | bytes 1622016 | tf_op jit(solution)/shard_map/reduce_scatter | solution.py:769
  514.9 319.6 %reduce-scatter.9.cloned.1.call-start = ((), (), s32[]{:S(2)}) async-start(), calls=%async_computation.8 | async-start | bytes 1622016 | tf_op jit(solution)/shard_map/reduce_scatter | solution.py:769
  555.1 43.0 %copy-start.34 = (f32[1,768]{1,0:T(1,128)S(1)}, f32[1,768]{1,0:T(1,128)}, u32[]{:S(2)}) copy-start(f32[1,768]{1,0:T(1,128)} %get-tuple-element.69) | copy-start | bytes 9220
  555.1 43.3 %copy-start.5 = (bf16[4,256,192]{2,1,0:T(8,128)(2,1)S(1)}, bf16[4,256,192]{2,1,0:T(8,128)(2,1)}, u32[]{:S(2)}) copy-start(bf16[4,256,192]{2,1,0:T(8,128)(2,1)} %get-tuple-element.66) | copy-start | bytes 1179652
  555.1 43.3 %copy-start.6 = (bf16[256,768]{1,0:T(8,128)(2,1)S(1)}, bf16[256,768]{1,0:T(8,128)(2,1)}, u32[]{:S(2)}) copy-start(bf16[256,768]{1,0:T(8,128)(2,1)} %get-tuple-element.67) | copy-start | bytes 1179652
  600.4 267.7 %reduce-scatter.15.cloned.1.call-start = ((), (), s32[]{:S(2)}) async-start(), calls=%async_computation.11 | async-start | bytes 1105920 | tf_op jit(solution)/shard_map/reduce_scatter | solution.py:779
  604.6 296.3 %reduce-scatter.13.cloned.1.call-start = ((), (), s32[]{:S(2)}) async-start(), calls=%async_computation.10 | async-start | bytes 1105920 | tf_op jit(solution)/shard_map/reduce_scatter | solution.py:779
  608.5 329.7 %all-gather.39.cloned.1.call-start = ((), (), s32[]{:S(2)}) async-start(), calls=%async_computation.23 | async-start | bytes 2949120 | tf_op jit(solution)/shard_map/all_gather | solution.py:751
  609.1 368.2 %all-gather.37.cloned.1.call-start = ((), (), s32[]{:S(2)}) async-start(), calls=%async_computation.22 | async-start | bytes 2949120 | tf_op jit(solution)/shard_map/all_gather | solution.py:751
  609.7 406.7 %all-gather.43.cloned.1.call-start = ((), (), s32[]{:S(2)}) async-start(), calls=%async_computation.25 | async-start | bytes 2949120 | tf_op jit(solution)/shard_map/all_gather | solution.py:751
  610.3 445.1 %all-gather.41.cloned.1.call-start = ((), (), s32[]{:S(2)}) async-start(), calls=%async_computation.24 | async-start | bytes 2949120 | tf_op jit(solution)/shard_map/all_gather | solution.py:751
  (31 other events, 201.7 us)
Sparse Core Ops, SparseCore 0:
  11.4 58.2 all-gather.30
  73.1 54.1 all-gather.24
  129.4 49.0 all-gather.26
  180.5 48.8 all-gather.28
  231.4 48.6 all-gather.32
  282.0 48.7 all-gather.34
  363.1 46.2 reduce-scatter.18
  485.5 44.9 reduce-scatter.16
  532.8 47.0 reduce-scatter.22
  582.1 47.0 reduce-scatter.20
  635.0 97.2 reduce-scatter.10
  737.4 96.9 reduce-scatter.8
  836.7 31.3 reduce-scatter.14
  870.2 30.6 reduce-scatter.12
  902.6 35.6 all-gather.38
  939.9 37.3 all-gather.36
  979.0 37.3 all-gather.42
  1018.1 37.3 all-gather.40

commit v3 on v2

--- a/solution.py
+++ b/solution.py
@@ -66,15 +66,19 @@
     qkv_ref, segr_ref, segc_ref, line_ref = refs[:4]
     midway = None
     if spread:
-        rows_ref, out_ref, lse_ref, gathered_ref = refs[4:8]
-        wires = Wires(*refs[12:])
+        rows_ref, qkv_next, out_next, out_ref, lse_ref, gathered_ref, qkv_all, out_all = refs[4:12]
+        wires = Wires(*refs[16:])
         place = plane_place()
-        greet(*plane_peers(place))
-        gathered_ref[place[0], place[1]] = rows_ref[...].astype(jnp.bfloat16)
+        core = place[1]
+        line_me, targets, sources = dp_peers()
+        greet(*plane_peers(place), *[{"dp": spot} for spot in targets])
+        gathered_ref[place[0], core] = rows_ref[...].astype(jnp.bfloat16)
         first = plane_gather_start(wires, gathered_ref, place)
+        qkvs = line_start(wires, qkv_next, qkv_all, core, line_me, targets)
+        outs = line_start(wires, out_next, out_all, core, line_me, targets)
         second = []
         midway = lambda: second.extend(plane_gather_forward(wires, gathered_ref, place, first))
-        refs = refs[8:12]
+        refs = refs[12:16]
     else:
         out_ref, lse_ref = refs[4:6]
         refs = refs[6:10]
@@ -106,11 +110,30 @@
     out_ref[...] = jnp.concatenate([mixed_ref[h] for h in range(heads)], axis=1)
     if spread:
         plane_gather_finish(wires, gathered_ref, place, first, second)
+        onward = line_forward(wires, qkv_all, core, qkvs, sources)
+        onward += line_forward(wires, out_all, core, outs, sources)
+        for one in onward:
+            one.wait_recv()
         wires.finish()
 
 
-def attn_bwd_kernel(heads, span, qkv_ref, segr_ref, segc_ref, line_ref, lse_ref, grad_ref, out_ref, band_ref,
-                    parts_ref, gparts_ref, qgrad_ref, kgrad_ref, vgrad_ref, slab_ref, mask_ref, band_acc):
+def attn_bwd_kernel(heads, span, spread, *refs):
+    qkv_ref, segr_ref, segc_ref, line_ref, lse_ref, grad_ref = refs[:6]
+    midway = None
+    if spread:
+        shard_ref, out_ref, band_ref, shared_ref = refs[6:10]
+        wires = Wires(*refs[18:])
+        place = plane_place()
+        greet({"seq": place[2]}, {"seq": place[3]})
+        shared_ref[place[0]] = shard_ref[...]
+        first = seq_gather_start(wires, shared_ref, place)
+        second = []
+        midway = lambda: second.extend(seq_gather_forward(wires, shared_ref, place, first))
+        refs = refs[10:18]
+    else:
+        out_ref, band_ref = refs[6:8]
+        refs = refs[8:16]
+    parts_ref, gparts_ref, qgrad_ref, kgrad_ref, vgrad_ref, slab_ref, mask_ref, band_acc = refs
     length = qkv_ref.shape[0]
     fill_slab(slab_ref, line_ref, heads, span)
     split_heads(qkv_ref, parts_ref, heads)
@@ -146,7 +169,7 @@
 
         lax.fori_loop(0, heads, one_head, 0)
 
-    visit_blocks(length, span, one_block)
+    visit_blocks(length, span, one_block, midway)
     parts = [qgrad_ref[h] for h in range(heads)]
     parts += [kgrad_ref[h].astype(jnp.bfloat16) for h in range(heads)]
     parts += [vgrad_ref[h].astype(jnp.bfloat16) for h in range(heads)]
@@ -159,6 +182,10 @@
             acc = jnp.where((row & bit) != 0, pltpu.roll(acc, span - bit, 1), acc)
             bit *= 2
         band_ref[h : h + 1, :] = jnp.sum(acc, axis=0, keepdims=True)
+    if spread:
+        for one in second:
+            one.wait_recv()
+        wires.finish()
 
 
 def vmem(count):
@@ -191,30 +218,34 @@
     )(qkv, seg_row, seg_col, line)
 
 
-def attend_back(qkv, seg_row, seg_col, line, lse, grad):
+def attend_back(qkv, seg_row, seg_col, line, lse, grad, shard=None):
     length, width = qkv.shape
     heads, span = line.shape
+    outs = [low_array(length, width), wide_array(heads, span)]
+    scratch = [
+        pltpu.VMEM((3 * heads, length, HD), jnp.bfloat16),
+        pltpu.VMEM((heads, length, HD), jnp.bfloat16),
+        pltpu.VMEM((heads, length, HD), jnp.bfloat16),
+        pltpu.VMEM((heads, length, HD), jnp.float32),
+        pltpu.VMEM((heads, length, HD), jnp.float32),
+        pltpu.VMEM((heads, ROWS, span), jnp.float32),
+        pltpu.VMEM((ROWS, span), jnp.float32),
+        pltpu.VMEM((heads, ROWS, span), jnp.float32),
+    ]
+    operands = [qkv, seg_row, seg_col, line, lse, grad]
+    if shard is not None:
+        outs.append(low_array(4, *shard.shape))
+        kernel = functools.partial(attn_bwd_kernel, heads, span, True)
+        return comm_call(kernel, "attend_back_share", 9, 25.0, outs, scratch, 4, *operands, shard)
     return pl.pallas_call(
-        functools.partial(attn_bwd_kernel, heads, span),
-        out_shape=(
-            jax.ShapeDtypeStruct((length, width), jnp.bfloat16),
-            jax.ShapeDtypeStruct((heads, span), jnp.float32),
-        ),
+        functools.partial(attn_bwd_kernel, heads, span, False),
+        out_shape=tuple(outs),
         in_specs=vmem(6),
         out_specs=tuple(vmem(2)),
-        scratch_shapes=[
-            pltpu.VMEM((3 * heads, length, HD), jnp.bfloat16),
-            pltpu.VMEM((heads, length, HD), jnp.bfloat16),
-            pltpu.VMEM((heads, length, HD), jnp.bfloat16),
-            pltpu.VMEM((heads, length, HD), jnp.float32),
-            pltpu.VMEM((heads, length, HD), jnp.float32),
-            pltpu.VMEM((heads, ROWS, span), jnp.float32),
-            pltpu.VMEM((ROWS, span), jnp.float32),
-            pltpu.VMEM((heads, ROWS, span), jnp.float32),
-        ],
+        scratch_shapes=scratch,
         cost_estimate=cost(21.0),
         name="attend_back",
-    )(qkv, seg_row, seg_col, line, lse, grad)
+    )(*operands)
 
 
 MESH_ID = pl.DeviceIdType.MESH
@@ -523,22 +554,240 @@
     return jax.ShapeDtypeStruct(shape, jnp.float32)
 
 
-def attend_gather(qkv, seg_row, seg_col, line, rows, n_tensor):
+def attend_gather(qkv, seg_row, seg_col, line, rows, qkv_next, out_next, n_tensor, n_dp):
     length, width = qkv.shape
     heads, span = line.shape
     piece, depth = rows.shape
-    outs = [low_array(length, heads * HD), wide_array(heads, length, 1), low_array(length // piece, n_tensor, piece, depth)]
-    return comm_call(functools.partial(attn_fwd_kernel, heads, span, True), "attend_gather", 6, 16.0, outs,
-                     attend_scratch(heads, length, span), 9, qkv, seg_row, seg_col, line, rows)
+    outs = [low_array(length, heads * HD), wide_array(heads, length, 1), low_array(length // piece, n_tensor, piece, depth),
+            low_array(n_dp, *qkv_next.shape), low_array(n_dp, *out_next.shape)]
+    return comm_call(functools.partial(attn_fwd_kernel, heads, span, True), "attend_gather", 6, 20.0, outs,
+                     attend_scratch(heads, length, span), 9 + 4 * (n_dp - 1), qkv, seg_row, seg_col, line, rows, qkv_next, out_next)
 
 
 def gelu_parts(values):
-    cubic = values * values * 0.044715
-    inner = jnp.tanh(0.7978845608028654 * values * (1.0 + cubic))
-    slope = 0.5 * (1.0 + inner) + 0.5 * values * (1.0 - inner * inner) * 0.7978845608028654 * (1.0 + 3.0 * cubic)
-    return 0.5 * values * (1.0 + inner), slope
-
-
+    square = values * values
+    inner = jnp.tanh(values * (0.7978845608028654 + (0.7978845608028654 * 0.044715) * square))
+    lift = 0.5 + 0.5 * inner
+    slope = lift + (0.5 * values) * (1.0 - inner * inner) * (0.7978845608028654 + (3.0 * 0.7978845608028654 * 0.044715) * square)
+    return values * lift, slope
+
+
+def slot_hot(slot_row, capacity):
+    rows = lax.broadcasted_iota(jnp.int32, (capacity, slot_row.shape[1]), 0)
+    return (rows == slot_row).astype(jnp.bfloat16)
+
+
+def experts_kernel(tokens_ref, slot_ref, chosen_ref, own_ref, router_ref, up_ref, down_ref, part_ref, slots_ref, pre_ref, shares_ref):
+    capacity = slots_ref.shape[0]
+    tokens = tokens_ref[...]
+    logits = jnp.where(chosen_ref[...] > 0, dot_nt(tokens, router_ref[...]), negative)
+    raised = jnp.exp(logits - jnp.max(logits, axis=1, keepdims=True))
+    shares = raised / jnp.sum(raised, axis=1, keepdims=True)
+    shares_ref[...] = shares
+    own_share = jnp.sum(shares * own_ref[...], axis=1, keepdims=True)
+    hot = slot_hot(slot_ref[...], capacity)
+    slots = dot(hot, tokens).astype(jnp.bfloat16)
+    slots_ref[...] = slots
+    pre = dot(slots, up_ref[...])
+    pre_ref[...] = pre.astype(jnp.bfloat16)
+    hidden = gelu_parts(pre)[0].astype(jnp.bfloat16)
+    result = dot_nt(hidden, down_ref[...]).astype(jnp.bfloat16)
+    part_ref[...] = (own_share * dot_tn(hot, result)).astype(jnp.bfloat16)
+
+
+def experts_back_kernel(rows_ref, tokens_ref, slot_ref, shares_ref, own_ref, router_ref, up_ref, down_ref, slots_ref, pre_ref,
+                        part_ref, up_grad_ref, down_grad_ref, router_grad_ref, up_acc, down_acc):
+    group = pl.program_id(0)
+
+    @pl.when(group == 0)
+    def _():
+        up_acc[...] = jnp.zeros_like(up_acc)
+        down_acc[...] = jnp.zeros_like(down_acc)
+        router_grad_ref[...] = jnp.zeros_like(router_grad_ref)
+
+    capacity = slots_ref.shape[0]
+    shares = shares_ref[...]
+    own = own_ref[...]
+    own_share = jnp.sum(shares * own, axis=1, keepdims=True)
+    hot = slot_hot(slot_ref[...], capacity)
+    scaled_rows = (own_share * rows_ref[...].astype(jnp.float32)).astype(jnp.bfloat16)
+    result_grad = dot(hot, scaled_rows).astype(jnp.bfloat16)
+    hidden_grad = dot(result_grad, down_ref[...])
+    hidden, slope = gelu_parts(pre_ref[...].astype(jnp.float32))
+    pre_grad = (slope * hidden_grad).astype(jnp.bfloat16)
+    pair_sum = jnp.sum(hidden * hidden_grad, axis=1, keepdims=True)
+    down_acc[...] += dot_tn(result_grad, hidden.astype(jnp.bfloat16))
+    up_acc[...] += dot_tn(slots_ref[...], pre_grad)
+    slot_grad = dot_nt(pre_grad, up_ref[...]).astype(jnp.bfloat16)
+    high = pair_sum.astype(jnp.bfloat16)
+    rest = (pair_sum - high.astype(jnp.float32)).astype(jnp.bfloat16)
+    token_pair = dot_tn(hot, jnp.concatenate([jnp.broadcast_to(high, (capacity, 128)), jnp.broadcast_to(rest, (capacity, 128))], axis=1))
+    token_pair = token_pair[:, :1] + token_pair[:, 128:129]
+    logit_grad = (token_pair * (own - shares)).astype(jnp.bfloat16)
+    router_grad_ref[...] += dot_tn(logit_grad, tokens_ref[...])
+    part_ref[...] = (dot_tn(hot, slot_grad) + dot(logit_grad, router_ref[...])).astype(jnp.bfloat16)
+
+    @pl.when(group == pl.num_programs(0) - 1)
+    def _():
+        up_grad_ref[...] = up_acc[...].astype(jnp.bfloat16)
+        down_grad_ref[...] = down_acc[...].astype(jnp.bfloat16)
+
+
+def by_group(*shape):
+    return pl.BlockSpec((None,) + shape, lambda g: (g,) + (0,) * len(shape))
+
+
+def held(*shape):
+    return pl.BlockSpec(shape, lambda g: (0,) * len(shape), pipeline_mode=pl.Buffered(1))
+
+
+def run_experts(tokens, slot, chosen, own, router, up, down, capacity):
+    groups, rows, width = tokens.shape
+    experts, wide_ff = router.shape[0], up.shape[1]
+    return pl.pallas_call(
+        experts_kernel,
+        grid=(groups,),
+        out_shape=(low_array(groups, rows, width), low_array(groups, capacity, width), low_array(groups, capacity, wide_ff),
+                   wide_array(groups, rows, experts)),
+        in_specs=[by_group(rows, width), by_group(1, rows), by_group(rows, experts), held(1, experts), held(experts, width),
+                  held(width, wide_ff), held(width, wide_ff)],
+        out_specs=(by_group(rows, width), by_group(capacity, width), by_group(capacity, wide_ff), by_group(rows, experts)),
+        compiler_params=pltpu.CompilerParams(dimension_semantics=("arbitrary",)),
+        cost_estimate=cost(14.0),
+        name="experts",
+    )(tokens, slot, chosen, own, router, up, down)
+
+
+def run_experts_back(rows_grad, tokens, slot, shares, own, router, up, down, slots, pre):
+    groups, rows, width = tokens.shape
+    experts, wide_ff = router.shape[0], up.shape[1]
+    capacity = slots.shape[1]
+    return pl.pallas_call(
+        experts_back_kernel,
+        grid=(groups,),
+        out_shape=(low_array(groups, rows, width), low_array(width, wide_ff), low_array(width, wide_ff), wide_array(experts, width)),
+        in_specs=[by_group(rows, width), by_group(rows, width), by_group(1, rows), by_group(rows, experts), held(1, experts),
+                  held(experts, width), held(width, wide_ff), held(width, wide_ff), by_group(capacity, width), by_group(capacity, wide_ff)],
+        out_specs=(by_group(rows, width), held(width, wide_ff), held(width, wide_ff), held(experts, width)),
+        scratch_shapes=[pltpu.VMEM((width, wide_ff), jnp.float32), pltpu.VMEM((width, wide_ff), jnp.float32)],
+        compiler_params=pltpu.CompilerParams(dimension_semantics=("arbitrary",)),
+        cost_estimate=cost(26.0),
+        name="experts_back",
+    )(rows_grad, tokens, slot, shares, own, router, up, down, slots, pre)
+
+
+def dp_peers():
+    me, count = lax.axis_index("dp"), lax.axis_size("dp")
+    return me, [lax.rem(me + step, count) for step in range(1, count)], [lax.rem(me + count - step, count) for step in range(1, count)]
+
+
+def line_start(wires, own_ref, all_ref, core, me, targets):
+    half = own_ref.at[core]
+    copies = [wires.copy(half, all_ref.at[me, core], {"dp": spot}) for spot in targets]
+    all_ref[me] = own_ref[...]
+    return copies
+
+
+def line_forward(wires, all_ref, core, copies, sources):
+    onward = []
+    for one, spot in zip(copies, sources):
+        one.wait_recv()
+        block = all_ref.at[spot, core]
+        onward.append(wires.copy(block, block, {"tensor": 1 - core}))
+    return onward
+
+
+def weights_kernel(small_ref, qkv_ref, out_ref, small_all, qkv_all, out_all, send, recv):
+    core = lax.axis_index("tensor")
+    me, targets, sources = dp_peers()
+    wires = Wires(send, recv)
+    greet(*[{"dp": spot} for spot in targets], {"tensor": 1 - core})
+    smalls = [wires.copy(small_ref, small_all.at[me], {"dp": spot}) for spot in targets]
+    small_all[me] = small_ref[...]
+    qkvs = line_start(wires, qkv_ref, qkv_all, core, me, targets)
+    outs = line_start(wires, out_ref, out_all, core, me, targets)
+    onward = line_forward(wires, qkv_all, core, qkvs, sources)
+    onward += line_forward(wires, out_all, core, outs, sources)
+    for one in smalls + onward:
+        one.wait_recv()
+    wires.finish()
+
+
+def reduce_kernel(layers, *refs):
+    q_refs, o_refs = refs[:layers], refs[layers : 2 * layers]
+    refs = refs[2 * layers :]
+    q_outs, o_outs = refs[:layers], refs[layers : 2 * layers]
+    refs = refs[2 * layers :]
+    scratch = [refs[6 * layer : 6 * layer + 6] for layer in range(layers)]
+    send, recv = refs[6 * layers :]
+    place = plane_place()
+    me, core, near, far, cross = place
+    others = (cross, near, far)
+    line_me, targets, sources = dp_peers()
+    wires = Wires(send, recv)
+    partner = {"tensor": 1 - core}
+    greet({"seq": near}, {"seq": far}, {"seq": cross}, partner, *[{"dp": spot} for spot in targets])
+    n_dp = len(targets) + 1
+    first = []
+    for layer in range(layers):
+        q_in, q_sum, q_line, o_in, o_seq, o_line = scratch[layer]
+        first.append((wires.copy(q_refs[layer].at[1 - core], q_in, partner), wires.copy(o_refs[layer].at[1 - core], o_in, partner)))
+    q_copies, o_copies = [], []
+    for layer in range(layers):
+        q_in, q_sum, q_line, o_in, o_seq, o_line = scratch[layer]
+        q_ref, o_ref = q_refs[layer], o_refs[layer]
+        first[layer][0].wait_recv()
+        q_sum[...] = (wide(q_ref[core]) + wide(q_in[...])).astype(jnp.bfloat16)
+        q_copies.append([wires.copy(q_sum.at[spot], q_line.at[line_me], {"dp": spot}) for spot in targets])
+        q_line[line_me] = q_sum[line_me]
+        first[layer][1].wait_recv()
+        o_in[...] = (wide(o_ref[core]) + wide(o_in[...])).astype(jnp.bfloat16)
+        o_copies.append([wires.copy(o_in.at[spot], o_seq.at[me], {"seq": spot}) for spot in others])
+        o_seq[me] = o_in[me]
+    line_copies, last = [], []
+    for layer in range(layers):
+        q_in, q_sum, q_line, o_in, o_seq, o_line = scratch[layer]
+        for one in o_copies[layer]:
+            one.wait_recv()
+        o_seq[me] = (wide(o_seq[0]) + wide(o_seq[1]) + wide(o_seq[2]) + wide(o_seq[3])).astype(jnp.bfloat16)
+        line_copies.append([wires.copy(o_seq.at[me, spot], o_line.at[line_me], {"dp": spot}) for spot in targets])
+        o_line[line_me] = o_seq[me, line_me]
+    for layer in range(layers):
+        q_in, q_sum, q_line, o_in, o_seq, o_line = scratch[layer]
+        for refs_in, copies, out in ((q_line, q_copies[layer], q_outs[layer]), (o_line, line_copies[layer], o_outs[layer])):
+            for one in copies:
+                one.wait_recv()
+            total = wide(refs_in[0])
+            for spot in range(1, n_dp):
+                total = total + wide(refs_in[spot])
+            out[core, me] = total.astype(jnp.bfloat16)
+            mine = out.at[core, me]
+            last.append((out, [wires.copy(mine, mine, {"seq": spot}) for spot in others], [wires.copy(mine, mine, partner)]))
+    for out, copies, onward in last:
+        for one, spot in zip(copies, others):
+            one.wait_recv()
+            block = out.at[core, spot]
+            onward.append(wires.copy(block, block, partner))
+    for out, copies, onward in last:
+        for one in onward:
+            one.wait_recv()
+    wires.finish()
+
+
+def share_kernel(count, *refs):
+    in_refs, out_refs, (send, recv) = refs[:count], refs[count : 2 * count], refs[2 * count :]
+    place = plane_place()
+    wires = Wires(send, recv)
+    greet({"seq": place[2]}, {"seq": place[3]})
+    first, second = [], []
+    for src, dst in zip(in_refs, out_refs):
+        dst[place[0]] = src[...]
+        first.append(seq_gather_start(wires, dst, place))
+    for dst, one in zip(out_refs, first):
+        second.extend(seq_gather_forward(wires, dst, place, one))
+    for one in second:
+        one.wait_recv()
+    wires.finish()
 def body(
     block_input,
     segments,
@@ -569,52 +818,49 @@
     group_rows = n_tensor * piece
     capacity = group_rows * routes.shape[-1] // experts
     seq_index = lax.axis_index("seq")
-    plane_index = seq_index * n_tensor + lax.axis_index("tensor")
     span = ROWS + length // 2
+
+
+    assert n_seq == 4 and n_tensor == 2
+    half = shard // n_tensor
+
+    def padded(values):
+        return jnp.pad(values, ((0, 0), (0, shard - values.shape[1])))
 
     small = jnp.concatenate(
         [
-            first_gain.reshape(LAYERS, -1),
-            second_gain.reshape(LAYERS, -1),
-            bias_table.reshape(LAYERS, -1),
-            router_weights.reshape(LAYERS, -1),
-        ],
-        axis=1,
+            first_gain,
+            second_gain,
+            router_weights.swapaxes(1, 2).reshape(-1, shard),
+            padded(bias_table.reshape(LAYERS, -1)),
+        ]
     )
-    small = lax.all_gather(small, "dp", axis=0)
-    cuts = [shard, 2 * shard, 2 * shard + bucket_shard * HEADS]
-    gains_one, gains_two, tables, routers = jnp.split(small, cuts, axis=2)
-
-    def whole(values, trailing):
-        return jnp.moveaxis(values, 1, 0).reshape((LAYERS, -1) + trailing)
-
-    gains_one = whole(gains_one, ()).astype(jnp.float32)
-    gains_two = whole(gains_two, ()).astype(jnp.float32)
-    tables = whole(tables, (HEADS,)).astype(jnp.float32)
-    routers = whole(routers, (experts,))
-
+    small_rows = small.shape[0]
+    small = jnp.pad(small, ((0, -small_rows % 16), (0, 0)))
     own_qkv = lax.dynamic_index_in_dim(
         query_key_value.reshape(LAYERS, shard, 3, n_seq, head_width), seq_index, 3, keepdims=False
-    ).reshape(LAYERS, shard, 3 * head_width)
-    out_columns = width // n_plane
-    own_out = lax.dynamic_index_in_dim(
-        attention_out.reshape(LAYERS, shard, n_plane, out_columns), plane_index, 2, keepdims=False
-    )
+    ).reshape(LAYERS, n_tensor, half, 3 * head_width)
+    own_out = attention_out.reshape(LAYERS, n_tensor, half, width)
     own_up = lax.dynamic_index_in_dim(expert_up, seq_index, 1, keepdims=False)
     own_down = lax.dynamic_index_in_dim(expert_down, seq_index, 1, keepdims=False).swapaxes(1, 2)
-
-    def attention_weights(layer):
-        qkv = lax.all_gather(own_qkv[layer], "dp", axis=0, tiled=True)
-        out = lax.all_gather(own_out[layer], ("dp", "seq", "tensor"), axis=0)
-        out = out.reshape(n_dp, n_plane, shard, out_columns)
-        return qkv, jnp.moveaxis(out, 1, 2).reshape(n_seq, head_width, width)
 
     def expert_weights(layer):
         up = lax.all_gather(own_up[layer], "dp", axis=0, tiled=True)
         down = lax.all_gather(own_down[layer], "dp", axis=0, tiled=True)
         return up, down
 
-    assert n_seq == 4 and n_tensor == 2
+    small_all, qkv_all, out_all = comm_call(
+        weights_kernel, "weights", 10, 25.0,
+        [low_array(n_dp, *small.shape), low_array(n_dp, *own_qkv.shape[1:]), low_array(n_dp, *own_out.shape[1:])], [], 5 * (n_dp - 1),
+        small, own_qkv[0], own_out[0]
+    )
+    qkv_weights, out_weights = [qkv_all], [out_all]
+    whole_rows = small_all.swapaxes(0, 1).reshape(-1, width)
+    gains = whole_rows[: 2 * LAYERS].astype(jnp.float32).reshape(2, LAYERS, 1, width)
+    routers = whole_rows[2 * LAYERS : 2 * LAYERS + LAYERS * experts].reshape(LAYERS, experts, width)
+    tables = whole_rows[2 * LAYERS + LAYERS * experts : small_rows].reshape(LAYERS, n_dp, shard)[:, :, : bucket_shard * HEADS]
+    tables = tables.reshape(LAYERS, bucket_count, HEADS).astype(jnp.float32)
+    own_tables = lax.dynamic_slice_in_dim(tables, seq_index * local_heads, local_heads, 2)
     routes_own = routes.reshape(-1, 128)
     seg_row = segments
     seg_col = segments.reshape(length, 1)
@@ -623,113 +869,87 @@
         [jnp.full((1,), -1, jnp.int32), bucket_line, jnp.full((span - 1 - length // 2,), -1, jnp.int32)]
     )
     line_hot = (bucket_line[None, :] == lax.iota(jnp.int32, bucket_count)[:, None]).astype(jnp.float32)
+    lines = jnp.einsum("lbh,bs->lhs", own_tables, line_hot, precision=highest_precision)
     strict_upper = (
         lax.iota(jnp.int32, group_rows)[:, None] < lax.iota(jnp.int32, group_rows)[None, :]
     ).astype(low)
 
-    def routing(layer, routes_all):
-        layer_routes = routes_all[layer]
-        mine = jnp.any(layer_routes == seq_index, axis=-1)
-        slot = dot(mine.astype(low), strict_upper).astype(jnp.int32)
-        slot = jnp.where(mine & (slot < capacity), slot, -1)
-        hot = (slot[:, None, :] == lax.iota(jnp.int32, capacity)[None, :, None]).astype(low)
-        chosen = jnp.any(layer_routes[..., None] == lax.iota(jnp.int32, experts), axis=2)
-        return hot, chosen.reshape(n_seq * group_rows, experts)
-
-    def to_slots(hot, rows):
-        rows = rows.reshape(n_seq, group_rows, width)
-        out = jnp.einsum("gct,gtd->gcd", hot, rows, preferred_element_type=jnp.float32)
-        return out.astype(low).reshape(n_seq * capacity, width)
-
-    def from_slots(hot, rows):
-        rows = rows.reshape(n_seq, capacity, -1)
-        out = jnp.einsum("gct,gcd->gtd", hot, rows, preferred_element_type=jnp.float32)
-        return out.reshape(n_seq * group_rows, -1)
+    own_hot = (lax.iota(jnp.int32, experts) == seq_index).astype(jnp.float32)[None]
 
     current = block_input[0]
     grad = cotangent[0]
     saved = []
     for layer in range(LAYERS):
-        qkv_weight, out_weight = attention_weights(layer)
         up, down = expert_weights(layer)
-        gain_one, gain_two = gains_one[layer][None], gains_two[layer][None]
+        gain_one, gain_two = gains[0, layer], gains[1, layer]
+        qkv_weight = qkv_weights[layer].reshape(width, 3 * head_width)
+        out_weight = out_weights[layer].reshape(n_seq, head_width, width)
         outs = [low_array(n_seq, piece, width), low_array(n_seq, piece, 3 * head_width)]
         if layer == 0:
             outs.append(jax.ShapeDtypeStruct((n_seq,) + routes_own.shape, jnp.int32))
             normed_all, qkv, routes_all = comm_call(
                 project_kernel, "project", 1, 16.0, outs, [], 7, current, gain_one, qkv_weight, routes_own
             )
-            routes_all = routes_all.reshape((n_seq,) + routes.shape)
-            routes_all = jnp.moveaxis(routes_all, 0, 1).reshape(LAYERS, n_seq, group_rows, -1)
+            routes_all = jnp.moveaxis(routes_all.reshape((n_seq,) + routes.shape), 0, 1).reshape(LAYERS, n_seq, group_rows, -1)
+            mine = jnp.any(routes_all == seq_index, axis=-1)
+            slot = dot(mine.reshape(-1, group_rows).astype(low), strict_upper).astype(jnp.int32).reshape(mine.shape)
+            slot = jnp.where(mine & (slot < capacity), slot, -1)[:, :, None]
+            chosen = jnp.any(routes_all[..., None] == lax.iota(jnp.int32, experts), axis=3).astype(jnp.float32)
         else:
             current, normed_all, qkv = comm_call(
                 sum_project_kernel, "sum_project", 2, 32.0, [wide_array(piece, width)] + outs,
                 [pltpu.VMEM((n_seq, piece, width), low)] + sum_scratch(piece, width), 14, part, middle, gain_one, qkv_weight
             )
         qkv = qkv.reshape(length, 3 * head_width)
-        own_table = lax.dynamic_slice_in_dim(tables[layer], seq_index * local_heads, local_heads, 1)
-        line = jnp.dot(own_table.T, line_hot, precision=highest_precision)
         if layer == 0:
-            mixed, log_total, grad_rows = attend_gather(qkv, seg_row, seg_col, line, grad, n_tensor)
+            mixed, log_total, grad_rows, qkv_all, out_all = attend_gather(
+                qkv, seg_row, seg_col, lines[layer], grad, own_qkv[1], own_out[1], n_tensor, n_dp
+            )
+            qkv_weights.append(qkv_all)
+            out_weights.append(out_all)
         else:
-            mixed, log_total = attend(qkv, seg_row, seg_col, line)
+            mixed, log_total = attend(qkv, seg_row, seg_col, lines[layer])
         merged, middle, tokens = comm_call(
             merge_kernel, "merge", 3, 21.0,
             [low_array(n_seq, piece, head_width), wide_array(piece, width), low_array(n_seq, n_tensor, piece, width)], [], 12,
             mixed.reshape(n_seq, piece, head_width), current, out_weight, gain_two
         )
-        tokens = tokens.reshape(n_plane * piece, width)
-        hot, chosen = routing(layer, routes_all)
-        router_logits = dot(tokens, routers[layer])
-        router_logits = jnp.where(chosen, router_logits, negative)
-        raised = jnp.exp(router_logits - jnp.max(router_logits, axis=1, keepdims=True))
-        shares = raised / jnp.sum(raised, axis=1, keepdims=True)
-        own_share = lax.dynamic_slice_in_dim(shares, seq_index, 1, 1)
-        slots = to_slots(hot, tokens)
-        pre = dot(slots, up)
-        hidden = gelu_parts(pre)[0].astype(low)
-        pre = pre.astype(low)
-        result = dot_nt(hidden, down).astype(low)
-        part = (own_share * from_slots(hot, result)).astype(low)
+        tokens = tokens.reshape(n_seq, group_rows, width)
+        part, slots, pre, shares = run_experts(tokens, slot[layer], chosen[layer], own_hot, routers[layer], up, down, capacity)
         part = part.reshape(n_seq, n_tensor, piece, width)
-        saved.append(
-            (current, normed_all, qkv, line, log_total, merged, middle, tokens, hot, shares, own_share, slots, pre, hidden,
-             qkv_weight, out_weight, up, down)
-        )
+        saved.append((current, normed_all, qkv, log_total, merged, middle, tokens, shares, slots, pre, qkv_weight, out_weight, up, down))
 
     (block_output,) = comm_call(
         sum_kernel, "sum_last", 4, 16.0, [wide_array(piece, width)], [pltpu.VMEM((n_seq, piece, width), low)] + sum_scratch(piece, width),
         10, part, middle
     )
-    results = [None] * LAYERS
+
+    def shard_sum(values):
+        return lax.psum_scatter(values, "dp", scatter_dimension=0, tiled=True)
+
+    up_shards, down_shards, qkv_grads, out_grads = ([None] * LAYERS for _ in range(4))
+    out_rows = half // n_seq
+    packed_rows = -(-(out_rows + 1) // 16) * 16
     for layer in range(LAYERS - 1, -1, -1):
-        (layer_in, normed_all, qkv, line, log_total, merged, middle, tokens, hot, shares, own_share, slots, pre, hidden,
-         qkv_weight, out_weight, up, down) = saved[layer]
-        gain_one, gain_two = gains_one[layer][None], gains_two[layer][None]
-        grad_rows = grad_rows.reshape(n_plane * piece, width).astype(jnp.float32)
-        result_grad = to_slots(hot, (own_share * grad_rows).astype(low))
-        hidden_grad = dot(result_grad, down)
-        down_grad = dot_tn(result_grad, hidden)
-        pair_sum = jnp.sum(hidden.astype(jnp.float32) * hidden_grad, axis=1)
-        pre_grad = (gelu_parts(pre.astype(jnp.float32))[1] * hidden_grad).astype(low)
-        up_grad = dot_tn(slots, pre_grad)
-        slot_grad = dot_nt(pre_grad, up).astype(low)
-        token_pair = jnp.einsum(
-            "gct,gc->gt", hot.astype(jnp.float32), pair_sum.reshape(n_seq, capacity), precision=highest_precision
-        ).reshape(-1, 1)
-        own_hot = (lax.iota(jnp.int32, experts) == seq_index).astype(jnp.float32)
-        logit_grad = (token_pair * (own_hot[None, :] - shares)).astype(low)
-        part = from_slots(hot, slot_grad) + dot_nt(logit_grad, routers[layer])
-        router_grad = dot_tn(tokens, logit_grad)
-        part = part.astype(low).reshape(n_seq, n_tensor, piece, width)
+        (layer_in, normed_all, qkv, log_total, merged, middle, tokens, shares, slots, pre, qkv_weight, out_weight, up, down) = saved[layer]
+        gain_one, gain_two = gains[0, layer], gains[1, layer]
+        part, up_grad, down_grad, router_grad = run_experts_back(
+            grad_rows.reshape(n_seq, group_rows, width), tokens, slot[layer], shares, own_hot, routers[layer], up, down, slots, pre
+        )
+        down_shards[layer] = shard_sum(down_grad)
+        up_shards[layer] = shard_sum(up_grad)
         middle_grad, out_grad, gain_two_grad, mixed_grad = comm_call(
             split_kernel, "split", 5, 22.0,
             [wide_array(piece, width), low_array(piece, width), wide_array(1, width), low_array(n_seq, piece, head_width)],
             [pltpu.VMEM((n_seq, piece, head_width), low), pltpu.VMEM((n_seq, piece, width), low)] + sum_scratch(piece, width), 13,
-            part, middle, gain_two, grad, out_weight
+            part.reshape(n_seq, n_tensor, piece, width), middle, gain_two, grad, out_weight
         )
-        out_weight_grad = jnp.einsum("gtd,te->gde", merged, out_grad, preferred_element_type=jnp.float32).reshape(width, width)
-        qkv_grad, band = attend_back(qkv, seg_row, seg_col, line, log_total, mixed_grad.reshape(length, head_width))
+        out_weight_grad = jnp.einsum("gtd,te->gde", merged, out_grad, preferred_element_type=jnp.float32)
+        operands = (qkv, seg_row, seg_col, lines[layer], log_total, mixed_grad.reshape(length, head_width))
+        if layer == 0:
+            qkv_grad, band, up_last = attend_back(*operands, up_shards[1])
+        else:
+            qkv_grad, band = attend_back(*operands)
         qkv_weight_grad = dot_tn(normed_all.reshape(length, width), qkv_grad)
         spread = layer > 0
         outs = [wide_array(piece, width), wide_array(1, width)]
@@ -744,46 +964,39 @@
         table_grad = lax.dynamic_update_slice_in_dim(
             jnp.zeros((bucket_count, HEADS), jnp.float32), table_grad, seq_index * local_heads, 1
         )
-
-        expert_grads = []
-        for piece_grad in (up_grad, down_grad):
-            piece_grad = lax.psum_scatter(piece_grad.astype(low), "dp", scatter_dimension=0, tiled=True)
-            expert_grads.append(lax.all_gather(piece_grad, "seq", axis=0).astype(jnp.float32))
-        up_total, down_total = expert_grads[0], expert_grads[1].swapaxes(1, 2)
-
-        packed = jnp.concatenate(
-            [
-                gain_one_grad.reshape(n_dp, -1),
-                gain_two_grad.reshape(n_dp, -1),
-                table_grad.reshape(n_dp, -1),
-                router_grad.reshape(n_dp, -1),
-            ],
-            axis=1,
-        )
-        packed_width = packed.shape[1]
-        lanes = width
-        per_row = n_plane * lanes
-        extra = -(-packed_width // per_row) * per_row - packed_width
-        packed = jnp.pad(packed, ((0, 0), (0, extra))).reshape(n_dp, n_plane, -1, lanes)
-        both = jnp.concatenate([out_weight_grad.reshape(n_dp, n_plane, -1, width), packed], axis=2).astype(low)
-        both = lax.psum_scatter(both.reshape((n_dp * n_plane,) + both.shape[2:]), ("dp", "seq", "tensor"), scatter_dimension=0, tiled=True)
-        both = lax.all_gather(both, ("seq", "tensor"), axis=0, tiled=True).astype(jnp.float32)
-        out_rows = shard // n_plane
-        out_total = both[:, :out_rows].reshape(shard, width)
-        packed_total = both[:, out_rows:].reshape(-1)[:packed_width]
-        gain_one_total = packed_total[: cuts[0]]
-        gain_two_total = packed_total[cuts[0] : cuts[1]]
-        table_total = packed_total[cuts[1] : cuts[2]].reshape(bucket_shard, HEADS)
-        router_total = packed_total[cuts[2] :].reshape(shard, experts)
-
-        qkv_total = lax.psum_scatter(qkv_weight_grad.astype(low), ("dp", "tensor"), scatter_dimension=0, tiled=True)
-        qkv_total = lax.all_gather(qkv_total, ("seq", "tensor"), axis=0).astype(jnp.float32)
-        qkv_total = qkv_total.reshape(n_seq, shard, 3, head_width)
-        qkv_total = jnp.moveaxis(qkv_total, 0, 2).reshape(shard, 3 * width)
-        results[layer] = (gain_one_total, qkv_total, out_total, table_total, gain_two_total, router_total, up_total, down_total)
-
-    stacked = [jnp.stack([results[layer][member] for layer in range(LAYERS)]) for member in range(8)]
-    return (block_output[None], grad[None]) + tuple(stacked)
+        table_grad = padded(table_grad.reshape(n_dp, -1)).reshape(1, width)
+        packed = jnp.concatenate([gain_one_grad, gain_two_grad, router_grad, table_grad, jnp.zeros((1, width), jnp.float32)])
+        packed = packed.reshape(n_plane, n_dp, shard).swapaxes(0, 1)[:, :, None]
+        packed = jnp.pad(packed, ((0, 0), (0, 0), (0, packed_rows - out_rows - 1), (0, width - shard)))
+        both = jnp.concatenate([out_weight_grad.reshape(n_dp, n_plane, out_rows, width), packed], axis=2).astype(low)
+        out_grads[layer] = both.reshape(n_dp, n_tensor, n_seq, packed_rows, width).transpose(1, 2, 0, 3, 4)
+        qkv_grads[layer] = qkv_weight_grad.astype(low).reshape(n_dp, n_tensor, half, 3 * head_width).swapaxes(0, 1)
+
+    down_last = lax.all_gather(down_shards[1], "seq", axis=0)
+    q_lines = [pltpu.VMEM((n_dp, half, 3 * head_width), low)] * 3
+    o_blocks = [
+        pltpu.VMEM((n_seq, n_dp, packed_rows, width), low),
+        pltpu.VMEM((n_seq, n_dp, packed_rows, width), low),
+        pltpu.VMEM((n_dp, packed_rows, width), low),
+    ]
+    totals = comm_call(
+        functools.partial(reduce_kernel, LAYERS), "reduce_grads", 11, 40.0,
+        [low_array(n_tensor, n_seq, half, 3 * head_width)] * LAYERS + [low_array(n_tensor, n_seq, packed_rows, width)] * LAYERS,
+        (q_lines + o_blocks) * LAYERS, LAYERS * (2 * (n_dp - 1) + 19), *qkv_grads, *out_grads
+    )
+    up_first, down_first = comm_call(
+        functools.partial(share_kernel, 2), "share", 12, 38.0, [low_array(n_seq, shard, up.shape[1])] * 2, [], 8, up_shards[0], down_shards[0]
+    )
+    qkv_total = jnp.stack(totals[:LAYERS]).astype(jnp.float32).reshape(LAYERS, n_tensor, n_seq, half, 3, head_width)
+    qkv_total = qkv_total.transpose(0, 1, 3, 4, 2, 5).reshape(LAYERS, shard, 3 * width)
+    both = jnp.stack(totals[LAYERS:]).astype(jnp.float32).reshape(LAYERS, n_plane, packed_rows, width)
+    out_total = both[:, :, :out_rows].reshape(LAYERS, shard, width)
+    small = both[:, :, out_rows, :shard]
+    router_total = small[:, 2 : 2 + experts].swapaxes(1, 2)
+    table_total = small[:, 2 + experts, : bucket_shard * HEADS].reshape(LAYERS, bucket_shard, HEADS)
+    up_total = jnp.stack([up_first, up_last]).astype(jnp.float32)
+    down_total = jnp.stack([down_first, down_last]).astype(jnp.float32).swapaxes(2, 3)
+    return (block_output[None], grad[None], small[:, 0], qkv_total, out_total, table_total, small[:, 1], router_total, up_total, down_total)
 
 
 def solution(mesh):

time: 1080 us -> 717 us (0.66)
  waiting for transfers between devices: 386 us -> 2.58 us
  Pallas kernels: 334 us -> 598 us
  matrix products: 139 us -> 9.48 us
  blocking collectives: 101 us -> 0 us
    reduce_scatter x8 -> x4, waiting for transfers between devices: 220 us -> 0.03 us  [shard_sum(): return lax.psum_scatter(values, 'dp', scatter_dimension=0, tiled=True)]
    pallas_call x10 -> x14, Pallas kernels: 277 us -> 487 us  [comm_call(): pl.pallas_call(kernel, out_shape=tuple(outs), in_specs=vmem(len(operands)...]
    all_gather x6 -> x1, waiting for transfers between devices: 131 us -> 0.01 us  [body(): down_last = lax.all_gather(down_shards[1], 'seq', axis=0)]
    all_gather x7 -> x0, blocking collectives: 101 us -> none  [the longest x2 44.7 us: attention_weights(): qkv = lax.all_gather(own_qkv[layer], 'dp', axis=0, tiled=True)]
    dot_general x18 -> x1, matrix products: 55.7 us -> 0.26 us  [body(): jnp.einsum('lbh,bs->lhs', own_tables, line_hot, precision=highest_precision)]
    pallas_call x2 -> x5, Pallas kernels: 41.9 us -> 95.6 us  [the longest x2 49 us: run_experts_back(): pl.pallas_call(experts_back_kernel, grid=(groups,), out_shape=(low_array(...]
    dot_general x8 -> x1, matrix products: 44.5 us -> 0.18 us  [dot(): return jnp.dot(left, right, preferred_element_type=jnp.float32)]
    all_gather x2, waiting for transfers between devices: 32.8 us -> 0.02 us  [expert_weights(): down = lax.all_gather(own_down[layer], 'dp', axis=0, tiled=True)]
  transfers between devices with their start and end apart: 18 -> 9, of which waited for: 10 -> 0; matrix products, arithmetic and copies ran while one was open for 19% -> 11% of each run, Pallas kernels for 31% -> 79%
where the time goes in v3:
time: 717 us; the launch traced here: 707 us
  Pallas kernels  598 us (83%)
  local copies, waits for them, and re-layouts  57.5 us (8%)
  other arithmetic  23.9 us (3%)
  between operations  15 us (2%)
  matrix products  9.48 us (1%)
    pallas_call x14, Pallas kernels, comm_call(): pl.pallas_call(kernel, out_shape=tuple(outs), in_specs=vmem(len(operands)...  487 us
    pallas_call x2, Pallas kernels, run_experts_back(): pl.pallas_call(experts_back_kernel, grid=(groups,), out_shape=(low_array(...  49 us
    pallas_call x2, Pallas kernels, run_experts(): pl.pallas_call(experts_kernel, grid=(groups,), out_shape=(low_array(group...  25.6 us
    pallas_call x1, Pallas kernels, attend_back(): pl.pallas_call(functools.partial(attn_bwd_kernel, heads, span, False), ou...  21 us
    pallas_call x1, Pallas kernels, attend(): pl.pallas_call(functools.partial(attn_fwd_kernel, heads, span, False), ou...  15.5 us
  transfers between devices with their start and end apart: 9, of which 0 were waited for; matrix products, arithmetic and copies ran while one was open for 11% of the time, Pallas kernels for 79%

profile of v3, /device:TPU:0, one launch (start us, length us, event | category | flops | bytes accessed | tf_op | source)
XLA Modules:
  0.0 707.2 jit_solution(6038038017301805819)
XLA Ops:
  7.2 2.3 constant_dynamic-slice_fusion.1
  13.6 4.7 reshape.245
  18.4 4.1 dynamic-slice_reduce_fusion
  26.1 51.8 %weights.1 = (bf16[4,16,192]{2,1,0:T(8,128)(2,1)}, bf16[4,2,96,576]{3,2,1,0:T(8,128)(2,1)}, bf16[4,2,96,768]{3,2,1,0:T(8,128)(2,1)}) custom-call(bf16[16,192]{1,0:T(8,128)(2,1)} %pad.27.small_ref, bf16[2,96,576]{2,1,0:T(8,128)(2,1)} %reshape.294.qkv_ref, bf16[2,96,768]{2,1,0:T(8,128)(2,1)} %bitcast.194), custom_call_target="tpu_custom_call" | custom-call | bytes 75000000 | tf_op jit(solution)/shard_map/weights/pallas_call | solution.py:533
  83.4 22.5 %project.1 = (bf16[4,256,768]{2,1,0:T(8,128)(2,1)}, bf16[4,256,576]{2,1,0:T(8,128)(2,1)}, s32[4,16,128]{2,1,0:T(8,128)}) custom-call(f32[256,768]{1,0:T(8,128)} %bitcast.150, f32[1,768]{1,0:T(1,128)} %get-tuple-element.156.gain_ref, bf16[768,576]{1,0:T(8,128)(2,1)} %bitcast.169, s32[16,128]{1,0:T(8,128)} %reshape.247.routes_ref), custom_call_target="tpu_custom_call" | custom-call | bytes 48000000 | tf_op jit(solution)/shard_map/project/pallas_call | solution.py:533
  113.8 48.4 %attend_gather.1 = (bf16[1024,192]{1,0:T(8,128)(2,1)}, f32[3,1024,1]{2,1,0:T(8,128)}, bf16[4,2,256,768]{3,2,1,0:T(8,128)(2,1)}, bf16[4,2,96,576]{3,2,1,0:T(8,128)(2,1)}, bf16[4,2,96,768]{3,2,1,0:T(8,128)(2,1)}) custom-call(bf16[1024,576]{1,0:T(8,128)(2,1)} %bitcast.153, s32[1,1024]{1,0:T(1,128)} %refs_1_.7, s32[1024,1]{1,0:T(8,128)} %copy.165.refs_2_, ...), custom_call_target="tpu_custom_call" | custom-call | bytes 60000000 | tf_op jit(solution)/shard_map/attend_gather/pallas_call | solution.py:533
  162.2 30.8 %merge.2 = (bf16[4,256,192]{2,1,0:T(8,128)(2,1)}, f32[256,768]{1,0:T(8,128)}, bf16[4,2,256,768]{3,2,1,0:T(8,128)(2,1)}) custom-call(bf16[4,256,192]{2,1,0:T(8,128)(2,1)} %bitcast.199, f32[256,768]{1,0:T(8,128)} %bitcast.151, bf16[4,192,768]{2,1,0:T(8,128)(2,1)} %bitcast.159, f32[1,768]{1,0:T(1,128)} %get-tuple-element.155.gain_ref), custom_call_target="tpu_custom_call" | custom-call | bytes 63000000 | tf_op jit(solution)/shard_map/merge/pallas_call | solution.py:533
  195.6 12.8 %experts.2 = (bf16[4,512,768]{2,1,0:T(8,128)(2,1)}, bf16[4,256,768]{2,1,0:T(8,128)(2,1)}, bf16[4,256,1536]{2,1,0:T(8,128)(2,1)}, f32[4,512,4]{2,1,0:T(8,128)}) custom-call(bf16[4,512,768]{2,1,0:T(8,128)(2,1)} %bitcast.136, s32[4,1,512]{2,1,0:T(1,128)} %get-tuple-element.152.slot_ref, f32[4,512,4]{2,1,0:T(8,128)} %get-tuple-element.139.chosen_ref, ...), custom_call_target="tpu_custom_call" | custom-call | bytes 42000000 | tf_op jit(solution)/shard_map/experts/pallas_call | solution.py:647
  208.4 39.0 %sum_project.1 = (f32[256,768]{1,0:T(8,128)}, bf16[4,256,768]{2,1,0:T(8,128)(2,1)}, bf16[4,256,576]{2,1,0:T(8,128)(2,1)}) custom-call(bf16[4,2,256,768]{3,2,1,0:T(8,128)(2,1)} %bitcast.175, f32[256,768]{1,0:T(8,128)} %get-tuple-element.80.base_ref.middle_ref, f32[1,768]{1,0:T(1,128)} %get-tuple-element.154.gain_ref, bf16[768,576]{1,0:T(8,128)(2,1)} %bitcast.165), custom_call_target="tpu_custom_call" | custom-call | bytes 96000000 | tf_op jit(solution)/shard_map/sum_project/pallas_call | solution.py:533
  247.4 15.5 %attend.1 = (bf16[1024,192]{1,0:T(8,128)(2,1)}, f32[3,1024,1]{2,1,0:T(8,128)}) custom-call(bf16[1024,576]{1,0:T(8,128)(2,1)} %bitcast.155, s32[1,1024]{1,0:T(1,128)} %refs_1_.7, s32[1024,1]{1,0:T(8,128)} %copy.165.refs_2_, f32[3,640]{1,0:T(4,128)} %get-tuple-element.147.refs_3_), custom_call_target="tpu_custom_call" | custom-call | bytes 45000000 | tf_op jit(solution)/shard_map/attend/pallas_call | solution.py:207
  262.9 30.3 %merge.3 = (bf16[4,256,192]{2,1,0:T(8,128)(2,1)}, f32[256,768]{1,0:T(8,128)}, bf16[4,2,256,768]{3,2,1,0:T(8,128)(2,1)}) custom-call(bf16[4,256,192]{2,1,0:T(8,128)(2,1)} %bitcast.200, f32[256,768]{1,0:T(8,128)} %get-tuple-element.84.base_ref.x_ref, bf16[4,192,768]{2,1,0:T(8,128)(2,1)} %bitcast.161, f32[1,768]{1,0:T(1,128)} %get-tuple-element.153.gain_ref), custom_call_target="tpu_custom_call" | custom-call | bytes 63000000 | tf_op jit(solution)/shard_map/merge/pallas_call | solution.py:533
  293.3 12.8 %experts.3 = (bf16[4,512,768]{2,1,0:T(8,128)(2,1)}, bf16[4,256,768]{2,1,0:T(8,128)(2,1)}, bf16[4,256,1536]{2,1,0:T(8,128)(2,1)}, f32[4,512,4]{2,1,0:T(8,128)}) custom-call(bf16[4,512,768]{2,1,0:T(8,128)(2,1)} %bitcast.138, s32[4,1,512]{2,1,0:T(1,128)} %get-tuple-element.151.slot_ref, f32[4,512,4]{2,1,0:T(8,128)} %get-tuple-element.138.chosen_ref, ...), custom_call_target="tpu_custom_call" | custom-call | bytes 42000000 | tf_op jit(solution)/shard_map/experts/pallas_call | solution.py:647
  306.1 24.4 %experts_back.2 = (bf16[4,512,768]{2,1,0:T(8,128)(2,1)}, bf16[768,1536]{1,0:T(8,128)(2,1)}, bf16[768,1536]{1,0:T(8,128)(2,1)}, f32[4,768]{1,0:T(4,128)}) custom-call(bf16[4,512,768]{2,1,0:T(8,128)(2,1)} %bitcast.178, bf16[4,512,768]{2,1,0:T(8,128)(2,1)} %bitcast.139, s32[4,1,512]{2,1,0:T(1,128)} %get-tuple-element.151.slot_ref, ...), custom_call_target="tpu_custom_call" | custom-call | bytes 78000000 | tf_op jit(solution)/shard_map/experts_back/pallas_call | solution.py:665
  331.2 30.1 %split.2 = (f32[256,768]{1,0:T(8,128)}, bf16[256,768]{1,0:T(8,128)(2,1)}, f32[1,768]{1,0:T(1,128)}, bf16[4,256,192]{2,1,0:T(8,128)(2,1)}) custom-call(bf16[4,2,256,768]{3,2,1,0:T(8,128)(2,1)} %bitcast.174, f32[256,768]{1,0:T(8,128)} %get-tuple-element.88.base_ref.middle_ref, f32[1,768]{1,0:T(1,128)} %get-tuple-element.153.gain_ref, f32[256,768]{1,0:T(8,128)} %bitcast.177, ...), custom_call_target="tpu_custom_call" | custom-call | bytes 66000000 | tf_op jit(solution)/shard_map/split/pallas_call | solution.py:533
  361.3 21.0 %attend_back.1 = (bf16[1024,576]{1,0:T(8,128)(2,1)}, f32[3,640]{1,0:T(4,128)}) custom-call(bf16[1024,576]{1,0:T(8,128)(2,1)} %bitcast.156, s32[1,1024]{1,0:T(1,128)} %refs_1_.7, s32[1024,1]{1,0:T(8,128)} %copy.165.refs_2_, f32[3,640]{1,0:T(4,128)} %get-tuple-element.147.refs_3_, f32[3,1024,1]{2,1,0:T(8,128)} %get-tuple-element.90.refs_4_, ...), custom_call_target="tpu_custom_call" | custom-call | bytes 63000000 | tf_op jit(solution)/shard_map/attend_back/pallas_call | solution.py:240
  382.3 37.0 %input_grad_spread.1 = (f32[256,768]{1,0:T(8,128)}, f32[1,768]{1,0:T(1,128)}, bf16[4,2,256,768]{3,2,1,0:T(8,128)(2,1)}) custom-call(bf16[4,256,576]{2,1,0:T(8,128)(2,1)} %bitcast.190, bf16[768,576]{1,0:T(8,128)(2,1)} %bitcast.166, f32[256,768]{1,0:T(8,128)} %get-tuple-element.84.base_ref.x_ref, f32[1,768]{1,0:T(1,128)} %get-tuple-element.154.gain_ref, ...), custom_call_target="tpu_custom_call" | custom-call | bytes 96000000 | tf_op jit(solution)/shard_map/input_grad_spread/pallas_call | solution.py:533
  419.3 24.6 %experts_back.3 = (bf16[4,512,768]{2,1,0:T(8,128)(2,1)}, bf16[768,1536]{1,0:T(8,128)(2,1)}, bf16[768,1536]{1,0:T(8,128)(2,1)}, f32[4,768]{1,0:T(4,128)}) custom-call(bf16[4,512,768]{2,1,0:T(8,128)(2,1)} %bitcast.179, bf16[4,512,768]{2,1,0:T(8,128)(2,1)} %bitcast.137, s32[4,1,512]{2,1,0:T(1,128)} %get-tuple-element.152.slot_ref, ...), custom_call_target="tpu_custom_call" | custom-call | bytes 78000000 | tf_op jit(solution)/shard_map/experts_back/pallas_call | solution.py:665
  444.9 20.8 %sum_last.1 = f32[256,768]{1,0:T(8,128)} custom-call(bf16[4,2,256,768]{3,2,1,0:T(8,128)(2,1)} %bitcast.172, f32[256,768]{1,0:T(8,128)} %get-tuple-element.88.base_ref.middle_ref), custom_call_target="tpu_custom_call" | custom-call | bytes 48000000 | tf_op jit(solution)/shard_map/sum_last/pallas_call | solution.py:533
  465.7 2.5 convolution_convert_fusion.2
  469.0 30.4 %split.3 = (f32[256,768]{1,0:T(8,128)}, bf16[256,768]{1,0:T(8,128)(2,1)}, f32[1,768]{1,0:T(1,128)}, bf16[4,256,192]{2,1,0:T(8,128)(2,1)}) custom-call(bf16[4,2,256,768]{3,2,1,0:T(8,128)(2,1)} %bitcast.173, f32[256,768]{1,0:T(8,128)} %get-tuple-element.80.base_ref.middle_ref, f32[1,768]{1,0:T(1,128)} %get-tuple-element.155.gain_ref, ...), custom_call_target="tpu_custom_call" | custom-call | bytes 66000000 | tf_op jit(solution)/shard_map/split/pallas_call | solution.py:533
  504.7 27.3 %attend_back_share.1 = (bf16[1024,576]{1,0:T(8,128)(2,1)}, f32[3,640]{1,0:T(4,128)}, bf16[4,192,1536]{2,1,0:T(8,128)(2,1)}) custom-call(bf16[1024,576]{1,0:T(8,128)(2,1)} %bitcast.154, s32[1,1024]{1,0:T(1,128)} %refs_1_.7, s32[1024,1]{1,0:T(8,128)} %copy.165.refs_2_, f32[3,640]{1,0:T(4,128)} %get-tuple-element.148.refs_3_, ...), custom_call_target="tpu_custom_call" | custom-call | bytes 75000000 | tf_op jit(solution)/shard_map/attend_back_share/pallas_call | solution.py:533
  532.0 18.7 %input_grad.1 = (f32[256,768]{1,0:T(8,128)}, f32[1,768]{1,0:T(1,128)}) custom-call(bf16[4,256,576]{2,1,0:T(8,128)(2,1)} %bitcast.191, bf16[768,576]{1,0:T(8,128)(2,1)} %bitcast.170, f32[256,768]{1,0:T(8,128)} %bitcast.152, f32[1,768]{1,0:T(1,128)} %get-tuple-element.156.gain_ref, f32[256,768]{1,0:T(8,128)} %get-tuple-element.108.middle_grad_ref), custom_call_target="tpu_custom_call" | custom-call | bytes 48000000 | tf_op jit(solution)/shard_map/input_grad/pallas_call | solution.py:533
  550.7 4.0 convolution_convert_fusion.3
  554.8 2.2 copy.180
  557.7 2.8 copy_bitcast_fusion
  562.5 55.4 %reduce_grads.1 = (bf16[2,4,96,576]{3,2,1,0:T(8,128)(2,1)}, bf16[2,4,96,576]{3,2,1,0:T(8,128)(2,1)}, bf16[2,4,32,768]{3,2,1,0:T(8,128)(2,1)}, bf16[2,4,32,768]{3,2,1,0:T(8,128)(2,1)}) custom-call(bf16[2,4,96,576]{3,2,1,0:T(8,128)(2,1)} %get-tuple-element.160.refs_0_, bf16[2,4,96,576]{3,2,1,0:T(8,128)(2,1)} %get-tuple-element.159.refs_1_, ...), custom_call_target="tpu_custom_call" | custom-call | bytes 120000000 | tf_op jit(solution)/shard_map/reduce_grads/pallas_call | solution.py:533
  621.8 2.9 convert_bitcast_fusion.1
  624.7 6.8 copy.202
  631.5 6.0 reshape.283
  638.8 44.6 %share.1 = (bf16[4,192,1536]{2,1,0:T(8,128)(2,1)}, bf16[4,192,1536]{2,1,0:T(8,128)(2,1)}) custom-call(bf16[192,1536]{1,0:T(8,128)(2,1)} %reduce-scatter.7.cloned.1.call-done.refs_0_, bf16[192,1536]{1,0:T(8,128)(2,1)} %reduce-scatter.9.cloned.1.call-done.refs_1_), custom_call_target="tpu_custom_call" | custom-call | bytes 114000000 | tf_op jit(solution)/shard_map/share/pallas_call | solution.py:533
  685.1 6.0 maximum_convert_fusion
  691.1 6.8 convert_bitcast_fusion
  (170 shorter events, 42.8 us)
Async XLA Ops:
  7.2 188.4 %all-gather.11.cloned.1.call-start = ((), (), s32[]{:S(2)}) async-start(), calls=%async_computation.8 | async-start | bytes 2949120 | tf_op jit(solution)/shard_map/all_gather | solution.py:848
  9.6 186.0 %all-gather.13.cloned.1.call-start = ((), (), s32[]{:S(2)}) async-start(), calls=%async_computation.9 | async-start | bytes 2949120 | tf_op jit(solution)/shard_map/all_gather | solution.py:849
  11.0 2.5 copy-start.15
  11.0 2.6 copy-start.16
  12.1 281.1 %all-gather.15.cloned.1.call-start = ((), (), s32[]{:S(2)}) async-start(), calls=%async_computation.10 | async-start | bytes 2949120 | tf_op jit(solution)/shard_map/all_gather | solution.py:848
  12.9 280.4 %all-gather.17.cloned.1.call-start = ((), (), s32[]{:S(2)}) async-start(), calls=%async_computation.11 | async-start | bytes 2949120 | tf_op jit(solution)/shard_map/all_gather | solution.py:849
  13.4 488.6 %reduce-scatter.11.cloned.1.call-start = ((), (), s32[]{:S(2)}) async-start(), calls=%async_computation.7 | async-start | bytes 2949120 | tf_op jit(solution)/shard_map/reduce_scatter | solution.py:928
  18.4 5.2 copy-start.20
  18.4 5.2 copy-start.21
  18.4 61.1 %copy-start.14 = (s32[2,2,256,2]{2,3,1,0:T(2,128)S(1)}, s32[2,2,256,2]{2,3,1,0:T(2,128)}, u32[]{:S(2)}) copy-start(s32[2,2,256,2]{2,3,1,0:T(2,128)} %param.15) | copy-start | bytes 24580
  22.5 58.0 %copy-start.11 = (s32[1,1024]{1,0:T(1,128)S(1)}, s32[1,1024]{1,0:T(1,128)}, u32[]{:S(2)}) copy-start(s32[1,1024]{1,0:T(1,128)} %refs_1_.7) | copy-start | bytes 12292
  22.6 59.1 %slice-start = ((s32[1024]{0:T(1024)}), s32[512]{0:T(512)S(1)}, s32[]{:S(2)}) async-start(s32[1024]{0:T(1024)} %param.16), calls=%async_computation.13 | async-start | bytes 4096 | tf_op jit(solution)/shard_map/slice | solution.py:867
  330.6 174.1 %reduce-scatter.5.cloned.1.call-start = ((), (), s32[]{:S(2)}) async-start(), calls=%async_computation.4 | async-start | bytes 2949120 | tf_op jit(solution)/shard_map/reduce_scatter | solution.py:928
  331.1 307.6 %reduce-scatter.7.cloned.1.call-start = ((), (), s32[]{:S(2)}) async-start(), calls=%async_computation.5 | async-start | bytes 2949120 | tf_op jit(solution)/shard_map/reduce_scatter | solution.py:928
  443.9 194.9 %reduce-scatter.9.cloned.1.call-start = ((), (), s32[]{:S(2)}) async-start(), calls=%async_computation.6 | async-start | bytes 2949120 | tf_op jit(solution)/shard_map/reduce_scatter | solution.py:928
  444.7 246.4 %all-gather.19.cloned.1.call-start = ((), (), s32[]{:S(2)}) async-start(), calls=%async_computation.12 | async-start | bytes 2949120 | tf_op jit(solution)/shard_map/all_gather | solution.py:975
  444.9 20.8 %copy-start.5 = (bf16[1024,576]{1,0:T(8,128)(2,1)S(1)}, bf16[1024,576]{1,0:T(8,128)(2,1)}, u32[]{:S(2)}) copy-start(bf16[1024,576]{1,0:T(8,128)(2,1)} %get-tuple-element.97) | copy-start | bytes 3538948
  468.9 31.3 %copy-start.13 = (f32[4,768]{1,0:T(4,128)S(1)}, f32[4,768]{1,0:T(4,128)}, u32[]{:S(2)}) copy-start(f32[4,768]{1,0:T(4,128)} %get-tuple-element.116) | copy-start | bytes 36868
  468.9 31.4 %copy-start.18 = (f32[1,768]{1,0:T(1,128)S(1)}, f32[1,768]{1,0:T(1,128)}, u32[]{:S(2)}) copy-start(f32[1,768]{1,0:T(1,128)} %get-tuple-element.120) | copy-start | bytes 9220
  468.9 31.5 %copy-start.17 = (f32[1,768]{1,0:T(1,128)S(1)}, f32[1,768]{1,0:T(1,128)}, u32[]{:S(2)}) copy-start(f32[1,768]{1,0:T(1,128)} %get-tuple-element.121) | copy-start | bytes 9220
  469.0 31.6 %copy-start.12 = (f32[4,768]{1,0:T(4,128)S(1)}, f32[4,768]{1,0:T(4,128)}, u32[]{:S(2)}) copy-start(f32[4,768]{1,0:T(4,128)} %get-tuple-element.122) | copy-start | bytes 36868
  469.0 31.7 %copy-start.22 = (f32[3,640]{1,0:T(4,128)S(1)}, f32[3,640]{1,0:T(4,128)}, u32[]{:S(2)}) copy-start(f32[3,640]{1,0:T(4,128)} %get-tuple-element.123) | copy-start | bytes 23044
  469.0 33.1 %copy-start.8 = (bf16[4,256,192]{2,1,0:T(8,128)(2,1)S(1)}, bf16[4,256,192]{2,1,0:T(8,128)(2,1)}, u32[]{:S(2)}) copy-start(bf16[4,256,192]{2,1,0:T(8,128)(2,1)} %get-tuple-element.118) | copy-start | bytes 1179652
  469.0 33.1 %copy-start.9 = (bf16[256,768]{1,0:T(8,128)(2,1)S(1)}, bf16[256,768]{1,0:T(8,128)(2,1)}, u32[]{:S(2)}) copy-start(bf16[256,768]{1,0:T(8,128)(2,1)} %get-tuple-element.119) | copy-start | bytes 1179652
  550.7 6.3 copy-start.19
  550.7 6.4 copy-start.23
  557.6 2.8 copy-start.2
  617.9 3.1 copy-start.6
  631.5 51.9 %copy-start.3 = (bf16[2,4,32,768]{3,2,1,0:T(8,128)(2,1)S(1)}, bf16[2,4,32,768]{3,2,1,0:T(8,128)(2,1)}, u32[]{:S(2)}) copy-start(bf16[2,4,32,768]{3,2,1,0:T(8,128)(2,1)} %get-tuple-element.124) | copy-start | bytes 1179652
  631.5 51.9 %copy-start.4 = (bf16[2,4,32,768]{3,2,1,0:T(8,128)(2,1)S(1)}, bf16[2,4,32,768]{3,2,1,0:T(8,128)(2,1)}, u32[]{:S(2)}) copy-start(bf16[2,4,32,768]{3,2,1,0:T(8,128)(2,1)} %get-tuple-element.125) | copy-start | bytes 1179652
  637.5 47.6 %copy-start.1 = (bf16[4,192,1536]{2,1,0:T(8,128)(2,1)S(1)}, bf16[4,192,1536]{2,1,0:T(8,128)(2,1)}, u32[]{:S(2)}) copy-start(bf16[4,192,1536]{2,1,0:T(8,128)(2,1)} %get-tuple-element.131) | copy-start | bytes 7077892
  691.1 6.8 copy-start
  (2 other events, 2.4 us)
Sparse Core Ops, SparseCore 0:
  10.1 76.5 all-gather.10
  88.9 65.7 all-gather.12
  156.8 48.3 all-gather.14
  206.7 48.7 all-gather.16
  330.7 48.4 reduce-scatter.10
  381.3 47.0 reduce-scatter.4
  444.0 48.4 reduce-scatter.6
  494.8 47.0 reduce-scatter.8
  543.8 52.8 all-gather.18

commit v4 on v3

--- a/solution.py
+++ b/solution.py
@@ -24,23 +24,32 @@
 TN = (((0,), (0,)), ((), ()))
 
 
-def visit_blocks(length, span, one_block, midway=None):
-    full = span // ROWS
-    for i in range(min(full - 1, length // ROWS)):
-        one_block(i * ROWS, 0, (i + 1) * ROWS)
+def visit_blocks(length, span, one_block, hook, hooks_at):
+    full, count = span // ROWS, length // ROWS
 
     def step(i, carry):
         start = pl.multiple_of(i * ROWS, ROWS)
         one_block(start, pl.multiple_of(start + ROWS - span, ROWS), span)
         return carry
 
-    middle = (full + length // ROWS) // 2
-    if midway is None:
-        lax.fori_loop(full - 1, length // ROWS, step, 0)
-    else:
-        lax.fori_loop(full - 1, middle, step, 0)
-        midway()
-        lax.fori_loop(middle, length // ROWS, step, 0)
+    for i in range(full - 1):
+        if i in hooks_at:
+            hook()
+        one_block(i * ROWS, 0, (i + 1) * ROWS)
+    stops = [full - 1] + [i for i in range(full - 1, count) if i in hooks_at] + [count]
+    for low, high in zip(stops, stops[1:]):
+        if low in hooks_at:
+            hook()
+        lax.fori_loop(low, high, step, 0)
+
+
+def background(tasks):
+    tasks = list(tasks)
+
+    def hook():
+        tasks[:] = [task for task in tasks if next(task, wires_done) is not wires_done]
+
+    return hook, lambda: run_all(*tasks)
 
 
 def fill_mask(mask_ref, segr_ref, segc_ref, start, low, width):
@@ -62,27 +71,41 @@
         parts_ref[h] = part * jnp.bfloat16(0.125) if h < heads else part
 
 
-def attn_fwd_kernel(heads, span, spread, *refs):
+def fetch_steps(wires, place, own, whole):
+    me, core, near, far, cross = place
+    width = whole.shape[-1]
+    columns = pl.ds(pl.multiple_of(core * (width // 2), width // 2), width // 2)
+    around = [wires.copy(own, whole.at[:, me, :, columns], {"seq": spot}) for spot in (cross, near, far)]
+    whole[:, me, :, columns] = own[...]
+    yield
+    for one in around:
+        one.wait_recv()
+    block = whole.at[:, :, :, columns]
+    onward = wires.copy(block, block, {"tensor": 1 - core})
+    yield
+    onward.wait_recv()
+
+
+def attn_fwd_kernel(heads, span, mode, *refs):
     qkv_ref, segr_ref, segc_ref, line_ref = refs[:4]
-    midway = None
-    if spread:
-        rows_ref, qkv_next, out_next, out_ref, lse_ref, gathered_ref, qkv_all, out_all = refs[4:12]
-        wires = Wires(*refs[16:])
-        place = plane_place()
-        core = place[1]
-        line_me, targets, sources = dp_peers()
-        greet(*plane_peers(place), *[{"dp": spot} for spot in targets])
-        gathered_ref[place[0], core] = rows_ref[...].astype(jnp.bfloat16)
-        first = plane_gather_start(wires, gathered_ref, place)
-        qkvs = line_start(wires, qkv_next, qkv_all, core, line_me, targets)
-        outs = line_start(wires, out_next, out_all, core, line_me, targets)
-        second = []
-        midway = lambda: second.extend(plane_gather_forward(wires, gathered_ref, place, first))
-        refs = refs[12:16]
+    place = plane_place()
+    me, core, near, far, cross = place
+    wires = Wires(*refs[-2:])
+    if mode == "fetch":
+        own_refs, (out_ref, lse_ref), whole_refs, scratch = refs[4:6], refs[6:8], refs[8:10], refs[10:14]
+        greet({"seq": near}, {"seq": far}, {"seq": cross}, {"tensor": 1 - core})
+        tasks = [fetch_steps(wires, place, *pair) for pair in zip(own_refs, whole_refs)]
+        hooks_at = (6,)
     else:
-        out_ref, lse_ref = refs[4:6]
-        refs = refs[6:10]
-    parts_ref, mixed_ref, slab_ref, mask_ref = refs
+        rows_ref, out_ref, lse_ref, gathered_ref = refs[4:8]
+        scratch = refs[8:12]
+        greet(*plane_peers(place))
+        gathered_ref[me, core] = rows_ref[...].astype(jnp.bfloat16)
+        tasks = [gather_steps(wires, gathered_ref, place, True)]
+        hooks_at = (4, 6)
+    hook, finish = background(tasks)
+    hook()
+    parts_ref, mixed_ref, slab_ref, mask_ref = scratch
     length = qkv_ref.shape[0]
     fill_slab(slab_ref, line_ref, heads, span)
     split_heads(qkv_ref, parts_ref, heads)
@@ -106,33 +129,30 @@
 
         lax.fori_loop(0, heads, one_head, 0)
 
-    visit_blocks(length, span, one_block, midway)
+    visit_blocks(length, span, one_block, hook, hooks_at)
     out_ref[...] = jnp.concatenate([mixed_ref[h] for h in range(heads)], axis=1)
-    if spread:
-        plane_gather_finish(wires, gathered_ref, place, first, second)
-        onward = line_forward(wires, qkv_all, core, qkvs, sources)
-        onward += line_forward(wires, out_all, core, outs, sources)
-        for one in onward:
-            one.wait_recv()
-        wires.finish()
-
-
-def attn_bwd_kernel(heads, span, spread, *refs):
+    finish()
+    wires.finish()
+
+
+def attn_bwd_kernel(heads, span, mode, *refs):
     qkv_ref, segr_ref, segc_ref, line_ref, lse_ref, grad_ref = refs[:6]
-    midway = None
-    if spread:
+    place = plane_place()
+    me, core, near, far, cross = place
+    wires = Wires(*refs[-2:])
+    if mode == "share":
         shard_ref, out_ref, band_ref, shared_ref = refs[6:10]
-        wires = Wires(*refs[18:])
-        place = plane_place()
-        greet({"seq": place[2]}, {"seq": place[3]})
-        shared_ref[place[0]] = shard_ref[...]
-        first = seq_gather_start(wires, shared_ref, place)
-        second = []
-        midway = lambda: second.extend(seq_gather_forward(wires, shared_ref, place, first))
+        greet({"seq": near}, {"seq": far})
+        shared_ref[me] = shard_ref[...]
+        tasks = [gather_steps(wires, shared_ref, place, False)]
         refs = refs[10:18]
     else:
-        out_ref, band_ref = refs[6:8]
-        refs = refs[8:16]
+        part_ref, base_ref, out_ref, band_ref, total_ref = refs[6:11]
+        greet(*plane_peers(place))
+        tasks = [plane_sum_steps(wires, place, part_ref, refs[19], refs[20:26], add_to(total_ref, base_ref))]
+        refs = refs[11:19]
+    hook, finish = background(tasks)
+    hook()
     parts_ref, gparts_ref, qgrad_ref, kgrad_ref, vgrad_ref, slab_ref, mask_ref, band_acc = refs
     length = qkv_ref.shape[0]
     fill_slab(slab_ref, line_ref, heads, span)
@@ -169,7 +189,7 @@
 
         lax.fori_loop(0, heads, one_head, 0)
 
-    visit_blocks(length, span, one_block, midway)
+    visit_blocks(length, span, one_block, hook, (5, 7) if mode == "share" else (3, 6))
     parts = [qgrad_ref[h] for h in range(heads)]
     parts += [kgrad_ref[h].astype(jnp.bfloat16) for h in range(heads)]
     parts += [vgrad_ref[h].astype(jnp.bfloat16) for h in range(heads)]
@@ -182,10 +202,8 @@
             acc = jnp.where((row & bit) != 0, pltpu.roll(acc, span - bit, 1), acc)
             bit *= 2
         band_ref[h : h + 1, :] = jnp.sum(acc, axis=0, keepdims=True)
-    if spread:
-        for one in second:
-            one.wait_recv()
-        wires.finish()
+    finish()
+    wires.finish()
 
 
 def vmem(count):
@@ -201,27 +219,18 @@
     ]
 
 
-def attend(qkv, seg_row, seg_col, line):
+def attend(qkv, seg_row, seg_col, line, extra, extra_outs, mode, number, wire_count):
     length, width = qkv.shape
     heads, span = line.shape
-    return pl.pallas_call(
-        functools.partial(attn_fwd_kernel, heads, span, False),
-        out_shape=(
-            jax.ShapeDtypeStruct((length, heads * HD), jnp.bfloat16),
-            jax.ShapeDtypeStruct((heads, length, 1), jnp.float32),
-        ),
-        in_specs=vmem(4),
-        out_specs=tuple(vmem(2)),
-        scratch_shapes=attend_scratch(heads, length, span),
-        cost_estimate=cost(15.0),
-        name="attend",
-    )(qkv, seg_row, seg_col, line)
-
-
-def attend_back(qkv, seg_row, seg_col, line, lse, grad, shard=None):
+    outs = [low_array(length, heads * HD), wide_array(heads, length, 1)] + extra_outs
+    return comm_call(functools.partial(attn_fwd_kernel, heads, span, mode), "attend_" + mode, number, 18.0, outs,
+                     attend_scratch(heads, length, span), wire_count, qkv, seg_row, seg_col, line, *extra)
+
+
+def attend_back(qkv, seg_row, seg_col, line, lse, grad, extra, extra_outs, extra_scratch, mode, number, wire_count):
     length, width = qkv.shape
     heads, span = line.shape
-    outs = [low_array(length, width), wide_array(heads, span)]
+    outs = [low_array(length, width), wide_array(heads, span)] + extra_outs
     scratch = [
         pltpu.VMEM((3 * heads, length, HD), jnp.bfloat16),
         pltpu.VMEM((heads, length, HD), jnp.bfloat16),
@@ -232,20 +241,8 @@
         pltpu.VMEM((ROWS, span), jnp.float32),
         pltpu.VMEM((heads, ROWS, span), jnp.float32),
     ]
-    operands = [qkv, seg_row, seg_col, line, lse, grad]
-    if shard is not None:
-        outs.append(low_array(4, *shard.shape))
-        kernel = functools.partial(attn_bwd_kernel, heads, span, True)
-        return comm_call(kernel, "attend_back_share", 9, 25.0, outs, scratch, 4, *operands, shard)
-    return pl.pallas_call(
-        functools.partial(attn_bwd_kernel, heads, span, False),
-        out_shape=tuple(outs),
-        in_specs=vmem(6),
-        out_specs=tuple(vmem(2)),
-        scratch_shapes=scratch,
-        cost_estimate=cost(21.0),
-        name="attend_back",
-    )(*operands)
+    return comm_call(functools.partial(attn_bwd_kernel, heads, span, mode), "attend_back_" + mode, number, 23.0, outs,
+                     scratch + extra_scratch, wire_count, qkv, seg_row, seg_col, line, lse, grad, *extra)
 
 
 MESH_ID = pl.DeviceIdType.MESH
@@ -285,69 +282,57 @@
     pl.semaphore_wait(barrier, len(places))
 
 
-def seq_gather_start(wires, ref, place):
-    me, core, near, far, cross = place
-    mine = ref.at[me]
-    return wires.copy(mine, mine, {"seq": near}), wires.copy(mine, mine, {"seq": far})
-
-
-def seq_gather_forward(wires, ref, place, first):
-    me, core, near, far, cross = place
-    half = ref.shape[1] // 2
-    first[0].wait_recv()
-    upper = ref.at[near, pl.ds(0, half)]
-    one = wires.copy(upper, upper, {"seq": far})
-    first[1].wait_recv()
-    lower = ref.at[far, pl.ds(half, half)]
-    return one, wires.copy(lower, lower, {"seq": near})
-
-
-def plane_gather_start(wires, ref, place):
-    me, core, near, far, cross = place
-    mine = ref.at[me, core]
-    return (
-        wires.copy(mine, mine, {"seq": near}),
-        wires.copy(mine, mine, {"seq": far}),
-        wires.copy(mine, mine, {"tensor": 1 - core}),
-    )
-
-
-def plane_gather_forward(wires, ref, place, first):
-    me, core, near, far, cross = place
-    half = ref.shape[2] // 2
-    partner = {"tensor": 1 - core}
-    first[0].wait_recv()
-    upper = ref.at[near, core, pl.ds(0, half)]
-    one = wires.copy(upper, upper, {"seq": far})
-    first[1].wait_recv()
-    lower = ref.at[far, core, pl.ds(half, half)]
-    two = wires.copy(lower, lower, {"seq": near})
-    block = ref.at[near, core]
-    three = wires.copy(block, block, partner)
-    block = ref.at[far, core]
-    four = wires.copy(block, block, partner)
-    return one, two, three, four
-
-
-def plane_gather_finish(wires, ref, place, first, second):
-    me, core, near, far, cross = place
-    half = ref.shape[2] // 2
-    partner = {"tensor": 1 - core}
-    second[0].wait_recv()
-    upper = ref.at[cross, core, pl.ds(0, half)]
-    one = wires.copy(upper, upper, partner)
-    second[1].wait_recv()
-    lower = ref.at[cross, core, pl.ds(half, half)]
-    two = wires.copy(lower, lower, partner)
-    for other in (first[2], second[2], second[3], one, two):
-        other.wait_recv()
+def gather_steps(wires, ref, place, paired):
+    me, core, near, far, cross = place
+    half = ref.shape[-2] // 2
+    to_near, to_far, partner = {"seq": near}, {"seq": far}, {"tensor": 1 - core}
+
+    def part(spot, start, size):
+        return ref.at[spot, core, pl.ds(start, size)] if paired else ref.at[spot, pl.ds(start, size)]
+
+    def send(spot, start, size, where):
+        block = part(spot, start, size)
+        return wires.copy(block, block, where)
+
+    near_top = send(me, 0, half, to_near)
+    far_low = send(me, half, half, to_far)
+    near_low = send(me, half, half, to_near)
+    far_top = send(me, 0, half, to_far)
+    inside = [send(me, 0, 2 * half, partner)] if paired else []
+    yield
+    near_top.wait_recv()
+    cross_top = send(near, 0, half, to_far)
+    far_low.wait_recv()
+    cross_low = send(far, half, half, to_near)
+    yield
+    near_low.wait_recv()
+    inside += [send(near, 0, 2 * half, partner)] if paired else []
+    far_top.wait_recv()
+    inside += [send(far, 0, 2 * half, partner)] if paired else []
+    yield
+    cross_top.wait_recv()
+    inside += [send(cross, 0, half, partner)] if paired else []
+    cross_low.wait_recv()
+    inside += [send(cross, half, half, partner)] if paired else []
+    yield
+    for one in inside:
+        one.wait_recv()
+
+
+def run_all(*tasks):
+    tasks = list(tasks)
+    while tasks:
+        tasks = [task for task in tasks if next(task, wires_done) is not wires_done]
+
+
+wires_done = object()
 
 
 def wide(values):
     return values.astype(jnp.float32)
 
 
-def cross_sum(wires, place, total_of, out_refs):
+def cross_steps(wires, place, total_of, out_refs, done):
     me, core, near, far, cross = place
     cross_ref, near_ref, far_ref, cross_in, near_in, far_in = out_refs
     half = near_ref.shape[0] // 2
@@ -359,19 +344,21 @@
     near_one = wires.copy(near_ref.at[top], near_in.at[top], {"seq": near})
     far_ref[...] = total_of(far).astype(far_ref.dtype)
     far_one = wires.copy(far_ref.at[bottom], far_in.at[bottom], {"seq": far})
-    own = total_of(me)
+    yield
     to_near.wait_recv()
     far_ref[top, :] = (wide(far_ref[top, :]) + wide(cross_in[top, :])).astype(far_ref.dtype)
     far_two = wires.copy(far_ref.at[top], far_in.at[top], {"seq": far})
     to_far.wait_recv()
     near_ref[bottom, :] = (wide(near_ref[bottom, :]) + wide(cross_in[bottom, :])).astype(near_ref.dtype)
     near_two = wires.copy(near_ref.at[bottom], near_in.at[bottom], {"seq": near})
+    own = total_of(me)
+    yield
     for one in (near_one, far_one, far_two, near_two):
         one.wait_recv()
-    return own + wide(near_in[...]) + wide(far_in[...])
-
-
-def plane_sum(wires, place, part_ref, partner_in, out_refs):
+    done(own + wide(near_in[...]) + wide(far_in[...]))
+
+
+def plane_sum_steps(wires, place, part_ref, partner_in, out_refs, done):
     me, core, near, far, cross = place
     arrivals = {}
     for name, spot in (("cross", cross), ("near", near), ("far", far), ("me", me)):
@@ -382,7 +369,14 @@
         arrivals[next(order)].wait_recv()
         return wide(part_ref[spot, core]) + wide(partner_in[spot])
 
-    return cross_sum(wires, place, total_of, out_refs)
+    yield
+    yield from cross_steps(wires, place, total_of, out_refs, done)
+
+
+def plane_sum(wires, place, part_ref, partner_in, out_refs):
+    totals = []
+    run_all(plane_sum_steps(wires, place, part_ref, partner_in, out_refs, totals.append))
+    return totals[0]
 
 
 def sum_scratch(piece, width):
@@ -425,14 +419,22 @@
 def project_steps(place, x_ref, gain_ref, w_ref, normed_ref, qkv_ref, wires):
     me, core, near, far, cross = place
     normed_ref[me] = norm_of(x_ref[...], gain_ref[...]).astype(jnp.bfloat16)
-    first = seq_gather_start(wires, normed_ref, place)
+    task = gather_steps(wires, normed_ref, place, False)
+    next(task)
     qkv_ref[me] = dot(normed_ref[me], w_ref[...]).astype(jnp.bfloat16)
-    second = seq_gather_forward(wires, normed_ref, place, first)
+    next(task)
+    next(task)
     qkv_ref[near] = dot(normed_ref[near], w_ref[...]).astype(jnp.bfloat16)
     qkv_ref[far] = dot(normed_ref[far], w_ref[...]).astype(jnp.bfloat16)
-    second[0].wait_recv()
-    second[1].wait_recv()
+    next(task)
     qkv_ref[cross] = dot(normed_ref[cross], w_ref[...]).astype(jnp.bfloat16)
+
+
+def add_to(out_ref, base_ref):
+    def done(total):
+        out_ref[...] = base_ref[...] + total
+
+    return done
 
 
 def project_kernel(x_ref, gain_ref, w_ref, routes_ref, normed_ref, qkv_ref, routes_all_ref, send, recv):
@@ -458,20 +460,19 @@
     wires.finish()
 
 
-def sum_kernel(part_ref, base_ref, x_ref, partner_in, *rest):
-    out_refs, (send, recv) = rest[:6], rest[6:]
+def merge_kernel(fetch, mixed_ref, base_ref, w_ref, gain_ref, *refs):
     place = plane_place()
+    me, core, near, far, cross = place
+    if fetch:
+        qkv_next, merged_ref, middle_ref, tokens_ref, qkv_all, send, recv = refs
+        line_me, targets, sources = dp_peers()
+    else:
+        merged_ref, middle_ref, tokens_ref, send, recv = refs
+        targets = []
     wires = Wires(send, recv)
-    greet(*plane_peers(place))
-    x_ref[...] = base_ref[...] + plane_sum(wires, place, part_ref, partner_in, out_refs)
-    wires.finish()
-
-
-def merge_kernel(mixed_ref, base_ref, w_ref, gain_ref, merged_ref, middle_ref, tokens_ref, send, recv):
-    place = plane_place()
-    me, core, near, far, cross = place
-    wires = Wires(send, recv)
-    greet({"seq": near}, {"seq": far}, {"seq": cross}, {"tensor": 1 - core})
+    greet({"seq": near}, {"seq": far}, {"seq": cross}, {"tensor": 1 - core}, *[{"dp": spot} for spot in targets])
+    if fetch:
+        lines = line_start(wires, qkv_next, qkv_all, core, line_me, targets)
     copies = [wires.copy(mixed_ref.at[spot], merged_ref.at[me], {"seq": spot}) for spot in (cross, near, far)]
     merged_ref[me] = mixed_ref[me]
     total = base_ref[...] + dot(mixed_ref[me], w_ref[me])
@@ -480,9 +481,10 @@
         total = total + dot(merged_ref[spot], w_ref[spot])
     middle_ref[...] = total
     tokens_ref[me, core] = norm_of(total, gain_ref[...]).astype(jnp.bfloat16)
-    first = plane_gather_start(wires, tokens_ref, place)
-    second = plane_gather_forward(wires, tokens_ref, place, first)
-    plane_gather_finish(wires, tokens_ref, place, first, second)
+    run_all(gather_steps(wires, tokens_ref, place, True))
+    if fetch:
+        for one in line_forward(wires, qkv_all, core, lines, sources):
+            one.wait_recv()
     wires.finish()
 
 
@@ -517,15 +519,15 @@
     me, core, near, far, cross = place
     wires = Wires(send, recv)
     greet(*plane_peers(place)[: 3 if spread else 2])
-    normed_grad = cross_sum(wires, place, lambda spot: dot_nt(qkv_grad_ref[spot], w_ref[...]), out_refs)
+    totals = []
+    run_all(cross_steps(wires, place, lambda spot: dot_nt(qkv_grad_ref[spot], w_ref[...]), out_refs, totals.append))
+    normed_grad = totals[0]
     part, gain_grad_ref[...] = norm_back(x_ref[...], gain_ref[...], normed_grad)
     grad = middle_grad_ref[...] + part
     grad_ref[...] = grad
     if spread:
         rows_ref[me, core] = grad.astype(jnp.bfloat16)
-        first = plane_gather_start(wires, rows_ref, place)
-        second = plane_gather_forward(wires, rows_ref, place, first)
-        plane_gather_finish(wires, rows_ref, place, first, second)
+        run_all(gather_steps(wires, rows_ref, place, True))
     wires.finish()
 
 
@@ -552,16 +554,6 @@
 
 def wide_array(*shape):
     return jax.ShapeDtypeStruct(shape, jnp.float32)
-
-
-def attend_gather(qkv, seg_row, seg_col, line, rows, qkv_next, out_next, n_tensor, n_dp):
-    length, width = qkv.shape
-    heads, span = line.shape
-    piece, depth = rows.shape
-    outs = [low_array(length, heads * HD), wide_array(heads, length, 1), low_array(length // piece, n_tensor, piece, depth),
-            low_array(n_dp, *qkv_next.shape), low_array(n_dp, *out_next.shape)]
-    return comm_call(functools.partial(attn_fwd_kernel, heads, span, True), "attend_gather", 6, 20.0, outs,
-                     attend_scratch(heads, length, span), 9 + 4 * (n_dp - 1), qkv, seg_row, seg_col, line, rows, qkv_next, out_next)
 
 
 def gelu_parts(values):
@@ -595,9 +587,57 @@
     part_ref[...] = (own_share * dot_tn(hot, result)).astype(jnp.bfloat16)
 
 
+class Replay(Wires):
+    def __init__(self, send, recv, ref, place, stage):
+        super().__init__(send, recv)
+        self.stage, self.now = stage, 0
+        task = gather_steps(self, ref, place, False)
+        for self.now in range(1, stage + 1):
+            next(task, None)
+        if stage == 5:
+            self.finish()
+
+    def copy(self, src, dst, where):
+        one = pltpu.make_async_remote_copy(
+            src_ref=src, dst_ref=dst, send_sem=self.send.at[self.next], recv_sem=self.recv.at[self.next],
+            device_id=where, device_id_type=MESH_ID,
+        )
+        self.next += 1
+        if self.now == self.stage:
+            one.start()
+        self.started.append(one)
+        return Held(one, self)
+
+
+class Held:
+    def __init__(self, one, owner):
+        self.one, self.owner = one, owner
+
+    def wait_recv(self):
+        if self.owner.now == self.owner.stage or self.owner.stage == 5 and self.owner.now > 2:
+            self.one.wait_recv()
+
+
 def experts_back_kernel(rows_ref, tokens_ref, slot_ref, shares_ref, own_ref, router_ref, up_ref, down_ref, slots_ref, pre_ref,
-                        part_ref, up_grad_ref, down_grad_ref, router_grad_ref, up_acc, down_acc):
-    group = pl.program_id(0)
+                        *refs):
+    group, last = pl.program_id(0), pl.num_programs(0) - 1
+    if len(refs) > 6:
+        shard_ref, part_ref, up_grad_ref, down_grad_ref, router_grad_ref, shared_ref, up_acc, down_acc, landing, send, recv = refs
+
+        @pl.when(group == 0)
+        def _():
+            place = plane_place()
+            greet({"seq": place[2]}, {"seq": place[3]})
+            landing[place[0]] = shard_ref[...]
+            Replay(send, recv, landing, plane_place(), 1)
+
+        @pl.when(group == 2)
+        def _():
+            Replay(send, recv, landing, plane_place(), 2)
+
+    else:
+        part_ref, up_grad_ref, down_grad_ref, router_grad_ref, up_acc, down_acc = refs
+        shared_ref = None
 
     @pl.when(group == 0)
     def _():
@@ -627,10 +667,17 @@
     router_grad_ref[...] += dot_tn(logit_grad, tokens_ref[...])
     part_ref[...] = (dot_tn(hot, slot_grad) + dot(logit_grad, router_ref[...])).astype(jnp.bfloat16)
 
-    @pl.when(group == pl.num_programs(0) - 1)
+    @pl.when(group == last)
     def _():
         up_grad_ref[...] = up_acc[...].astype(jnp.bfloat16)
         down_grad_ref[...] = down_acc[...].astype(jnp.bfloat16)
+
+    if shared_ref is not None:
+
+        @pl.when(group == last)
+        def _():
+            Replay(send, recv, landing, plane_place(), 5)
+            shared_ref[...] = landing[...]
 
 
 def by_group(*shape):
@@ -658,22 +705,35 @@
     )(tokens, slot, chosen, own, router, up, down)
 
 
-def run_experts_back(rows_grad, tokens, slot, shares, own, router, up, down, slots, pre):
+def run_experts_back(rows_grad, tokens, slot, shares, own, router, up, down, slots, pre, shard=None):
     groups, rows, width = tokens.shape
     experts, wide_ff = router.shape[0], up.shape[1]
     capacity = slots.shape[1]
+    outs = [low_array(groups, rows, width), low_array(width, wide_ff), low_array(width, wide_ff), wide_array(experts, width)]
+    out_specs = [by_group(rows, width), held(width, wide_ff), held(width, wide_ff), held(experts, width)]
+    in_specs = [by_group(rows, width), by_group(rows, width), by_group(1, rows), by_group(rows, experts), held(1, experts),
+                held(experts, width), held(width, wide_ff), held(width, wide_ff), by_group(capacity, width), by_group(capacity, wide_ff)]
+    scratch = [pltpu.VMEM((width, wide_ff), jnp.float32), pltpu.VMEM((width, wide_ff), jnp.float32)]
+    operands = [rows_grad, tokens, slot, shares, own, router, up, down, slots, pre]
+    options = {}
+    if shard is not None:
+        operands.append(shard)
+        in_specs.append(held(*shard.shape))
+        outs.append(low_array(4, *shard.shape))
+        out_specs.append(held(4, *shard.shape))
+        scratch += [pltpu.VMEM((4,) + shard.shape, jnp.bfloat16)] + sems(6)
+        options = {"collective_id": 13, "has_side_effects": True}
     return pl.pallas_call(
         experts_back_kernel,
         grid=(groups,),
-        out_shape=(low_array(groups, rows, width), low_array(width, wide_ff), low_array(width, wide_ff), wide_array(experts, width)),
-        in_specs=[by_group(rows, width), by_group(rows, width), by_group(1, rows), by_group(rows, experts), held(1, experts),
-                  held(experts, width), held(width, wide_ff), held(width, wide_ff), by_group(capacity, width), by_group(capacity, wide_ff)],
-        out_specs=(by_group(rows, width), held(width, wide_ff), held(width, wide_ff), held(experts, width)),
-        scratch_shapes=[pltpu.VMEM((width, wide_ff), jnp.float32), pltpu.VMEM((width, wide_ff), jnp.float32)],
-        compiler_params=pltpu.CompilerParams(dimension_semantics=("arbitrary",)),
-        cost_estimate=cost(26.0),
-        name="experts_back",
-    )(rows_grad, tokens, slot, shares, own, router, up, down, slots, pre)
+        out_shape=tuple(outs),
+        in_specs=in_specs,
+        out_specs=tuple(out_specs),
+        scratch_shapes=scratch,
+        compiler_params=pltpu.CompilerParams(dimension_semantics=("arbitrary",), **options),
+        cost_estimate=cost(25.0),
+        name="experts_back" if shard is None else "experts_back_share",
+    )(*operands)
 
 
 def dp_peers():
@@ -697,96 +757,137 @@
     return onward
 
 
-def weights_kernel(small_ref, qkv_ref, out_ref, small_all, qkv_all, out_all, send, recv):
-    core = lax.axis_index("tensor")
+def weights_kernel(small_ref, whole_ref, outs_ref, small_all, qkv_all, qkv_next, one_piece, two_piece, own_ref, send, recv):
+    core, place = lax.axis_index("tensor"), lax.axis_index("seq")
     me, targets, sources = dp_peers()
     wires = Wires(send, recv)
     greet(*[{"dp": spot} for spot in targets], {"tensor": 1 - core})
     smalls = [wires.copy(small_ref, small_all.at[me], {"dp": spot}) for spot in targets]
     small_all[me] = small_ref[...]
-    qkvs = line_start(wires, qkv_ref, qkv_all, core, me, targets)
-    outs = line_start(wires, out_ref, out_all, core, me, targets)
+    layers, rows, columns = whole_ref.shape
+    part, parts = columns // 3, lax.axis_size("seq")
+    size = part // parts
+    for spot in range(parts):
+
+        @pl.when(place == spot)
+        def _():
+            for layer, target in enumerate((own_ref, qkv_next)):
+                pieces = [whole_ref[layer, :, kind * part + spot * size : kind * part + (spot + 1) * size] for kind in range(3)]
+                pieces = jnp.concatenate(pieces, axis=1)
+                target[0] = pieces[: rows // 2]
+                target[1] = pieces[rows // 2 :]
+
+    qkvs = line_start(wires, own_ref, qkv_all, core, me, targets)
+    half = one_piece.shape[-1]
+    chosen = pl.ds(pl.multiple_of(core * half, half), half)
+    for layer, piece in enumerate((one_piece, two_piece)):
+        smalls += [wires.copy(outs_ref.at[layer, place, :, chosen], piece.at[me], {"dp": spot}) for spot in targets]
+        piece[me] = outs_ref[layer, place, :, chosen]
     onward = line_forward(wires, qkv_all, core, qkvs, sources)
-    onward += line_forward(wires, out_all, core, outs, sources)
     for one in smalls + onward:
         one.wait_recv()
     wires.finish()
 
 
-def reduce_kernel(layers, *refs):
-    q_refs, o_refs = refs[:layers], refs[layers : 2 * layers]
-    refs = refs[2 * layers :]
-    q_outs, o_outs = refs[:layers], refs[layers : 2 * layers]
-    refs = refs[2 * layers :]
-    scratch = [refs[6 * layer : 6 * layer + 6] for layer in range(layers)]
-    send, recv = refs[6 * layers :]
-    place = plane_place()
-    me, core, near, far, cross = place
-    others = (cross, near, far)
-    line_me, targets, sources = dp_peers()
-    wires = Wires(send, recv)
-    partner = {"tensor": 1 - core}
-    greet({"seq": near}, {"seq": far}, {"seq": cross}, partner, *[{"dp": spot} for spot in targets])
-    n_dp = len(targets) + 1
-    first = []
-    for layer in range(layers):
-        q_in, q_sum, q_line, o_in, o_seq, o_line = scratch[layer]
-        first.append((wires.copy(q_refs[layer].at[1 - core], q_in, partner), wires.copy(o_refs[layer].at[1 - core], o_in, partner)))
-    q_copies, o_copies = [], []
-    for layer in range(layers):
-        q_in, q_sum, q_line, o_in, o_seq, o_line = scratch[layer]
-        q_ref, o_ref = q_refs[layer], o_refs[layer]
-        first[layer][0].wait_recv()
-        q_sum[...] = (wide(q_ref[core]) + wide(q_in[...])).astype(jnp.bfloat16)
-        q_copies.append([wires.copy(q_sum.at[spot], q_line.at[line_me], {"dp": spot}) for spot in targets])
-        q_line[line_me] = q_sum[line_me]
-        first[layer][1].wait_recv()
-        o_in[...] = (wide(o_ref[core]) + wide(o_in[...])).astype(jnp.bfloat16)
-        o_copies.append([wires.copy(o_in.at[spot], o_seq.at[me], {"seq": spot}) for spot in others])
-        o_seq[me] = o_in[me]
-    line_copies, last = [], []
-    for layer in range(layers):
-        q_in, q_sum, q_line, o_in, o_seq, o_line = scratch[layer]
-        for one in o_copies[layer]:
+def reduce_steps(wires, place, line, plane_first, q_ref, o_ref, o_out, scratch):
+    me, core, near, far, cross = place
+    line_me, targets, sources = line
+    q_in, q_sum, q_line, q_out, o_in, o_line, o_sum, o_seq = scratch
+    others, partner = (cross, near, far), {"tensor": 1 - core}
+    q_first = wires.copy(q_ref.at[1 - core], q_in, partner)
+    o_first = wires.copy(o_ref.at[1 - core], o_in, partner)
+    yield
+    q_first.wait_recv()
+    q_sum[...] = (wide(q_ref[core]) + wide(q_in[...])).astype(jnp.bfloat16)
+    q_copies = [wires.copy(q_sum.at[spot], q_line.at[line_me], {"dp": spot}) for spot in targets]
+    q_line[line_me] = q_sum[line_me]
+    o_first.wait_recv()
+    o_in[...] = (wide(o_ref[core]) + wide(o_in[...])).astype(jnp.bfloat16)
+    if plane_first:
+        o_copies = [wires.copy(o_in.at[:, spot], o_seq.at[me], {"seq": spot}) for spot in others]
+        o_seq[me] = o_in[:, me]
+    else:
+        o_copies = [wires.copy(o_in.at[spot], o_line.at[line_me], {"dp": spot}) for spot in targets]
+        o_line[line_me] = o_in[line_me]
+    yield
+
+    def line_total(ref, copies):
+        for one in copies:
             one.wait_recv()
-        o_seq[me] = (wide(o_seq[0]) + wide(o_seq[1]) + wide(o_seq[2]) + wide(o_seq[3])).astype(jnp.bfloat16)
-        line_copies.append([wires.copy(o_seq.at[me, spot], o_line.at[line_me], {"dp": spot}) for spot in targets])
-        o_line[line_me] = o_seq[me, line_me]
-    for layer in range(layers):
-        q_in, q_sum, q_line, o_in, o_seq, o_line = scratch[layer]
-        for refs_in, copies, out in ((q_line, q_copies[layer], q_outs[layer]), (o_line, line_copies[layer], o_outs[layer])):
-            for one in copies:
-                one.wait_recv()
-            total = wide(refs_in[0])
-            for spot in range(1, n_dp):
-                total = total + wide(refs_in[spot])
-            out[core, me] = total.astype(jnp.bfloat16)
-            mine = out.at[core, me]
-            last.append((out, [wires.copy(mine, mine, {"seq": spot}) for spot in others], [wires.copy(mine, mine, partner)]))
+        total = wide(ref[0])
+        for spot in range(1, len(targets) + 1):
+            total = total + wide(ref[spot])
+        return total.astype(jnp.bfloat16)
+
+    def spread(out):
+        mine = out.at[core, me]
+        return (out, [wires.copy(mine, mine, {"seq": spot}) for spot in others], [wires.copy(mine, mine, partner)])
+
+    def plane_total(copies):
+        for one in copies:
+            one.wait_recv()
+        return (wide(o_seq[0]) + wide(o_seq[1]) + wide(o_seq[2]) + wide(o_seq[3])).astype(jnp.bfloat16)
+
+    if plane_first:
+        o_sum[...] = plane_total(o_copies)
+        next_copies = [wires.copy(o_sum.at[spot], o_line.at[line_me], {"dp": spot}) for spot in targets]
+        o_line[line_me] = o_sum[line_me]
+        yield
+        q_out[core, me] = line_total(q_line, q_copies)
+        last = [spread(q_out)]
+        yield
+        o_out[core, me] = line_total(o_line, next_copies)
+    else:
+        q_out[core, me] = line_total(q_line, q_copies)
+        last = [spread(q_out)]
+        yield
+        o_sum[...] = line_total(o_line, o_copies)
+        next_copies = [wires.copy(o_sum.at[spot], o_seq.at[me], {"seq": spot}) for spot in others]
+        o_seq[me] = o_sum[me]
+        yield
+        o_out[core, me] = plane_total(next_copies)
+    last.append(spread(o_out))
+    yield
     for out, copies, onward in last:
         for one, spot in zip(copies, others):
             one.wait_recv()
             block = out.at[core, spot]
             onward.append(wires.copy(block, block, partner))
+    yield
     for out, copies, onward in last:
         for one in onward:
             one.wait_recv()
-    wires.finish()
-
-
-def share_kernel(count, *refs):
-    in_refs, out_refs, (send, recv) = refs[:count], refs[count : 2 * count], refs[2 * count :]
-    place = plane_place()
-    wires = Wires(send, recv)
-    greet({"seq": place[2]}, {"seq": place[3]})
-    first, second = [], []
-    for src, dst in zip(in_refs, out_refs):
-        dst[place[0]] = src[...]
-        first.append(seq_gather_start(wires, dst, place))
-    for dst, one in zip(out_refs, first):
-        second.extend(seq_gather_forward(wires, dst, place, one))
-    for one in second:
-        one.wait_recv()
+
+
+def finish_kernel(layers, count, *refs):
+    def take(number):
+        nonlocal refs
+        first, refs = refs[:number], refs[number:]
+        return first
+
+    q_refs, o_refs, shard_refs = take(layers), take(layers), take(count)
+    (total_ref,), o_outs, share_outs = take(1), take(layers), take(count)
+    scratch = [take(8) for _ in range(layers)]
+    place, line = plane_place(), dp_peers()
+    me, core, near, far, cross = place
+    wires = Wires(*refs)
+    greet({"seq": near}, {"seq": far}, {"seq": cross}, {"tensor": 1 - core}, *[{"dp": spot} for spot in line[1]])
+    tasks = [reduce_steps(wires, place, line, at > 0, *one) for at, one in enumerate(zip(q_refs, o_refs, o_outs, scratch))]
+    for _ in range(2):
+        for task in tasks:
+            next(task)
+    shares = []
+    for src, dst in zip(shard_refs, share_outs):
+        dst[me] = src[...]
+        shares.append(gather_steps(wires, dst, place, False))
+    run_all(*shares, *tasks)
+    rows = total_ref.shape[1] // 2
+    for layer in range(layers):
+        whole = scratch[layer][3]
+        size = whole.shape[-1] // 3
+        for half in range(2):
+            pieces = [whole[half, spot][:, kind * size : (kind + 1) * size] for kind in range(3) for spot in range(4)]
+            total_ref[layer, half * rows : (half + 1) * rows, :] = wide(jnp.concatenate(pieces, axis=1))
     wires.finish()
 def body(
     block_input,
@@ -837,10 +938,7 @@
     )
     small_rows = small.shape[0]
     small = jnp.pad(small, ((0, -small_rows % 16), (0, 0)))
-    own_qkv = lax.dynamic_index_in_dim(
-        query_key_value.reshape(LAYERS, shard, 3, n_seq, head_width), seq_index, 3, keepdims=False
-    ).reshape(LAYERS, n_tensor, half, 3 * head_width)
-    own_out = attention_out.reshape(LAYERS, n_tensor, half, width)
+    own_out = attention_out.reshape(LAYERS, n_seq, shard // n_seq, width)
     own_up = lax.dynamic_index_in_dim(expert_up, seq_index, 1, keepdims=False)
     own_down = lax.dynamic_index_in_dim(expert_down, seq_index, 1, keepdims=False).swapaxes(1, 2)
 
@@ -849,12 +947,15 @@
         down = lax.all_gather(own_down[layer], "dp", axis=0, tiled=True)
         return up, down
 
-    small_all, qkv_all, out_all = comm_call(
-        weights_kernel, "weights", 10, 25.0,
-        [low_array(n_dp, *small.shape), low_array(n_dp, *own_qkv.shape[1:]), low_array(n_dp, *own_out.shape[1:])], [], 5 * (n_dp - 1),
-        small, own_qkv[0], own_out[0]
+    own_shape = (n_tensor, half, 3 * head_width)
+    small_all, qkv_all, qkv_next, *out_pieces = comm_call(
+        weights_kernel, "weights", 10, 22.0,
+        [low_array(n_dp, *small.shape), low_array(n_dp, *own_shape), low_array(*own_shape)]
+        + [low_array(n_dp, shard // n_seq, width // n_tensor)] * LAYERS,
+        [pltpu.VMEM(own_shape, low)], 5 * (n_dp - 1), small, query_key_value, own_out
     )
-    qkv_weights, out_weights = [qkv_all], [out_all]
+    own_up, own_down, small_all = lax.optimization_barrier((own_up, own_down, small_all))
+    qkv_weights = [qkv_all]
     whole_rows = small_all.swapaxes(0, 1).reshape(-1, width)
     gains = whole_rows[: 2 * LAYERS].astype(jnp.float32).reshape(2, LAYERS, 1, width)
     routers = whole_rows[2 * LAYERS : 2 * LAYERS + LAYERS * experts].reshape(LAYERS, experts, width)
@@ -883,12 +984,11 @@
         up, down = expert_weights(layer)
         gain_one, gain_two = gains[0, layer], gains[1, layer]
         qkv_weight = qkv_weights[layer].reshape(width, 3 * head_width)
-        out_weight = out_weights[layer].reshape(n_seq, head_width, width)
         outs = [low_array(n_seq, piece, width), low_array(n_seq, piece, 3 * head_width)]
         if layer == 0:
             outs.append(jax.ShapeDtypeStruct((n_seq,) + routes_own.shape, jnp.int32))
             normed_all, qkv, routes_all = comm_call(
-                project_kernel, "project", 1, 16.0, outs, [], 7, current, gain_one, qkv_weight, routes_own
+                project_kernel, "project", 1, 16.0, outs, [], 9, current, gain_one, qkv_weight, routes_own
             )
             routes_all = jnp.moveaxis(routes_all.reshape((n_seq,) + routes.shape), 0, 1).reshape(LAYERS, n_seq, group_rows, -1)
             mine = jnp.any(routes_all == seq_index, axis=-1)
@@ -898,31 +998,31 @@
         else:
             current, normed_all, qkv = comm_call(
                 sum_project_kernel, "sum_project", 2, 32.0, [wide_array(piece, width)] + outs,
-                [pltpu.VMEM((n_seq, piece, width), low)] + sum_scratch(piece, width), 14, part, middle, gain_one, qkv_weight
+                [pltpu.VMEM((n_seq, piece, width), low)] + sum_scratch(piece, width), 16, part, middle, gain_one, qkv_weight
             )
         qkv = qkv.reshape(length, 3 * head_width)
         if layer == 0:
-            mixed, log_total, grad_rows, qkv_all, out_all = attend_gather(
-                qkv, seg_row, seg_col, lines[layer], grad, own_qkv[1], own_out[1], n_tensor, n_dp
-            )
-            qkv_weights.append(qkv_all)
-            out_weights.append(out_all)
+            outs = [low_array(n_dp, *own_out.shape[1:])] * LAYERS
+            mixed, log_total, *out_weights = attend(qkv, seg_row, seg_col, lines[layer], out_pieces, outs, "fetch", 6, 8)
         else:
-            mixed, log_total = attend(qkv, seg_row, seg_col, lines[layer])
-        merged, middle, tokens = comm_call(
-            merge_kernel, "merge", 3, 21.0,
-            [low_array(n_seq, piece, head_width), wide_array(piece, width), low_array(n_seq, n_tensor, piece, width)], [], 12,
-            mixed.reshape(n_seq, piece, head_width), current, out_weight, gain_two
+            outs = [low_array(n_seq, n_tensor, piece, width)]
+            mixed, log_total, grad_rows = attend(qkv, seg_row, seg_col, lines[layer], (grad,), outs, "gather", 14, 11)
+        out_weight = out_weights[layer].reshape(n_seq, head_width, width)
+        fetch = layer == 0
+        outs = [low_array(n_seq, piece, head_width), wide_array(piece, width), low_array(n_seq, n_tensor, piece, width)]
+        outs += [low_array(n_dp, *own_shape)] if fetch else []
+        operands = (mixed.reshape(n_seq, piece, head_width), current, out_weight, gain_two) + ((qkv_next,) if fetch else ())
+        merged, middle, tokens, *more = comm_call(
+            functools.partial(merge_kernel, fetch), "merge_fetch" if fetch else "merge", 15 if fetch else 3, 25.0, outs, [],
+            14 + (2 * (n_dp - 1) if fetch else 0), *operands
         )
+        qkv_weights += more
         tokens = tokens.reshape(n_seq, group_rows, width)
         part, slots, pre, shares = run_experts(tokens, slot[layer], chosen[layer], own_hot, routers[layer], up, down, capacity)
         part = part.reshape(n_seq, n_tensor, piece, width)
         saved.append((current, normed_all, qkv, log_total, merged, middle, tokens, shares, slots, pre, qkv_weight, out_weight, up, down))
 
-    (block_output,) = comm_call(
-        sum_kernel, "sum_last", 4, 16.0, [wide_array(piece, width)], [pltpu.VMEM((n_seq, piece, width), low)] + sum_scratch(piece, width),
-        10, part, middle
-    )
+    last_part, last_middle = part, middle
 
     def shard_sum(values):
         return lax.psum_scatter(values, "dp", scatter_dimension=0, tiled=True)
@@ -933,8 +1033,9 @@
     for layer in range(LAYERS - 1, -1, -1):
         (layer_in, normed_all, qkv, log_total, merged, middle, tokens, shares, slots, pre, qkv_weight, out_weight, up, down) = saved[layer]
         gain_one, gain_two = gains[0, layer], gains[1, layer]
-        part, up_grad, down_grad, router_grad = run_experts_back(
-            grad_rows.reshape(n_seq, group_rows, width), tokens, slot[layer], shares, own_hot, routers[layer], up, down, slots, pre
+        part, up_grad, down_grad, router_grad, *shared = run_experts_back(
+            grad_rows.reshape(n_seq, group_rows, width), tokens, slot[layer], shares, own_hot, routers[layer], up, down, slots, pre,
+            down_shards[1] if layer == 0 else None
         )
         down_shards[layer] = shard_sum(down_grad)
         up_shards[layer] = shard_sum(up_grad)
@@ -947,16 +1048,20 @@
         out_weight_grad = jnp.einsum("gtd,te->gde", merged, out_grad, preferred_element_type=jnp.float32)
         operands = (qkv, seg_row, seg_col, lines[layer], log_total, mixed_grad.reshape(length, head_width))
         if layer == 0:
-            qkv_grad, band, up_last = attend_back(*operands, up_shards[1])
+            (down_last,) = shared
+            outs = [low_array(n_seq, *up_shards[1].shape)]
+            qkv_grad, band, up_last = attend_back(*operands, (up_shards[1],), outs, [], "share", 9, 6)
         else:
-            qkv_grad, band = attend_back(*operands)
+            outs = [wide_array(piece, width)]
+            extra_scratch = [pltpu.VMEM((n_seq, piece, width), low)] + sum_scratch(piece, width)
+            qkv_grad, band, block_output = attend_back(*operands, (last_part, last_middle), outs, extra_scratch, "sum", 4, 10)
         qkv_weight_grad = dot_tn(normed_all.reshape(length, width), qkv_grad)
         spread = layer > 0
         outs = [wide_array(piece, width), wide_array(1, width)]
         outs += [low_array(n_seq, n_tensor, piece, width)] if spread else []
         outs = comm_call(
             functools.partial(input_grad_kernel, spread), "input_grad_spread" if spread else "input_grad", 7 + spread, 32.0 if spread else 16.0,
-            outs, sum_scratch(piece, width), 15, qkv_grad.reshape(n_seq, piece, -1), qkv_weight, layer_in, gain_one, middle_grad
+            outs, sum_scratch(piece, width), 17, qkv_grad.reshape(n_seq, piece, -1), qkv_weight, layer_in, gain_one, middle_grad
         )
         grad, gain_one_grad = outs[:2]
         grad_rows = outs[2] if spread else None
@@ -969,27 +1074,26 @@
         packed = packed.reshape(n_plane, n_dp, shard).swapaxes(0, 1)[:, :, None]
         packed = jnp.pad(packed, ((0, 0), (0, 0), (0, packed_rows - out_rows - 1), (0, width - shard)))
         both = jnp.concatenate([out_weight_grad.reshape(n_dp, n_plane, out_rows, width), packed], axis=2).astype(low)
-        out_grads[layer] = both.reshape(n_dp, n_tensor, n_seq, packed_rows, width).transpose(1, 2, 0, 3, 4)
+        out_grads[layer] = both.reshape(n_dp, n_tensor, n_seq, packed_rows, width).swapaxes(0, 1)
         qkv_grads[layer] = qkv_weight_grad.astype(low).reshape(n_dp, n_tensor, half, 3 * head_width).swapaxes(0, 1)
 
-    down_last = lax.all_gather(down_shards[1], "seq", axis=0)
-    q_lines = [pltpu.VMEM((n_dp, half, 3 * head_width), low)] * 3
-    o_blocks = [
-        pltpu.VMEM((n_seq, n_dp, packed_rows, width), low),
-        pltpu.VMEM((n_seq, n_dp, packed_rows, width), low),
-        pltpu.VMEM((n_dp, packed_rows, width), low),
-    ]
-    totals = comm_call(
-        functools.partial(reduce_kernel, LAYERS), "reduce_grads", 11, 40.0,
-        [low_array(n_tensor, n_seq, half, 3 * head_width)] * LAYERS + [low_array(n_tensor, n_seq, packed_rows, width)] * LAYERS,
-        (q_lines + o_blocks) * LAYERS, LAYERS * (2 * (n_dp - 1) + 19), *qkv_grads, *out_grads
+    def reduce_scratch(plane_first):
+        line = pltpu.VMEM((n_dp, half, 3 * head_width), low)
+        blocks = pltpu.VMEM((n_dp, n_seq, packed_rows, width), low)
+        over_dp, over_seq = (pltpu.VMEM((count, packed_rows, width), low) for count in (n_dp, n_seq))
+        found = [line] * 3 + [pltpu.VMEM((n_tensor, n_seq, half, 3 * head_width), low), blocks]
+        if plane_first:
+            return found + [over_dp, over_dp, pltpu.VMEM((n_seq, n_dp, packed_rows, width), low)]
+        return found + [blocks, over_seq, over_seq]
+
+    qkv_total, *totals = comm_call(
+        functools.partial(finish_kernel, LAYERS, 2), "finish", 11, 70.0,
+        [wide_array(LAYERS, shard, 3 * width)] + [low_array(n_tensor, n_seq, packed_rows, width)] * LAYERS
+        + [low_array(n_seq, shard, up.shape[1])] * 2,
+        reduce_scratch(False) + reduce_scratch(True), LAYERS * (2 * (n_dp - 1) + 19) + 12, *qkv_grads, *out_grads, up_shards[0], down_shards[0]
     )
-    up_first, down_first = comm_call(
-        functools.partial(share_kernel, 2), "share", 12, 38.0, [low_array(n_seq, shard, up.shape[1])] * 2, [], 8, up_shards[0], down_shards[0]
-    )
-    qkv_total = jnp.stack(totals[:LAYERS]).astype(jnp.float32).reshape(LAYERS, n_tensor, n_seq, half, 3, head_width)
-    qkv_total = qkv_total.transpose(0, 1, 3, 4, 2, 5).reshape(LAYERS, shard, 3 * width)
-    both = jnp.stack(totals[LAYERS:]).astype(jnp.float32).reshape(LAYERS, n_plane, packed_rows, width)
+    up_first, down_first = totals[LAYERS:]
+    both = jnp.stack(totals[:LAYERS]).astype(jnp.float32).reshape(LAYERS, n_plane, packed_rows, width)
     out_total = both[:, :, :out_rows].reshape(LAYERS, shard, width)
     small = both[:, :, out_rows, :shard]
     router_total = small[:, 2 : 2 + experts].swapaxes(1, 2)

time: 717 us -> 623 us (0.87)
  Pallas kernels: 598 us -> 518 us
  local copies, waits for them, and re-layouts: 57.5 us -> 32.2 us
  waiting for transfers between devices: 2.58 us -> 22.8 us
    pallas_call x14, Pallas kernels: 487 us -> 438 us  [comm_call(): pl.pallas_call(kernel, out_shape=tuple(outs), in_specs=vmem(len(operands)...]
    pallas_call x4 -> x2, Pallas kernels: 85.5 us -> 53.8 us  [run_experts_back(): pl.pallas_call(experts_back_kernel, grid=(groups,), out_shape=tuple(outs)...]
    all_gather x2, waiting for transfers between devices: 0.02 us -> 20.2 us  [expert_weights(): down = lax.all_gather(own_down[layer], 'dp', axis=0, tiled=True)]
    reshape x3 -> x0, local copies, waits for them, and re-layouts: 17.6 us -> none  [the longest x2 12.8 us: body(): qkv_total.transpose(0, 1, 3, 4, 2, 5).reshape(LAYERS, shard, 3 * width)]
  transfers between devices with their start and end apart: 9 -> 8, of which waited for: 0 -> 1; matrix products, arithmetic and copies ran while one was open for 11% -> 6% of each run, Pallas kernels for 79% -> 61%
where the time goes in v4:
time: 623 us; the launch traced here: 618 us
  Pallas kernels  518 us (83%)
  local copies, waits for them, and re-layouts  32.2 us (5%)
  waiting for transfers between devices  22.8 us (4%)
  other arithmetic  19.3 us (3%)
  between operations  15.3 us (2%)
  matrix products  10.1 us (2%)
    pallas_call x14, Pallas kernels, comm_call(): pl.pallas_call(kernel, out_shape=tuple(outs), in_specs=vmem(len(operands)...  438 us
    pallas_call x2, Pallas kernels, run_experts_back(): pl.pallas_call(experts_back_kernel, grid=(groups,), out_shape=tuple(outs)...  53.8 us
    pallas_call x2, Pallas kernels, run_experts(): pl.pallas_call(experts_kernel, grid=(groups,), out_shape=(low_array(group...  25.6 us
    all_gather x2, waiting for transfers between devices, expert_weights(): down = lax.all_gather(own_down[layer], 'dp', axis=0, tiled=True)  20.2 us
  transfers between devices with their start and end apart: 8, of which 1 were waited for; matrix products, arithmetic and copies ran while one was open for 6% of the time, Pallas kernels for 61%

profile of v4, /device:TPU:0, one launch (start us, length us, event | category | flops | bytes accessed | tf_op | source)
XLA Modules:
  0.0 617.7 jit_solution(6588898897725412983)
XLA Ops:
  8.6 1.4 dynamic-slice_bitcast_fusion
  10.8 26.3 %weights.1 = (bf16[4,16,192]{2,1,0:T(8,128)(2,1)}, bf16[4,2,96,576]{3,2,1,0:T(8,128)(2,1)}, bf16[2,96,576]{2,1,0:T(8,128)(2,1)}, bf16[4,48,384]{2,1,0:T(8,128)(2,1)}, bf16[4,48,384]{2,1,0:T(8,128)(2,1)}) custom-call(bf16[16,192]{1,0:T(8,128)(2,1)} %pad.27.small_ref, bf16[2,192,2304]{2,1,0:T(8,128)(2,1)} %whole_ref.1, bf16[2,4,48,768]{3,2,1,0:T(8,128)(2,1)} %bitcast.190), custom_call_target="tpu_custom_call" | custom-call | bytes 66000000 | tf_op jit(solution)/shard_map/weights/pallas_call | solution.py:535
  43.8 19.2 %project.1 = (bf16[4,256,768]{2,1,0:T(8,128)(2,1)}, bf16[4,256,576]{2,1,0:T(8,128)(2,1)}, s32[4,16,128]{2,1,0:T(8,128)}) custom-call(f32[256,768]{1,0:T(8,128)} %bitcast.147, f32[1,768]{1,0:T(1,128)} %get-tuple-element.166.gain_ref, bf16[768,576]{1,0:T(8,128)(2,1)} %bitcast.164, s32[16,128]{1,0:T(8,128)} %reshape.221.routes_ref), custom_call_target="tpu_custom_call" | custom-call | bytes 48000000 | tf_op jit(solution)/shard_map/project/pallas_call | solution.py:535
  64.2 1.7 compare_reduce_fusion
  70.9 22.6 %attend_fetch.1 = (bf16[1024,192]{1,0:T(8,128)(2,1)}, f32[3,1024,1]{2,1,0:T(8,128)}, bf16[4,4,48,768]{3,2,1,0:T(8,128)(2,1)}, bf16[4,4,48,768]{3,2,1,0:T(8,128)(2,1)}) custom-call(bf16[1024,576]{1,0:T(8,128)(2,1)} %bitcast.150, s32[1,1024]{1,0:T(1,128)} %refs_1_.7, s32[1024,1]{1,0:T(8,128)} %copy.148.refs_2_, f32[3,640]{1,0:T(4,128)} %get-tuple-element.158.refs_3_, ...), custom_call_target="tpu_custom_call" | custom-call | bytes 54000000 | tf_op jit(solution)/shard_map/attend_fetch/pallas_call | solution.py:535
  93.5 32.2 %merge_fetch.1 = (bf16[4,256,192]{2,1,0:T(8,128)(2,1)}, f32[256,768]{1,0:T(8,128)}, bf16[4,2,256,768]{3,2,1,0:T(8,128)(2,1)}, bf16[4,2,96,576]{3,2,1,0:T(8,128)(2,1)}) custom-call(bf16[4,256,192]{2,1,0:T(8,128)(2,1)} %bitcast.193, f32[256,768]{1,0:T(8,128)} %bitcast.148, bf16[4,192,768]{2,1,0:T(8,128)(2,1)} %bitcast.154, ...), custom_call_target="tpu_custom_call" | custom-call | bytes 75000000 | tf_op jit(solution)/shard_map/merge_fetch/pallas_call | solution.py:535
  126.9 1.5 slice_bitcast_fusion
  128.4 20.2 %all-gather.11.cloned.1.call-done = bf16[1,768,1536]{2,1,0:T(8,128)(2,1)} async-done(((bf16[1,192,1536]{2,1,0:T(8,128)(2,1)}), bf16[1,768,1536]{2,1,0:T(8,128)(2,1)}) %all-gather.11.cloned.1.call-update) | async-done | bytes 2359312 | tf_op jit(solution)/shard_map/all_gather | solution.py:947
  148.6 12.8 %experts.2 = (bf16[4,512,768]{2,1,0:T(8,128)(2,1)}, bf16[4,256,768]{2,1,0:T(8,128)(2,1)}, bf16[4,256,1536]{2,1,0:T(8,128)(2,1)}, f32[4,512,4]{2,1,0:T(8,128)}) custom-call(bf16[4,512,768]{2,1,0:T(8,128)(2,1)} %bitcast.133, s32[4,1,512]{2,1,0:T(1,128)} %get-tuple-element.162.slot_ref, f32[4,512,4]{2,1,0:T(8,128)} %get-tuple-element.149.chosen_ref, ...), custom_call_target="tpu_custom_call" | custom-call | bytes 42000000 | tf_op jit(solution)/shard_map/experts/pallas_call | solution.py:694
  161.4 35.7 %sum_project.1 = (f32[256,768]{1,0:T(8,128)}, bf16[4,256,768]{2,1,0:T(8,128)(2,1)}, bf16[4,256,576]{2,1,0:T(8,128)(2,1)}) custom-call(bf16[4,2,256,768]{3,2,1,0:T(8,128)(2,1)} %bitcast.169, f32[256,768]{1,0:T(8,128)} %get-tuple-element.93.base_ref.middle_ref, f32[1,768]{1,0:T(1,128)} %get-tuple-element.164.gain_ref, bf16[768,576]{1,0:T(8,128)(2,1)} %bitcast.160), custom_call_target="tpu_custom_call" | custom-call | bytes 96000000 | tf_op jit(solution)/shard_map/sum_project/pallas_call | solution.py:535
  197.1 24.5 %attend_gather.1 = (bf16[1024,192]{1,0:T(8,128)(2,1)}, f32[3,1024,1]{2,1,0:T(8,128)}, bf16[4,2,256,768]{3,2,1,0:T(8,128)(2,1)}) custom-call(bf16[1024,576]{1,0:T(8,128)(2,1)} %bitcast.152, s32[1,1024]{1,0:T(1,128)} %refs_1_.7, s32[1024,1]{1,0:T(8,128)} %copy.148.refs_2_, f32[3,640]{1,0:T(4,128)} %get-tuple-element.157.refs_3_, f32[256,768]{1,0:T(8,128)} %bitcast.170), custom_call_target="tpu_custom_call" | custom-call | bytes 54000000 | tf_op jit(solution)/shard_map/attend_gather/pallas_call | solution.py:535
  221.7 29.3 %merge.1 = (bf16[4,256,192]{2,1,0:T(8,128)(2,1)}, f32[256,768]{1,0:T(8,128)}, bf16[4,2,256,768]{3,2,1,0:T(8,128)(2,1)}) custom-call(bf16[4,256,192]{2,1,0:T(8,128)(2,1)} %bitcast.194, f32[256,768]{1,0:T(8,128)} %get-tuple-element.99.base_ref.x_ref, bf16[4,192,768]{2,1,0:T(8,128)(2,1)} %bitcast.156, f32[1,768]{1,0:T(1,128)} %get-tuple-element.163.gain_ref), custom_call_target="tpu_custom_call" | custom-call | bytes 75000000 | tf_op jit(solution)/shard_map/merge/pallas_call | solution.py:535
  251.0 12.8 %experts.3 = (bf16[4,512,768]{2,1,0:T(8,128)(2,1)}, bf16[4,256,768]{2,1,0:T(8,128)(2,1)}, bf16[4,256,1536]{2,1,0:T(8,128)(2,1)}, f32[4,512,4]{2,1,0:T(8,128)}) custom-call(bf16[4,512,768]{2,1,0:T(8,128)(2,1)} %bitcast.135, s32[4,1,512]{2,1,0:T(1,128)} %get-tuple-element.161.slot_ref, f32[4,512,4]{2,1,0:T(8,128)} %get-tuple-element.148.chosen_ref, ...), custom_call_target="tpu_custom_call" | custom-call | bytes 42000000 | tf_op jit(solution)/shard_map/experts/pallas_call | solution.py:694
  263.8 24.4 %experts_back.1 = (bf16[4,512,768]{2,1,0:T(8,128)(2,1)}, bf16[768,1536]{1,0:T(8,128)(2,1)}, bf16[768,1536]{1,0:T(8,128)(2,1)}, f32[4,768]{1,0:T(4,128)}) custom-call(bf16[4,512,768]{2,1,0:T(8,128)(2,1)} %bitcast.172, bf16[4,512,768]{2,1,0:T(8,128)(2,1)} %bitcast.136, s32[4,1,512]{2,1,0:T(1,128)} %get-tuple-element.161.slot_ref, ...), custom_call_target="tpu_custom_call" | custom-call | bytes 75000000 | tf_op jit(solution)/shard_map/experts_back/pallas_call | solution.py:726
  288.9 30.1 %split.2 = (f32[256,768]{1,0:T(8,128)}, bf16[256,768]{1,0:T(8,128)(2,1)}, f32[1,768]{1,0:T(1,128)}, bf16[4,256,192]{2,1,0:T(8,128)(2,1)}) custom-call(bf16[4,2,256,768]{3,2,1,0:T(8,128)(2,1)} %bitcast.168, f32[256,768]{1,0:T(8,128)} %get-tuple-element.106.middle_ref.refs_7_, f32[1,768]{1,0:T(1,128)} %get-tuple-element.163.gain_ref, f32[256,768]{1,0:T(8,128)} %bitcast.171, ...), custom_call_target="tpu_custom_call" | custom-call | bytes 66000000 | tf_op jit(solution)/shard_map/split/pallas_call | solution.py:535
  319.0 26.6 %attend_back_sum.1 = (bf16[1024,576]{1,0:T(8,128)(2,1)}, f32[3,640]{1,0:T(4,128)}, f32[256,768]{1,0:T(8,128)}) custom-call(bf16[1024,576]{1,0:T(8,128)(2,1)} %bitcast.153, s32[1,1024]{1,0:T(1,128)} %refs_1_.7, s32[1024,1]{1,0:T(8,128)} %copy.148.refs_2_, f32[3,640]{1,0:T(4,128)} %get-tuple-element.157.refs_3_, f32[3,1024,1]{2,1,0:T(8,128)} %get-tuple-element.96.refs_4_, ...), custom_call_target="tpu_custom_call" | custom-call | bytes 69000000 | tf_op jit(solution)/shard_map/attend_back_sum/pallas_call | solution.py:535
  345.6 35.6 %input_grad_spread.1 = (f32[256,768]{1,0:T(8,128)}, f32[1,768]{1,0:T(1,128)}, bf16[4,2,256,768]{3,2,1,0:T(8,128)(2,1)}) custom-call(bf16[4,256,576]{2,1,0:T(8,128)(2,1)} %bitcast.184, bf16[768,576]{1,0:T(8,128)(2,1)} %bitcast.161, f32[256,768]{1,0:T(8,128)} %get-tuple-element.99.base_ref.x_ref, f32[1,768]{1,0:T(1,128)} %get-tuple-element.164.gain_ref, ...), custom_call_target="tpu_custom_call" | custom-call | bytes 96000000 | tf_op jit(solution)/shard_map/input_grad_spread/pallas_call | solution.py:535
  381.3 29.4 %experts_back_share.1 = (bf16[4,512,768]{2,1,0:T(8,128)(2,1)}, bf16[768,1536]{1,0:T(8,128)(2,1)}, bf16[768,1536]{1,0:T(8,128)(2,1)}, f32[4,768]{1,0:T(4,128)}, bf16[4,192,1536]{2,1,0:T(8,128)(2,1)}) custom-call(bf16[4,512,768]{2,1,0:T(8,128)(2,1)} %bitcast.173, bf16[4,512,768]{2,1,0:T(8,128)(2,1)} %bitcast.134, s32[4,1,512]{2,1,0:T(1,128)} %get-tuple-element.162.slot_ref, ...), custom_call_target="tpu_custom_call" | custom-call | bytes 75000000 | tf_op jit(solution)/shard_map/experts_back_share/pallas_call | solution.py:726
  412.0 2.5 convolution_convert_fusion.2
  417.6 30.6 %split.3 = (f32[256,768]{1,0:T(8,128)}, bf16[256,768]{1,0:T(8,128)(2,1)}, f32[1,768]{1,0:T(1,128)}, bf16[4,256,192]{2,1,0:T(8,128)(2,1)}) custom-call(bf16[4,2,256,768]{3,2,1,0:T(8,128)(2,1)} %bitcast.166, f32[256,768]{1,0:T(8,128)} %get-tuple-element.93.base_ref.middle_ref, f32[1,768]{1,0:T(1,128)} %get-tuple-element.165.gain_ref, ...), custom_call_target="tpu_custom_call" | custom-call | bytes 66000000 | tf_op jit(solution)/shard_map/split/pallas_call | solution.py:535
  448.2 26.2 %attend_back_share.1 = (bf16[1024,576]{1,0:T(8,128)(2,1)}, f32[3,640]{1,0:T(4,128)}, bf16[4,192,1536]{2,1,0:T(8,128)(2,1)}) custom-call(bf16[1024,576]{1,0:T(8,128)(2,1)} %bitcast.151, s32[1,1024]{1,0:T(1,128)} %refs_1_.7, s32[1024,1]{1,0:T(8,128)} %copy.148.refs_2_, f32[3,640]{1,0:T(4,128)} %get-tuple-element.158.refs_3_, ...), custom_call_target="tpu_custom_call" | custom-call | bytes 69000000 | tf_op jit(solution)/shard_map/attend_back_share/pallas_call | solution.py:535
  474.4 19.4 %input_grad.1 = (f32[256,768]{1,0:T(8,128)}, f32[1,768]{1,0:T(1,128)}) custom-call(bf16[4,256,576]{2,1,0:T(8,128)(2,1)} %bitcast.185, bf16[768,576]{1,0:T(8,128)(2,1)} %bitcast.165, f32[256,768]{1,0:T(8,128)} %bitcast.149, f32[1,768]{1,0:T(1,128)} %get-tuple-element.166.gain_ref, f32[256,768]{1,0:T(8,128)} %get-tuple-element.123.middle_grad_ref), custom_call_target="tpu_custom_call" | custom-call | bytes 48000000 | tf_op jit(solution)/shard_map/input_grad/pallas_call | solution.py:535
  493.8 3.8 convolution_convert_fusion.3
  497.7 1.5 copy.162
  504.7 1.7 convolution_convert_fusion.1
  506.4 2.1 copy_bitcast_fusion
  508.5 1.5 copy_bitcast_fusion.2
  510.0 80.0 %finish.1 = (f32[2,192,2304]{2,1,0:T(8,128)}, bf16[2,4,32,768]{3,2,1,0:T(8,128)(2,1)}, bf16[2,4,32,768]{3,2,1,0:T(8,128)(2,1)}, bf16[4,192,1536]{2,1,0:T(8,128)(2,1)}, bf16[4,192,1536]{2,1,0:T(8,128)(2,1)}) custom-call(bf16[2,4,96,576]{3,2,1,0:T(8,128)(2,1)} %get-tuple-element.170.refs_0_, bf16[2,4,96,576]{3,2,1,0:T(8,128)(2,1)} %get-tuple-element.169.refs_1_, ...), custom_call_target="tpu_custom_call" | custom-call | bytes 210000000 | tf_op jit(solution)/shard_map/finish/pallas_call | solution.py:535
  590.9 2.2 fusion
  595.6 6.2 maximum_convert_fusion
  601.8 4.5 convert_bitcast_fusion
  608.6 1.8 copy.220
  (157 shorter events, 32.0 us)
Async XLA Ops:
  7.2 121.2 %all-gather.9.cloned.1.call-start = ((), (), s32[]{:S(2)}) async-start(), calls=%async_computation.8 | async-start | bytes 2949120 | tf_op jit(solution)/shard_map/all_gather | solution.py:946
  8.6 1.4 copy-start.15
  8.6 1.5 copy-start.16
  8.6 1.5 copy-start.21
  8.6 1.5 copy-start.22
  38.2 2.5 copy-start.11
  38.2 2.7 copy-start.14
  38.2 110.4 %all-gather.11.cloned.1.call-start = ((), (), s32[]{:S(2)}) async-start(), calls=%async_computation.9 | async-start | bytes 2949120 | tf_op jit(solution)/shard_map/all_gather | solution.py:947
  39.3 2.6 copy-start.9
  39.3 3.7 slice-start
  39.4 211.6 %all-gather.13.cloned.1.call-start = ((), (), s32[]{:S(2)}) async-start(), calls=%async_computation.10 | async-start | bytes 2949120 | tf_op jit(solution)/shard_map/all_gather | solution.py:946
  40.1 210.9 %all-gather.15.cloned.1.call-start = ((), (), s32[]{:S(2)}) async-start(), calls=%async_computation.11 | async-start | bytes 2949120 | tf_op jit(solution)/shard_map/all_gather | solution.py:947
  40.7 340.6 %reduce-scatter.5.cloned.1.call-start = ((), (), s32[]{:S(2)}) async-start(), calls=%async_computation.4 | async-start | bytes 2949120 | tf_op jit(solution)/shard_map/reduce_scatter | solution.py:1028
  70.1 345.8 %copy-start.12 = (s32[640]{0:T(1024)}, s32[640]{0:T(1024)S(1)}, u32[]{:S(2)}) copy-start(s32[640]{0:T(1024)S(1)} %pad_add_fusion) | copy-start | bytes 7684
  288.3 159.9 %reduce-scatter.7.cloned.1.call-start = ((), (), s32[]{:S(2)}) async-start(), calls=%async_computation.5 | async-start | bytes 2949120 | tf_op jit(solution)/shard_map/reduce_scatter | solution.py:1028
  288.9 221.1 %reduce-scatter.9.cloned.1.call-start = ((), (), s32[]{:S(2)}) async-start(), calls=%async_computation.6 | async-start | bytes 2949120 | tf_op jit(solution)/shard_map/reduce_scatter | solution.py:1028
  410.7 1.3 copy-start.4
  410.7 99.3 %reduce-scatter.11.cloned.1.call-start = ((), (), s32[]{:S(2)}) async-start(), calls=%async_computation.7 | async-start | bytes 2949120 | tf_op jit(solution)/shard_map/reduce_scatter | solution.py:1028
  414.5 1.0 copy-start.18
  414.6 1.1 copy-start.17
  414.6 1.2 copy-start.13
  414.6 1.3 copy-start.23
  414.6 2.4 copy-start.7
  414.6 2.4 copy-start.8
  497.7 1.6 copy-start.20
  497.7 2.3 copy-start.19
  590.0 5.6 copy-start.2
  595.6 6.2 copy-start.1
  595.6 6.2 copy-start.3
  601.8 4.6 copy-start.5
  601.8 6.9 %copy-start = (f32[2,192,2304]{2,1,0:T(8,128)S(1)}, f32[2,192,2304]{2,1,0:T(8,128)}, u32[]{:S(2)}) copy-start(f32[2,192,2304]{2,1,0:T(8,128)} %get-tuple-element.184) | copy-start | bytes 10616836
  606.3 1.4 copy-start.6
  (1 other events, 0.6 us)
Sparse Core Ops, SparseCore 0:
  38.3 50.3 all-gather.8
  90.8 57.7 all-gather.10
  150.7 49.0 all-gather.12
  201.2 49.1 all-gather.14
  288.4 46.7 reduce-scatter.4
  337.3 47.0 reduce-scatter.6
  410.8 46.7 reduce-scatter.8
  459.9 47.5 reduce-scatter.10

commit v5 on v4

--- a/solution.py
+++ b/solution.py
@@ -127,7 +127,7 @@
             lse_ref[h, pl.ds(start, ROWS), :] = top + jnp.log(total)
             return carry
 
-        lax.fori_loop(0, heads, one_head, 0)
+        lax.fori_loop(0, heads, one_head, 0, unroll=True)
 
     visit_blocks(length, span, one_block, hook, hooks_at)
     out_ref[...] = jnp.concatenate([mixed_ref[h] for h in range(heads)], axis=1)
@@ -136,21 +136,21 @@
 
 
 def attn_bwd_kernel(heads, span, mode, *refs):
-    qkv_ref, segr_ref, segc_ref, line_ref, lse_ref, grad_ref = refs[:6]
+    qkv_ref, segr_ref, segc_ref, line_ref, lse_ref, grad_ref, normed_ref = refs[:7]
     place = plane_place()
     me, core, near, far, cross = place
     wires = Wires(*refs[-2:])
     if mode == "share":
-        shard_ref, out_ref, band_ref, shared_ref = refs[6:10]
+        shard_ref, out_ref, band_ref, weight_ref, shared_ref = refs[7:12]
         greet({"seq": near}, {"seq": far})
-        shared_ref[me] = shard_ref[...]
+        shared_ref[me] = shard_ref[0]
         tasks = [gather_steps(wires, shared_ref, place, False)]
-        refs = refs[10:18]
+        refs = refs[12:20]
     else:
-        part_ref, base_ref, out_ref, band_ref, total_ref = refs[6:11]
+        part_ref, base_ref, out_ref, band_ref, weight_ref, total_ref = refs[7:13]
         greet(*plane_peers(place))
-        tasks = [plane_sum_steps(wires, place, part_ref, refs[19], refs[20:26], add_to(total_ref, base_ref))]
-        refs = refs[11:19]
+        tasks = [plane_sum_steps(wires, place, part_ref, refs[21], refs[22:28], add_to(total_ref, base_ref))]
+        refs = refs[13:21]
     hook, finish = background(tasks)
     hook()
     parts_ref, gparts_ref, qgrad_ref, kgrad_ref, vgrad_ref, slab_ref, mask_ref, band_acc = refs
@@ -187,13 +187,19 @@
             vgrad_ref[h, window, :] += lax.dot_general(p.astype(jnp.bfloat16), grad, TN, preferred_element_type=jnp.float32)
             return carry
 
-        lax.fori_loop(0, heads, one_head, 0)
+        lax.fori_loop(0, heads, one_head, 0, unroll=True)
 
     visit_blocks(length, span, one_block, hook, (5, 7) if mode == "share" else (3, 6))
     parts = [qgrad_ref[h] for h in range(heads)]
     parts += [kgrad_ref[h].astype(jnp.bfloat16) for h in range(heads)]
     parts += [vgrad_ref[h].astype(jnp.bfloat16) for h in range(heads)]
     out_ref[...] = jnp.concatenate(parts, axis=1)
+    weight_grad = dot_tn(normed_ref[...], out_ref[...])
+    rows = weight_ref.shape[2]
+    for at in range(weight_ref.shape[1]):
+        for core_at in range(weight_ref.shape[0]):
+            first = (at * weight_ref.shape[0] + core_at) * rows
+            weight_ref[core_at, at] = weight_grad[first : first + rows].astype(jnp.bfloat16)
     row = lax.broadcasted_iota(jnp.int32, (ROWS, span), 0)
     for h in range(heads):
         acc = band_acc[h]
@@ -227,10 +233,10 @@
                      attend_scratch(heads, length, span), wire_count, qkv, seg_row, seg_col, line, *extra)
 
 
-def attend_back(qkv, seg_row, seg_col, line, lse, grad, extra, extra_outs, extra_scratch, mode, number, wire_count):
+def attend_back(qkv, seg_row, seg_col, line, lse, grad, normed, weight_shape, extra, extra_outs, extra_scratch, mode, number, wire_count):
     length, width = qkv.shape
     heads, span = line.shape
-    outs = [low_array(length, width), wide_array(heads, span)] + extra_outs
+    outs = [low_array(length, width), wide_array(heads, span), low_array(*weight_shape)] + extra_outs
     scratch = [
         pltpu.VMEM((3 * heads, length, HD), jnp.bfloat16),
         pltpu.VMEM((heads, length, HD), jnp.bfloat16),
@@ -242,7 +248,7 @@
         pltpu.VMEM((heads, ROWS, span), jnp.float32),
     ]
     return comm_call(functools.partial(attn_bwd_kernel, heads, span, mode), "attend_back_" + mode, number, 23.0, outs,
-                     scratch + extra_scratch, wire_count, qkv, seg_row, seg_col, line, lse, grad, *extra)
+                     scratch + extra_scratch, wire_count, qkv, seg_row, seg_col, line, lse, grad, normed, *extra)
 
 
 MESH_ID = pl.DeviceIdType.MESH
@@ -488,8 +494,8 @@
     wires.finish()
 
 
-def split_kernel(part_ref, middle_ref, gain_ref, grad_ref, w_ref, middle_grad_ref, out_grad_ref, gain_grad_ref, mixed_grad_ref,
-                 outgoing, partner_in, *rest):
+def split_kernel(part_ref, middle_ref, gain_ref, grad_ref, w_ref, merged_ref, middle_grad_ref, gain_grad_ref, mixed_grad_ref,
+                 weight_ref, out_grad_ref, outgoing, partner_in, *rest):
     out_refs, (send, recv) = rest[:6], rest[6:]
     place = plane_place()
     me, core, near, far, cross = place
@@ -505,6 +511,14 @@
         outgoing[spot] = dot_nt(out_grad_ref[...], w_ref[spot]).astype(jnp.bfloat16)
         copies.append(wires.copy(outgoing.at[spot], mixed_grad_ref.at[me], {"seq": spot}))
     mixed_grad_ref[me] = dot_nt(out_grad_ref[...], w_ref[me]).astype(jnp.bfloat16)
+    cores, count, parts, rows = weight_ref.shape[:4]
+    block = merged_ref.shape[2]
+    for at in range(merged_ref.shape[0]):
+        weight_grad = dot_tn(merged_ref[at], out_grad_ref[...])
+        for inner in range(block // rows):
+            index = (at * block + inner * rows) // rows
+            dp_at, core_at, part_at = index // (cores * parts), index // parts % cores, index % parts
+            weight_ref[core_at, dp_at, part_at] = weight_grad[inner * rows : (inner + 1) * rows].astype(jnp.bfloat16)
     for one in copies:
         one.wait_recv()
     wires.finish()
@@ -569,7 +583,12 @@
     return (rows == slot_row).astype(jnp.bfloat16)
 
 
-def experts_kernel(tokens_ref, slot_ref, chosen_ref, own_ref, router_ref, up_ref, down_ref, part_ref, slots_ref, pre_ref, shares_ref):
+def one_of(pair_ref, index):
+    values = pair_ref[:, index]
+    return values.reshape(values.shape[0] * values.shape[1], values.shape[2])
+
+
+def experts_kernel(tokens_ref, slot_ref, chosen_ref, own_ref, router_ref, pair_ref, part_ref, slots_ref, pre_ref, shares_ref):
     capacity = slots_ref.shape[0]
     tokens = tokens_ref[...]
     logits = jnp.where(chosen_ref[...] > 0, dot_nt(tokens, router_ref[...]), negative)
@@ -580,10 +599,10 @@
     hot = slot_hot(slot_ref[...], capacity)
     slots = dot(hot, tokens).astype(jnp.bfloat16)
     slots_ref[...] = slots
-    pre = dot(slots, up_ref[...])
+    pre = dot(slots, one_of(pair_ref, 0))
     pre_ref[...] = pre.astype(jnp.bfloat16)
     hidden = gelu_parts(pre)[0].astype(jnp.bfloat16)
-    result = dot_nt(hidden, down_ref[...]).astype(jnp.bfloat16)
+    result = dot_nt(hidden, one_of(pair_ref, 1)).astype(jnp.bfloat16)
     part_ref[...] = (own_share * dot_tn(hot, result)).astype(jnp.bfloat16)
 
 
@@ -618,17 +637,17 @@
             self.one.wait_recv()
 
 
-def experts_back_kernel(rows_ref, tokens_ref, slot_ref, shares_ref, own_ref, router_ref, up_ref, down_ref, slots_ref, pre_ref,
+def experts_back_kernel(rows_ref, tokens_ref, slot_ref, shares_ref, own_ref, router_ref, pair_ref, slots_ref, pre_ref,
                         *refs):
     group, last = pl.program_id(0), pl.num_programs(0) - 1
     if len(refs) > 6:
-        shard_ref, part_ref, up_grad_ref, down_grad_ref, router_grad_ref, shared_ref, up_acc, down_acc, landing, send, recv = refs
+        shard_ref, part_ref, pair_grad_ref, router_grad_ref, shared_ref, up_acc, down_acc, landing, send, recv = refs
 
         @pl.when(group == 0)
         def _():
             place = plane_place()
             greet({"seq": place[2]}, {"seq": place[3]})
-            landing[place[0]] = shard_ref[...]
+            landing[place[0]] = shard_ref[1]
             Replay(send, recv, landing, plane_place(), 1)
 
         @pl.when(group == 2)
@@ -636,7 +655,7 @@
             Replay(send, recv, landing, plane_place(), 2)
 
     else:
-        part_ref, up_grad_ref, down_grad_ref, router_grad_ref, up_acc, down_acc = refs
+        part_ref, pair_grad_ref, router_grad_ref, up_acc, down_acc = refs
         shared_ref = None
 
     @pl.when(group == 0)
@@ -652,13 +671,13 @@
     hot = slot_hot(slot_ref[...], capacity)
     scaled_rows = (own_share * rows_ref[...].astype(jnp.float32)).astype(jnp.bfloat16)
     result_grad = dot(hot, scaled_rows).astype(jnp.bfloat16)
-    hidden_grad = dot(result_grad, down_ref[...])
+    hidden_grad = dot(result_grad, one_of(pair_ref, 1))
     hidden, slope = gelu_parts(pre_ref[...].astype(jnp.float32))
     pre_grad = (slope * hidden_grad).astype(jnp.bfloat16)
     pair_sum = jnp.sum(hidden * hidden_grad, axis=1, keepdims=True)
     down_acc[...] += dot_tn(result_grad, hidden.astype(jnp.bfloat16))
     up_acc[...] += dot_tn(slots_ref[...], pre_grad)
-    slot_grad = dot_nt(pre_grad, up_ref[...]).astype(jnp.bfloat16)
+    slot_grad = dot_nt(pre_grad, one_of(pair_ref, 0)).astype(jnp.bfloat16)
     high = pair_sum.astype(jnp.bfloat16)
     rest = (pair_sum - high.astype(jnp.float32)).astype(jnp.bfloat16)
     token_pair = dot_tn(hot, jnp.concatenate([jnp.broadcast_to(high, (capacity, 128)), jnp.broadcast_to(rest, (capacity, 128))], axis=1))
@@ -669,8 +688,9 @@
 
     @pl.when(group == last)
     def _():
-        up_grad_ref[...] = up_acc[...].astype(jnp.bfloat16)
-        down_grad_ref[...] = down_acc[...].astype(jnp.bfloat16)
+        shape = pair_grad_ref.shape[:1] + pair_grad_ref.shape[2:]
+        pair_grad_ref[:, 0] = up_acc[...].astype(jnp.bfloat16).reshape(shape)
+        pair_grad_ref[:, 1] = down_acc[...].astype(jnp.bfloat16).reshape(shape)
 
     if shared_ref is not None:
 
@@ -688,40 +708,40 @@
     return pl.BlockSpec(shape, lambda g: (0,) * len(shape), pipeline_mode=pl.Buffered(1))
 
 
-def run_experts(tokens, slot, chosen, own, router, up, down, capacity):
+def run_experts(tokens, slot, chosen, own, router, pair, capacity):
     groups, rows, width = tokens.shape
-    experts, wide_ff = router.shape[0], up.shape[1]
+    experts, wide_ff = router.shape[0], pair.shape[3]
     return pl.pallas_call(
         experts_kernel,
         grid=(groups,),
         out_shape=(low_array(groups, rows, width), low_array(groups, capacity, width), low_array(groups, capacity, wide_ff),
                    wide_array(groups, rows, experts)),
         in_specs=[by_group(rows, width), by_group(1, rows), by_group(rows, experts), held(1, experts), held(experts, width),
-                  held(width, wide_ff), held(width, wide_ff)],
+                  held(*pair.shape)],
         out_specs=(by_group(rows, width), by_group(capacity, width), by_group(capacity, wide_ff), by_group(rows, experts)),
         compiler_params=pltpu.CompilerParams(dimension_semantics=("arbitrary",)),
         cost_estimate=cost(14.0),
         name="experts",
-    )(tokens, slot, chosen, own, router, up, down)
-
-
-def run_experts_back(rows_grad, tokens, slot, shares, own, router, up, down, slots, pre, shard=None):
+    )(tokens, slot, chosen, own, router, pair)
+
+
+def run_experts_back(rows_grad, tokens, slot, shares, own, router, pair, slots, pre, shard=None):
     groups, rows, width = tokens.shape
-    experts, wide_ff = router.shape[0], up.shape[1]
+    experts, wide_ff = router.shape[0], pair.shape[3]
     capacity = slots.shape[1]
-    outs = [low_array(groups, rows, width), low_array(width, wide_ff), low_array(width, wide_ff), wide_array(experts, width)]
-    out_specs = [by_group(rows, width), held(width, wide_ff), held(width, wide_ff), held(experts, width)]
+    outs = [low_array(groups, rows, width), low_array(*pair.shape), wide_array(experts, width)]
+    out_specs = [by_group(rows, width), held(*pair.shape), held(experts, width)]
     in_specs = [by_group(rows, width), by_group(rows, width), by_group(1, rows), by_group(rows, experts), held(1, experts),
-                held(experts, width), held(width, wide_ff), held(width, wide_ff), by_group(capacity, width), by_group(capacity, wide_ff)]
+                held(experts, width), held(*pair.shape), by_group(capacity, width), by_group(capacity, wide_ff)]
     scratch = [pltpu.VMEM((width, wide_ff), jnp.float32), pltpu.VMEM((width, wide_ff), jnp.float32)]
-    operands = [rows_grad, tokens, slot, shares, own, router, up, down, slots, pre]
+    operands = [rows_grad, tokens, slot, shares, own, router, pair, slots, pre]
     options = {}
     if shard is not None:
         operands.append(shard)
         in_specs.append(held(*shard.shape))
-        outs.append(low_array(4, *shard.shape))
-        out_specs.append(held(4, *shard.shape))
-        scratch += [pltpu.VMEM((4,) + shard.shape, jnp.bfloat16)] + sems(6)
+        outs.append(low_array(4, *shard.shape[1:]))
+        out_specs.append(held(4, *shard.shape[1:]))
+        scratch += [pltpu.VMEM((4,) + shard.shape[1:], jnp.bfloat16)] + sems(6)
         options = {"collective_id": 13, "has_side_effects": True}
     return pl.pallas_call(
         experts_back_kernel,
@@ -859,28 +879,71 @@
             one.wait_recv()
 
 
-def finish_kernel(layers, count, *refs):
+def small_steps(wires, place, line, s_ref, s_out, scratch):
+    me, core, near, far, cross = place
+    line_me, targets, sources = line
+    s_in, s_sum, s_line, s_tot, s_seq = scratch
+    partner = {"tensor": 1 - core}
+    one = wires.copy(s_ref.at[1 - core], s_in, partner)
+    yield
+    one.wait_recv()
+    s_sum[...] = s_ref[core] + s_in[...]
+    copies = [wires.copy(s_sum.at[spot], s_line.at[line_me], {"dp": spot}) for spot in targets]
+    s_line[line_me] = s_sum[line_me]
+    yield
+    for one in copies:
+        one.wait_recv()
+    s_tot[...] = jnp.sum(s_line[...], axis=0)
+    copies = [wires.copy(s_tot, s_seq.at[me], {"seq": spot}) for spot in (cross, near, far)]
+    s_seq[me] = s_tot[...]
+    yield
+    for one in copies:
+        one.wait_recv()
+    s_out[core] = jnp.sum(s_seq[...], axis=0)
+    mine = s_out.at[core]
+    one = wires.copy(mine, mine, partner)
+    yield
+    one.wait_recv()
+
+
+def finish_kernel(layers, *refs):
     def take(number):
         nonlocal refs
         first, refs = refs[:number], refs[number:]
         return first
 
-    q_refs, o_refs, shard_refs = take(layers), take(layers), take(count)
-    (total_ref,), o_outs, share_outs = take(1), take(layers), take(count)
+    q_refs, o_refs, s_refs = take(layers), take(layers), take(layers)
+    qkv_grad_ref, w_ref, x_ref, gain_ref, middle_grad_ref = take(5)
+    (total_ref, grad_ref), o_outs, s_outs = take(2), take(layers), take(layers)
     scratch = [take(8) for _ in range(layers)]
+    small_scratch = [take(5) for _ in range(layers)]
+    (s_own,), out_refs = take(1), take(6)
     place, line = plane_place(), dp_peers()
     me, core, near, far, cross = place
     wires = Wires(*refs)
     greet({"seq": near}, {"seq": far}, {"seq": cross}, {"tensor": 1 - core}, *[{"dp": spot} for spot in line[1]])
-    tasks = [reduce_steps(wires, place, line, at > 0, *one) for at, one in enumerate(zip(q_refs, o_refs, o_outs, scratch))]
-    for _ in range(2):
-        for task in tasks:
-            next(task)
-    shares = []
-    for src, dst in zip(shard_refs, share_outs):
-        dst[me] = src[...]
-        shares.append(gather_steps(wires, dst, place, False))
-    run_all(*shares, *tasks)
+
+    def input_steps():
+        totals = []
+        yield from cross_steps(wires, place, lambda spot: dot_nt(qkv_grad_ref[spot], w_ref[...]), out_refs, totals.append)
+        part, gain_grad = norm_back(x_ref[...], gain_ref[...], totals[0])
+        grad_ref[...] = middle_grad_ref[...] + part
+        s_own[...] = s_refs[0][...]
+        size = s_own.shape[3]
+        for at in range(s_own.shape[1]):
+            s_own[0, at, 0:1, :] = gain_grad[:, at * size : (at + 1) * size]
+        yield
+        yield from small_steps(wires, place, line, s_own, s_outs[0], small_scratch[0])
+
+    reduces = [reduce_steps(wires, place, line, True, *one) for at, one in enumerate(zip(q_refs, o_refs, o_outs, scratch))]
+    inputs = input_steps()
+    for task in reduces:
+        next(task)
+    next(inputs)
+    for task in reduces:
+        next(task)
+    smalls = [small_steps(wires, place, line, s_refs[at], s_outs[at], small_scratch[at]) for at in range(1, layers)]
+    run_all(inputs, *reduces, *smalls)
     rows = total_ref.shape[1] // 2
     for layer in range(layers):
         whole = scratch[layer][3]
@@ -888,6 +951,18 @@
         for half in range(2):
             pieces = [whole[half, spot][:, kind * size : (kind + 1) * size] for kind in range(3) for spot in range(4)]
             total_ref[layer, half * rows : (half + 1) * rows, :] = wide(jnp.concatenate(pieces, axis=1))
+    wires.finish()
+
+
+def share_kernel(pair_ref, one_ref, two_ref, send, recv):
+    place = plane_place()
+    wires = Wires(send, recv)
+    greet({"seq": place[2]}, {"seq": place[3]})
+    tasks = []
+    for at, dst in enumerate((one_ref, two_ref)):
+        dst[place[0]] = pair_ref[at]
+        tasks.append(gather_steps(wires, dst, place, False))
+    run_all(*tasks)
     wires.finish()
 def body(
     block_input,
@@ -942,11 +1017,6 @@
     own_up = lax.dynamic_index_in_dim(expert_up, seq_index, 1, keepdims=False)
     own_down = lax.dynamic_index_in_dim(expert_down, seq_index, 1, keepdims=False).swapaxes(1, 2)
 
-    def expert_weights(layer):
-        up = lax.all_gather(own_up[layer], "dp", axis=0, tiled=True)
-        down = lax.all_gather(own_down[layer], "dp", axis=0, tiled=True)
-        return up, down
-
     own_shape = (n_tensor, half, 3 * head_width)
     small_all, qkv_all, qkv_next, *out_pieces = comm_call(
         weights_kernel, "weights", 10, 22.0,
@@ -954,8 +1024,8 @@
         + [low_array(n_dp, shard // n_seq, width // n_tensor)] * LAYERS,
         [pltpu.VMEM(own_shape, low)], 5 * (n_dp - 1), small, query_key_value, own_out
     )
-    own_up, own_down, small_all = lax.optimization_barrier((own_up, own_down, small_all))
     qkv_weights = [qkv_all]
+    own_pair, small_all = lax.optimization_barrier((jnp.stack([own_up, own_down], axis=1), small_all))
     whole_rows = small_all.swapaxes(0, 1).reshape(-1, width)
     gains = whole_rows[: 2 * LAYERS].astype(jnp.float32).reshape(2, LAYERS, 1, width)
     routers = whole_rows[2 * LAYERS : 2 * LAYERS + LAYERS * experts].reshape(LAYERS, experts, width)
@@ -981,7 +1051,7 @@
     grad = cotangent[0]
     saved = []
     for layer in range(LAYERS):
-        up, down = expert_weights(layer)
+        pair = lax.all_gather(own_pair[layer], "dp", axis=0)
         gain_one, gain_two = gains[0, layer], gains[1, layer]
         qkv_weight = qkv_weights[layer].reshape(width, 3 * head_width)
         outs = [low_array(n_seq, piece, width), low_array(n_seq, piece, 3 * head_width)]
@@ -990,11 +1060,6 @@
             normed_all, qkv, routes_all = comm_call(
                 project_kernel, "project", 1, 16.0, outs, [], 9, current, gain_one, qkv_weight, routes_own
             )
-            routes_all = jnp.moveaxis(routes_all.reshape((n_seq,) + routes.shape), 0, 1).reshape(LAYERS, n_seq, group_rows, -1)
-            mine = jnp.any(routes_all == seq_index, axis=-1)
-            slot = dot(mine.reshape(-1, group_rows).astype(low), strict_upper).astype(jnp.int32).reshape(mine.shape)
-            slot = jnp.where(mine & (slot < capacity), slot, -1)[:, :, None]
-            chosen = jnp.any(routes_all[..., None] == lax.iota(jnp.int32, experts), axis=3).astype(jnp.float32)
         else:
             current, normed_all, qkv = comm_call(
                 sum_project_kernel, "sum_project", 2, 32.0, [wide_array(piece, width)] + outs,
@@ -1017,90 +1082,95 @@
             14 + (2 * (n_dp - 1) if fetch else 0), *operands
         )
         qkv_weights += more
+        if layer == 0:
+            routes_all, tokens = lax.optimization_barrier((routes_all, tokens))
+            routes_all = jnp.moveaxis(routes_all.reshape((n_seq,) + routes.shape), 0, 1).reshape(LAYERS, n_seq, group_rows, -1)
+            mine = jnp.any(routes_all == seq_index, axis=-1)
+            slot = dot(mine.reshape(-1, group_rows).astype(low), strict_upper).astype(jnp.int32).reshape(mine.shape)
+            slot = jnp.where(mine & (slot < capacity), slot, -1)[:, :, None]
+            chosen = jnp.any(routes_all[..., None] == lax.iota(jnp.int32, experts), axis=3).astype(jnp.float32)
         tokens = tokens.reshape(n_seq, group_rows, width)
-        part, slots, pre, shares = run_experts(tokens, slot[layer], chosen[layer], own_hot, routers[layer], up, down, capacity)
+        part, slots, pre, shares = run_experts(tokens, slot[layer], chosen[layer], own_hot, routers[layer], pair, capacity)
         part = part.reshape(n_seq, n_tensor, piece, width)
-        saved.append((current, normed_all, qkv, log_total, merged, middle, tokens, shares, slots, pre, qkv_weight, out_weight, up, down))
+        saved.append((current, normed_all, qkv, log_total, merged, middle, tokens, shares, slots, pre, qkv_weight, out_weight, pair))
 
     last_part, last_middle = part, middle
 
-    def shard_sum(values):
-        return lax.psum_scatter(values, "dp", scatter_dimension=0, tiled=True)
-
-    up_shards, down_shards, qkv_grads, out_grads = ([None] * LAYERS for _ in range(4))
+    pair_shards, qkv_grads, out_grads, smalls = ([None] * LAYERS for _ in range(4))
     out_rows = half // n_seq
-    packed_rows = -(-(out_rows + 1) // 16) * 16
     for layer in range(LAYERS - 1, -1, -1):
-        (layer_in, normed_all, qkv, log_total, merged, middle, tokens, shares, slots, pre, qkv_weight, out_weight, up, down) = saved[layer]
+        (layer_in, normed_all, qkv, log_total, merged, middle, tokens, shares, slots, pre, qkv_weight, out_weight, pair) = saved[layer]
         gain_one, gain_two = gains[0, layer], gains[1, layer]
-        part, up_grad, down_grad, router_grad, *shared = run_experts_back(
-            grad_rows.reshape(n_seq, group_rows, width), tokens, slot[layer], shares, own_hot, routers[layer], up, down, slots, pre,
-            down_shards[1] if layer == 0 else None
+        part, pair_grad, router_grad, *shared = run_experts_back(
+            grad_rows.reshape(n_seq, group_rows, width), tokens, slot[layer], shares, own_hot, routers[layer], pair, slots, pre,
+            pair_shards[1] if layer == 0 else None
         )
-        down_shards[layer] = shard_sum(down_grad)
-        up_shards[layer] = shard_sum(up_grad)
-        middle_grad, out_grad, gain_two_grad, mixed_grad = comm_call(
-            split_kernel, "split", 5, 22.0,
-            [wide_array(piece, width), low_array(piece, width), wide_array(1, width), low_array(n_seq, piece, head_width)],
-            [pltpu.VMEM((n_seq, piece, head_width), low), pltpu.VMEM((n_seq, piece, width), low)] + sum_scratch(piece, width), 13,
-            part.reshape(n_seq, n_tensor, piece, width), middle, gain_two, grad, out_weight
+        pair_shards[layer] = lax.psum_scatter(pair_grad, "dp", scatter_dimension=0, tiled=True)[0]
+        middle_grad, gain_two_grad, mixed_grad, out_grads[layer] = comm_call(
+            split_kernel, "split", 5, 25.0,
+            [wide_array(piece, width), wide_array(1, width), low_array(n_seq, piece, head_width),
+             low_array(n_tensor, n_dp, n_seq, out_rows, width)],
+            [pltpu.VMEM((piece, width), low), pltpu.VMEM((n_seq, piece, head_width), low), pltpu.VMEM((n_seq, piece, width), low)]
+            + sum_scratch(piece, width), 13,
+            part.reshape(n_seq, n_tensor, piece, width), middle, gain_two, grad, out_weight, merged
         )
-        out_weight_grad = jnp.einsum("gtd,te->gde", merged, out_grad, preferred_element_type=jnp.float32)
         operands = (qkv, seg_row, seg_col, lines[layer], log_total, mixed_grad.reshape(length, head_width))
+        operands += (normed_all.reshape(length, width), (n_tensor, n_dp, half, 3 * head_width))
         if layer == 0:
             (down_last,) = shared
-            outs = [low_array(n_seq, *up_shards[1].shape)]
-            qkv_grad, band, up_last = attend_back(*operands, (up_shards[1],), outs, [], "share", 9, 6)
+            outs = [low_array(n_seq, *pair_shards[1].shape[1:])]
+            qkv_grad, band, qkv_grads[layer], up_last = attend_back(*operands, (pair_shards[1],), outs, [], "share", 9, 6)
+            gain_one_grad = jnp.zeros((1, width), jnp.float32)
         else:
             outs = [wide_array(piece, width)]
             extra_scratch = [pltpu.VMEM((n_seq, piece, width), low)] + sum_scratch(piece, width)
-            qkv_grad, band, block_output = attend_back(*operands, (last_part, last_middle), outs, extra_scratch, "sum", 4, 10)
-        qkv_weight_grad = dot_tn(normed_all.reshape(length, width), qkv_grad)
-        spread = layer > 0
-        outs = [wide_array(piece, width), wide_array(1, width)]
-        outs += [low_array(n_seq, n_tensor, piece, width)] if spread else []
-        outs = comm_call(
-            functools.partial(input_grad_kernel, spread), "input_grad_spread" if spread else "input_grad", 7 + spread, 32.0 if spread else 16.0,
-            outs, sum_scratch(piece, width), 17, qkv_grad.reshape(n_seq, piece, -1), qkv_weight, layer_in, gain_one, middle_grad
-        )
-        grad, gain_one_grad = outs[:2]
-        grad_rows = outs[2] if spread else None
+            qkv_grad, band, qkv_grads[layer], block_output = attend_back(
+                *operands, (last_part, last_middle), outs, extra_scratch, "sum", 4, 10
+            )
+            outs = [wide_array(piece, width), wide_array(1, width), low_array(n_seq, n_tensor, piece, width)]
+            grad, gain_one_grad, grad_rows = comm_call(
+                functools.partial(input_grad_kernel, True), "input_grad", 7, 32.0, outs, sum_scratch(piece, width), 17,
+                qkv_grad.reshape(n_seq, piece, -1), qkv_weight, layer_in, gain_one, middle_grad
+            )
         table_grad = jnp.dot(line_hot, band.T, precision=highest_precision)
         table_grad = lax.dynamic_update_slice_in_dim(
             jnp.zeros((bucket_count, HEADS), jnp.float32), table_grad, seq_index * local_heads, 1
         )
         table_grad = padded(table_grad.reshape(n_dp, -1)).reshape(1, width)
         packed = jnp.concatenate([gain_one_grad, gain_two_grad, router_grad, table_grad, jnp.zeros((1, width), jnp.float32)])
-        packed = packed.reshape(n_plane, n_dp, shard).swapaxes(0, 1)[:, :, None]
-        packed = jnp.pad(packed, ((0, 0), (0, 0), (0, packed_rows - out_rows - 1), (0, width - shard)))
-        both = jnp.concatenate([out_weight_grad.reshape(n_dp, n_plane, out_rows, width), packed], axis=2).astype(low)
-        out_grads[layer] = both.reshape(n_dp, n_tensor, n_seq, packed_rows, width).swapaxes(0, 1)
-        qkv_grads[layer] = qkv_weight_grad.astype(low).reshape(n_dp, n_tensor, half, 3 * head_width).swapaxes(0, 1)
+        smalls[layer] = packed.reshape(n_tensor, n_seq, n_dp, shard).swapaxes(1, 2)
 
     def reduce_scratch(plane_first):
         line = pltpu.VMEM((n_dp, half, 3 * head_width), low)
-        blocks = pltpu.VMEM((n_dp, n_seq, packed_rows, width), low)
-        over_dp, over_seq = (pltpu.VMEM((count, packed_rows, width), low) for count in (n_dp, n_seq))
+        blocks = pltpu.VMEM((n_dp, n_seq, out_rows, width), low)
+        over_dp, over_seq = (pltpu.VMEM((count, out_rows, width), low) for count in (n_dp, n_seq))
         found = [line] * 3 + [pltpu.VMEM((n_tensor, n_seq, half, 3 * head_width), low), blocks]
         if plane_first:
-            return found + [over_dp, over_dp, pltpu.VMEM((n_seq, n_dp, packed_rows, width), low)]
+            return found + [over_dp, over_dp, pltpu.VMEM((n_seq, n_dp, out_rows, width), low)]
         return found + [blocks, over_seq, over_seq]
 
-    qkv_total, *totals = comm_call(
-        functools.partial(finish_kernel, LAYERS, 2), "finish", 11, 70.0,
-        [wide_array(LAYERS, shard, 3 * width)] + [low_array(n_tensor, n_seq, packed_rows, width)] * LAYERS
-        + [low_array(n_seq, shard, up.shape[1])] * 2,
-        reduce_scratch(False) + reduce_scratch(True), LAYERS * (2 * (n_dp - 1) + 19) + 12, *qkv_grads, *out_grads, up_shards[0], down_shards[0]
+    small_scratch = [pltpu.VMEM((n_dp, n_seq, shard), jnp.float32)] * 3 + [pltpu.VMEM((n_seq, shard), jnp.float32)]
+    small_scratch += [pltpu.VMEM((n_seq, n_seq, shard), jnp.float32)]
+    qkv_total, input_grad, *totals = comm_call(
+        functools.partial(finish_kernel, LAYERS), "finish", 11, 75.0,
+        [wide_array(LAYERS, shard, 3 * width), wide_array(piece, width)]
+        + [low_array(n_tensor, n_seq, out_rows, width)] * LAYERS + [wide_array(n_tensor, n_seq, shard)] * LAYERS,
+        reduce_scratch(True) + reduce_scratch(True) + small_scratch * LAYERS
+        + [pltpu.VMEM((n_tensor, n_dp, n_seq, shard), jnp.float32)] + sum_scratch(piece, width),
+        LAYERS * (2 * (n_dp - 1) + 19 + n_dp + 4) + 6,
+        *qkv_grads, *out_grads, *smalls, qkv_grad.reshape(n_seq, piece, -1), qkv_weight, layer_in, gain_one, middle_grad
     )
-    up_first, down_first = totals[LAYERS:]
-    both = jnp.stack(totals[:LAYERS]).astype(jnp.float32).reshape(LAYERS, n_plane, packed_rows, width)
-    out_total = both[:, :, :out_rows].reshape(LAYERS, shard, width)
-    small = both[:, :, out_rows, :shard]
+    out_total = jnp.stack(totals[:LAYERS]).astype(jnp.float32).reshape(LAYERS, shard, width)
+    small = jnp.stack(totals[LAYERS : 2 * LAYERS]).reshape(LAYERS, n_plane, shard)
+    pair_last, small = lax.optimization_barrier((pair_shards[0], small))
+    up_first, down_first = comm_call(
+        share_kernel, "share", 12, 42.0, [low_array(n_seq, *pair_last.shape[1:])] * 2, [], 12, pair_last
+    )
     router_total = small[:, 2 : 2 + experts].swapaxes(1, 2)
     table_total = small[:, 2 + experts, : bucket_shard * HEADS].reshape(LAYERS, bucket_shard, HEADS)
     up_total = jnp.stack([up_first, up_last]).astype(jnp.float32)
     down_total = jnp.stack([down_first, down_last]).astype(jnp.float32).swapaxes(2, 3)
-    return (block_output[None], grad[None], small[:, 0], qkv_total, out_total, table_total, small[:, 1], router_total, up_total, down_total)
+    return (block_output[None], input_grad[None], small[:, 0], qkv_total, out_total, table_total, small[:, 1], router_total, up_total, down_total)
 
 
 def solution(mesh):

time: 623 us -> 604 us (0.970)
  waiting for transfers between devices: 22.8 us -> 14 us
  matrix products: 10.1 us -> 1.46 us
    dot_general x4 -> x0, matrix products: 8.63 us -> none  [the longest x2 6.38 us: dot_tn(): return lax.dot_general(left, right, TN, preferred_element_type=jnp.float32)]
    all_gather x4 -> x2, waiting for transfers between devices: 20.2 us -> 13.2 us  [body(): pair = lax.all_gather(own_pair[layer], 'dp', axis=0)]
  transfers between devices with their start and end apart: 8 -> 4, of which waited for: 1 -> 1; matrix products, arithmetic and copies ran while one was open for 6% -> 3% of each run, Pallas kernels for 61% -> 64%
where the time goes in v5:
time: 604 us; the launch traced here: 598 us
  Pallas kernels  524 us (87%)
  local copies, waits for them, and re-layouts  26.1 us (4%)
  other arithmetic  17.2 us (3%)
  between operations  14.5 us (2%)
  waiting for transfers between devices  14 us (2%)
    pallas_call x14, Pallas kernels, comm_call(): pl.pallas_call(kernel, out_shape=tuple(outs), in_specs=vmem(len(operands)...  444 us
    pallas_call x2, Pallas kernels, run_experts_back(): pl.pallas_call(experts_back_kernel, grid=(groups,), out_shape=tuple(outs)...  54.3 us
    pallas_call x2, Pallas kernels, run_experts(): pl.pallas_call(experts_kernel, grid=(groups,), out_shape=(low_array(group...  26 us
    all_gather x2, waiting for transfers between devices, body(): pair = lax.all_gather(own_pair[layer], 'dp', axis=0)  13.2 us
  transfers between devices with their start and end apart: 4, of which 1 were waited for; matrix products, arithmetic and copies ran while one was open for 3% of the time, Pallas kernels for 64%

profile of v5, /device:TPU:0, one launch (start us, length us, event | category | flops | bytes accessed | tf_op | source)
XLA Modules:
  0.0 598.0 jit_solution(15959103175639416933)
XLA Ops:
  7.2 1.4 dynamic-slice_bitcast_fusion
  8.6 2.4 constant_dynamic-slice_fusion
  11.1 1.5 pad_maximum_fusion
  13.3 26.4 %weights.1 = (bf16[4,16,192]{2,1,0:T(8,128)(2,1)}, bf16[4,2,96,576]{3,2,1,0:T(8,128)(2,1)}, bf16[2,96,576]{2,1,0:T(8,128)(2,1)}, bf16[4,48,384]{2,1,0:T(8,128)(2,1)}, bf16[4,48,384]{2,1,0:T(8,128)(2,1)}) custom-call(bf16[16,192]{1,0:T(8,128)(2,1)} %pad.16.small_ref, bf16[2,192,2304]{2,1,0:T(8,128)(2,1)} %whole_ref.1, bf16[2,4,48,768]{3,2,1,0:T(8,128)(2,1)} %bitcast.138), custom_call_target="tpu_custom_call" | custom-call | bytes 66000000 | tf_op jit(solution)/shard_map/weights/pallas_call | solution.py:549
  39.6 1.6 fusion.13
  43.3 1.0 copy.73.refs_2_
  45.1 19.2 %project.1 = (bf16[4,256,768]{2,1,0:T(8,128)(2,1)}, bf16[4,256,576]{2,1,0:T(8,128)(2,1)}, s32[4,16,128]{2,1,0:T(8,128)}) custom-call(f32[256,768]{1,0:T(8,128)} %bitcast.101, f32[1,768]{1,0:T(1,128)} %get-tuple-element.172.gain_ref.refs_9_, bf16[768,576]{1,0:T(8,128)(2,1)} %bitcast.116, s32[16,128]{1,0:T(8,128)} %reshape.189.routes_ref), custom_call_target="tpu_custom_call" | custom-call | bytes 48000000 | tf_op jit(solution)/shard_map/project/pallas_call | solution.py:549
  65.3 21.6 %attend_fetch.1 = (bf16[1024,192]{1,0:T(8,128)(2,1)}, f32[3,1024,1]{2,1,0:T(8,128)}, bf16[4,4,48,768]{3,2,1,0:T(8,128)(2,1)}, bf16[4,4,48,768]{3,2,1,0:T(8,128)(2,1)}) custom-call(bf16[1024,576]{1,0:T(8,128)(2,1)} %bitcast.104, s32[1,1024]{1,0:T(1,128)} %refs_1_.7, s32[1024,1]{1,0:T(8,128)} %copy.73.refs_2_, f32[3,640]{1,0:T(4,128)} %get-tuple-element.164.refs_3_, ...), custom_call_target="tpu_custom_call" | custom-call | bytes 54000000 | tf_op jit(solution)/shard_map/attend_fetch/pallas_call | solution.py:549
  86.9 32.8 %merge_fetch.1 = (bf16[4,256,192]{2,1,0:T(8,128)(2,1)}, f32[256,768]{1,0:T(8,128)}, bf16[4,2,256,768]{3,2,1,0:T(8,128)(2,1)}, bf16[4,2,96,576]{3,2,1,0:T(8,128)(2,1)}) custom-call(bf16[4,256,192]{2,1,0:T(8,128)(2,1)} %bitcast.140, f32[256,768]{1,0:T(8,128)} %bitcast.102, bf16[4,192,768]{2,1,0:T(8,128)(2,1)} %bitcast.110, ...), custom_call_target="tpu_custom_call" | custom-call | bytes 75000000 | tf_op jit(solution)/shard_map/merge_fetch/pallas_call | solution.py:549
  120.1 1.7 compare_reduce_fusion
  126.8 1.5 slice_bitcast_fusion
  128.3 13.2 %all-gather.3.cloned.1.call-done.pair_ref = bf16[4,2,192,1536]{3,2,1,0:T(8,128)(2,1)} async-done(((bf16[1,2,192,1536]{3,2,1,0:T(8,128)(2,1)}), bf16[4,2,192,1536]{3,2,1,0:T(8,128)(2,1)}) %all-gather.3.cloned.1.call-update) | async-done | bytes 4718608 | tf_op jit(solution)/shard_map/all_gather | solution.py:1054
  141.5 13.2 %experts.2 = (bf16[4,512,768]{2,1,0:T(8,128)(2,1)}, bf16[4,256,768]{2,1,0:T(8,128)(2,1)}, bf16[4,256,1536]{2,1,0:T(8,128)(2,1)}, f32[4,512,4]{2,1,0:T(8,128)}) custom-call(bf16[4,512,768]{2,1,0:T(8,128)(2,1)} %bitcast.95, s32[4,1,512]{2,1,0:T(1,128)} %get-tuple-element.168.slot_ref, f32[4,512,4]{2,1,0:T(8,128)} %get-tuple-element.159.chosen_ref, ...), custom_call_target="tpu_custom_call" | custom-call | bytes 42000000 | tf_op jit(solution)/shard_map/experts/pallas_call | solution.py:714
  154.7 37.7 %sum_project.1 = (f32[256,768]{1,0:T(8,128)}, bf16[4,256,768]{2,1,0:T(8,128)(2,1)}, bf16[4,256,576]{2,1,0:T(8,128)(2,1)}) custom-call(bf16[4,2,256,768]{3,2,1,0:T(8,128)(2,1)} %bitcast.120, f32[256,768]{1,0:T(8,128)} %get-tuple-element.98.base_ref.middle_ref, f32[1,768]{1,0:T(1,128)} %get-tuple-element.170.gain_ref, bf16[768,576]{1,0:T(8,128)(2,1)} %bitcast.114), custom_call_target="tpu_custom_call" | custom-call | bytes 96000000 | tf_op jit(solution)/shard_map/sum_project/pallas_call | solution.py:549
  192.5 21.9 %attend_gather.1 = (bf16[1024,192]{1,0:T(8,128)(2,1)}, f32[3,1024,1]{2,1,0:T(8,128)}, bf16[4,2,256,768]{3,2,1,0:T(8,128)(2,1)}) custom-call(bf16[1024,576]{1,0:T(8,128)(2,1)} %bitcast.106, s32[1,1024]{1,0:T(1,128)} %refs_1_.7, s32[1024,1]{1,0:T(8,128)} %copy.73.refs_2_, f32[3,640]{1,0:T(4,128)} %get-tuple-element.163.refs_3_, f32[256,768]{1,0:T(8,128)} %bitcast.121), custom_call_target="tpu_custom_call" | custom-call | bytes 54000000 | tf_op jit(solution)/shard_map/attend_gather/pallas_call | solution.py:549
  214.4 27.5 %merge.1 = (bf16[4,256,192]{2,1,0:T(8,128)(2,1)}, f32[256,768]{1,0:T(8,128)}, bf16[4,2,256,768]{3,2,1,0:T(8,128)(2,1)}) custom-call(bf16[4,256,192]{2,1,0:T(8,128)(2,1)} %bitcast.141, f32[256,768]{1,0:T(8,128)} %get-tuple-element.104.base_ref.x_ref, bf16[4,192,768]{2,1,0:T(8,128)(2,1)} %bitcast.112, f32[1,768]{1,0:T(1,128)} %get-tuple-element.169.gain_ref), custom_call_target="tpu_custom_call" | custom-call | bytes 75000000 | tf_op jit(solution)/shard_map/merge/pallas_call | solution.py:549
  242.0 12.8 %experts.3 = (bf16[4,512,768]{2,1,0:T(8,128)(2,1)}, bf16[4,256,768]{2,1,0:T(8,128)(2,1)}, bf16[4,256,1536]{2,1,0:T(8,128)(2,1)}, f32[4,512,4]{2,1,0:T(8,128)}) custom-call(bf16[4,512,768]{2,1,0:T(8,128)(2,1)} %bitcast.97, s32[4,1,512]{2,1,0:T(1,128)} %get-tuple-element.167.slot_ref, f32[4,512,4]{2,1,0:T(8,128)} %get-tuple-element.158.chosen_ref, ...), custom_call_target="tpu_custom_call" | custom-call | bytes 42000000 | tf_op jit(solution)/shard_map/experts/pallas_call | solution.py:714
  254.7 24.6 %experts_back.1 = (bf16[4,512,768]{2,1,0:T(8,128)(2,1)}, bf16[4,2,192,1536]{3,2,1,0:T(8,128)(2,1)}, f32[4,768]{1,0:T(4,128)}) custom-call(bf16[4,512,768]{2,1,0:T(8,128)(2,1)} %bitcast.124, bf16[4,512,768]{2,1,0:T(8,128)(2,1)} %bitcast.98, s32[4,1,512]{2,1,0:T(1,128)} %get-tuple-element.167.slot_ref, f32[4,512,4]{2,1,0:T(8,128)} %get-tuple-element.107.shares_ref, ...), custom_call_target="tpu_custom_call" | custom-call | bytes 75000000 | tf_op jit(solution)/shard_map/experts_back/pallas_call | solution.py:746
  279.6 32.0 %split.2 = (f32[256,768]{1,0:T(8,128)}, f32[1,768]{1,0:T(1,128)}, bf16[4,256,192]{2,1,0:T(8,128)(2,1)}, bf16[2,4,4,24,768]{4,3,2,1,0:T(8,128)(2,1)}) custom-call(bf16[4,2,256,768]{3,2,1,0:T(8,128)(2,1)} %bitcast.119, f32[256,768]{1,0:T(8,128)} %get-tuple-element.111.middle_ref.refs_8_, f32[1,768]{1,0:T(1,128)} %get-tuple-element.169.gain_ref, ...), custom_call_target="tpu_custom_call" | custom-call | bytes 75000000 | tf_op jit(solution)/shard_map/split/pallas_call | solution.py:549
  311.6 25.1 %attend_back_sum.1 = (bf16[1024,576]{1,0:T(8,128)(2,1)}, f32[3,640]{1,0:T(4,128)}, bf16[2,4,96,576]{3,2,1,0:T(8,128)(2,1)}, f32[256,768]{1,0:T(8,128)}) custom-call(bf16[1024,576]{1,0:T(8,128)(2,1)} %bitcast.107, s32[1,1024]{1,0:T(1,128)} %refs_1_.7, s32[1024,1]{1,0:T(8,128)} %copy.73.refs_2_, f32[3,640]{1,0:T(4,128)} %get-tuple-element.163.refs_3_, ...), custom_call_target="tpu_custom_call" | custom-call | bytes 69000000 | tf_op jit(solution)/shard_map/attend_back_sum/pallas_call | solution.py:549
  336.7 35.8 %input_grad.1 = (f32[256,768]{1,0:T(8,128)}, f32[1,768]{1,0:T(1,128)}, bf16[4,2,256,768]{3,2,1,0:T(8,128)(2,1)}) custom-call(bf16[4,256,576]{2,1,0:T(8,128)(2,1)} %bitcast.133, bf16[768,576]{1,0:T(8,128)(2,1)} %bitcast.115, f32[256,768]{1,0:T(8,128)} %get-tuple-element.104.base_ref.x_ref, f32[1,768]{1,0:T(1,128)} %get-tuple-element.170.gain_ref, ...), custom_call_target="tpu_custom_call" | custom-call | bytes 96000000 | tf_op jit(solution)/shard_map/input_grad/pallas_call | solution.py:549
  372.5 29.7 %experts_back_share.1 = (bf16[4,512,768]{2,1,0:T(8,128)(2,1)}, bf16[4,2,192,1536]{3,2,1,0:T(8,128)(2,1)}, f32[4,768]{1,0:T(4,128)}, bf16[4,192,1536]{2,1,0:T(8,128)(2,1)}) custom-call(bf16[4,512,768]{2,1,0:T(8,128)(2,1)} %bitcast.125, bf16[4,512,768]{2,1,0:T(8,128)(2,1)} %bitcast.96, s32[4,1,512]{2,1,0:T(1,128)} %get-tuple-element.168.slot_ref, ...), custom_call_target="tpu_custom_call" | custom-call | bytes 75000000 | tf_op jit(solution)/shard_map/experts_back_share/pallas_call | solution.py:746
  404.2 30.9 %split.3 = (f32[256,768]{1,0:T(8,128)}, f32[1,768]{1,0:T(1,128)}, bf16[4,256,192]{2,1,0:T(8,128)(2,1)}, bf16[2,4,4,24,768]{4,3,2,1,0:T(8,128)(2,1)}) custom-call(bf16[4,2,256,768]{3,2,1,0:T(8,128)(2,1)} %bitcast.118, f32[256,768]{1,0:T(8,128)} %get-tuple-element.98.base_ref.middle_ref, f32[1,768]{1,0:T(1,128)} %get-tuple-element.171.gain_ref, ...), custom_call_target="tpu_custom_call" | custom-call | bytes 75000000 | tf_op jit(solution)/shard_map/split/pallas_call | solution.py:549
  435.2 26.8 %attend_back_share.1 = (bf16[1024,576]{1,0:T(8,128)(2,1)}, f32[3,640]{1,0:T(4,128)}, bf16[2,4,96,576]{3,2,1,0:T(8,128)(2,1)}, bf16[4,192,1536]{2,1,0:T(8,128)(2,1)}) custom-call(bf16[1024,576]{1,0:T(8,128)(2,1)} %bitcast.105, s32[1,1024]{1,0:T(1,128)} %refs_1_.7, s32[1024,1]{1,0:T(8,128)} %copy.73.refs_2_, f32[3,640]{1,0:T(4,128)} %get-tuple-element.164.refs_3_, ...), custom_call_target="tpu_custom_call" | custom-call | bytes 69000000 | tf_op jit(solution)/shard_map/attend_back_share/pallas_call | solution.py:549
  464.0 60.6 %finish.1 = (f32[2,192,2304]{2,1,0:T(8,128)}, f32[256,768]{1,0:T(8,128)}, bf16[2,4,24,768]{3,2,1,0:T(8,128)(2,1)}, bf16[2,4,24,768]{3,2,1,0:T(8,128)(2,1)}, f32[2,4,192]{2,1,0:T(4,128)}, /*index=5*/f32[2,4,192]{2,1,0:T(4,128)}) custom-call(bf16[2,4,96,576]{3,2,1,0:T(8,128)(2,1)} %get-tuple-element.130.refs_0_, ...), custom_call_target="tpu_custom_call" | custom-call | bytes 225000000 | tf_op jit(solution)/shard_map/finish/pallas_call | solution.py:549
  526.2 2.1 maximum_convert_fusion.1
  530.8 45.9 %share.1 = (bf16[4,192,1536]{2,1,0:T(8,128)(2,1)}, bf16[4,192,1536]{2,1,0:T(8,128)(2,1)}) custom-call(bf16[2,192,1536]{2,1,0:T(8,128)(2,1)} %bitcast.135), custom_call_target="tpu_custom_call" | custom-call | bytes 126000000 | tf_op jit(solution)/shard_map/share/pallas_call | solution.py:549
  576.7 6.2 %maximum_convert_fusion = f32[2,4,192,1536]{3,2,1,0:T(8,128)} fusion(bf16[1,4,192,1536]{3,2,1,0:T(8,128)(2,1)S(1)} %bitcast.127, bf16[1,4,192,1536]{3,2,1,0:T(8,128)(2,1)} %bitcast.129), kind=kLoop, calls=%fused_computation.1 | loop fusion | flops 4718592 | bytes 14155776 | tf_op jit(solution)/shard_map/convert_element_type | solution.py:1171
  582.9 4.8 convert_bitcast_fusion
  587.7 0.9 copy.113
  588.6 0.9 copy.114
  589.5 1.8 copy.115
  (115 shorter events, 18.2 us)
Async XLA Ops:
  7.2 134.3 %all-gather.3.cloned.1.call-start = ((), (), s32[]{:S(2)}) async-start(), calls=%async_computation.2 | async-start | bytes 5898240 | tf_op jit(solution)/shard_map/all_gather | solution.py:1054
  7.2 3.8 copy-start.12
  7.2 3.8 copy-start.13
  11.1 1.5 copy-start.17
  11.1 1.5 copy-start.18
  41.2 0.8 copy-start.8
  41.2 1.0 copy-start.11
  41.2 2.1 copy-start.6
  41.2 3.1 slice-start
  41.2 200.8 %all-gather.5.cloned.1.call-start = ((), (), s32[]{:S(2)}) async-start(), calls=%async_computation.3 | async-start | bytes 5898240 | tf_op jit(solution)/shard_map/all_gather | solution.py:1054
  42.0 330.5 %reduce-scatter.3.cloned.1.call-start = ((), (), s32[]{:S(2)}) async-start(), calls=%async_computation.4 | async-start | bytes 5898240 | tf_op jit(solution)/shard_map/reduce_scatter | solution.py:1108
  65.3 54.4 %copy-start.7 = (s32[4,16,128]{2,1,0:T(8,128)S(1)}, s32[4,16,128]{2,1,0:T(8,128)}, u32[]{:S(2)}) copy-start(s32[4,16,128]{2,1,0:T(8,128)} %get-tuple-element.95) | copy-start | bytes 98308
  279.4 249.0 %reduce-scatter.5.cloned.1.call-start = ((), (), s32[]{:S(2)}) async-start(), calls=%async_computation.5 | async-start | bytes 5898240 | tf_op jit(solution)/shard_map/reduce_scatter | solution.py:1108
  402.2 0.7 copy-start.19
  402.3 1.8 copy-start.9
  402.3 1.8 copy-start.14
  402.3 1.8 copy-start.15
  435.1 28.1 %copy-start.10 = (f32[4,768]{1,0:T(4,128)S(1)}, f32[4,768]{1,0:T(4,128)}, u32[]{:S(2)}) copy-start(f32[4,768]{1,0:T(4,128)} %get-tuple-element.135) | copy-start | bytes 36868
  435.2 28.1 %copy-start.16 = (f32[1,768]{1,0:T(1,128)S(1)}, f32[1,768]{1,0:T(1,128)}, u32[]{:S(2)}) copy-start(f32[1,768]{1,0:T(1,128)} %get-tuple-element.134) | copy-start | bytes 9220
  524.6 52.1 %copy-start.2 = (bf16[4,192,1536]{2,1,0:T(8,128)(2,1)S(1)}, bf16[4,192,1536]{2,1,0:T(8,128)(2,1)}, u32[]{:S(2)}) copy-start(bf16[4,192,1536]{2,1,0:T(8,128)(2,1)} %get-tuple-element.153) | copy-start | bytes 7077892
  576.7 6.2 %copy-start.1 = (bf16[4,192,1536]{2,1,0:T(8,128)(2,1)S(1)}, bf16[4,192,1536]{2,1,0:T(8,128)(2,1)}, u32[]{:S(2)}) copy-start(bf16[4,192,1536]{2,1,0:T(8,128)(2,1)} %get-tuple-element.155) | copy-start | bytes 7077892
  576.7 6.2 %copy-start.3 = (bf16[4,192,1536]{2,1,0:T(8,128)(2,1)S(1)}, bf16[4,192,1536]{2,1,0:T(8,128)(2,1)}, u32[]{:S(2)}) copy-start(bf16[4,192,1536]{2,1,0:T(8,128)(2,1)} %get-tuple-element.154) | copy-start | bytes 7077892
  582.9 4.8 copy-start.4
  582.9 5.7 copy-start.5
  582.9 6.6 %copy-start = (f32[2,192,2304]{2,1,0:T(8,128)S(1)}, f32[2,192,2304]{2,1,0:T(8,128)}, u32[]{:S(2)}) copy-start(f32[2,192,2304]{2,1,0:T(8,128)} %get-tuple-element.188) | copy-start | bytes 10616836
Sparse Core Ops, SparseCore 0:
  41.3 100.0 all-gather.2
  143.6 87.7 all-gather.4
  279.5 83.9 reduce-scatter.2
  402.4 95.6 reduce-scatter.4

commit v6 on v5

--- a/solution.py
+++ b/solution.py
@@ -912,38 +912,26 @@
         first, refs = refs[:number], refs[number:]
         return first
 
-    q_refs, o_refs, s_refs = take(layers), take(layers), take(layers)
-    qkv_grad_ref, w_ref, x_ref, gain_ref, middle_grad_ref = take(5)
-    (total_ref, grad_ref), o_outs, s_outs = take(2), take(layers), take(layers)
+    q_refs, o_refs, s_refs, (pair_ref,) = take(layers), take(layers), take(layers), take(1)
+    (total_ref,), o_outs, s_outs, share_outs = take(1), take(layers), take(layers), take(2)
     scratch = [take(8) for _ in range(layers)]
     small_scratch = [take(5) for _ in range(layers)]
-    (s_own,), out_refs = take(1), take(6)
     place, line = plane_place(), dp_peers()
     me, core, near, far, cross = place
     wires = Wires(*refs)
     greet({"seq": near}, {"seq": far}, {"seq": cross}, {"tensor": 1 - core}, *[{"dp": spot} for spot in line[1]])
-
-    def input_steps():
-        totals = []
-        yield from cross_steps(wires, place, lambda spot: dot_nt(qkv_grad_ref[spot], w_ref[...]), out_refs, totals.append)
-        part, gain_grad = norm_back(x_ref[...], gain_ref[...], totals[0])
-        grad_ref[...] = middle_grad_ref[...] + part
-        s_own[...] = s_refs[0][...]
-        size = s_own.shape[3]
-        for at in range(s_own.shape[1]):
-            s_own[0, at, 0:1, :] = gain_grad[:, at * size : (at + 1) * size]
-        yield
-        yield from small_steps(wires, place, line, s_own, s_outs[0], small_scratch[0])
-
-    reduces = [reduce_steps(wires, place, line, True, *one) for at, one in enumerate(zip(q_refs, o_refs, o_outs, scratch))]
-    inputs = input_steps()
+    reduces = [reduce_steps(wires, place, line, True, *one) for one in zip(q_refs, o_refs, o_outs, scratch)]
+    smalls = [small_steps(wires, place, line, *one) for one in zip(s_refs, s_outs, small_scratch)]
+    for task in reduces + smalls:
+        next(task)
     for task in reduces:
         next(task)
-    next(inputs)
-    for task in reduces:
-        next(task)
-    smalls = [small_steps(wires, place, line, s_refs[at], s_outs[at], small_scratch[at]) for at in range(1, layers)]
-    run_all(inputs, *reduces, *smalls)
+    shares = []
+    for at, dst in enumerate(share_outs):
+        dst[me] = pair_ref[at]
+        shares.append(gather_steps(wires, dst, place, False))
+        next(shares[at])
+    run_all(*reduces, *smalls, *shares)
     rows = total_ref.shape[1] // 2
     for layer in range(layers):
         whole = scratch[layer][3]
@@ -953,17 +941,6 @@
             total_ref[layer, half * rows : (half + 1) * rows, :] = wide(jnp.concatenate(pieces, axis=1))
     wires.finish()
 
-
-def share_kernel(pair_ref, one_ref, two_ref, send, recv):
-    place = plane_place()
-    wires = Wires(send, recv)
-    greet({"seq": place[2]}, {"seq": place[3]})
-    tasks = []
-    for at, dst in enumerate((one_ref, two_ref)):
-        dst[place[0]] = pair_ref[at]
-        tasks.append(gather_steps(wires, dst, place, False))
-    run_all(*tasks)
-    wires.finish()
 def body(
     block_input,
     segments,
@@ -1120,7 +1097,10 @@
             (down_last,) = shared
             outs = [low_array(n_seq, *pair_shards[1].shape[1:])]
             qkv_grad, band, qkv_grads[layer], up_last = attend_back(*operands, (pair_shards[1],), outs, [], "share", 9, 6)
-            gain_one_grad = jnp.zeros((1, width), jnp.float32)
+            input_grad, gain_one_grad = comm_call(
+                functools.partial(input_grad_kernel, False), "input_grad_last", 12, 16.0, [wide_array(piece, width), wide_array(1, width)],
+                sum_scratch(piece, width), 6, qkv_grad.reshape(n_seq, piece, -1), qkv_weight, layer_in, gain_one, middle_grad
+            )
         else:
             outs = [wide_array(piece, width)]
             extra_scratch = [pltpu.VMEM((n_seq, piece, width), low)] + sum_scratch(piece, width)
@@ -1151,21 +1131,17 @@
 
     small_scratch = [pltpu.VMEM((n_dp, n_seq, shard), jnp.float32)] * 3 + [pltpu.VMEM((n_seq, shard), jnp.float32)]
     small_scratch += [pltpu.VMEM((n_seq, n_seq, shard), jnp.float32)]
-    qkv_total, input_grad, *totals = comm_call(
-        functools.partial(finish_kernel, LAYERS), "finish", 11, 75.0,
-        [wide_array(LAYERS, shard, 3 * width), wide_array(piece, width)]
-        + [low_array(n_tensor, n_seq, out_rows, width)] * LAYERS + [wide_array(n_tensor, n_seq, shard)] * LAYERS,
-        reduce_scratch(True) + reduce_scratch(True) + small_scratch * LAYERS
-        + [pltpu.VMEM((n_tensor, n_dp, n_seq, shard), jnp.float32)] + sum_scratch(piece, width),
-        LAYERS * (2 * (n_dp - 1) + 19 + n_dp + 4) + 6,
-        *qkv_grads, *out_grads, *smalls, qkv_grad.reshape(n_seq, piece, -1), qkv_weight, layer_in, gain_one, middle_grad
+    qkv_total, *totals = comm_call(
+        functools.partial(finish_kernel, LAYERS), "finish", 11, 70.0,
+        [wide_array(LAYERS, shard, 3 * width)]
+        + [low_array(n_tensor, n_seq, out_rows, width)] * LAYERS + [wide_array(n_tensor, n_seq, shard)] * LAYERS
+        + [low_array(n_seq, *pair_shards[0].shape[1:])] * 2,
+        reduce_scratch(True) + reduce_scratch(True) + small_scratch * LAYERS,
+        LAYERS * (2 * (n_dp - 1) + 19 + n_dp + 4) + 12, *qkv_grads, *out_grads, *smalls, pair_shards[0]
     )
     out_total = jnp.stack(totals[:LAYERS]).astype(jnp.float32).reshape(LAYERS, shard, width)
     small = jnp.stack(totals[LAYERS : 2 * LAYERS]).reshape(LAYERS, n_plane, shard)
-    pair_last, small = lax.optimization_barrier((pair_shards[0], small))
-    up_first, down_first = comm_call(
-        share_kernel, "share", 12, 42.0, [low_array(n_seq, *pair_last.shape[1:])] * 2, [], 12, pair_last
-    )
+    up_first, down_first = totals[2 * LAYERS :]
     router_total = small[:, 2 : 2 + experts].swapaxes(1, 2)
     table_total = small[:, 2 + experts, : bucket_shard * HEADS].reshape(LAYERS, bucket_shard, HEADS)
     up_total = jnp.stack([up_first, up_last]).astype(jnp.float32)

time: 604 us -> 600 us (level)
  transfers between devices with their start and end apart: 4 -> 4, of which waited for: 1 -> 2; matrix products, arithmetic and copies ran while one was open for 3% -> 3% of each run, Pallas kernels for 64% -> 58%
where the time goes in v6:
time: 600 us; the launch traced here: 594 us
  Pallas kernels  519 us (86%)
  local copies, waits for them, and re-layouts  26.6 us (4%)
  other arithmetic  17.2 us (3%)
  waiting for transfers between devices  15.9 us (3%)
  between operations  14.5 us (2%)
    pallas_call x14, Pallas kernels, comm_call(): pl.pallas_call(kernel, out_shape=tuple(outs), in_specs=vmem(len(operands)...  439 us
    pallas_call x2, Pallas kernels, run_experts_back(): pl.pallas_call(experts_back_kernel, grid=(groups,), out_shape=tuple(outs)...  54.4 us
    pallas_call x2, Pallas kernels, run_experts(): pl.pallas_call(experts_kernel, grid=(groups,), out_shape=(low_array(group...  26 us
    all_gather x2, waiting for transfers between devices, body(): pair = lax.all_gather(own_pair[layer], 'dp', axis=0)  13.2 us
  transfers between devices with their start and end apart: 4, of which 2 were waited for; matrix products, arithmetic and copies ran while one was open for 3% of the time, Pallas kernels for 58%

profile of v6, /device:TPU:0, one launch (start us, length us, event | category | flops | bytes accessed | tf_op | source)
XLA Modules:
  0.0 594.2 jit_solution(11778324762955603559)
XLA Ops:
  7.2 1.4 dynamic-slice_bitcast_fusion
  8.6 2.4 constant_dynamic-slice_fusion
  11.1 1.5 pad_maximum_fusion
  13.3 26.4 %weights.1 = (bf16[4,16,192]{2,1,0:T(8,128)(2,1)}, bf16[4,2,96,576]{3,2,1,0:T(8,128)(2,1)}, bf16[2,96,576]{2,1,0:T(8,128)(2,1)}, bf16[4,48,384]{2,1,0:T(8,128)(2,1)}, bf16[4,48,384]{2,1,0:T(8,128)(2,1)}) custom-call(bf16[16,192]{1,0:T(8,128)(2,1)} %pad.16.small_ref, bf16[2,192,2304]{2,1,0:T(8,128)(2,1)} %whole_ref.1, bf16[2,4,48,768]{3,2,1,0:T(8,128)(2,1)} %bitcast.138), custom_call_target="tpu_custom_call" | custom-call | bytes 66000000 | tf_op jit(solution)/shard_map/weights/pallas_call | solution.py:549
  39.6 1.6 fusion.13
  43.3 1.0 copy.73.refs_2_
  45.1 19.2 %project.1 = (bf16[4,256,768]{2,1,0:T(8,128)(2,1)}, bf16[4,256,576]{2,1,0:T(8,128)(2,1)}, s32[4,16,128]{2,1,0:T(8,128)}) custom-call(f32[256,768]{1,0:T(8,128)} %bitcast.101, f32[1,768]{1,0:T(1,128)} %get-tuple-element.170.gain_ref, bf16[768,576]{1,0:T(8,128)(2,1)} %bitcast.116, s32[16,128]{1,0:T(8,128)} %reshape.189.routes_ref), custom_call_target="tpu_custom_call" | custom-call | bytes 48000000 | tf_op jit(solution)/shard_map/project/pallas_call | solution.py:549
  65.3 21.6 %attend_fetch.1 = (bf16[1024,192]{1,0:T(8,128)(2,1)}, f32[3,1024,1]{2,1,0:T(8,128)}, bf16[4,4,48,768]{3,2,1,0:T(8,128)(2,1)}, bf16[4,4,48,768]{3,2,1,0:T(8,128)(2,1)}) custom-call(bf16[1024,576]{1,0:T(8,128)(2,1)} %bitcast.104, s32[1,1024]{1,0:T(1,128)} %refs_1_.7, s32[1024,1]{1,0:T(8,128)} %copy.73.refs_2_, f32[3,640]{1,0:T(4,128)} %get-tuple-element.162.refs_3_, ...), custom_call_target="tpu_custom_call" | custom-call | bytes 54000000 | tf_op jit(solution)/shard_map/attend_fetch/pallas_call | solution.py:549
  86.9 32.8 %merge_fetch.1 = (bf16[4,256,192]{2,1,0:T(8,128)(2,1)}, f32[256,768]{1,0:T(8,128)}, bf16[4,2,256,768]{3,2,1,0:T(8,128)(2,1)}, bf16[4,2,96,576]{3,2,1,0:T(8,128)(2,1)}) custom-call(bf16[4,256,192]{2,1,0:T(8,128)(2,1)} %bitcast.140, f32[256,768]{1,0:T(8,128)} %bitcast.102, bf16[4,192,768]{2,1,0:T(8,128)(2,1)} %bitcast.110, ...), custom_call_target="tpu_custom_call" | custom-call | bytes 75000000 | tf_op jit(solution)/shard_map/merge_fetch/pallas_call | solution.py:549
  120.1 1.7 compare_reduce_fusion
  126.8 1.5 slice_bitcast_fusion
  128.3 13.1 %all-gather.3.cloned.1.call-done.pair_ref = bf16[4,2,192,1536]{3,2,1,0:T(8,128)(2,1)} async-done(((bf16[1,2,192,1536]{3,2,1,0:T(8,128)(2,1)}), bf16[4,2,192,1536]{3,2,1,0:T(8,128)(2,1)}) %all-gather.3.cloned.1.call-update) | async-done | bytes 4718608 | tf_op jit(solution)/shard_map/all_gather | solution.py:1031
  141.5 13.2 %experts.2 = (bf16[4,512,768]{2,1,0:T(8,128)(2,1)}, bf16[4,256,768]{2,1,0:T(8,128)(2,1)}, bf16[4,256,1536]{2,1,0:T(8,128)(2,1)}, f32[4,512,4]{2,1,0:T(8,128)}) custom-call(bf16[4,512,768]{2,1,0:T(8,128)(2,1)} %bitcast.95, s32[4,1,512]{2,1,0:T(1,128)} %get-tuple-element.166.slot_ref, f32[4,512,4]{2,1,0:T(8,128)} %get-tuple-element.157.chosen_ref, ...), custom_call_target="tpu_custom_call" | custom-call | bytes 42000000 | tf_op jit(solution)/shard_map/experts/pallas_call | solution.py:714
  154.7 37.7 %sum_project.1 = (f32[256,768]{1,0:T(8,128)}, bf16[4,256,768]{2,1,0:T(8,128)(2,1)}, bf16[4,256,576]{2,1,0:T(8,128)(2,1)}) custom-call(bf16[4,2,256,768]{3,2,1,0:T(8,128)(2,1)} %bitcast.120, f32[256,768]{1,0:T(8,128)} %get-tuple-element.97.base_ref.middle_ref, f32[1,768]{1,0:T(1,128)} %get-tuple-element.168.gain_ref, bf16[768,576]{1,0:T(8,128)(2,1)} %bitcast.114), custom_call_target="tpu_custom_call" | custom-call | bytes 96000000 | tf_op jit(solution)/shard_map/sum_project/pallas_call | solution.py:549
  192.4 21.9 %attend_gather.1 = (bf16[1024,192]{1,0:T(8,128)(2,1)}, f32[3,1024,1]{2,1,0:T(8,128)}, bf16[4,2,256,768]{3,2,1,0:T(8,128)(2,1)}) custom-call(bf16[1024,576]{1,0:T(8,128)(2,1)} %bitcast.106, s32[1,1024]{1,0:T(1,128)} %refs_1_.7, s32[1024,1]{1,0:T(8,128)} %copy.73.refs_2_, f32[3,640]{1,0:T(4,128)} %get-tuple-element.161.refs_3_, f32[256,768]{1,0:T(8,128)} %bitcast.121), custom_call_target="tpu_custom_call" | custom-call | bytes 54000000 | tf_op jit(solution)/shard_map/attend_gather/pallas_call | solution.py:549
  214.4 27.6 %merge.1 = (bf16[4,256,192]{2,1,0:T(8,128)(2,1)}, f32[256,768]{1,0:T(8,128)}, bf16[4,2,256,768]{3,2,1,0:T(8,128)(2,1)}) custom-call(bf16[4,256,192]{2,1,0:T(8,128)(2,1)} %bitcast.141, f32[256,768]{1,0:T(8,128)} %get-tuple-element.103.base_ref.x_ref, bf16[4,192,768]{2,1,0:T(8,128)(2,1)} %bitcast.112, f32[1,768]{1,0:T(1,128)} %get-tuple-element.167.gain_ref), custom_call_target="tpu_custom_call" | custom-call | bytes 75000000 | tf_op jit(solution)/shard_map/merge/pallas_call | solution.py:549
  242.0 12.8 %experts.3 = (bf16[4,512,768]{2,1,0:T(8,128)(2,1)}, bf16[4,256,768]{2,1,0:T(8,128)(2,1)}, bf16[4,256,1536]{2,1,0:T(8,128)(2,1)}, f32[4,512,4]{2,1,0:T(8,128)}) custom-call(bf16[4,512,768]{2,1,0:T(8,128)(2,1)} %bitcast.97, s32[4,1,512]{2,1,0:T(1,128)} %get-tuple-element.165.slot_ref, f32[4,512,4]{2,1,0:T(8,128)} %get-tuple-element.156.chosen_ref, ...), custom_call_target="tpu_custom_call" | custom-call | bytes 42000000 | tf_op jit(solution)/shard_map/experts/pallas_call | solution.py:714
  254.8 24.6 %experts_back.1 = (bf16[4,512,768]{2,1,0:T(8,128)(2,1)}, bf16[4,2,192,1536]{3,2,1,0:T(8,128)(2,1)}, f32[4,768]{1,0:T(4,128)}) custom-call(bf16[4,512,768]{2,1,0:T(8,128)(2,1)} %bitcast.124, bf16[4,512,768]{2,1,0:T(8,128)(2,1)} %bitcast.98, s32[4,1,512]{2,1,0:T(1,128)} %get-tuple-element.165.slot_ref, f32[4,512,4]{2,1,0:T(8,128)} %get-tuple-element.106.shares_ref, ...), custom_call_target="tpu_custom_call" | custom-call | bytes 75000000 | tf_op jit(solution)/shard_map/experts_back/pallas_call | solution.py:746
  279.7 32.0 %split.2 = (f32[256,768]{1,0:T(8,128)}, f32[1,768]{1,0:T(1,128)}, bf16[4,256,192]{2,1,0:T(8,128)(2,1)}, bf16[2,4,4,24,768]{4,3,2,1,0:T(8,128)(2,1)}) custom-call(bf16[4,2,256,768]{3,2,1,0:T(8,128)(2,1)} %bitcast.119, f32[256,768]{1,0:T(8,128)} %get-tuple-element.110.middle_ref.refs_8_, f32[1,768]{1,0:T(1,128)} %get-tuple-element.167.gain_ref, ...), custom_call_target="tpu_custom_call" | custom-call | bytes 75000000 | tf_op jit(solution)/shard_map/split/pallas_call | solution.py:549
  311.6 25.1 %attend_back_sum.1 = (bf16[1024,576]{1,0:T(8,128)(2,1)}, f32[3,640]{1,0:T(4,128)}, bf16[2,4,96,576]{3,2,1,0:T(8,128)(2,1)}, f32[256,768]{1,0:T(8,128)}) custom-call(bf16[1024,576]{1,0:T(8,128)(2,1)} %bitcast.107, s32[1,1024]{1,0:T(1,128)} %refs_1_.7, s32[1024,1]{1,0:T(8,128)} %copy.73.refs_2_, f32[3,640]{1,0:T(4,128)} %get-tuple-element.161.refs_3_, ...), custom_call_target="tpu_custom_call" | custom-call | bytes 69000000 | tf_op jit(solution)/shard_map/attend_back_sum/pallas_call | solution.py:549
  336.7 35.8 %input_grad.1 = (f32[256,768]{1,0:T(8,128)}, f32[1,768]{1,0:T(1,128)}, bf16[4,2,256,768]{3,2,1,0:T(8,128)(2,1)}) custom-call(bf16[4,256,576]{2,1,0:T(8,128)(2,1)} %bitcast.132, bf16[768,576]{1,0:T(8,128)(2,1)} %bitcast.115, f32[256,768]{1,0:T(8,128)} %get-tuple-element.103.base_ref.x_ref, f32[1,768]{1,0:T(1,128)} %get-tuple-element.168.gain_ref, ...), custom_call_target="tpu_custom_call" | custom-call | bytes 96000000 | tf_op jit(solution)/shard_map/input_grad/pallas_call | solution.py:549
  372.6 29.7 %experts_back_share.1 = (bf16[4,512,768]{2,1,0:T(8,128)(2,1)}, bf16[4,2,192,1536]{3,2,1,0:T(8,128)(2,1)}, f32[4,768]{1,0:T(4,128)}, bf16[4,192,1536]{2,1,0:T(8,128)(2,1)}) custom-call(bf16[4,512,768]{2,1,0:T(8,128)(2,1)} %bitcast.125, bf16[4,512,768]{2,1,0:T(8,128)(2,1)} %bitcast.96, s32[4,1,512]{2,1,0:T(1,128)} %get-tuple-element.166.slot_ref, ...), custom_call_target="tpu_custom_call" | custom-call | bytes 75000000 | tf_op jit(solution)/shard_map/experts_back_share/pallas_call | solution.py:746
  404.3 31.0 %split.3 = (f32[256,768]{1,0:T(8,128)}, f32[1,768]{1,0:T(1,128)}, bf16[4,256,192]{2,1,0:T(8,128)(2,1)}, bf16[2,4,4,24,768]{4,3,2,1,0:T(8,128)(2,1)}) custom-call(bf16[4,2,256,768]{3,2,1,0:T(8,128)(2,1)} %bitcast.118, f32[256,768]{1,0:T(8,128)} %get-tuple-element.97.base_ref.middle_ref, f32[1,768]{1,0:T(1,128)} %get-tuple-element.169.gain_ref, ...), custom_call_target="tpu_custom_call" | custom-call | bytes 75000000 | tf_op jit(solution)/shard_map/split/pallas_call | solution.py:549
  435.3 26.8 %attend_back_share.1 = (bf16[1024,576]{1,0:T(8,128)(2,1)}, f32[3,640]{1,0:T(4,128)}, bf16[2,4,96,576]{3,2,1,0:T(8,128)(2,1)}, bf16[4,192,1536]{2,1,0:T(8,128)(2,1)}) custom-call(bf16[1024,576]{1,0:T(8,128)(2,1)} %bitcast.105, s32[1,1024]{1,0:T(1,128)} %refs_1_.7, s32[1024,1]{1,0:T(8,128)} %copy.73.refs_2_, f32[3,640]{1,0:T(4,128)} %get-tuple-element.162.refs_3_, ...), custom_call_target="tpu_custom_call" | custom-call | bytes 69000000 | tf_op jit(solution)/shard_map/attend_back_share/pallas_call | solution.py:549
  462.2 19.0 %input_grad_last.1 = (f32[256,768]{1,0:T(8,128)}, f32[1,768]{1,0:T(1,128)}) custom-call(bf16[4,256,576]{2,1,0:T(8,128)(2,1)} %bitcast.133, bf16[768,576]{1,0:T(8,128)(2,1)} %bitcast.117, f32[256,768]{1,0:T(8,128)} %bitcast.103, f32[1,768]{1,0:T(1,128)} %get-tuple-element.170.gain_ref, f32[256,768]{1,0:T(8,128)} %get-tuple-element.130.middle_grad_ref), custom_call_target="tpu_custom_call" | custom-call | bytes 48000000 | tf_op jit(solution)/shard_map/input_grad_last/pallas_call | solution.py:549
  483.2 1.9 reduce-scatter.5.cloned.1.call-done
  485.1 81.7 %finish.1 = (f32[2,192,2304]{2,1,0:T(8,128)}, bf16[2,4,24,768]{3,2,1,0:T(8,128)(2,1)}, bf16[2,4,24,768]{3,2,1,0:T(8,128)(2,1)}, f32[2,4,192]{2,1,0:T(4,128)}, f3...) custom-call(bf16[2,4,96,576]{3,2,1,0:T(8,128)(2,1)} %get-tuple-element.132.refs_0_, ...), custom_call_target="tpu_custom_call" | custom-call | bytes 210000000 | tf_op jit(solution)/shard_map/finish/pallas_call | solution.py:549
  570.8 2.1 maximum_convert_fusion.1
  572.9 6.2 %maximum_convert_fusion = f32[2,4,192,1536]{3,2,1,0:T(8,128)} fusion(bf16[1,4,192,1536]{3,2,1,0:T(8,128)(2,1)S(1)} %bitcast.127, bf16[1,4,192,1536]{3,2,1,0:T(8,128)(2,1)} %bitcast.129), kind=kLoop, calls=%fused_computation.1 | loop fusion | flops 4718592 | bytes 14155776 | tf_op jit(solution)/shard_map/convert_element_type | solution.py:1147
  579.1 4.8 convert_bitcast_fusion
  583.9 0.9 copy.114
  585.7 1.8 copy.116
  (118 shorter events, 18.9 us)
Async XLA Ops:
  7.2 134.3 %all-gather.3.cloned.1.call-start = ((), (), s32[]{:S(2)}) async-start(), calls=%async_computation.2 | async-start | bytes 5898240 | tf_op jit(solution)/shard_map/all_gather | solution.py:1031
  7.2 3.8 copy-start.12
  7.2 3.8 copy-start.13
  11.1 1.5 copy-start.17
  11.1 1.5 copy-start.18
  41.2 0.8 copy-start.8
  41.2 1.0 copy-start.11
  41.2 2.1 copy-start.6
  41.2 3.1 slice-start
  41.2 200.8 %all-gather.5.cloned.1.call-start = ((), (), s32[]{:S(2)}) async-start(), calls=%async_computation.3 | async-start | bytes 5898240 | tf_op jit(solution)/shard_map/all_gather | solution.py:1031
  42.0 330.6 %reduce-scatter.3.cloned.1.call-start = ((), (), s32[]{:S(2)}) async-start(), calls=%async_computation.4 | async-start | bytes 5898240 | tf_op jit(solution)/shard_map/reduce_scatter | solution.py:1085
  65.3 54.4 %copy-start.7 = (s32[4,16,128]{2,1,0:T(8,128)S(1)}, s32[4,16,128]{2,1,0:T(8,128)}, u32[]{:S(2)}) copy-start(s32[4,16,128]{2,1,0:T(8,128)} %get-tuple-element.94) | copy-start | bytes 98308
  279.4 205.7 %reduce-scatter.5.cloned.1.call-start = ((), (), s32[]{:S(2)}) async-start(), calls=%async_computation.5 | async-start | bytes 5898240 | tf_op jit(solution)/shard_map/reduce_scatter | solution.py:1085
  402.3 0.7 copy-start.19
  402.3 1.8 copy-start.9
  402.3 1.8 copy-start.14
  402.3 1.8 copy-start.15
  462.1 19.0 %copy-start.20 = (f32[3,640]{1,0:T(4,128)S(1)}, f32[3,640]{1,0:T(4,128)}, u32[]{:S(2)}) copy-start(f32[3,640]{1,0:T(4,128)} %get-tuple-element.139) | copy-start | bytes 23044
  462.2 19.6 %copy-start.10 = (f32[4,768]{1,0:T(4,128)S(1)}, f32[4,768]{1,0:T(4,128)}, u32[]{:S(2)}) copy-start(f32[4,768]{1,0:T(4,128)} %get-tuple-element.138) | copy-start | bytes 36868
  462.2 19.6 %copy-start.16 = (f32[1,768]{1,0:T(1,128)S(1)}, f32[1,768]{1,0:T(1,128)}, u32[]{:S(2)}) copy-start(f32[1,768]{1,0:T(1,128)} %get-tuple-element.137) | copy-start | bytes 9220
  485.1 87.8 %copy-start.2 = (bf16[4,192,1536]{2,1,0:T(8,128)(2,1)S(1)}, bf16[4,192,1536]{2,1,0:T(8,128)(2,1)}, u32[]{:S(2)}) copy-start(bf16[4,192,1536]{2,1,0:T(8,128)(2,1)} %get-tuple-element.151) | copy-start | bytes 7077892
  572.9 6.2 %copy-start.1 = (bf16[4,192,1536]{2,1,0:T(8,128)(2,1)S(1)}, bf16[4,192,1536]{2,1,0:T(8,128)(2,1)}, u32[]{:S(2)}) copy-start(bf16[4,192,1536]{2,1,0:T(8,128)(2,1)} %get-tuple-element.153) | copy-start | bytes 7077892
  572.9 6.2 %copy-start.3 = (bf16[4,192,1536]{2,1,0:T(8,128)(2,1)S(1)}, bf16[4,192,1536]{2,1,0:T(8,128)(2,1)}, u32[]{:S(2)}) copy-start(bf16[4,192,1536]{2,1,0:T(8,128)(2,1)} %get-tuple-element.152) | copy-start | bytes 7077892
  579.1 4.8 copy-start.4
  579.1 5.7 copy-start.5
  579.1 6.6 %copy-start = (f32[2,192,2304]{2,1,0:T(8,128)S(1)}, f32[2,192,2304]{2,1,0:T(8,128)}, u32[]{:S(2)}) copy-start(f32[2,192,2304]{2,1,0:T(8,128)} %get-tuple-element.186) | copy-start | bytes 10616836
Sparse Core Ops, SparseCore 0:
  41.3 100.0 all-gather.2
  143.6 87.7 all-gather.4
  279.5 83.9 reduce-scatter.2
  402.5 82.6 reduce-scatter.4

commit v7 on v6

--- a/solution.py
+++ b/solution.py
@@ -920,7 +920,7 @@
     me, core, near, far, cross = place
     wires = Wires(*refs)
     greet({"seq": near}, {"seq": far}, {"seq": cross}, {"tensor": 1 - core}, *[{"dp": spot} for spot in line[1]])
-    reduces = [reduce_steps(wires, place, line, True, *one) for one in zip(q_refs, o_refs, o_outs, scratch)]
+    reduces = [reduce_steps(wires, place, line, at > 0, *one) for at, one in enumerate(zip(q_refs, o_refs, o_outs, scratch))]
     smalls = [small_steps(wires, place, line, *one) for one in zip(s_refs, s_outs, small_scratch)]
     for task in reduces + smalls:
         next(task)
@@ -1136,7 +1136,7 @@
         [wide_array(LAYERS, shard, 3 * width)]
         + [low_array(n_tensor, n_seq, out_rows, width)] * LAYERS + [wide_array(n_tensor, n_seq, shard)] * LAYERS
         + [low_array(n_seq, *pair_shards[0].shape[1:])] * 2,
-        reduce_scratch(True) + reduce_scratch(True) + small_scratch * LAYERS,
+        reduce_scratch(False) + reduce_scratch(True) + small_scratch * LAYERS,
         LAYERS * (2 * (n_dp - 1) + 19 + n_dp + 4) + 12, *qkv_grads, *out_grads, *smalls, pair_shards[0]
     )
     out_total = jnp.stack(totals[:LAYERS]).astype(jnp.float32).reshape(LAYERS, shard, width)

time: 600 us -> 597 us (level)
  no operation moved by 1% of the time
where the time goes in v7:
time: 597 us; the launch traced here: 591 us
  Pallas kernels  516 us (86%)
  local copies, waits for them, and re-layouts  26.6 us (4%)
  other arithmetic  17.2 us (3%)
  waiting for transfers between devices  15.9 us (3%)
  between operations  14.5 us (2%)
    pallas_call x14, Pallas kernels, comm_call(): pl.pallas_call(kernel, out_shape=tuple(outs), in_specs=vmem(len(operands)...  435 us
    pallas_call x2, Pallas kernels, run_experts_back(): pl.pallas_call(experts_back_kernel, grid=(groups,), out_shape=tuple(outs)...  54.4 us
    pallas_call x2, Pallas kernels, run_experts(): pl.pallas_call(experts_kernel, grid=(groups,), out_shape=(low_array(group...  26 us
    all_gather x2, waiting for transfers between devices, body(): pair = lax.all_gather(own_pair[layer], 'dp', axis=0)  13.2 us
  transfers between devices with their start and end apart: 4, of which 2 were waited for; matrix products, arithmetic and copies ran while one was open for 3% of the time, Pallas kernels for 58%

profile of v7, /device:TPU:0, one launch (start us, length us, event | category | flops | bytes accessed | tf_op | source)
XLA Modules:
  0.0 590.9 jit_solution(7633869038842162790)
XLA Ops:
  7.2 1.4 dynamic-slice_bitcast_fusion
  8.6 2.4 constant_dynamic-slice_fusion
  11.1 1.5 pad_maximum_fusion
  13.3 26.4 %weights.1 = (bf16[4,16,192]{2,1,0:T(8,128)(2,1)}, bf16[4,2,96,576]{3,2,1,0:T(8,128)(2,1)}, bf16[2,96,576]{2,1,0:T(8,128)(2,1)}, bf16[4,48,384]{2,1,0:T(8,128)(2,1)}, bf16[4,48,384]{2,1,0:T(8,128)(2,1)}) custom-call(bf16[16,192]{1,0:T(8,128)(2,1)} %pad.16.small_ref, bf16[2,192,2304]{2,1,0:T(8,128)(2,1)} %whole_ref.1, bf16[2,4,48,768]{3,2,1,0:T(8,128)(2,1)} %bitcast.138), custom_call_target="tpu_custom_call" | custom-call | bytes 66000000 | tf_op jit(solution)/shard_map/weights/pallas_call | solution.py:549
  39.6 1.6 fusion.13
  43.3 1.0 copy.73.refs_2_
  45.1 19.2 %project.1 = (bf16[4,256,768]{2,1,0:T(8,128)(2,1)}, bf16[4,256,576]{2,1,0:T(8,128)(2,1)}, s32[4,16,128]{2,1,0:T(8,128)}) custom-call(f32[256,768]{1,0:T(8,128)} %bitcast.101, f32[1,768]{1,0:T(1,128)} %get-tuple-element.170.gain_ref, bf16[768,576]{1,0:T(8,128)(2,1)} %bitcast.116, s32[16,128]{1,0:T(8,128)} %reshape.189.routes_ref), custom_call_target="tpu_custom_call" | custom-call | bytes 48000000 | tf_op jit(solution)/shard_map/project/pallas_call | solution.py:549
  65.3 21.6 %attend_fetch.1 = (bf16[1024,192]{1,0:T(8,128)(2,1)}, f32[3,1024,1]{2,1,0:T(8,128)}, bf16[4,4,48,768]{3,2,1,0:T(8,128)(2,1)}, bf16[4,4,48,768]{3,2,1,0:T(8,128)(2,1)}) custom-call(bf16[1024,576]{1,0:T(8,128)(2,1)} %bitcast.104, s32[1,1024]{1,0:T(1,128)} %refs_1_.7, s32[1024,1]{1,0:T(8,128)} %copy.73.refs_2_, f32[3,640]{1,0:T(4,128)} %get-tuple-element.162.refs_3_, ...), custom_call_target="tpu_custom_call" | custom-call | bytes 54000000 | tf_op jit(solution)/shard_map/attend_fetch/pallas_call | solution.py:549
  86.9 32.8 %merge_fetch.1 = (bf16[4,256,192]{2,1,0:T(8,128)(2,1)}, f32[256,768]{1,0:T(8,128)}, bf16[4,2,256,768]{3,2,1,0:T(8,128)(2,1)}, bf16[4,2,96,576]{3,2,1,0:T(8,128)(2,1)}) custom-call(bf16[4,256,192]{2,1,0:T(8,128)(2,1)} %bitcast.140, f32[256,768]{1,0:T(8,128)} %bitcast.102, bf16[4,192,768]{2,1,0:T(8,128)(2,1)} %bitcast.110, ...), custom_call_target="tpu_custom_call" | custom-call | bytes 75000000 | tf_op jit(solution)/shard_map/merge_fetch/pallas_call | solution.py:549
  120.1 1.7 compare_reduce_fusion
  126.8 1.5 slice_bitcast_fusion
  128.3 13.1 %all-gather.3.cloned.1.call-done.pair_ref = bf16[4,2,192,1536]{3,2,1,0:T(8,128)(2,1)} async-done(((bf16[1,2,192,1536]{3,2,1,0:T(8,128)(2,1)}), bf16[4,2,192,1536]{3,2,1,0:T(8,128)(2,1)}) %all-gather.3.cloned.1.call-update) | async-done | bytes 4718608 | tf_op jit(solution)/shard_map/all_gather | solution.py:1031
  141.5 13.2 %experts.2 = (bf16[4,512,768]{2,1,0:T(8,128)(2,1)}, bf16[4,256,768]{2,1,0:T(8,128)(2,1)}, bf16[4,256,1536]{2,1,0:T(8,128)(2,1)}, f32[4,512,4]{2,1,0:T(8,128)}) custom-call(bf16[4,512,768]{2,1,0:T(8,128)(2,1)} %bitcast.95, s32[4,1,512]{2,1,0:T(1,128)} %get-tuple-element.166.slot_ref, f32[4,512,4]{2,1,0:T(8,128)} %get-tuple-element.157.chosen_ref, ...), custom_call_target="tpu_custom_call" | custom-call | bytes 42000000 | tf_op jit(solution)/shard_map/experts/pallas_call | solution.py:714
  154.7 37.7 %sum_project.1 = (f32[256,768]{1,0:T(8,128)}, bf16[4,256,768]{2,1,0:T(8,128)(2,1)}, bf16[4,256,576]{2,1,0:T(8,128)(2,1)}) custom-call(bf16[4,2,256,768]{3,2,1,0:T(8,128)(2,1)} %bitcast.120, f32[256,768]{1,0:T(8,128)} %get-tuple-element.97.base_ref.middle_ref, f32[1,768]{1,0:T(1,128)} %get-tuple-element.168.gain_ref, bf16[768,576]{1,0:T(8,128)(2,1)} %bitcast.114), custom_call_target="tpu_custom_call" | custom-call | bytes 96000000 | tf_op jit(solution)/shard_map/sum_project/pallas_call | solution.py:549
  192.4 21.9 %attend_gather.1 = (bf16[1024,192]{1,0:T(8,128)(2,1)}, f32[3,1024,1]{2,1,0:T(8,128)}, bf16[4,2,256,768]{3,2,1,0:T(8,128)(2,1)}) custom-call(bf16[1024,576]{1,0:T(8,128)(2,1)} %bitcast.106, s32[1,1024]{1,0:T(1,128)} %refs_1_.7, s32[1024,1]{1,0:T(8,128)} %copy.73.refs_2_, f32[3,640]{1,0:T(4,128)} %get-tuple-element.161.refs_3_, f32[256,768]{1,0:T(8,128)} %bitcast.121), custom_call_target="tpu_custom_call" | custom-call | bytes 54000000 | tf_op jit(solution)/shard_map/attend_gather/pallas_call | solution.py:549
  214.4 27.6 %merge.1 = (bf16[4,256,192]{2,1,0:T(8,128)(2,1)}, f32[256,768]{1,0:T(8,128)}, bf16[4,2,256,768]{3,2,1,0:T(8,128)(2,1)}) custom-call(bf16[4,256,192]{2,1,0:T(8,128)(2,1)} %bitcast.141, f32[256,768]{1,0:T(8,128)} %get-tuple-element.103.base_ref.x_ref, bf16[4,192,768]{2,1,0:T(8,128)(2,1)} %bitcast.112, f32[1,768]{1,0:T(1,128)} %get-tuple-element.167.gain_ref), custom_call_target="tpu_custom_call" | custom-call | bytes 75000000 | tf_op jit(solution)/shard_map/merge/pallas_call | solution.py:549
  242.0 12.8 %experts.3 = (bf16[4,512,768]{2,1,0:T(8,128)(2,1)}, bf16[4,256,768]{2,1,0:T(8,128)(2,1)}, bf16[4,256,1536]{2,1,0:T(8,128)(2,1)}, f32[4,512,4]{2,1,0:T(8,128)}) custom-call(bf16[4,512,768]{2,1,0:T(8,128)(2,1)} %bitcast.97, s32[4,1,512]{2,1,0:T(1,128)} %get-tuple-element.165.slot_ref, f32[4,512,4]{2,1,0:T(8,128)} %get-tuple-element.156.chosen_ref, ...), custom_call_target="tpu_custom_call" | custom-call | bytes 42000000 | tf_op jit(solution)/shard_map/experts/pallas_call | solution.py:714
  254.8 24.6 %experts_back.1 = (bf16[4,512,768]{2,1,0:T(8,128)(2,1)}, bf16[4,2,192,1536]{3,2,1,0:T(8,128)(2,1)}, f32[4,768]{1,0:T(4,128)}) custom-call(bf16[4,512,768]{2,1,0:T(8,128)(2,1)} %bitcast.124, bf16[4,512,768]{2,1,0:T(8,128)(2,1)} %bitcast.98, s32[4,1,512]{2,1,0:T(1,128)} %get-tuple-element.165.slot_ref, f32[4,512,4]{2,1,0:T(8,128)} %get-tuple-element.106.shares_ref, ...), custom_call_target="tpu_custom_call" | custom-call | bytes 75000000 | tf_op jit(solution)/shard_map/experts_back/pallas_call | solution.py:746
  279.7 32.0 %split.2 = (f32[256,768]{1,0:T(8,128)}, f32[1,768]{1,0:T(1,128)}, bf16[4,256,192]{2,1,0:T(8,128)(2,1)}, bf16[2,4,4,24,768]{4,3,2,1,0:T(8,128)(2,1)}) custom-call(bf16[4,2,256,768]{3,2,1,0:T(8,128)(2,1)} %bitcast.119, f32[256,768]{1,0:T(8,128)} %get-tuple-element.110.middle_ref.refs_8_, f32[1,768]{1,0:T(1,128)} %get-tuple-element.167.gain_ref, ...), custom_call_target="tpu_custom_call" | custom-call | bytes 75000000 | tf_op jit(solution)/shard_map/split/pallas_call | solution.py:549
  311.6 25.1 %attend_back_sum.1 = (bf16[1024,576]{1,0:T(8,128)(2,1)}, f32[3,640]{1,0:T(4,128)}, bf16[2,4,96,576]{3,2,1,0:T(8,128)(2,1)}, f32[256,768]{1,0:T(8,128)}) custom-call(bf16[1024,576]{1,0:T(8,128)(2,1)} %bitcast.107, s32[1,1024]{1,0:T(1,128)} %refs_1_.7, s32[1024,1]{1,0:T(8,128)} %copy.73.refs_2_, f32[3,640]{1,0:T(4,128)} %get-tuple-element.161.refs_3_, ...), custom_call_target="tpu_custom_call" | custom-call | bytes 69000000 | tf_op jit(solution)/shard_map/attend_back_sum/pallas_call | solution.py:549
  336.7 35.8 %input_grad.1 = (f32[256,768]{1,0:T(8,128)}, f32[1,768]{1,0:T(1,128)}, bf16[4,2,256,768]{3,2,1,0:T(8,128)(2,1)}) custom-call(bf16[4,256,576]{2,1,0:T(8,128)(2,1)} %bitcast.132, bf16[768,576]{1,0:T(8,128)(2,1)} %bitcast.115, f32[256,768]{1,0:T(8,128)} %get-tuple-element.103.base_ref.x_ref, f32[1,768]{1,0:T(1,128)} %get-tuple-element.168.gain_ref, ...), custom_call_target="tpu_custom_call" | custom-call | bytes 96000000 | tf_op jit(solution)/shard_map/input_grad/pallas_call | solution.py:549
  372.6 29.7 %experts_back_share.1 = (bf16[4,512,768]{2,1,0:T(8,128)(2,1)}, bf16[4,2,192,1536]{3,2,1,0:T(8,128)(2,1)}, f32[4,768]{1,0:T(4,128)}, bf16[4,192,1536]{2,1,0:T(8,128)(2,1)}) custom-call(bf16[4,512,768]{2,1,0:T(8,128)(2,1)} %bitcast.125, bf16[4,512,768]{2,1,0:T(8,128)(2,1)} %bitcast.96, s32[4,1,512]{2,1,0:T(1,128)} %get-tuple-element.166.slot_ref, ...), custom_call_target="tpu_custom_call" | custom-call | bytes 75000000 | tf_op jit(solution)/shard_map/experts_back_share/pallas_call | solution.py:746
  404.3 31.0 %split.3 = (f32[256,768]{1,0:T(8,128)}, f32[1,768]{1,0:T(1,128)}, bf16[4,256,192]{2,1,0:T(8,128)(2,1)}, bf16[2,4,4,24,768]{4,3,2,1,0:T(8,128)(2,1)}) custom-call(bf16[4,2,256,768]{3,2,1,0:T(8,128)(2,1)} %bitcast.118, f32[256,768]{1,0:T(8,128)} %get-tuple-element.97.base_ref.middle_ref, f32[1,768]{1,0:T(1,128)} %get-tuple-element.169.gain_ref, ...), custom_call_target="tpu_custom_call" | custom-call | bytes 75000000 | tf_op jit(solution)/shard_map/split/pallas_call | solution.py:549
  435.3 26.8 %attend_back_share.1 = (bf16[1024,576]{1,0:T(8,128)(2,1)}, f32[3,640]{1,0:T(4,128)}, bf16[2,4,96,576]{3,2,1,0:T(8,128)(2,1)}, bf16[4,192,1536]{2,1,0:T(8,128)(2,1)}) custom-call(bf16[1024,576]{1,0:T(8,128)(2,1)} %bitcast.105, s32[1,1024]{1,0:T(1,128)} %refs_1_.7, s32[1024,1]{1,0:T(8,128)} %copy.73.refs_2_, f32[3,640]{1,0:T(4,128)} %get-tuple-element.162.refs_3_, ...), custom_call_target="tpu_custom_call" | custom-call | bytes 69000000 | tf_op jit(solution)/shard_map/attend_back_share/pallas_call | solution.py:549
  462.2 19.0 %input_grad_last.1 = (f32[256,768]{1,0:T(8,128)}, f32[1,768]{1,0:T(1,128)}) custom-call(bf16[4,256,576]{2,1,0:T(8,128)(2,1)} %bitcast.133, bf16[768,576]{1,0:T(8,128)(2,1)} %bitcast.117, f32[256,768]{1,0:T(8,128)} %bitcast.103, f32[1,768]{1,0:T(1,128)} %get-tuple-element.170.gain_ref, f32[256,768]{1,0:T(8,128)} %get-tuple-element.130.middle_grad_ref), custom_call_target="tpu_custom_call" | custom-call | bytes 48000000 | tf_op jit(solution)/shard_map/input_grad_last/pallas_call | solution.py:549
  483.2 1.9 reduce-scatter.5.cloned.1.call-done
  485.1 78.5 %finish.1 = (f32[2,192,2304]{2,1,0:T(8,128)}, bf16[2,4,24,768]{3,2,1,0:T(8,128)(2,1)}, bf16[2,4,24,768]{3,2,1,0:T(8,128)(2,1)}, f32[2,4,192]{2,1,0:T(4,128)}, f3...) custom-call(bf16[2,4,96,576]{3,2,1,0:T(8,128)(2,1)} %get-tuple-element.132.refs_0_, ...), custom_call_target="tpu_custom_call" | custom-call | bytes 210000000 | tf_op jit(solution)/shard_map/finish/pallas_call | solution.py:549
  567.5 2.1 maximum_convert_fusion.1
  569.7 6.2 %maximum_convert_fusion = f32[2,4,192,1536]{3,2,1,0:T(8,128)} fusion(bf16[1,4,192,1536]{3,2,1,0:T(8,128)(2,1)S(1)} %bitcast.127, bf16[1,4,192,1536]{3,2,1,0:T(8,128)(2,1)} %bitcast.129), kind=kLoop, calls=%fused_computation.1 | loop fusion | flops 4718592 | bytes 14155776 | tf_op jit(solution)/shard_map/convert_element_type | solution.py:1147
  575.8 4.8 convert_bitcast_fusion
  581.5 0.9 copy.115
  582.4 1.8 copy.116
  (118 shorter events, 18.9 us)
Async XLA Ops:
  7.2 134.3 %all-gather.3.cloned.1.call-start = ((), (), s32[]{:S(2)}) async-start(), calls=%async_computation.2 | async-start | bytes 5898240 | tf_op jit(solution)/shard_map/all_gather | solution.py:1031
  7.2 3.8 copy-start.12
  7.2 3.8 copy-start.13
  11.1 1.5 copy-start.17
  11.1 1.5 copy-start.18
  41.2 0.8 copy-start.8
  41.2 1.0 copy-start.11
  41.2 2.1 copy-start.6
  41.2 3.1 slice-start
  41.2 200.8 %all-gather.5.cloned.1.call-start = ((), (), s32[]{:S(2)}) async-start(), calls=%async_computation.3 | async-start | bytes 5898240 | tf_op jit(solution)/shard_map/all_gather | solution.py:1031
  42.0 330.6 %reduce-scatter.3.cloned.1.call-start = ((), (), s32[]{:S(2)}) async-start(), calls=%async_computation.4 | async-start | bytes 5898240 | tf_op jit(solution)/shard_map/reduce_scatter | solution.py:1085
  65.3 54.4 %copy-start.7 = (s32[4,16,128]{2,1,0:T(8,128)S(1)}, s32[4,16,128]{2,1,0:T(8,128)}, u32[]{:S(2)}) copy-start(s32[4,16,128]{2,1,0:T(8,128)} %get-tuple-element.94) | copy-start | bytes 98308
  279.4 205.7 %reduce-scatter.5.cloned.1.call-start = ((), (), s32[]{:S(2)}) async-start(), calls=%async_computation.5 | async-start | bytes 5898240 | tf_op jit(solution)/shard_map/reduce_scatter | solution.py:1085
  402.3 0.7 copy-start.19
  402.3 1.8 copy-start.9
  402.3 1.8 copy-start.14
  402.3 1.8 copy-start.15
  462.1 19.0 %copy-start.20 = (f32[3,640]{1,0:T(4,128)S(1)}, f32[3,640]{1,0:T(4,128)}, u32[]{:S(2)}) copy-start(f32[3,640]{1,0:T(4,128)} %get-tuple-element.139) | copy-start | bytes 23044
  462.2 19.6 %copy-start.10 = (f32[4,768]{1,0:T(4,128)S(1)}, f32[4,768]{1,0:T(4,128)}, u32[]{:S(2)}) copy-start(f32[4,768]{1,0:T(4,128)} %get-tuple-element.138) | copy-start | bytes 36868
  462.2 19.6 %copy-start.16 = (f32[1,768]{1,0:T(1,128)S(1)}, f32[1,768]{1,0:T(1,128)}, u32[]{:S(2)}) copy-start(f32[1,768]{1,0:T(1,128)} %get-tuple-element.137) | copy-start | bytes 9220
  485.1 84.5 %copy-start.2 = (bf16[4,192,1536]{2,1,0:T(8,128)(2,1)S(1)}, bf16[4,192,1536]{2,1,0:T(8,128)(2,1)}, u32[]{:S(2)}) copy-start(bf16[4,192,1536]{2,1,0:T(8,128)(2,1)} %get-tuple-element.151) | copy-start | bytes 7077892
  569.6 6.2 %copy-start.1 = (bf16[4,192,1536]{2,1,0:T(8,128)(2,1)S(1)}, bf16[4,192,1536]{2,1,0:T(8,128)(2,1)}, u32[]{:S(2)}) copy-start(bf16[4,192,1536]{2,1,0:T(8,128)(2,1)} %get-tuple-element.153) | copy-start | bytes 7077892
  569.7 6.2 %copy-start.3 = (bf16[4,192,1536]{2,1,0:T(8,128)(2,1)S(1)}, bf16[4,192,1536]{2,1,0:T(8,128)(2,1)}, u32[]{:S(2)}) copy-start(bf16[4,192,1536]{2,1,0:T(8,128)(2,1)} %get-tuple-element.152) | copy-start | bytes 7077892
  575.8 4.8 copy-start.4
  575.8 5.7 copy-start.5
  575.8 6.6 %copy-start = (f32[2,192,2304]{2,1,0:T(8,128)S(1)}, f32[2,192,2304]{2,1,0:T(8,128)}, u32[]{:S(2)}) copy-start(f32[2,192,2304]{2,1,0:T(8,128)} %get-tuple-element.186) | copy-start | bytes 10616836
Sparse Core Ops, SparseCore 0:
  41.3 100.0 all-gather.2
  143.6 87.7 all-gather.4
  279.5 83.9 reduce-scatter.2
  402.5 82.6 reduce-scatter.4
